TPU v7x, 32 devices: a whole 2x2x4 slice. The times are simulated.
32 devices in a mesh: dp: 2 (over core), ctx: 4 (over z), fsdp: 4 (over y, x).
Axes of the slice: x: 2, y: 2, z: 4, core: 2. Of those that a mesh axis runs over, the one named last changes fastest.
Arguments:
- tokens: bfloat16 [2, 2, 1024, 1536], P(None, 'dp', ('ctx', 'fsdp')), may hold values from -6 to 6
- cotangent: bfloat16 [2, 2, 1024, 1536], P(None, 'dp', ('ctx', 'fsdp')), may hold values from -6 to 6
- attn_gain: bfloat16 [1536], P(('dp', 'ctx', 'fsdp')), may hold values from 0.5 to 1.5
- w_qkv: bfloat16 [1536, 3072], P(None, ('dp', 'ctx', 'fsdp')), may hold values from -5 to 5
- w_out: bfloat16 [1536, 1536], P(('dp', 'ctx', 'fsdp')), may hold values from -1.5 to 1.5
- mlp_gain: bfloat16 [1536], P(('dp', 'ctx', 'fsdp')), may hold values from 0.5 to 1.5
- w_gate_up: bfloat16 [1536, 8192], P(None, ('dp', 'ctx', 'fsdp')), may hold values from -0.15625 to 0.15625
- w_down: bfloat16 [4096, 1536], P(('dp', 'ctx', 'fsdp')), may hold values from -0.09375 to 0.09375
Outputs:
- block_out: bfloat16 [2, 2, 1024, 1536], P(None, 'dp', ('ctx', 'fsdp'))
- grad_tokens: bfloat16 [2, 2, 1024, 1536], P(None, 'dp', ('ctx', 'fsdp'))
- grad_attn_gain: float32 [1536], P(('dp', 'ctx', 'fsdp'))
- grad_w_qkv: float32 [1536, 3072], P(None, ('dp', 'ctx', 'fsdp'))
- grad_w_out: float32 [1536, 1536], P(('dp', 'ctx', 'fsdp'))
- grad_mlp_gain: float32 [1536], P(('dp', 'ctx', 'fsdp'))
- grad_w_gate_up: float32 [1536, 8192], P(None, ('dp', 'ctx', 'fsdp'))
- grad_w_down: float32 [4096, 1536], P(('dp', 'ctx', 'fsdp'))
All inputs are finite; a program needn't handle non-finite values.
Results may differ from a plain program's by a relative error of at most 0.02.
Values may be sent and summed in bfloat16 or wider, within the bound.
A program may use at most 320 MiB of HBM per device.

v0:
```python
import jax
import jax.numpy as jnp
from jax import lax
from jax.sharding import PartitionSpec as P

D = 1536
H = 16
KVH = 8
HD = 96
FF = 4096


EPS = 1e-05
THETA = 100000.0
NEG = -1e30


def in_blocks(value, dim, length):
    lengths = value.shape
    pieces = value.reshape(*lengths[:dim], length, lengths[dim] // length, *lengths[dim + 1 :])
    return jnp.moveaxis(pieces, dim, 0)


def sum_at_owner(value, axis, dim):
    pieces = in_blocks(value, dim, lax.axis_size(axis))
    arrived = lax.all_to_all(pieces, axis, split_axis=0, concat_axis=0, tiled=True)
    return arrived.astype(jnp.float32).sum(axis=0)


def side_by_side(arrays, axis, dim, along):
    both = jnp.concatenate(arrays, axis=along)
    whole, at, finished = (sum_at_owner(both, axis, dim), 0, [])
    for a in arrays:
        finished.append(lax.slice_in_dim(whole, at, at + a.shape[along], axis=along))
        at += a.shape[along]
    return tuple(finished)


def rms_norm(values, gain_vec):
    return values * lax.rsqrt(jnp.mean(values * values, axis=-1, keepdims=True) + EPS) * gain_vec


def tables(start, length, width):
    half_width = width // 2
    frequency = THETA ** (-(jnp.arange(half_width, dtype=jnp.float32) * 2.0) / width)
    angles = (start + jnp.arange(length, dtype=jnp.int32)).astype(jnp.float32)[:, None] * frequency[
        None, :
    ]
    return (jnp.cos(angles), jnp.sin(angles))


def rotate(values, cosine, sine_table):
    half_width = values.shape[-1] // 2
    first_half = values[..., :half_width]
    second_half = values[..., half_width:]
    cos_b = cosine[:, None, :]
    sin_b = sine_table[:, None, :]
    return jnp.concatenate(
        [first_half * cos_b - second_half * sin_b, second_half * cos_b + first_half * sin_b],
        axis=-1,
    )


def swiglu(both):
    return jax.nn.silu(both[:, :FF]) * both[:, FF:]


def inner(left, right):
    return lax.dot_general(
        left, right, (((0,), (0,)), ((), ())), preferred_element_type=jnp.float32
    )


def outer(left, right):
    return lax.dot_general(
        left, right, (((1,), (1,)), ((), ())), preferred_element_type=jnp.float32
    )


def unchanged(state):
    return state


def on_device(tokens, cotangent, attn_gain, w_qkv, w_out, mlp_gain, w_gate_up, w_down):
    tok_count = tokens.shape[2]
    groups = H // KVH
    factor = HD ** (-0.5)
    seq_length = tok_count * lax.axis_size(("ctx", "fsdp"))
    pos_first = lax.axis_index(("ctx", "fsdp")) * tok_count
    positions = pos_first + jnp.arange(tok_count, dtype=jnp.int32)
    pos_last = pos_first + tok_count - 1
    cosine, sine_table = tables(pos_first, tok_count, HD)
    sums = [
        jnp.zeros((D,), jnp.float32),
        jnp.zeros((D, (H + 2 * KVH) * HD), jnp.float32),
        jnp.zeros((H * HD, D), jnp.float32),
        jnp.zeros((D,), jnp.float32),
        jnp.zeros((D, 2 * FF), jnp.float32),
        jnp.zeros((FF, D), jnp.float32),
    ]
    outputs = []
    in_grads = []
    whole = (
        lax.all_gather(attn_gain, ("dp", "ctx", "fsdp"), axis=0, tiled=True),
        lax.all_gather(w_qkv, ("dp", "ctx", "fsdp"), axis=1, tiled=True),
        lax.all_gather(w_out, ("dp", "ctx", "fsdp"), axis=0, tiled=True),
        lax.all_gather(mlp_gain, ("dp", "ctx", "fsdp"), axis=0, tiled=True),
        lax.all_gather(w_gate_up, ("dp", "ctx", "fsdp"), axis=1, tiled=True),
        lax.all_gather(w_down, ("dp", "ctx", "fsdp"), axis=0, tiled=True),
    )
    for step_index in range(tokens.shape[0]):
        gain_one, mix_qkv, mix_out, gain_two, mix_gate_up, mix_down = whole
        inputs = tokens[step_index, 0].astype(jnp.float32)
        normed = rms_norm(inputs, gain_one.astype(jnp.float32)).astype(jnp.bfloat16)
        mixed = jnp.dot(normed, mix_qkv, preferred_element_type=jnp.float32)
        queries = rotate(mixed[:, : H * HD].reshape(tok_count, H, HD), cosine, sine_table).astype(
            jnp.bfloat16
        )
        key_rows = rotate(
            mixed[:, H * HD : (H + KVH) * HD].reshape(tok_count, KVH, HD), cosine, sine_table
        )
        key_rows = key_rows.astype(jnp.bfloat16).reshape(tok_count, KVH * HD)
        value_rows = mixed[:, (H + KVH) * HD :].astype(jnp.bfloat16)
        grouped = queries.reshape(tok_count, KVH, groups, HD)
        start_state = (
            jnp.full((KVH, groups, tok_count), NEG, jnp.float32),
            jnp.zeros((KVH, groups, tok_count), jnp.float32),
            jnp.zeros((KVH, groups, tok_count, HD), jnp.float32),
        )
        piece = (
            lax.all_gather(key_rows, ("ctx", "fsdp"), axis=0, tiled=True),
            lax.all_gather(value_rows, ("ctx", "fsdp"), axis=0, tiled=True),
        )

        def work(state):
            best, total, summed = state
            key_count = piece[0].shape[0]
            keys = piece[0].reshape(key_count, KVH, HD)
            values = piece[1].reshape(key_count, KVH, HD)
            scores = (
                jnp.einsum("qkgd,tkd->kgqt", grouped, keys, preferred_element_type=jnp.float32)
                * factor
            )
            allowed = jnp.arange(key_count, dtype=jnp.int32)[None, :] <= positions[:, None]
            scores = jnp.where(allowed, scores, NEG)
            new_best = jnp.maximum(best, jnp.max(scores, axis=-1))
            weights = jnp.where(allowed, jnp.exp(scores - new_best[..., None]), 0.0)
            total = jnp.sum(weights, axis=-1)
            summed = jnp.einsum(
                "kgqt,tkd->kgqd",
                weights.astype(jnp.bfloat16),
                values,
                preferred_element_type=jnp.float32,
            )
            return (new_best, total, summed)

        best, total, summed = lax.cond(jnp.int32(0) <= pos_last, work, unchanged, start_state)
        head_out = summed / total[..., None]
        log_total = best + jnp.log(total)
        attended = (
            jnp.transpose(head_out, (2, 0, 1, 3)).reshape(tok_count, H * HD).astype(jnp.bfloat16)
        )
        resid = inputs + jnp.dot(attended, mix_out, preferred_element_type=jnp.float32)
        normed_two = rms_norm(resid, gain_two.astype(jnp.float32)).astype(jnp.bfloat16)
        both = jnp.dot(normed_two, mix_gate_up, preferred_element_type=jnp.float32)
        acted = swiglu(both).astype(jnp.bfloat16)
        result = resid + jnp.dot(acted, mix_down, preferred_element_type=jnp.float32)
        outputs.append(result.astype(jnp.bfloat16))
        gain_one, mix_qkv, mix_out, gain_two, mix_gate_up, mix_down = whole
        up_low = cotangent[step_index, 0]
        upstream = up_low.astype(jnp.float32)
        sums[5] = sums[5] + inner(acted, up_low)
        d_act = outer(up_low, mix_down)
        _, pull_glu = jax.vjp(swiglu, both)
        d_both = pull_glu(d_act)[0].astype(jnp.bfloat16)
        sums[4] = sums[4] + inner(normed_two, d_both)
        d_normed_two = outer(d_both, mix_gate_up)
        _, pull_two = jax.vjp(rms_norm, resid, gain_two.astype(jnp.float32))
        d_resid_norm, d_gain_two = pull_two(d_normed_two)
        sums[3] = sums[3] + d_gain_two
        d_resid = upstream + d_resid_norm
        d_resid_low = d_resid.astype(jnp.bfloat16)
        sums[2] = sums[2] + inner(attended, d_resid_low)
        d_attended = outer(d_resid_low, mix_out).astype(jnp.bfloat16)
        d_grouped = d_attended.reshape(tok_count, KVH, groups, HD)
        delta = jnp.einsum("qkgd,kgqd->kgq", d_grouped.astype(jnp.float32), head_out)
        zero_q = jnp.zeros((tok_count, KVH, groups, HD), jnp.float32)
        back_state = (
            zero_q,
            jnp.zeros((seq_length, KVH * HD), jnp.float32),
            jnp.zeros((seq_length, KVH * HD), jnp.float32),
        )
        attend_piece = (
            lax.all_gather(key_rows, ("ctx", "fsdp"), axis=0, tiled=True),
            lax.all_gather(value_rows, ("ctx", "fsdp"), axis=0, tiled=True),
        )

        def attend_work(state):
            key_count = attend_piece[0].shape[0]
            keys = attend_piece[0].reshape(key_count, KVH, HD)
            values = attend_piece[1].reshape(key_count, KVH, HD)
            scores = (
                jnp.einsum("qkgd,tkd->kgqt", grouped, keys, preferred_element_type=jnp.float32)
                * factor
            )
            allowed = jnp.arange(key_count, dtype=jnp.int32)[None, :] <= positions[:, None]
            scores = jnp.where(allowed, scores, NEG)
            probs = jnp.where(allowed, jnp.exp(scores - log_total[..., None]), 0.0)
            d_probs = jnp.einsum(
                "qkgd,tkd->kgqt", d_grouped, values, preferred_element_type=jnp.float32
            )
            d_scores = (probs * (d_probs - delta[..., None])).astype(jnp.bfloat16)
            grad_q = jnp.einsum(
                "kgqt,tkd->qkgd", d_scores, keys, preferred_element_type=jnp.float32
            )
            piece_k = (
                jnp.einsum("kgqt,qkgd->tkd", d_scores, grouped, preferred_element_type=jnp.float32)
                * factor
            )
            piece_v = jnp.einsum(
                "kgqt,qkgd->tkd",
                probs.astype(jnp.bfloat16),
                d_grouped,
                preferred_element_type=jnp.float32,
            )
            grad_k = piece_k.reshape(key_count, KVH * HD)
            grad_v = piece_v.reshape(key_count, KVH * HD)
            return (grad_q, grad_k, grad_v)

        back_result = lax.cond(jnp.int32(0) <= pos_last, attend_work, unchanged, back_state)
        grad_q = back_result[0]
        summed_k, summed_v = side_by_side(
            (back_result[1].astype(jnp.bfloat16), back_result[2].astype(jnp.bfloat16)),
            ("ctx", "fsdp"),
            0,
            1,
        )
        d_q_raw = rotate(grad_q.reshape(tok_count, H, HD) * factor, cosine, -sine_table).reshape(
            tok_count, H * HD
        )
        d_k_raw = rotate(summed_k.reshape(tok_count, KVH, HD), cosine, -sine_table).reshape(
            tok_count, KVH * HD
        )
        d_mixed = jnp.concatenate([d_q_raw, d_k_raw, summed_v], axis=1).astype(jnp.bfloat16)
        sums[1] = sums[1] + inner(normed, d_mixed)
        d_normed = outer(d_mixed, mix_qkv)
        _, pull_one = jax.vjp(rms_norm, inputs, gain_one.astype(jnp.float32))
        d_inputs_norm, d_gain_one = pull_one(d_normed)
        sums[0] = sums[0] + d_gain_one
        in_grads.append((d_resid + d_inputs_norm).astype(jnp.bfloat16))
    grad_gain_one, grad_qkv, grad_out, grad_gain_two, grad_gate_up, grad_down = (
        lax.psum_scatter(sums[0], ("dp", "ctx", "fsdp"), scatter_dimension=0, tiled=True),
        lax.psum_scatter(sums[1], ("dp", "ctx", "fsdp"), scatter_dimension=1, tiled=True),
        lax.psum_scatter(sums[2], ("dp", "ctx", "fsdp"), scatter_dimension=0, tiled=True),
        lax.psum_scatter(sums[3], ("dp", "ctx", "fsdp"), scatter_dimension=0, tiled=True),
        lax.psum_scatter(sums[4], ("dp", "ctx", "fsdp"), scatter_dimension=1, tiled=True),
        lax.psum_scatter(sums[5], ("dp", "ctx", "fsdp"), scatter_dimension=0, tiled=True),
    )
    block_out = jnp.stack(outputs)[:, None]
    grad_tokens = jnp.stack(in_grads)[:, None]
    return (
        block_out,
        grad_tokens,
        grad_gain_one,
        grad_qkv,
        grad_out,
        grad_gain_two,
        grad_gate_up,
        grad_down,
    )


def solution(mesh):
    placed = (
        P(None, "dp", ("ctx", "fsdp"), None),
        P(None, "dp", ("ctx", "fsdp"), None),
        P(("dp", "ctx", "fsdp")),
        P(None, ("dp", "ctx", "fsdp")),
        P(("dp", "ctx", "fsdp"), None),
        P(("dp", "ctx", "fsdp")),
        P(None, ("dp", "ctx", "fsdp")),
        P(("dp", "ctx", "fsdp"), None),
    )
    return jax.shard_map(
        on_device,
        mesh=mesh,
        in_specs=placed,
        out_specs=(
            P(None, "dp", ("ctx", "fsdp"), None),
            P(None, "dp", ("ctx", "fsdp"), None),
            P(("dp", "ctx", "fsdp")),
            P(None, ("dp", "ctx", "fsdp")),
            P(("dp", "ctx", "fsdp"), None),
            P(("dp", "ctx", "fsdp")),
            P(None, ("dp", "ctx", "fsdp")),
            P(("dp", "ctx", "fsdp"), None),
        ),
        check_vma=False,
    )
```

profile of v0, /device:TPU:13, one launch (start us, length us, event | category | flops | bytes accessed | tf_op | source)
XLA Modules:
  0.0 1849.3 jit_solution(17228387076068626405)
XLA Ops:
  9.7 40.8 %all-reduce.9 = (bf16[1536]{0:T(1024)(128)(2,1)S(1)}, bf16[1536]{0:T(1024)(128)(2,1)S(1)}) all-reduce(bf16[1536]{0:T(1024)(128)(2,1)S(1)} %dynamic-update-slice, bf16[1536]{0:T(1024)(128)(2,1)S(1)} %dynamic-update-slice.1), channel_id=1, replica_groups=mesh['dp'=2,'ctx'=4,'fsdp'=4] {'dp','ctx','fsdp'}, use_global_device_ids=true, to_apply=%add.4 | all-reduce | flops 3072 | bytes 12288
  51.7 42.8 %all-gather.9.cloned.1.call-done = bf16[1536,3072]{0,1:T(8,128)(2,1)} async-done(((bf16[1536,96]{0,1:T(8,128)(2,1)}), bf16[1536,3072]{0,1:T(8,128)(2,1)}) %all-gather.9.cloned.1.call-update) | async-done | bytes 9437200 | tf_op jit(solution)/shard_map/all_gather | solution.py:105
  116.8 39.7 %all-gather.23.cloned.1.call-done = bf16[1024,768]{1,0:T(8,128)(2,1)} async-done(((bf16[64,768]{1,0:T(8,128)(2,1)}), bf16[1024,768]{1,0:T(8,128)(2,1)}) %all-gather.23.cloned.1.call-update) | async-done | bytes 1572880 | tf_op jit(solution)/shard_map/all_gather | solution.py:132
  156.5 60.1 %all-gather.21.cloned.1.call-done = bf16[1024,768]{1,0:T(8,128)(2,1)} async-done(((bf16[64,768]{1,0:T(8,128)(2,1)}), bf16[1024,768]{1,0:T(8,128)(2,1)}) %all-gather.21.cloned.1.call-update) | async-done | bytes 1572880 | tf_op jit(solution)/shard_map/all_gather | solution.py:131
  216.5 12.8 conditional.5
  232.3 43.6 %all-gather.13.cloned.1.call-done = bf16[1024,768]{1,0:T(8,128)(2,1)} async-done(((bf16[64,768]{1,0:T(8,128)(2,1)}), bf16[1024,768]{1,0:T(8,128)(2,1)}) %all-gather.13.cloned.1.call-update) | async-done | bytes 1572880 | tf_op jit(solution)/shard_map/all_gather | solution.py:132
  275.8 59.9 %all-gather.11.cloned.1.call-done = bf16[1024,768]{1,0:T(8,128)(2,1)} async-done(((bf16[64,768]{1,0:T(8,128)(2,1)}), bf16[1024,768]{1,0:T(8,128)(2,1)}) %all-gather.11.cloned.1.call-update) | async-done | bytes 1572880 | tf_op jit(solution)/shard_map/all_gather | solution.py:131
  335.7 12.7 conditional.4
  350.7 52.2 %all-gather.15.cloned.1.call-done = bf16[1536,1536]{1,0:T(8,128)(2,1)} async-done(((bf16[48,1536]{1,0:T(8,128)(2,1)}), bf16[1536,1536]{1,0:T(8,128)(2,1)}) %all-gather.15.cloned.1.call-update) | async-done | bytes 4718608 | tf_op jit(solution)/shard_map/all_gather | solution.py:106
  407.9 149.9 %all-gather.17.cloned.1.call-done = bf16[1536,8192]{1,0:T(8,128)(2,1)} async-done(((bf16[1536,256]{1,0:T(8,128)(2,1)}), bf16[1536,8192]{1,0:T(8,128)(2,1)}) %all-gather.17.cloned.1.call-update) | async-done | bytes 25165840 | tf_op jit(solution)/shard_map/all_gather | solution.py:108
  557.8 12.0 fusion.136
  569.8 11.9 fusion.137
  581.7 72.9 %all-gather.19.cloned.1.call-done = bf16[4096,1536]{1,0:T(8,128)(2,1)} async-done(((bf16[128,1536]{1,0:T(8,128)(2,1)}), bf16[4096,1536]{1,0:T(8,128)(2,1)}) %all-gather.19.cloned.1.call-update) | async-done | bytes 12582928 | tf_op jit(solution)/shard_map/all_gather | solution.py:109
  654.7 10.7 fusion.109
  672.4 13.2 fusion.104
  685.7 14.4 multiply_reduce_fusion.1
  710.8 18.6 %conditional.7 = (f32[64,16,96]{2,0,1:T(8,128)}, bf16[1024,768]{1,0:T(8,128)(2,1)}, bf16[1024,768]{1,0:T(8,128)(2,1)S(1)}) conditional(s32[]{:T(128)} %convert_element_type.201, () %tuple.65, (s32[64]{0:T(128)S(1)}, bf16[1024,768]{1,0:T(8,128)(2,1)}, bf16[64,8,2,96]{3,0,2,1:T(8,128)(2,1)}, f32[8,2,64]{2,1,0:T(2,128)}, f32[8,2,64]{2,1,0:T(2,128)S(1)}, ...), branch_computations={%region_18.19_spmd, %region_19.20_spmd} | conditional | flops 1021837312 | bytes 48853360 | solution.py:230
  752.2 17.8 conditional.6
  773.5 54.5 %all-to-all-done.1 = bf16[16,64,1536]{2,1,0:T(8,128)(2,1)} async-done(((bf16[16,64,1536]{2,1,0:T(8,128)(2,1)}), bf16[16,64,1536]{2,1,0:T(8,128)(2,1)}, u32[]{:S(2)}, u32[]{:S(2)}) %all-to-all-start.1) | async-done | bytes 3145760 | tf_op jit(solution)/shard_map/all_to_all | solution.py:26
  827.9 9.3 all-to-all-start
  846.2 78.9 %all-to-all-done = bf16[16,64,1536]{2,1,0:T(8,128)(2,1)} async-done(((bf16[16,64,1536]{2,1,0:T(8,128)(2,1)}), bf16[16,64,1536]{2,1,0:T(8,128)(2,1)}, u32[]{:S(2)}, u32[]{:S(2)}) %all-to-all-start) | async-done | bytes 3145760 | tf_op jit(solution)/shard_map/all_to_all | solution.py:26
  932.4 9.0 fusion.100
  941.4 12.0 convolution_add_fusion.2
  954.5 12.5 fusion.95
  967.0 21.0 %convolution_add_fusion.1 = f32[4096,1536]{1,0:T(8,128)} fusion(f32[4096,1536]{1,0:T(8,128)} %fusion.95, bf16[64,4096]{1,0:T(8,128)(2,1)S(1)} %copy-done.6, bf16[2,1,64,1536]{3,2,1,0:T(8,128)(2,1)S(1)} %copy-done.21), kind=kOutput, calls=%fused_computation.75 | convolution fusion | flops 811597824 | bytes 51052544 | tf_op jit(solution)/shard_map/dot_general | solution.py:69
  988.4 22.9 %fusion.102 = f32[1536,8192]{1,0:T(8,128)} fusion(f32[64,4096]{1,0:T(8,128)} %get-tuple-element.253, f32[64,4096]{1,0:T(8,128)S(1)} %copy-done.7, f32[64,1536]{1,0:T(8,128)S(1)} %copy-done.3, f32[1536]{0:T(1024)S(1)} %convert_element_type.209, f32[64]{0:T(128)S(1)} %copy-done.48), kind=kOutput, calls=%fused_computation.192 | convolution fusion | flops 1611956224 | bytes 52828416 | tf_op jit(solution)/shard_map/dot_general | solution.py:69
  1011.3 34.5 %convolution_add_fusion = f32[1536,8192]{1,0:T(8,128)} fusion(f32[1536,8192]{1,0:T(8,128)} %fusion.102, f32[64,4096]{1,0:T(8,128)} %get-tuple-element.255, f32[64,4096]{1,0:T(8,128)} %get-tuple-element.254, f32[64,1536]{1,0:T(8,128)S(1)} %get-tuple-element.296, f32[64]{0:T(128)S(1)} %copy-done.46, f32[1536]{0:T(1024)S(1)} %convert_element_type.209), kind=kOutput, calls=%fused_computation.74 | convolution fusion | flops 1624539136 | bytes 103160064 | tf_op jit(solution)/shard_map/dot_general | solution.py:69
  1053.6 7.1 fusion.64
  1065.3 41.5 %all-reduce.8 = (f32[1536]{0:T(1024)S(1)}, f32[1536]{0:T(1024)S(1)}) all-reduce(f32[1536]{0:T(1024)S(1)} %add.192, f32[1536]{0:T(1024)S(1)} %add.195), channel_id=2, replica_groups=mesh['dp'=2,'ctx'=4,'fsdp'=4] {'dp','ctx','fsdp'}, use_global_device_ids=true, to_apply=%region_24.25.clone | all-reduce | flops 3072 | bytes 24576
  1109.1 49.2 %reduce-scatter.5.cloned.1.call-done = f32[1536,96]{0,1:T(8,128)} async-done(((f32[1536,3072]{0,1:T(8,128)}), f32[1536,96]{0,1:T(8,128)}) %reduce-scatter.5.cloned.1.call-update) | async-done | bytes 589840 | tf_op jit(solution)/shard_map/reduce_scatter | solution.py:253
  1158.3 250.4 %reduce-scatter.11.cloned.1.call-done = f32[128,1536]{1,0:T(8,128)} async-done(((f32[4096,1536]{1,0:T(8,128)}), f32[128,1536]{1,0:T(8,128)}) %reduce-scatter.11.cloned.1.call-update) | async-done | bytes 786448 | tf_op jit(solution)/shard_map/reduce_scatter | solution.py:257
  1408.7 433.3 %reduce-scatter.9.cloned.1.call-done = f32[1536,256]{1,0:T(8,128)} async-done(((f32[1536,8192]{1,0:T(8,128)}), f32[1536,256]{1,0:T(8,128)}) %reduce-scatter.9.cloned.1.call-update) | async-done | bytes 1572880 | tf_op jit(solution)/shard_map/reduce_scatter | solution.py:256
  (291 shorter events, 173.3 us)
Async XLA Ops:
  7.2 87.3 %all-gather.9.cloned.1.call-start = ((), (), s32[]{:S(2)}) async-start(), calls=%async_computation.6 | async-start | bytes 9732096 | tf_op jit(solution)/shard_map/all_gather | solution.py:105
  7.9 148.6 %all-gather.23.cloned.1.call-start = ((), (), s32[]{:S(2)}) async-start(), calls=%async_computation.13 | async-start | bytes 1671168 | tf_op jit(solution)/shard_map/all_gather | solution.py:132
  51.6 49.6 %copy-start.57 = (f32[64]{0:T(128)}, f32[64]{0:T(128)S(1)}, u32[]{:S(2)}) copy-start(f32[64]{0:T(128)S(1)} %get-tuple-element.239) | copy-start | bytes 772
  51.6 50.4 %copy-start.55 = (f32[64]{0:T(128)}, f32[64]{0:T(128)S(1)}, u32[]{:S(2)}) copy-start(f32[64]{0:T(128)S(1)} %get-tuple-element.238) | copy-start | bytes 772
  51.7 49.6 %copy-start.51 = (f32[64]{0:T(128)}, f32[64]{0:T(128)S(1)}, u32[]{:S(2)}) copy-start(f32[64]{0:T(128)S(1)} %fusion.125) | copy-start | bytes 772
  51.7 50.7 %copy-start.4 = (bf16[2,1,64,1536]{3,2,1,0:T(8,128)(2,1)S(1)}, bf16[2,1,64,1536]{3,2,1,0:T(8,128)(2,1)}, u32[]{:S(2)}) copy-start(bf16[2,1,64,1536]{3,2,1,0:T(8,128)(2,1)} %param.16) | copy-start | bytes 1179652
  101.9 114.6 %all-gather.21.cloned.1.call-start = ((), (), s32[]{:S(2)}) async-start(), calls=%async_computation.12 | async-start | bytes 1671168 | tf_op jit(solution)/shard_map/all_gather | solution.py:131
  110.4 165.4 %all-gather.13.cloned.1.call-start = ((), (), s32[]{:S(2)}) async-start(), calls=%async_computation.8 | async-start | bytes 1671168 | tf_op jit(solution)/shard_map/all_gather | solution.py:132
  111.1 224.6 %all-gather.11.cloned.1.call-start = ((), (), s32[]{:S(2)}) async-start(), calls=%async_computation.7 | async-start | bytes 1671168 | tf_op jit(solution)/shard_map/all_gather | solution.py:131
  112.1 290.8 %all-gather.15.cloned.1.call-start = ((), (), s32[]{:S(2)}) async-start(), calls=%async_computation.9 | async-start | bytes 4866048 | tf_op jit(solution)/shard_map/all_gather | solution.py:106
  112.7 445.1 %all-gather.17.cloned.1.call-start = ((), (), s32[]{:S(2)}) async-start(), calls=%async_computation.10 | async-start | bytes 25952256 | tf_op jit(solution)/shard_map/all_gather | solution.py:108
  113.4 541.2 %all-gather.19.cloned.1.call-start = ((), (), s32[]{:S(2)}) async-start(), calls=%async_computation.11 | async-start | bytes 12976128 | tf_op jit(solution)/shard_map/all_gather | solution.py:109
  114.2 221.5 %copy-start.53 = (s32[64]{0:T(128)}, s32[64]{0:T(128)S(1)}, u32[]{:S(2)}) copy-start(s32[64]{0:T(128)S(1)} %iota_add_fusion) | copy-start | bytes 772
  115.9 219.8 %copy-start.19 = (bf16[64,8,2,96]{3,0,2,1:T(8,128)(2,1)}, bf16[64,8,2,96]{3,0,2,1:T(8,128)(2,1)S(1)}, u32[]{:S(2)}) copy-start(bf16[64,8,2,96]{3,0,2,1:T(8,128)(2,1)S(1)} %pad_maximum_fusion.4) | copy-start | bytes 589828
  350.7 57.1 %copy-start.23 = (bf16[64,1536]{1,0:T(8,128)(2,1)}, bf16[64,1536]{1,0:T(8,128)(2,1)S(1)}, u32[]{:S(2)}) copy-start(bf16[64,1536]{1,0:T(8,128)(2,1)S(1)} %convert_element_type.208) | copy-start | bytes 589828
  406.5 163.2 %copy-start.59 = (f32[64]{0:T(128)}, f32[64]{0:T(128)S(1)}, u32[]{:S(2)}) copy-start(f32[64]{0:T(128)S(1)} %get-tuple-element.295) | copy-start | bytes 772
  406.8 163.0 %copy-start.45 = (f32[64]{0:T(128)}, f32[64]{0:T(128)S(1)}, u32[]{:S(2)}) copy-start(f32[64]{0:T(128)S(1)} %fusion.126) | copy-start | bytes 772
  407.8 162.0 %copy-start.2 = (f32[64,1536]{1,0:T(8,128)}, f32[64,1536]{1,0:T(8,128)S(1)}, u32[]{:S(2)}) copy-start(f32[64,1536]{1,0:T(8,128)S(1)} %get-tuple-element.298) | copy-start | bytes 1179652
  407.8 162.0 %copy-start.61 = (f32[64]{0:T(128)}, f32[64]{0:T(128)S(1)}, u32[]{:S(2)}) copy-start(f32[64]{0:T(128)S(1)} %get-tuple-element.297) | copy-start | bytes 772
  407.9 161.9 %copy-start.47 = (f32[64]{0:T(128)}, f32[64]{0:T(128)S(1)}, u32[]{:S(2)}) copy-start(f32[64]{0:T(128)S(1)} %fusion.124) | copy-start | bytes 772
  732.7 95.2 %all-to-all-start.1 = ((bf16[16,64,1536]{2,1,0:T(8,128)(2,1)}), bf16[16,64,1536]{2,1,0:T(8,128)(2,1)}, u32[]{:S(2)}, u32[]{:S(2)}) async-start(bf16[16,64,1536]{2,1,0:T(8,128)(2,1)} %bitcast.254), calls=%async_computation.1 | async-start | bytes 6291456 | tf_op jit(solution)/shard_map/all_to_all | solution.py:26
  737.6 371.5 %reduce-scatter.7.cloned.1.call-start = ((), (), s32[]{:S(2)}) async-start(), calls=%async_computation.15 | async-start | bytes 9732096 | tf_op jit(solution)/shard_map/reduce_scatter | solution.py:254
  827.9 97.2 %all-to-all-start = ((bf16[16,64,1536]{2,1,0:T(8,128)(2,1)}), bf16[16,64,1536]{2,1,0:T(8,128)(2,1)}, u32[]{:S(2)}, u32[]{:S(2)}) async-start(bf16[16,64,1536]{2,1,0:T(8,128)(2,1)} %bitcast.255), calls=%async_computation | async-start | bytes 6291456 | tf_op jit(solution)/shard_map/all_to_all | solution.py:26
  837.2 321.1 %reduce-scatter.5.cloned.1.call-start = ((), (), s32[]{:S(2)}) async-start(), calls=%async_computation.14 | async-start | bytes 19464192 | tf_op jit(solution)/shard_map/reduce_scatter | solution.py:253
  841.4 91.0 %copy-start.25 = (bf16[64,1536]{1,0:T(8,128)(2,1)}, bf16[64,1536]{1,0:T(8,128)(2,1)S(1)}, u32[]{:S(2)}) copy-start(bf16[64,1536]{1,0:T(8,128)(2,1)S(1)} %reshape.313) | copy-start | bytes 589828
  843.0 98.4 %copy-start.28 = (bf16[64,1536]{1,0:T(8,128)(2,1)}, bf16[64,1536]{1,0:T(8,128)(2,1)S(1)}, u32[]{:S(2)}) copy-start(bf16[64,1536]{1,0:T(8,128)(2,1)S(1)} %reshape.318) | copy-start | bytes 589828
  846.2 86.2 %copy-start.5 = (bf16[2,1,64,1536]{3,2,1,0:T(8,128)(2,1)S(1)}, bf16[2,1,64,1536]{3,2,1,0:T(8,128)(2,1)}, u32[]{:S(2)}) copy-start(bf16[2,1,64,1536]{3,2,1,0:T(8,128)(2,1)} %param.16) | copy-start | bytes 1179652
  846.2 86.2 %copy-start.50 = (f32[64]{0:T(128)S(1)}, f32[64]{0:T(128)}, u32[]{:S(2)}) copy-start(f32[64]{0:T(128)} %copy-done.49) | copy-start | bytes 772
  953.5 455.2 %reduce-scatter.11.cloned.1.call-start = ((), (), s32[]{:S(2)}) async-start(), calls=%async_computation.17 | async-start | bytes 25952256 | tf_op jit(solution)/shard_map/reduce_scatter | solution.py:257
  988.1 853.9 %reduce-scatter.9.cloned.1.call-start = ((), (), s32[]{:S(2)}) async-start(), calls=%async_computation.16 | async-start | bytes 51904512 | tf_op jit(solution)/shard_map/reduce_scatter | solution.py:256
  1063.3 44.7 %copy-start.56 = (f32[64]{0:T(128)S(1)}, f32[64]{0:T(128)}, u32[]{:S(2)}) copy-start(f32[64]{0:T(128)} %copy-done.55) | copy-start | bytes 772
  1063.4 44.7 %copy-start.15 = (f32[64,1536]{1,0:T(8,128)S(1)}, f32[64,1536]{1,0:T(8,128)}, u32[]{:S(2)}) copy-start(f32[64,1536]{1,0:T(8,128)} %get-tuple-element.272) | copy-start | bytes 1179652
  (48 other events, 402.5 us)
Sparse Core Ops, SparseCore 0:
  10.9 83.5 all-gather.8
  102.1 54.3 all-gather.22
  159.8 56.6 all-gather.20
  219.1 56.6 all-gather.12
  279.0 56.6 all-gather.10
  338.5 64.3 all-gather.14
  404.4 153.3 all-gather.16
  560.7 93.9 all-gather.18
  744.9 181.9 reduce-scatter.6
  953.6 204.6 reduce-scatter.4
  1165.3 243.3 reduce-scatter.10
  1415.6 426.3 reduce-scatter.8
where the time goes:
time: 1860 us; the launch traced here: 1850 us
  waiting for transfers between devices  1390 us (75%)
  matrix products  259 us (14%)
  blocking collectives  82.3 us (4%)
  other arithmetic  43.9 us (2%)
  local copies, waits for them, and re-layouts  43 us (2%)
    reduce_scatter x1, waiting for transfers between devices, on_device(): lax.psum_scatter(sums[4], ('dp', 'ctx', 'fsdp'), scatter_dimension=1, til...  433 us
    reduce_scatter x1, waiting for transfers between devices, on_device(): lax.psum_scatter(sums[5], ('dp', 'ctx', 'fsdp'), scatter_dimension=0, til...  250 us
    all_gather x1, waiting for transfers between devices, on_device(): lax.all_gather(w_gate_up, ('dp', 'ctx', 'fsdp'), axis=1, tiled=True)  150 us
    all_to_all x2, waiting for transfers between devices, sum_at_owner(): lax.all_to_all(pieces, axis, split_axis=0, concat_axis=0, tiled=True)  133 us
    all_gather x2, waiting for transfers between devices, on_device(): lax.all_gather(key_rows, ('ctx', 'fsdp'), axis=0, tiled=True)  120 us
    dot_general x8, matrix products, inner(): lax.dot_general(left, right, (((0,), (0,)), ((), ())), preferred_element_...  118 us
    all_gather x2, waiting for transfers between devices, on_device(): lax.all_gather(value_rows, ('ctx', 'fsdp'), axis=0, tiled=True)  83.2 us
    unnamed x2, blocking collectives  82.3 us
  transfers between devices with their start and end apart: 14, of which 13 were waited for; matrix products, arithmetic and copies ran while one was open for 14% of the time, Pallas kernels for 0%

commit v1 on v0

--- a/solution.py
+++ b/solution.py
@@ -81,7 +81,7 @@
     return state
 
 
-def on_device(tokens, cotangent, attn_gain, w_qkv, w_out, mlp_gain, w_gate_up, w_down):
+def on_device_gathered(tokens, cotangent, attn_gain, w_qkv, w_out, mlp_gain, w_gate_up, w_down):
     tok_count = tokens.shape[2]
     groups = H // KVH
     factor = HD ** (-0.5)
@@ -270,6 +270,208 @@
     )
 
 
+TP = ("dp", "ctx")
+ALL = ("dp", "ctx", "fsdp")
+
+
+def dot(left, right):
+    return jnp.dot(left, right, preferred_element_type=jnp.float32)
+
+
+def qkv_owner(sizes):
+    moves = []
+    for head in range(H + 2 * KVH):
+        if head < H:
+            group, slot = head // 2, head % 2
+        elif head < H + KVH:
+            group, slot = head - H, 2
+        else:
+            group, slot = head - H - KVH, 3
+        moves.append((head, group * sizes["fsdp"] + slot))
+    return moves
+
+
+def hidden_of(device, sizes):
+    ctx = sizes["ctx"]
+    return (device % ctx) * sizes["dp"] + device // ctx
+
+
+def down_owner(sizes):
+    n, f = sizes["dp"] * sizes["ctx"], sizes["fsdp"]
+    return [
+        (hidden_of(device, sizes) * f + slot, device * f + slot)
+        for device in range(n)
+        for slot in range(f)
+    ]
+
+
+def up_owner(sizes):
+    n, f = sizes["dp"] * sizes["ctx"], sizes["fsdp"]
+    half = n * f // 2
+    moves = []
+    for device in range(n):
+        first = hidden_of(device, sizes) * (f // 2)
+        for slot in range(f):
+            source = first + slot if slot < f // 2 else half + first + slot - f // 2
+            moves.append((source, device * f + slot))
+    return moves
+
+
+def back(moves):
+    return [(to, source) for source, to in moves]
+
+
+def gather_tp(value):
+    return lax.all_gather(value, TP, axis=0, tiled=True)
+
+
+def sum_tp(value):
+    return lax.psum_scatter(value.astype(jnp.bfloat16), TP, scatter_dimension=0, tiled=True).astype(
+        jnp.float32
+    )
+
+
+def norm_back(values, scale, gain, incoming):
+    weighted = incoming * gain
+    mean = jnp.mean(weighted * values, axis=-1, keepdims=True)
+    return scale * weighted - values * (scale * scale * scale) * mean
+
+
+def on_device(tokens, cotangent, attn_gain, w_qkv, w_out, mlp_gain, w_gate_up, w_down):
+    sizes = {name: lax.axis_size(name) for name in ALL}
+    dp, ctx, fs = sizes["dp"], sizes["ctx"], sizes["fsdp"]
+    mb, _, span, _ = tokens.shape
+    rows = mb * span
+    f_index = lax.axis_index("fsdp")
+    length = span * ctx * fs
+    factor = HD ** (-0.5)
+    hidden = FF // (dp * ctx)
+
+    gains = lax.all_gather(jnp.stack([attn_gain, mlp_gain]), ALL, axis=1, tiled=True)
+    gain_one = gains[0].astype(jnp.float32)
+    gain_two = gains[1].astype(jnp.float32)
+    qkv = lax.all_gather(lax.ppermute(w_qkv, ALL, qkv_owner(sizes)), "fsdp", axis=0)
+    out_w = lax.all_gather(w_out, "fsdp", axis=0, tiled=True)
+    gate_up = lax.all_gather(lax.ppermute(w_gate_up, ALL, up_owner(sizes)), "fsdp", axis=1, tiled=True)
+    down = lax.all_gather(lax.ppermute(w_down, ALL, down_owner(sizes)), "fsdp", axis=0, tiled=True)
+
+    x = tokens.reshape(rows, D).astype(jnp.float32)
+    dy = cotangent.reshape(rows, D)
+    scale_one = lax.rsqrt(jnp.mean(x * x, axis=-1, keepdims=True) + EPS)
+    normed = gather_tp((x * scale_one * gain_one).astype(jnp.bfloat16))
+    dy_all = gather_tp(dy)
+
+    heads = jnp.stack([dot(normed, qkv[h]) for h in range(4)])
+    positions = (
+        (jnp.arange(ctx, dtype=jnp.int32)[:, None] * fs + f_index) * span
+        + jnp.arange(span, dtype=jnp.int32)[None, :]
+    )
+    frequency = THETA ** (-(jnp.arange(HD // 2, dtype=jnp.float32) * 2.0) / HD)
+    angles = positions.astype(jnp.float32)[:, :, None] * frequency
+    cosine = jnp.cos(angles)[None, None, :, None]
+    sine = jnp.sin(angles)[None, None, :, None]
+
+    def turn(values, sin_b):
+        a, b = values[..., : HD // 2], values[..., HD // 2 :]
+        return jnp.concatenate([a * cosine - b * sin_b, b * cosine + a * sin_b], axis=-1)
+
+    heads = heads.reshape(4, dp, ctx, mb, span, HD)
+    turned = turn(heads[:3], sine)
+    heads = jnp.concatenate([turned, heads[3:]]).astype(jnp.bfloat16)
+
+    def to_units(values):
+        count = values.shape[0]
+        values = values.transpose(1, 3, 0, 2, 4, 5)
+        values = values.reshape(dp * mb, count, ctx, span, HD)
+        values = lax.all_to_all(values, "fsdp", split_axis=0, concat_axis=0, tiled=True)
+        return values.transpose(1, 2, 0, 3, 4).reshape(count, length, HD)
+
+    def to_rows(values):
+        count = values.shape[0]
+        values = values.reshape(count, ctx, fs, span, HD).transpose(2, 0, 1, 3, 4)
+        values = lax.all_to_all(values, "fsdp", split_axis=0, concat_axis=0, tiled=True)
+        values = values.reshape(dp, mb, count, ctx, span, HD).transpose(2, 0, 3, 1, 4, 5)
+        return values.reshape(count, dp * ctx * rows, HD)
+
+    unit = to_units(heads)
+    q, k, v = unit[:2], unit[2], unit[3]
+    scores = jnp.einsum("hqd,kd->hqk", q, k, preferred_element_type=jnp.float32) * factor
+    allowed = jnp.arange(length)[None, :] <= jnp.arange(length)[:, None]
+    scores = jnp.where(allowed, scores, NEG)
+    best = jnp.max(scores, axis=-1, keepdims=True)
+    weights = jnp.where(allowed, jnp.exp(scores - best), 0.0)
+    probs = weights / jnp.sum(weights, axis=-1, keepdims=True)
+    probs_low = probs.astype(jnp.bfloat16)
+    att = jnp.einsum("hqk,kd->hqd", probs_low, v, preferred_element_type=jnp.float32)
+    attended = to_rows(att.astype(jnp.bfloat16))
+    out_heads = out_w.reshape(2, HD, D)
+    partial = dot(attended[0], out_heads[0]) + dot(attended[1], out_heads[1])
+    resid = x + sum_tp(partial)
+    scale_two = lax.rsqrt(jnp.mean(resid * resid, axis=-1, keepdims=True) + EPS)
+    normed_two = gather_tp((resid * scale_two * gain_two).astype(jnp.bfloat16))
+    gate = dot(normed_two, gate_up[:, :hidden])
+    up = dot(normed_two, gate_up[:, hidden:])
+    sig = 1.0 / (1.0 + jnp.exp(-gate))
+    silu = gate * sig
+    act = (silu * up).astype(jnp.bfloat16)
+    block_out = (resid + sum_tp(dot(act, down))).astype(jnp.bfloat16)
+
+    grad_down = inner(act, dy_all)
+    d_act = outer(dy_all, down)
+    d_gate = d_act * up * (sig * (1.0 + gate * (1.0 - sig)))
+    d_up = d_act * silu
+    d_both = jnp.concatenate([d_gate, d_up], axis=1).astype(jnp.bfloat16)
+    grad_gate_up = inner(normed_two, d_both)
+    d_two = sum_tp(outer(d_both, gate_up))
+    grad_two = jnp.sum(d_two * resid * scale_two, axis=0)
+    d_resid = dy.astype(jnp.float32) + norm_back(resid, scale_two, gain_two, d_two)
+    d_resid_all = gather_tp(d_resid.astype(jnp.bfloat16))
+    grad_out = jnp.concatenate([inner(attended[h], d_resid_all) for h in range(2)], axis=0)
+    d_att = jnp.stack([outer(d_resid_all, out_heads[h]) for h in range(2)]).astype(jnp.bfloat16)
+    d_unit = to_units(d_att.reshape(2, dp, ctx, mb, span, HD))
+    d_probs = jnp.einsum("hqd,kd->hqk", d_unit, v, preferred_element_type=jnp.float32)
+    delta = jnp.sum(probs * d_probs, axis=-1, keepdims=True)
+    d_scores = (probs * (d_probs - delta)).astype(jnp.bfloat16)
+    d_q = jnp.einsum("hqk,kd->hqd", d_scores, k, preferred_element_type=jnp.float32) * factor
+    d_k = jnp.einsum("hqk,hqd->kd", d_scores, q, preferred_element_type=jnp.float32) * factor
+    d_v = jnp.einsum("hqk,hqd->kd", probs_low, d_unit, preferred_element_type=jnp.float32)
+    all_pos = jnp.arange(length, dtype=jnp.float32)[:, None] * frequency
+    cos_u, sin_u = jnp.cos(all_pos), jnp.sin(all_pos)
+
+    def unturn(values):
+        a, b = values[..., : HD // 2], values[..., HD // 2 :]
+        return jnp.concatenate([a * cos_u + b * sin_u, b * cos_u - a * sin_u], axis=-1)
+
+    d_heads = jnp.concatenate([unturn(d_q), unturn(d_k)[None], d_v[None]]).astype(jnp.bfloat16)
+    d_mixed = to_rows(d_heads)
+    grad_qkv = jnp.stack([inner(normed, d_mixed[h]) for h in range(4)])
+    d_normed = sum_tp(sum(outer(d_mixed[h], qkv[h]) for h in range(4)))
+    grad_one = jnp.sum(d_normed * x * scale_one, axis=0)
+    grad_tokens = (d_resid + norm_back(x, scale_one, gain_one, d_normed)).astype(jnp.bfloat16)
+
+    def reduce_rows(value, dim, moves):
+        value = lax.psum_scatter(value.astype(jnp.bfloat16), "fsdp", scatter_dimension=dim, tiled=True)
+        if moves is not None:
+            value = lax.ppermute(value, ALL, back(moves))
+        return value.astype(jnp.float32)
+
+    gain_grads = lax.psum_scatter(jnp.stack([grad_one, grad_two]), ALL, scatter_dimension=1, tiled=True)
+    return (
+        block_out.reshape(tokens.shape),
+        grad_tokens.reshape(tokens.shape),
+        gain_grads[0],
+        reduce_rows(grad_qkv, 0, qkv_owner(sizes)).reshape(D, HD),
+        reduce_rows(grad_out, 0, None),
+        gain_grads[1],
+        reduce_rows(grad_gate_up, 1, up_owner(sizes)),
+        reduce_rows(grad_down, 0, down_owner(sizes)),
+    )
+
+
+def fits(mesh):
+    return mesh.shape["dp"] * mesh.shape["ctx"] == KVH and mesh.shape["fsdp"] == 4
+
+
 def solution(mesh):
     placed = (
         P(None, "dp", ("ctx", "fsdp"), None),
@@ -282,7 +484,7 @@
         P(("dp", "ctx", "fsdp"), None),
     )
     return jax.shard_map(
-        on_device,
+        on_device if fits(mesh) else on_device_gathered,
         mesh=mesh,
         in_specs=placed,
         out_specs=(

time: 1860 us -> 971 us (0.52)
  waiting for transfers between devices: 1390 us -> 650 us
  matrix products: 259 us -> 82.4 us
  starting transfers between devices: 15.3 us -> 39.4 us
    reduce_scatter x4 -> x7, waiting for transfers between devices: 733 us -> 272 us  [the longest x4 248 us: sum_tp(): lax.psum_scatter(value.astype(jnp.bfloat16), TP, scatter_dimension=0, til...]
    all_gather x8 -> x7, waiting for transfers between devices: 521 us -> 215 us  [the longest x4 149 us: gather_tp(): return lax.all_gather(value, TP, axis=0, tiled=True)]
    unnamed x12 -> x18, waiting for transfers between devices: 2.72 us -> 118 us
    all_to_all x2 -> x3, waiting for transfers between devices: 133 us -> 20.3 us  [the longest x2 20.3 us: to_units(): lax.all_to_all(values, 'fsdp', split_axis=0, concat_axis=0, tiled=True)]
    dot_general x8, matrix products: 118 us -> 18 us  [inner(): lax.dot_general(left, right, (((0,), (0,)), ((), ())), preferred_element_...]
    unnamed x2 -> x0, blocking collectives: 82.3 us -> none
    all_gather x0 -> x2, blocking collectives: none -> 75.3 us  [the longest x1 62.4 us: on_device(): lax.all_gather(jnp.stack([attn_gain, mlp_gain]), ALL, axis=1, tiled=True)]
    dot_general x22 -> x15, matrix products: 82.2 us -> 39.9 us  [the longest x9 23.1 us: dot(): return jnp.dot(left, right, preferred_element_type=jnp.float32)]
  transfers between devices with their start and end apart: 14 -> 25, of which waited for: 13 -> 17; matrix products, arithmetic and copies ran while one was open for 14% -> 10% of each run, Pallas kernels for 0% -> 0%
where the time goes in v1:
time: 971 us; the launch traced here: 957 us
  waiting for transfers between devices  650 us (67%)
  blocking collectives  97.5 us (10%)
  matrix products  82.4 us (8%)
  other arithmetic  43 us (4%)
  starting transfers between devices  39.4 us (4%)
  local copies, waits for them, and re-layouts  28.7 us (3%)
  between operations  15.1 us (2%)
    reduce_scatter x4, waiting for transfers between devices, sum_tp(): lax.psum_scatter(value.astype(jnp.bfloat16), TP, scatter_dimension=0, til...  248 us
    all_gather x4, waiting for transfers between devices, gather_tp(): return lax.all_gather(value, TP, axis=0, tiled=True)  149 us
    unnamed x18, waiting for transfers between devices  118 us
    all_gather x1, blocking collectives, on_device(): lax.all_gather(jnp.stack([attn_gain, mlp_gain]), ALL, axis=1, tiled=True)  62.4 us
    all_gather x1, waiting for transfers between devices, on_device(): lax.all_gather(lax.ppermute(w_gate_up, ALL, up_owner(sizes)), 'fsdp', axi...  39.1 us
    all_gather x1, waiting for transfers between devices, on_device(): lax.all_gather(lax.ppermute(w_down, ALL, down_owner(sizes)), 'fsdp', axis...  26.7 us
    dot_general x8, matrix products, outer(): lax.dot_general(left, right, (((1,), (1,)), ((), ())), preferred_element_...  24.5 us
    reduce_scatter x3, waiting for transfers between devices, reduce_rows(): lax.psum_scatter(value.astype(jnp.bfloat16), 'fsdp', scatter_dimension=di...  23.9 us
  transfers between devices with their start and end apart: 25, of which 17 were waited for; matrix products, arithmetic and copies ran while one was open for 10% of the time, Pallas kernels for 0%

profile of v1, /device:TPU:13, one launch (start us, length us, event | category | flops | bytes accessed | tf_op | source)
XLA Modules:
  0.0 956.7 jit_solution(13701603334139968594)
XLA Ops:
  10.4 8.5 collective-permute-done
  20.4 62.4 %all-gather.1 = bf16[32,48,2]{1,2,0:T(2,128)(2,1)S(1)} all-gather(bf16[1,48,2]{1,2,0:T(2,128)(2,1)S(1)} %maximum_bitcast_fusion.3), channel_id=1, replica_groups=mesh['dp'=2,'ctx'=4,'fsdp'=4] {'dp','ctx','fsdp'}, dimensions={0}, use_global_device_ids=true | all-gather | bytes 6336 | tf_op jit(solution)/shard_map/all_gather | solution.py:350
  86.9 45.4 %all-gather.10.cloned.1.call-done = bf16[1024,1536]{1,0:T(8,128)(2,1)} async-done(((bf16[128,1536]{1,0:T(8,128)(2,1)}), bf16[1024,1536]{1,0:T(8,128)(2,1)}) %all-gather.10.cloned.1.call-update) | async-done | bytes 3145744 | tf_op jit(solution)/shard_map/all_gather | solution.py:325
  141.5 4.5 all-to-all-start
  147.3 12.0 %all-to-all-done = bf16[4,4,4,64,96]{4,3,2,1,0:T(8,128)(2,1)} async-done(((bf16[4,4,4,64,96]{4,3,2,1,0:T(8,128)(2,1)}), bf16[4,4,4,64,96]{4,3,2,1,0:T(8,128)(2,1)}, u32[]{:S(2)}, u32[]{:S(2)}) %all-to-all-start) | async-done | bytes 786464 | tf_op jit(solution)/shard_map/all_to_all | solution.py:386
  172.7 4.4 all-to-all-start.1
  177.1 12.8 %all_gather.34 = bf16[192,1536]{1,0:T(8,128)(2,1)} all-gather(bf16[48,1536]{1,0:T(8,128)(2,1)} %param.12), channel_id=1, replica_groups=mesh['dp'=2,'ctx'=4,'fsdp'=4] {'fsdp'}, dimensions={0}, use_global_device_ids=true | all-gather | bytes 737280 | tf_op jit(solution)/shard_map/all_gather | solution.py:354
  198.9 16.3 %collective-permute-done.2 = bf16[128,1536]{1,0:T(8,128)(2,1)} collective-permute-done((bf16[128,1536]{1,0:T(8,128)(2,1)}, bf16[128,1536]{1,0:T(8,128)(2,1)}, u32[]{:S(2)}, u32[]{:S(2)}) %collective-permute-start.2) | collective-permute-done | bytes 393248 | tf_op jit(solution)/shard_map/ppermute | solution.py:356
  215.9 7.5 collective-permute-start.1
  223.6 47.2 %reduce-scatter.14.cloned.1.call-done = bf16[128,1536]{1,0:T(8,128)(2,1)} async-done(((bf16[1024,1536]{1,0:T(8,128)(2,1)}), bf16[128,1536]{1,0:T(8,128)(2,1)}) %reduce-scatter.14.cloned.1.call-update) | async-done | bytes 393232 | tf_op jit(solution)/shard_map/reduce_scatter | solution.py:329
  275.1 26.7 %all-gather.16.cloned.1.call-done = bf16[512,1536]{1,0:T(8,128)(2,1)} async-done(((bf16[128,1536]{1,0:T(8,128)(2,1)}), bf16[512,1536]{1,0:T(8,128)(2,1)}) %all-gather.16.cloned.1.call-update) | async-done | bytes 1572880 | tf_op jit(solution)/shard_map/all_gather | solution.py:356
  301.7 39.4 %all-gather.18.cloned.1.call-done = bf16[1024,1536]{1,0:T(8,128)(2,1)} async-done(((bf16[128,1536]{1,0:T(8,128)(2,1)}), bf16[1024,1536]{1,0:T(8,128)(2,1)}) %all-gather.18.cloned.1.call-update) | async-done | bytes 3145744 | tf_op jit(solution)/shard_map/all_gather | solution.py:325
  341.2 5.5 fusion.78
  346.7 39.1 %all-gather.14.cloned.1.call-done = bf16[1536,1024]{1,0:T(8,128)(2,1)} async-done(((bf16[1536,256]{1,0:T(8,128)(2,1)}), bf16[1536,1024]{1,0:T(8,128)(2,1)}) %all-gather.14.cloned.1.call-update) | async-done | bytes 3145744 | tf_op jit(solution)/shard_map/all_gather | solution.py:355
  385.8 40.1 %all-gather.12.cloned.1.call-done = bf16[1024,1536]{1,0:T(8,128)(2,1)} async-done(((bf16[128,1536]{1,0:T(8,128)(2,1)}), bf16[1024,1536]{1,0:T(8,128)(2,1)}) %all-gather.12.cloned.1.call-update) | async-done | bytes 3145744 | tf_op jit(solution)/shard_map/all_gather | solution.py:325
  425.9 4.3 fusion.14
  435.8 5.0 convolution_convert_fusion.2
  440.8 66.5 %reduce-scatter.18.cloned.1.call-done = bf16[128,1536]{1,0:T(8,128)(2,1)} async-done(((bf16[1024,1536]{1,0:T(8,128)(2,1)}), bf16[128,1536]{1,0:T(8,128)(2,1)}) %reduce-scatter.18.cloned.1.call-update) | async-done | bytes 393232 | tf_op jit(solution)/shard_map/reduce_scatter | solution.py:329
  512.7 7.6 convolution_convert_fusion.1
  520.6 6.4 fusion.4
  527.0 24.1 %all-gather.20.cloned.1.call-done = bf16[1024,1536]{1,0:T(8,128)(2,1)} async-done(((bf16[128,1536]{1,0:T(8,128)(2,1)}), bf16[1024,1536]{1,0:T(8,128)(2,1)}) %all-gather.20.cloned.1.call-update) | async-done | bytes 3145744 | tf_op jit(solution)/shard_map/all_gather | solution.py:325
  564.1 4.4 all-to-all-start.2
  568.4 5.4 convolution_convert_fusion.3
  574.0 8.3 all-to-all-done.2
  583.5 6.1 multiply_reduce_fusion
  607.6 22.3 %all_to_all.20 = bf16[4,4,4,64,96]{4,3,2,1,0:T(8,128)(2,1)S(1)} all-to-all(bf16[4,4,4,64,96]{4,3,2,1,0:T(8,128)(2,1)S(1)} %copy.78), channel_id=1, replica_groups=mesh['dp'=2,'ctx'=4,'fsdp'=4] {'fsdp'}, dimensions={0} | all-to-all | bytes 1572864 | tf_op jit(solution)/shard_map/all_to_all | solution.py:392
  652.6 6.0 collective-permute-start.5
  658.6 19.9 %reduce-scatter.30.cloned.1.call-done = bf16[1,1536,96]{1,2,0:T(8,128)(2,1)} async-done(((bf16[4,1536,96]{1,2,0:T(8,128)(2,1)}), bf16[1,1536,96]{1,2,0:T(8,128)(2,1)}) %reduce-scatter.30.cloned.1.call-update) | async-done | bytes 294928
  684.0 23.9 %reduce-scatter.22.cloned.1.call-done = bf16[48,1536]{1,0:T(8,128)(2,1)} async-done(((bf16[192,1536]{1,0:T(8,128)(2,1)}), bf16[48,1536]{1,0:T(8,128)(2,1)}) %reduce-scatter.22.cloned.1.call-update) | async-done | bytes 147472 | tf_op jit(solution)/shard_map/reduce_scatter | solution.py:453
  710.4 67.0 %reduce-scatter.20.cloned.1.call-done = bf16[128,1536]{1,0:T(8,128)(2,1)} async-done(((bf16[1024,1536]{1,0:T(8,128)(2,1)}), bf16[128,1536]{1,0:T(8,128)(2,1)}) %reduce-scatter.20.cloned.1.call-update) | async-done | bytes 393232 | tf_op jit(solution)/shard_map/reduce_scatter | solution.py:329
  779.9 67.7 %reduce-scatter.16.cloned.1.call-done = bf16[128,1536]{1,0:T(8,128)(2,1)} async-done(((bf16[1024,1536]{1,0:T(8,128)(2,1)}), bf16[128,1536]{1,0:T(8,128)(2,1)}) %reduce-scatter.16.cloned.1.call-update) | async-done | bytes 393232 | tf_op jit(solution)/shard_map/reduce_scatter | solution.py:329
  850.2 97.6 %reduce-scatter.28.cloned.1.call-done = f32[48,2]{1,0:T(8,128)} async-done(((f32[1536,2]{1,0:T(8,128)}), f32[48,2]{1,0:T(8,128)}) %reduce-scatter.28.cloned.1.call-update) | async-done | bytes 400
  (245 shorter events, 127.3 us)
Async XLA Ops:
  7.2 79.7 %all-gather.22.cloned.1.call-start = ((), (), s32[]{:S(2)}) async-start(), calls=%async_computation.26 | async-start | bytes 1474560 | tf_op jit(solution)/shard_map/all_gather | solution.py:353
  7.2 11.7 %collective-permute-start = (bf16[1536,96]{0,1:T(8,128)(2,1)}, bf16[1536,96]{0,1:T(8,128)(2,1)S(1)}, u32[]{:S(2)}, u32[]{:S(2)}) collective-permute-start(bf16[1536,96]{0,1:T(8,128)(2,1)} %param.11), channel_id=1, source_target_pairs={{0,0},{1,1},{2,4},{3,5},{4,8},{5,9},{6,12},{7,13},{8,16},{9,17},{1... | collective-permute-start | bytes 884744 | tf_op jit(solution)/shard_map/ppermute | solution.py:353
  19.7 112.6 %all-gather.10.cloned.1.call-start = ((), (), s32[]{:S(2)}) async-start(), calls=%async_computation.13 | async-start | bytes 3538944 | tf_op jit(solution)/shard_map/all_gather | solution.py:325
  141.5 17.8 %all-to-all-start = ((bf16[4,4,4,64,96]{4,3,2,1,0:T(8,128)(2,1)}), bf16[4,4,4,64,96]{4,3,2,1,0:T(8,128)(2,1)}, u32[]{:S(2)}, u32[]{:S(2)}) async-start(bf16[4,4,4,64,96]{4,3,2,1,0:T(8,128)(2,1)} %bitcast.219), calls=%async_computation | async-start | bytes 2097152 | tf_op jit(solution)/shard_map/all_to_all | solution.py:386
  172.7 17.2 %all-to-all-start.1 = ((bf16[4,2,4,64,96]{4,3,2,1,0:T(8,128)(2,1)}), bf16[4,2,4,64,96]{4,3,2,1,0:T(8,128)(2,1)}, u32[]{:S(2)}, u32[]{:S(2)}) async-start(bf16[4,2,4,64,96]{4,3,2,1,0:T(8,128)(2,1)} %copy.61), calls=%async_computation.1 | async-start | bytes 1048576 | tf_op jit(solution)/shard_map/all_to_all | solution.py:392
  177.1 93.7 %reduce-scatter.14.cloned.1.call-start = ((), (), s32[]{:S(2)}) async-start(), calls=%async_computation.14 | async-start | bytes 3538944 | tf_op jit(solution)/shard_map/reduce_scatter | solution.py:329
  195.8 75.0 %copy-start.3 = (bf16[2,1,64,1536]{3,2,1,0:T(8,128)(2,1)S(1)}, bf16[2,1,64,1536]{3,2,1,0:T(8,128)(2,1)}, u32[]{:S(2)}) copy-start(bf16[2,1,64,1536]{3,2,1,0:T(8,128)(2,1)} %param.8) | copy-start | bytes 1179652
  195.8 105.9 %all-gather.16.cloned.1.call-start = ((), (), s32[]{:S(2)}) async-start(), calls=%async_computation.17 | async-start | bytes 1966080 | tf_op jit(solution)/shard_map/all_gather | solution.py:356
  195.9 19.3 %collective-permute-start.2 = (bf16[128,1536]{1,0:T(8,128)(2,1)}, bf16[128,1536]{1,0:T(8,128)(2,1)}, u32[]{:S(2)}, u32[]{:S(2)}) collective-permute-start(bf16[128,1536]{1,0:T(8,128)(2,1)} %param.15), channel_id=1, source_target_pairs={{0,0},{1,1},{2,2},{3,3},{8,4},{9,5},{10,6},{11,7},{16,8},{17,9},{1... | collective-permute-start | bytes 1179656 | tf_op jit(solution)/shard_map/ppermute | solution.py:356
  215.2 125.9 %all-gather.18.cloned.1.call-start = ((), (), s32[]{:S(2)}) async-start(), calls=%async_computation.19 | async-start | bytes 3538944 | tf_op jit(solution)/shard_map/all_gather | solution.py:325
  215.8 169.9 %all-gather.14.cloned.1.call-start = ((), (), s32[]{:S(2)}) async-start(), calls=%async_computation.16 | async-start | bytes 3932160 | tf_op jit(solution)/shard_map/all_gather | solution.py:355
  215.9 7.5 collective-permute-start.1
  223.4 202.5 %all-gather.12.cloned.1.call-start = ((), (), s32[]{:S(2)}) async-start(), calls=%async_computation.15 | async-start | bytes 3538944 | tf_op jit(solution)/shard_map/all_gather | solution.py:325
  275.0 232.3 %reduce-scatter.18.cloned.1.call-start = ((), (), s32[]{:S(2)}) async-start(), calls=%async_computation.20 | async-start | bytes 3538944 | tf_op jit(solution)/shard_map/reduce_scatter | solution.py:329
  440.8 110.3 %all-gather.20.cloned.1.call-start = ((), (), s32[]{:S(2)}) async-start(), calls=%async_computation.21 | async-start | bytes 3538944 | tf_op jit(solution)/shard_map/all_gather | solution.py:325
  512.2 138.5 %reduce-scatter.24.cloned.1.call-start = ((), (), s32[]{:S(2)}) async-start(), calls=%async_computation.24 | async-start | bytes 3932160 | tf_op jit(solution)/shard_map/reduce_scatter | solution.py:453
  564.1 18.3 %all-to-all-start.2 = ((bf16[4,2,4,64,96]{4,3,2,1,0:T(8,128)(2,1)}), bf16[4,2,4,64,96]{4,3,2,1,0:T(8,128)(2,1)}, u32[]{:S(2)}, u32[]{:S(2)}) async-start(bf16[4,2,4,64,96]{4,3,2,1,0:T(8,128)(2,1)} %bitcast.240), calls=%async_computation.5 | async-start | bytes 1048576 | tf_op jit(solution)/shard_map/all_to_all | solution.py:386
  568.4 84.1 %reduce-scatter.26.cloned.1.call-start = ((), (), s32[]{:S(2)}) async-start(), calls=%async_computation.25 | async-start | bytes 1966080 | tf_op jit(solution)/shard_map/reduce_scatter | solution.py:453
  573.8 104.7 %reduce-scatter.30.cloned.1.call-start = ((), (), s32[]{:S(2)}) async-start(), calls=%async_computation.28 | async-start | bytes 1474560
  634.1 73.7 %reduce-scatter.22.cloned.1.call-start = ((), (), s32[]{:S(2)}) async-start(), calls=%async_computation.23 | async-start | bytes 737280 | tf_op jit(solution)/shard_map/reduce_scatter | solution.py:453
  638.5 138.9 %reduce-scatter.20.cloned.1.call-start = ((), (), s32[]{:S(2)}) async-start(), calls=%async_computation.22 | async-start | bytes 3538944 | tf_op jit(solution)/shard_map/reduce_scatter | solution.py:329
  645.5 202.1 %reduce-scatter.16.cloned.1.call-start = ((), (), s32[]{:S(2)}) async-start(), calls=%async_computation.18 | async-start | bytes 3538944 | tf_op jit(solution)/shard_map/reduce_scatter | solution.py:329
  650.7 297.1 %reduce-scatter.28.cloned.1.call-start = ((), (), s32[]{:S(2)}) async-start(), calls=%async_computation.27 | async-start | bytes 811008
  650.8 31.9 %collective-permute-start.4 = (bf16[1536,256]{1,0:T(8,128)(2,1)}, bf16[1536,256]{1,0:T(8,128)(2,1)S(1)}, u32[]{:S(2)}, u32[]{:S(2)}) collective-permute-start(bf16[1536,256]{1,0:T(8,128)(2,1)} %reduce-scatter.24.cloned.1.call-done), channel_id=1, source_target_pairs={{0,0},{1,1},{2,16},{3,17},{4,4},{5,5},{6,20},{7,21},{8,8},{9,9},{1... | collective-permute-start | bytes 2359304 | tf_op jit(solution)/shard_map/ppermute | solution.py:455
  652.6 29.1 %collective-permute-start.5 = (bf16[128,1536]{1,0:T(8,128)(2,1)}, bf16[128,1536]{1,0:T(8,128)(2,1)S(1)}, u32[]{:S(2)}, u32[]{:S(2)}) collective-permute-start(bf16[128,1536]{1,0:T(8,128)(2,1)} %reduce-scatter.26.cloned.1.call-done), channel_id=1, source_target_pairs={{0,0},{1,1},{2,2},{3,3},{4,8},{5,9},{6,10},{7,11},{8,16},{9,17},{1... | collective-permute-start | bytes 1179656 | tf_op jit(solution)/shard_map/ppermute | solution.py:455
  678.5 31.0 %collective-permute-start.3 = (bf16[1,1536,96]{1,2,0:T(8,128)(2,1)}, bf16[1,1536,96]{1,2,0:T(8,128)(2,1)S(1)}, u32[]{:S(2)}, u32[]{:S(2)}) collective-permute-start(bf16[1,1536,96]{1,2,0:T(8,128)(2,1)} %reduce-scatter.30.cloned.1.call-done), channel_id=1, source_target_pairs={{0,0},{1,1},{4,2},{5,3},{8,4},{9,5},{12,6},{13,7},{16,8},{17,9},{2... | collective-permute-start | bytes 884744 | tf_op jit(solution)/shard_map/ppermute | solution.py:455
  682.6 164.9 %copy-start.4 = (bf16[128,1536]{1,0:T(8,128)(2,1)S(1)}, bf16[128,1536]{1,0:T(8,128)(2,1)}, u32[]{:S(2)}) copy-start(bf16[128,1536]{1,0:T(8,128)(2,1)} %reduce-scatter.14.cloned.1.call-done) | copy-start | bytes 1179652
  682.6 164.9 %copy-start.17 = (bf16[2,1,64,1536]{3,2,1,0:T(8,128)(2,1)S(1)}, bf16[2,1,64,1536]{3,2,1,0:T(8,128)(2,1)}, u32[]{:S(2)}) copy-start(bf16[2,1,64,1536]{3,2,1,0:T(8,128)(2,1)} %param.9) | copy-start | bytes 1179652
  682.6 164.9 %copy-start.18 = (bf16[128,1536]{1,0:T(8,128)(2,1)S(1)}, bf16[128,1536]{1,0:T(8,128)(2,1)}, u32[]{:S(2)}) copy-start(bf16[128,1536]{1,0:T(8,128)(2,1)} %reduce-scatter.18.cloned.1.call-done) | copy-start | bytes 1179652
  682.6 164.9 %copy-start.37 = (f32[128]{0:T(128)S(1)}, f32[128]{0:T(128)}, u32[]{:S(2)}) copy-start(f32[128]{0:T(128)} %copy-done.36) | copy-start | bytes 1540
  682.6 164.9 %copy-start.42 = (f32[128]{0:T(128)S(1)}, f32[128]{0:T(128)}, u32[]{:S(2)}) copy-start(f32[128]{0:T(128)} %get-tuple-element.65) | copy-start | bytes 1540
  682.7 164.9 %copy-start.44 = (f32[128]{0:T(128)S(1)}, f32[128]{0:T(128)}, u32[]{:S(2)}) copy-start(f32[128]{0:T(128)} %copy-done.43) | copy-start | bytes 1540
  (47 other events, 238.8 us)
Sparse Core Ops, SparseCore 0:
  19.8 34.5 all-gather.21
  86.3 45.8 all-gather.9
  196.0 74.7 reduce-scatter.13
  272.5 29.1 all-gather.15
  303.2 37.9 all-gather.17
  342.8 42.8 all-gather.13
  387.9 37.9 all-gather.11
  440.9 66.3 reduce-scatter.17
  512.4 38.7 all-gather.19
  554.0 48.6 reduce-scatter.23
  606.2 38.5 reduce-scatter.25
  647.6 30.8 reduce-scatter.29
  682.0 25.8 reduce-scatter.21
  710.0 67.3 reduce-scatter.19
  779.5 67.9 reduce-scatter.15
  852.5 95.2 reduce-scatter.27

commit v2 on v1

--- a/solution.py
+++ b/solution.py
@@ -1,6 +1,10 @@
+import functools
+
 import jax
 import jax.numpy as jnp
 from jax import lax
+from jax.experimental import pallas as pl
+from jax.experimental.pallas import tpu as pltpu
 from jax.sharding import PartitionSpec as P
 
 D = 1536
@@ -287,7 +291,8 @@
             group, slot = head - H, 2
         else:
             group, slot = head - H - KVH, 3
-        moves.append((head, group * sizes["fsdp"] + slot))
+        device = group % sizes["dp"] * sizes["ctx"] + group // sizes["dp"]
+        moves.append((head, device * sizes["fsdp"] + slot))
     return moves
 
 
@@ -321,6 +326,437 @@
     return [(to, source) for source, to in moves]
 
 
+MESH = pl.DeviceIdType.MESH
+VM = pltpu.VMEM
+ANY = pl.ANY
+
+
+def place():
+    return lax.axis_index("dp"), lax.axis_index("ctx"), lax.axis_index("fsdp")
+
+
+def at_device(dp, ctx, fs):
+    return {"dp": dp, "ctx": ctx, "fsdp": fs}
+
+
+def remote(src, dst, send, recv, device):
+    return pltpu.make_async_remote_copy(
+        src_ref=src, dst_ref=dst, send_sem=send, recv_sem=recv, device_id=device, device_id_type=MESH
+    )
+
+
+def arrived(dst, recv, device):
+    remote(dst, dst, recv, recv, device).wait_recv()
+
+
+def left(src, send, device):
+    remote(src, src, send, send, device).wait_send()
+
+
+def greet_all(sizes):
+    dp, ctx, fs = sizes
+    n = dp * ctx * fs
+    d, c, f = place()
+    me = (d * ctx + c) * fs + f
+    barrier = pltpu.get_barrier_semaphore()
+
+    def tell(step, carry):
+        other = lax.rem(me + step, n)
+        pl.semaphore_signal(
+            barrier,
+            inc=1,
+            device_id=at_device(other // (ctx * fs), lax.rem(other // fs, ctx), lax.rem(other, fs)),
+            device_id_type=MESH,
+        )
+        return carry
+
+    lax.fori_loop(1, n, tell, 0)
+    pl.semaphore_wait(barrier, n - 1)
+
+
+class LineGather:
+    def __init__(self, n, own, whole, send, recv, local):
+        self.n, self.own, self.whole, self.send, self.recv, self.local = n, own, whole, send, recv, local
+        self.d, self.c, self.f = place()
+
+    def slot(self, at):
+        return self.whole.at[self.d, at]
+
+    def up(self, src, at):
+        return remote(src, self.slot(at), self.send.at[0, at], self.recv.at[self.d, at], at_device(self.d, self.c + 1, self.f))
+
+    def down(self, src, at):
+        return remote(src, self.slot(at), self.send.at[1, at], self.recv.at[self.d, at], at_device(self.d, self.c - 1, self.f))
+
+    def across(self, src, at):
+        return remote(src, self.slot(at), self.send.at[2, at], self.recv.at[self.d, at], at_device(1 - self.d, self.c, self.f))
+
+    def start(self):
+        c = self.c
+
+        @pl.when(c < self.n - 1)
+        def _():
+            self.up(self.own, c).start()
+
+        @pl.when(c > 0)
+        def _():
+            self.down(self.own, c).start()
+
+        self.across(self.own, c).start()
+        if self.local is not None:
+            pltpu.make_async_copy(self.own, self.slot(c), self.local).start()
+
+    def forward(self, k):
+        c = self.c
+
+        @pl.when(c - k >= 0)
+        def _():
+            arrived(self.slot(c - k), self.recv.at[self.d, c - k], at_device(self.d, c, self.f))
+
+            @pl.when(c < self.n - 1)
+            def _():
+                self.up(self.slot(c - k), c - k).start()
+
+            self.across(self.slot(c - k), c - k).start()
+
+        @pl.when(c + k < self.n)
+        def _():
+            arrived(self.slot(c + k), self.recv.at[self.d, c + k], at_device(self.d, c, self.f))
+
+            @pl.when(c > 0)
+            def _():
+                self.down(self.slot(c + k), c + k).start()
+
+            self.across(self.slot(c + k), c + k).start()
+
+    def other(self, at):
+        arrived(self.whole.at[1 - self.d, at], self.recv.at[1 - self.d, at], at_device(self.d, self.c, self.f))
+
+    def finish(self):
+        c = self.c
+        for at in range(self.n):
+
+            @pl.when(jnp.logical_and(at <= c, c < self.n - 1))
+            def _():
+                left(self.slot(at), self.send.at[0, at], at_device(self.d, c, self.f))
+
+            @pl.when(jnp.logical_and(at >= c, c > 0))
+            def _():
+                left(self.slot(at), self.send.at[1, at], at_device(self.d, c, self.f))
+
+            left(self.slot(at), self.send.at[2, at], at_device(self.d, c, self.f))
+        if self.local is not None:
+            pltpu.make_async_copy(self.own, self.slot(c), self.local).wait()
+
+
+FACTOR = HD ** (-0.5)
+LANES = 128
+
+
+def ordered(c, step, n):
+    at = jnp.int32(0)
+    for here in range(n):
+        near = sorted(range(n), key=lambda place_: (abs(place_ - here), place_))
+        for index, value in enumerate(near):
+            at = jnp.where(jnp.logical_and(c == here, step == index), value, at)
+    return at
+
+
+def first_kernel(
+    sizes, x_ref, gains_ref, w_ref, cos_ref, sin_up_ref, sin_down_ref,
+    normed_out, unit_out, att_out, wide_out, gains_out,
+    x_all, w_all, wide, normed, stage, unit, att_stage, att, gain_all, gain_vec,
+    line_send, line_recv, line_local, w_send, w_recv, w_pass, g_send, g_recv, u_send, u_recv, a_send, a_recv, out_sem,
+):
+    dp, ctx, fs = sizes
+    n = dp * ctx * fs
+    d, c, f = place()
+    here = at_device(d, c, f)
+    span = stage.shape[2]
+    greet_all(sizes)
+
+    q_core = f // 2
+    kv_slot = 2 + c // 2
+    kv_ctx = 2 * lax.rem(c, 2) + f // 2
+    kv_core = lax.rem(f, 2)
+    relay = f == 2 * lax.rem(c, 2) + d
+
+    @pl.when(jnp.logical_and(d == 1, jnp.logical_or(kv_core != 1, kv_ctx != c)))
+    def _():
+        remote(w_ref, w_all.at[kv_slot], w_send.at[0], w_recv.at[kv_slot], at_device(kv_core, kv_ctx, f)).start()
+
+    @pl.when(jnp.logical_and(d == 1, jnp.logical_and(kv_core == 1, kv_ctx == c)))
+    def _():
+        pltpu.make_async_copy(w_ref, w_all.at[kv_slot], w_recv.at[kv_slot]).start()
+
+    line = LineGather(ctx, x_ref, x_all, line_send, line_recv, line_local)
+    line.start()
+
+    @pl.when(d == 0)
+    def _():
+        slot = lax.rem(f, 2)
+        for to in range(fs):
+
+            @pl.when(jnp.logical_or(q_core != 0, to != f))
+            def _():
+                remote(w_ref, w_all.at[slot], w_send.at[to], w_recv.at[slot], at_device(q_core, c, to)).start()
+
+            @pl.when(jnp.logical_and(q_core == 0, to == f))
+            def _():
+                pltpu.make_async_copy(w_ref, w_all.at[slot], w_recv.at[slot]).start()
+
+    me = (d * ctx + c) * fs + f
+
+    def gain_to(step, carry):
+        other = lax.rem(me + step, n)
+        remote(
+            gains_ref, gain_all.at[me], g_send.at[other], g_recv.at[me],
+            at_device(other // (ctx * fs), lax.rem(other // fs, ctx), lax.rem(other, fs)),
+        ).start()
+        return carry
+
+    lax.fori_loop(1, n, gain_to, 0)
+    gain_all[me] = gains_ref[...]
+
+    @pl.when(relay)
+    def _():
+        for slot in (2, 3):
+            arrived(w_all.at[slot], w_recv.at[slot], here)
+            for step in range(1, fs):
+                to = lax.rem(f + step, fs)
+                remote(w_all.at[slot], w_all.at[slot], w_pass.at[slot - 2, step], w_recv.at[slot], at_device(d, c, to)).start()
+
+    def gain_from(step, carry):
+        other = lax.rem(me + step, n)
+        arrived(gain_all.at[other], g_recv.at[other], here)
+        return carry
+
+    lax.fori_loop(1, n, gain_from, 0)
+    each = D // n
+    for index in range(n):
+        gain_vec[:, index * each : (index + 1) * each] = gain_all[index][:, :each]
+    gain = gain_vec[0:1, :]
+
+    wide[...] = jnp.zeros_like(wide)
+    for slot in (0, 1, 2, 3):
+        if slot < 2:
+            arrived(w_all.at[slot], w_recv.at[slot], here)
+        else:
+
+            @pl.when(jnp.logical_not(relay))
+            def _():
+                arrived(w_all.at[slot], w_recv.at[slot], here)
+
+        wide[:, slot * LANES : slot * LANES + HD] = w_all[slot]
+
+    pltpu.make_async_copy(line.own, line.slot(c), line.local).wait()
+
+    def block(step, carry):
+        at = ordered(c, step, ctx)
+
+        @pl.when(at != c)
+        def _():
+            arrived(line.slot(at), line_recv.at[d, at], here)
+
+            @pl.when(jnp.logical_and(at < c, c < ctx - 1))
+            def _():
+                line.up(line.slot(at), at).start()
+
+            @pl.when(jnp.logical_and(at > c, c > 0))
+            def _():
+                line.down(line.slot(at), at).start()
+
+            line.across(line.slot(at), at).start()
+
+        line.other(at)
+        values = x_all[:, at].reshape(dp * 2 * span, D).astype(jnp.float32)
+        scale = lax.rsqrt(jnp.mean(values * values, axis=-1, keepdims=True) + EPS)
+        low = (values * scale * gain).astype(jnp.bfloat16)
+        normed[:, at] = low.reshape(dp, 2 * span, D)
+        heads = jnp.dot(low, wide[...], preferred_element_type=jnp.float32)
+        cosine, sine_up, sine_down = cos_ref[at], sin_up_ref[at], sin_down_ref[at]
+        for slot in range(4):
+            head = heads[:, slot * LANES : (slot + 1) * LANES]
+            if slot < 3:
+                turned_up = pltpu.roll(head, HD // 2, 1).reshape(2 * dp, span, LANES)
+                turned_down = pltpu.roll(head, LANES - HD // 2, 1).reshape(2 * dp, span, LANES)
+                head = head.reshape(2 * dp, span, LANES)
+                head = head * cosine[None] + turned_up * sine_up[None] + turned_down * sine_down[None]
+            else:
+                head = head.reshape(2 * dp, span, LANES)
+            stage[at, :, :, slot * LANES : (slot + 1) * LANES] = head.astype(jnp.bfloat16)
+        for to in range(2 * dp):
+
+            @pl.when(to != f)
+            def _():
+                remote(stage.at[at, to], unit.at[at, f], u_send.at[at, to], u_recv.at[at, f], at_device(d, c, to)).start()
+
+            @pl.when(to == f)
+            def _():
+                unit[at, f] = stage[at, to]
+
+        return carry
+
+    lax.fori_loop(0, ctx, block, 0)
+    normed_copy = pltpu.make_async_copy(normed, normed_out, out_sem.at[0])
+    wide_copy = pltpu.make_async_copy(wide, wide_out, out_sem.at[1])
+    gains_copy = pltpu.make_async_copy(gain_vec, gains_out, out_sem.at[2])
+    normed_copy.start()
+    wide_copy.start()
+    gains_copy.start()
+
+    for at in range(ctx):
+        for step in range(1, fs):
+            other = lax.rem(f + step, fs)
+            arrived(unit.at[at, other], u_recv.at[at, other], here)
+    unit_copy = pltpu.make_async_copy(unit, unit_out, out_sem.at[3])
+    unit_copy.start()
+
+    rows = fs * span
+    for at in range(ctx):
+        keys = rows * (at + 1)
+        k_rows = unit[0 : at + 1, :, :, 2 * LANES : 3 * LANES].reshape(keys, LANES)
+        v_rows = unit[0 : at + 1, :, :, 3 * LANES : 4 * LANES].reshape(keys, LANES)
+        allowed = lax.broadcasted_iota(jnp.int32, (rows, keys), 1) <= rows * at + lax.broadcasted_iota(
+            jnp.int32, (rows, keys), 0
+        )
+        for head in range(2):
+            q_rows = unit[at, :, :, head * LANES : (head + 1) * LANES].reshape(rows, LANES)
+            scores = outer(q_rows, k_rows) * FACTOR
+            scores = jnp.where(allowed, scores, NEG)
+            best = jnp.max(scores, axis=-1, keepdims=True)
+            weights = jnp.exp(scores - best)
+            probs = weights / jnp.sum(weights, axis=-1, keepdims=True)
+            mixed = jnp.dot(probs.astype(jnp.bfloat16), v_rows, preferred_element_type=jnp.float32)
+            att_stage[at, :, :, head * LANES : (head + 1) * LANES] = mixed.astype(jnp.bfloat16).reshape(fs, span, LANES)
+        for to in range(fs):
+
+            @pl.when(to != f)
+            def _():
+                remote(
+                    att_stage.at[at, to], att.at[f // 2, at, lax.rem(f, 2)], a_send.at[at, to], a_recv.at[f, at], at_device(d, c, to)
+                ).start()
+
+            @pl.when(to == f)
+            def _():
+                att[f // 2, at, lax.rem(f, 2)] = att_stage[at, to]
+
+    for at in range(ctx):
+        for step in range(1, fs):
+            other = lax.rem(f + step, fs)
+            arrived(att.at[other // 2, at, lax.rem(other, 2)], a_recv.at[other, at], here)
+    att_copy = pltpu.make_async_copy(att, att_out, out_sem.at[4])
+    att_copy.start()
+
+    for at in range(ctx):
+
+        @pl.when(jnp.logical_and(at <= c, c < ctx - 1))
+        def _():
+            left(line.slot(at), line_send.at[0, at], here)
+
+        @pl.when(jnp.logical_and(at >= c, c > 0))
+        def _():
+            left(line.slot(at), line_send.at[1, at], here)
+
+        left(line.slot(at), line_send.at[2, at], here)
+        for to in range(fs):
+
+            @pl.when(to != f)
+            def _():
+                left(stage.at[at, to], u_send.at[at, to], here)
+                left(att_stage.at[at, to], a_send.at[at, to], here)
+
+    @pl.when(jnp.logical_and(d == 1, jnp.logical_or(kv_core != 1, kv_ctx != c)))
+    def _():
+        left(w_ref, w_send.at[0], here)
+
+    @pl.when(d == 0)
+    def _():
+        for to in range(fs):
+
+            @pl.when(jnp.logical_or(q_core != 0, to != f))
+            def _():
+                left(w_ref, w_send.at[to], here)
+
+    @pl.when(relay)
+    def _():
+        for slot in (2, 3):
+            for step in range(1, fs):
+                left(w_all.at[slot], w_pass.at[slot - 2, step], here)
+
+    def gain_left(step, carry):
+        other = lax.rem(me + step, n)
+        left(gains_ref, g_send.at[other], here)
+        return carry
+
+    lax.fori_loop(1, n, gain_left, 0)
+    for copy in (normed_copy, wide_copy, gains_copy, unit_copy, att_copy):
+        copy.wait()
+
+
+def first(sizes, x, gains, w_qkv, cosine, sine_up, sine_down):
+    dp, ctx, fs = sizes
+    n = dp * ctx * fs
+    rows = x.shape[0]
+    span = rows // 2
+    low, wide_t = jnp.bfloat16, jnp.float32
+    dma = pltpu.SemaphoreType.DMA
+    shapes = (
+        jax.ShapeDtypeStruct((dp, ctx, rows, D), low),
+        jax.ShapeDtypeStruct((ctx, fs, span, 4 * LANES), low),
+        jax.ShapeDtypeStruct((dp, ctx, 2, span, 2 * LANES), low),
+        jax.ShapeDtypeStruct((D, 4 * LANES), low),
+        jax.ShapeDtypeStruct((8, D), wide_t),
+    )
+    any_spec, vm_spec = pl.BlockSpec(memory_space=ANY), pl.BlockSpec(memory_space=VM)
+    return pl.pallas_call(
+        functools.partial(first_kernel, sizes),
+        name="first",
+        out_shape=shapes,
+        in_specs=[vm_spec, vm_spec, any_spec, vm_spec, vm_spec, vm_spec],
+        out_specs=[any_spec] * 5,
+        scratch_shapes=[
+            VM((dp, ctx, rows, D), low),
+            VM((4, D, HD), low),
+            VM((D, 4 * LANES), low),
+            VM((dp, ctx, rows, D), low),
+            VM((ctx, 2 * dp, span, 4 * LANES), low),
+            VM((ctx, fs, span, 4 * LANES), low),
+            VM((ctx, fs, span, 2 * LANES), low),
+            VM((dp, ctx, 2, span, 2 * LANES), low),
+            VM((n, 8, LANES), wide_t),
+            VM((8, D), wide_t),
+            dma((3, ctx)), dma((dp, ctx)), dma,
+            dma((fs,)), dma((4,)), dma((2, fs)),
+            dma((n,)), dma((n,)),
+            dma((ctx, 2 * dp)), dma((ctx, fs)),
+            dma((ctx, fs)), dma((fs, ctx)),
+            dma((5,)),
+        ],
+        compiler_params=pltpu.CompilerParams(collective_id=1, has_side_effects=True, vmem_limit_bytes=60 * 1024 * 1024),
+    )(x, gains, w_qkv, cosine, sine_up, sine_down)
+
+
+def angle_tables(ctx, fs, span):
+    f_index = lax.axis_index("fsdp")
+    positions = (jnp.arange(ctx, dtype=jnp.int32)[:, None] * fs + f_index) * span + jnp.arange(span, dtype=jnp.int32)[None, :]
+    return lane_tables(positions)
+
+
+def lane_tables(positions):
+    lane = jnp.arange(LANES, dtype=jnp.int32)
+    pair = (lane % (HD // 2)).astype(jnp.float32)
+    frequency = THETA ** (-(pair * 2.0) / HD)
+    angles = positions.astype(jnp.float32)[..., None] * frequency
+    inside = lane < HD
+    low_half = lane < HD // 2
+    cosine = jnp.where(inside, jnp.cos(angles), 0.0)
+    sine = jnp.sin(angles)
+    sine_up = jnp.where(jnp.logical_and(inside, jnp.logical_not(low_half)), sine, 0.0)
+    sine_down = jnp.where(low_half, -sine, 0.0)
+    return cosine, sine_up, sine_down
+
+
 def gather_tp(value):
     return lax.all_gather(value, TP, axis=0, tiled=True)
 
@@ -347,54 +783,43 @@
     factor = HD ** (-0.5)
     hidden = FF // (dp * ctx)
 
-    gains = lax.all_gather(jnp.stack([attn_gain, mlp_gain]), ALL, axis=1, tiled=True)
-    gain_one = gains[0].astype(jnp.float32)
-    gain_two = gains[1].astype(jnp.float32)
-    qkv = lax.all_gather(lax.ppermute(w_qkv, ALL, qkv_owner(sizes)), "fsdp", axis=0)
-    out_w = lax.all_gather(w_out, "fsdp", axis=0, tiled=True)
+    x_low = tokens.reshape(rows, D)
+    gain_rows = jnp.zeros((8, LANES), jnp.float32)
+    gain_rows = gain_rows.at[0, : attn_gain.shape[0]].set(attn_gain.astype(jnp.float32))
+    gain_rows = gain_rows.at[1, : mlp_gain.shape[0]].set(mlp_gain.astype(jnp.float32))
+    cosine, sine_up, sine_down = angle_tables(ctx, fs, span)
+    normed, unit, att, qkv, gains = first((dp, ctx, fs), x_low, gain_rows, w_qkv, cosine, sine_up, sine_down)
+    gain_one, gain_two = gains[0], gains[1]
+    normed = normed.reshape(dp * ctx * rows, D)
+    unit = unit.reshape(length, 4, LANES)
+    attended = att.reshape(dp * ctx * rows, 2 * LANES)
+
+    out_w = lax.all_gather(lax.ppermute(w_out, ALL, down_owner(sizes)), "fsdp", axis=0, tiled=True)
+    out_w = jnp.pad(out_w.reshape(2, HD, D), ((0, 0), (0, LANES - HD), (0, 0))).reshape(2 * LANES, D)
     gate_up = lax.all_gather(lax.ppermute(w_gate_up, ALL, up_owner(sizes)), "fsdp", axis=1, tiled=True)
     down = lax.all_gather(lax.ppermute(w_down, ALL, down_owner(sizes)), "fsdp", axis=0, tiled=True)
 
-    x = tokens.reshape(rows, D).astype(jnp.float32)
+    x = x_low.astype(jnp.float32)
     dy = cotangent.reshape(rows, D)
     scale_one = lax.rsqrt(jnp.mean(x * x, axis=-1, keepdims=True) + EPS)
-    normed = gather_tp((x * scale_one * gain_one).astype(jnp.bfloat16))
     dy_all = gather_tp(dy)
-
-    heads = jnp.stack([dot(normed, qkv[h]) for h in range(4)])
-    positions = (
-        (jnp.arange(ctx, dtype=jnp.int32)[:, None] * fs + f_index) * span
-        + jnp.arange(span, dtype=jnp.int32)[None, :]
-    )
-    frequency = THETA ** (-(jnp.arange(HD // 2, dtype=jnp.float32) * 2.0) / HD)
-    angles = positions.astype(jnp.float32)[:, :, None] * frequency
-    cosine = jnp.cos(angles)[None, None, :, None]
-    sine = jnp.sin(angles)[None, None, :, None]
-
-    def turn(values, sin_b):
-        a, b = values[..., : HD // 2], values[..., HD // 2 :]
-        return jnp.concatenate([a * cosine - b * sin_b, b * cosine + a * sin_b], axis=-1)
-
-    heads = heads.reshape(4, dp, ctx, mb, span, HD)
-    turned = turn(heads[:3], sine)
-    heads = jnp.concatenate([turned, heads[3:]]).astype(jnp.bfloat16)
 
     def to_units(values):
         count = values.shape[0]
         values = values.transpose(1, 3, 0, 2, 4, 5)
-        values = values.reshape(dp * mb, count, ctx, span, HD)
+        values = values.reshape(dp * mb, count, ctx, span, -1)
         values = lax.all_to_all(values, "fsdp", split_axis=0, concat_axis=0, tiled=True)
-        return values.transpose(1, 2, 0, 3, 4).reshape(count, length, HD)
+        return values.transpose(1, 2, 0, 3, 4).reshape(count, length, -1)
 
     def to_rows(values):
         count = values.shape[0]
-        values = values.reshape(count, ctx, fs, span, HD).transpose(2, 0, 1, 3, 4)
+        values = values.reshape(count, ctx, fs, span, -1).transpose(2, 0, 1, 3, 4)
         values = lax.all_to_all(values, "fsdp", split_axis=0, concat_axis=0, tiled=True)
-        values = values.reshape(dp, mb, count, ctx, span, HD).transpose(2, 0, 3, 1, 4, 5)
-        return values.reshape(count, dp * ctx * rows, HD)
-
-    unit = to_units(heads)
-    q, k, v = unit[:2], unit[2], unit[3]
+        values = values.reshape(dp, mb, count, ctx, span, -1).transpose(2, 0, 3, 1, 4, 5)
+        return values.reshape(count, dp * ctx * rows, -1)
+
+    q = jnp.stack([unit[:, 0], unit[:, 1]])
+    k, v = unit[:, 2], unit[:, 3]
     scores = jnp.einsum("hqd,kd->hqk", q, k, preferred_element_type=jnp.float32) * factor
     allowed = jnp.arange(length)[None, :] <= jnp.arange(length)[:, None]
     scores = jnp.where(allowed, scores, NEG)
@@ -402,10 +827,7 @@
     weights = jnp.where(allowed, jnp.exp(scores - best), 0.0)
     probs = weights / jnp.sum(weights, axis=-1, keepdims=True)
     probs_low = probs.astype(jnp.bfloat16)
-    att = jnp.einsum("hqk,kd->hqd", probs_low, v, preferred_element_type=jnp.float32)
-    attended = to_rows(att.astype(jnp.bfloat16))
-    out_heads = out_w.reshape(2, HD, D)
-    partial = dot(attended[0], out_heads[0]) + dot(attended[1], out_heads[1])
+    partial = dot(attended, out_w)
     resid = x + sum_tp(partial)
     scale_two = lax.rsqrt(jnp.mean(resid * resid, axis=-1, keepdims=True) + EPS)
     normed_two = gather_tp((resid * scale_two * gain_two).astype(jnp.bfloat16))
@@ -426,26 +848,25 @@
     grad_two = jnp.sum(d_two * resid * scale_two, axis=0)
     d_resid = dy.astype(jnp.float32) + norm_back(resid, scale_two, gain_two, d_two)
     d_resid_all = gather_tp(d_resid.astype(jnp.bfloat16))
-    grad_out = jnp.concatenate([inner(attended[h], d_resid_all) for h in range(2)], axis=0)
-    d_att = jnp.stack([outer(d_resid_all, out_heads[h]) for h in range(2)]).astype(jnp.bfloat16)
-    d_unit = to_units(d_att.reshape(2, dp, ctx, mb, span, HD))
+    grad_out = inner(attended, d_resid_all).reshape(2, LANES, D)[:, :HD].reshape(2 * HD, D)
+    d_att = outer(d_resid_all, out_w).astype(jnp.bfloat16)
+    d_unit = to_units(jnp.moveaxis(d_att.reshape(dp, ctx, mb, span, 2, LANES), 4, 0))
     d_probs = jnp.einsum("hqd,kd->hqk", d_unit, v, preferred_element_type=jnp.float32)
     delta = jnp.sum(probs * d_probs, axis=-1, keepdims=True)
     d_scores = (probs * (d_probs - delta)).astype(jnp.bfloat16)
     d_q = jnp.einsum("hqk,kd->hqd", d_scores, k, preferred_element_type=jnp.float32) * factor
     d_k = jnp.einsum("hqk,hqd->kd", d_scores, q, preferred_element_type=jnp.float32) * factor
     d_v = jnp.einsum("hqk,hqd->kd", probs_low, d_unit, preferred_element_type=jnp.float32)
-    all_pos = jnp.arange(length, dtype=jnp.float32)[:, None] * frequency
-    cos_u, sin_u = jnp.cos(all_pos), jnp.sin(all_pos)
+    cos_u, up_u, down_u = lane_tables(jnp.arange(length, dtype=jnp.int32))
 
     def unturn(values):
-        a, b = values[..., : HD // 2], values[..., HD // 2 :]
-        return jnp.concatenate([a * cos_u + b * sin_u, b * cos_u - a * sin_u], axis=-1)
+        return values * cos_u - jnp.roll(values, HD // 2, -1) * up_u - jnp.roll(values, -(HD // 2), -1) * down_u
 
     d_heads = jnp.concatenate([unturn(d_q), unturn(d_k)[None], d_v[None]]).astype(jnp.bfloat16)
     d_mixed = to_rows(d_heads)
-    grad_qkv = jnp.stack([inner(normed, d_mixed[h]) for h in range(4)])
-    d_normed = sum_tp(sum(outer(d_mixed[h], qkv[h]) for h in range(4)))
+    d_mixed = jnp.moveaxis(d_mixed, 0, 1).reshape(dp * ctx * rows, 4 * LANES)
+    grad_qkv = jnp.moveaxis(inner(normed, d_mixed).reshape(D, 4, LANES)[:, :, :HD], 1, 0)
+    d_normed = sum_tp(outer(d_mixed, qkv))
     grad_one = jnp.sum(d_normed * x * scale_one, axis=0)
     grad_tokens = (d_resid + norm_back(x, scale_one, gain_one, d_normed)).astype(jnp.bfloat16)
 
@@ -461,7 +882,7 @@
         grad_tokens.reshape(tokens.shape),
         gain_grads[0],
         reduce_rows(grad_qkv, 0, qkv_owner(sizes)).reshape(D, HD),
-        reduce_rows(grad_out, 0, None),
+        reduce_rows(grad_out, 0, down_owner(sizes)),
         gain_grads[1],
         reduce_rows(grad_gate_up, 1, up_owner(sizes)),
         reduce_rows(grad_down, 0, down_owner(sizes)),

time: 971 us -> 796 us (0.82)
  waiting for transfers between devices: 650 us -> 522 us
  blocking collectives: 97.5 us -> 27.2 us
  Pallas kernels: 0 us -> 65 us
  matrix products: 82.4 us -> 68.3 us
  starting transfers between devices: 39.4 us -> 27.8 us
  other arithmetic: 43 us -> 32.1 us
    all_gather x4 -> x3, waiting for transfers between devices: 149 us -> 70 us  [gather_tp(): return lax.all_gather(value, TP, axis=0, tiled=True)]
    all_gather x2 -> x1, blocking collectives: 75.3 us -> 7.69 us  [on_device(): lax.all_gather(lax.ppermute(w_out, ALL, down_owner(sizes)), 'fsdp', axis=...]
    pallas_call x0 -> x1, Pallas kernels: none -> 65 us  [first(): pl.pallas_call(functools.partial(first_kernel, sizes), name='first', out_...]
    all_gather x1, waiting for transfers between devices: 26.7 us -> 0.03 us  [on_device(): lax.all_gather(lax.ppermute(w_down, ALL, down_owner(sizes)), 'fsdp', axis...]
    all_to_all x2 -> x1, waiting for transfers between devices: 20.3 us -> 3.08 us  [to_units(): lax.all_to_all(values, 'fsdp', split_axis=0, concat_axis=0, tiled=True)]
    unnamed x18 -> x16, waiting for transfers between devices: 118 us -> 106 us
    reduce_scatter x4, waiting for transfers between devices: 248 us -> 260 us  [sum_tp(): lax.psum_scatter(value.astype(jnp.bfloat16), TP, scatter_dimension=0, til...]
    dot_general x9 -> x4, matrix products: 23.1 us -> 16.5 us  [dot(): return jnp.dot(left, right, preferred_element_type=jnp.float32)]
  transfers between devices with their start and end apart: 25 -> 22, of which waited for: 17 -> 14; matrix products, arithmetic and copies ran while one was open for 10% -> 12% of each run, Pallas kernels for 0% -> 8%
where the time goes in v2:
time: 796 us; the launch traced here: 785 us
  waiting for transfers between devices  522 us (66%)
  matrix products  68.3 us (9%)
  Pallas kernels  65 us (8%)
  other arithmetic  32.1 us (4%)
  starting transfers between devices  27.8 us (3%)
  blocking collectives  27.2 us (3%)
  local copies, waits for them, and re-layouts  25.2 us (3%)
  between operations  16.5 us (2%)
    reduce_scatter x4, waiting for transfers between devices, sum_tp(): lax.psum_scatter(value.astype(jnp.bfloat16), TP, scatter_dimension=0, til...  260 us
    unnamed x16, waiting for transfers between devices  106 us
    all_gather x3, waiting for transfers between devices, gather_tp(): return lax.all_gather(value, TP, axis=0, tiled=True)  70 us
    pallas_call x1, Pallas kernels, first(): pl.pallas_call(functools.partial(first_kernel, sizes), name='first', out_...  65 us
    all_gather x1, waiting for transfers between devices, on_device(): lax.all_gather(lax.ppermute(w_gate_up, ALL, up_owner(sizes)), 'fsdp', axi...  40 us
    reduce_scatter x3, waiting for transfers between devices, reduce_rows(): lax.psum_scatter(value.astype(jnp.bfloat16), 'fsdp', scatter_dimension=di...  27.2 us
    all_to_all x1, blocking collectives, to_rows(): lax.all_to_all(values, 'fsdp', split_axis=0, concat_axis=0, tiled=True)  19.5 us
    dot_general x4, matrix products, outer(): lax.dot_general(left, right, (((1,), (1,)), ((), ())), preferred_element_...  19.1 us
  transfers between devices with their start and end apart: 22, of which 14 were waited for; matrix products, arithmetic and copies ran while one was open for 12% of the time, Pallas kernels for 8%

profile of v2, /device:TPU:13, one launch (start us, length us, event | category | flops | bytes accessed | tf_op | source)
XLA Modules:
  0.0 784.5 jit_solution(10607267714563104618)
XLA Ops:
  16.1 65.0 %first.1 = (bf16[2,4,128,1536]{3,2,1,0:T(8,128)(2,1)}, bf16[4,4,64,512]{3,2,1,0:T(8,128)(2,1)}, bf16[2,4,2,64,256]{4,3,2,1,0:T(8,128)(2,1)}, bf16[1536,512]{1,0:T(8,128)(2,1)}, f32[8,1536]{1,0:T(8,128)}) custom-call(bf16[128,1536]{1,0:T(8,128)(2,1)} %bitcast.156, f32[8,128]{1,0:T(8,128)} %copy-done.22, bf16[1536,96]{1,0:T(8,128)(2,1)} %copy.86.w_ref, ...), custom_call_target="tpu_custom_call" | custom-call | tf_op jit(solution)/shard_map/first/pallas_call | solution.py:712
  81.1 7.7 all_gather.18
  88.9 3.6 convolution_convert_fusion
  95.5 14.3 %collective-permute-done.2 = bf16[128,1536]{1,0:T(8,128)(2,1)S(1)} collective-permute-done((bf16[128,1536]{1,0:T(8,128)(2,1)S(1)}, bf16[128,1536]{1,0:T(8,128)(2,1)S(1)}, u32[]{:S(2)}, u32[]{:S(2)}) %collective-permute-start.2) | collective-permute-done | bytes 393248 | tf_op jit(solution)/shard_map/ppermute | solution.py:800
  114.9 67.0 %reduce-scatter.14.cloned.1.call-done = bf16[128,1536]{1,0:T(8,128)(2,1)} async-done(((bf16[1024,1536]{1,0:T(8,128)(2,1)}), bf16[128,1536]{1,0:T(8,128)(2,1)}) %reduce-scatter.14.cloned.1.call-update) | async-done | bytes 393232 | tf_op jit(solution)/shard_map/reduce_scatter | solution.py:765
  185.3 13.5 %all-gather.12.cloned.1.call-done = bf16[1024,1536]{1,0:T(8,128)(2,1)} async-done(((bf16[128,1536]{1,0:T(8,128)(2,1)}), bf16[1024,1536]{1,0:T(8,128)(2,1)}) %all-gather.12.cloned.1.call-update) | async-done | bytes 3145744 | tf_op jit(solution)/shard_map/all_gather | solution.py:761
  198.8 5.5 fusion.69
  204.3 40.0 %all-gather.8.cloned.1.call-done = bf16[1536,1024]{1,0:T(8,128)(2,1)} async-done(((bf16[1536,256]{1,0:T(8,128)(2,1)}), bf16[1536,1024]{1,0:T(8,128)(2,1)}) %all-gather.8.cloned.1.call-update) | async-done | bytes 3145744 | tf_op jit(solution)/shard_map/all_gather | solution.py:799
  244.4 40.1 %all-gather.6.cloned.1.call-done = bf16[1024,1536]{1,0:T(8,128)(2,1)} async-done(((bf16[128,1536]{1,0:T(8,128)(2,1)}), bf16[1024,1536]{1,0:T(8,128)(2,1)}) %all-gather.6.cloned.1.call-update) | async-done | bytes 3145744 | tf_op jit(solution)/shard_map/all_gather | solution.py:761
  284.5 4.3 fusion.10
  289.4 3.8 multiply_convert_fusion.2
  294.1 5.0 convolution_convert_fusion.4
  299.2 66.4 %reduce-scatter.18.cloned.1.call-done = bf16[128,1536]{1,0:T(8,128)(2,1)} async-done(((bf16[1024,1536]{1,0:T(8,128)(2,1)}), bf16[128,1536]{1,0:T(8,128)(2,1)}) %reduce-scatter.18.cloned.1.call-update) | async-done | bytes 393232 | tf_op jit(solution)/shard_map/reduce_scatter | solution.py:765
  370.1 7.3 convolution_convert_fusion.3
  388.4 3.8 fusion.4
  392.2 16.3 %all-gather.14.cloned.1.call-done = bf16[1024,1536]{1,0:T(8,128)(2,1)} async-done(((bf16[128,1536]{1,0:T(8,128)(2,1)}), bf16[1024,1536]{1,0:T(8,128)(2,1)}) %all-gather.14.cloned.1.call-update) | async-done | bytes 3145744 | tf_op jit(solution)/shard_map/all_gather | solution.py:761
  408.6 3.7 convolution_convert_fusion.6
  414.3 3.7 all-to-all-start
  418.1 5.2 convolution_convert_fusion.5
  426.7 6.0 multiply_reduce_fusion
  445.1 3.5 fusion.70
  448.8 19.5 %all_to_all.10 = bf16[4,4,4,64,128]{4,3,2,1,0:T(8,128)(2,1)S(1)} all-to-all(bf16[4,4,4,64,128]{4,3,2,1,0:T(8,128)(2,1)S(1)} %copy.101), channel_id=1, replica_groups=mesh['dp'=2,'ctx'=4,'fsdp'=4] {'fsdp'}, dimensions={0} | all-to-all | bytes 2097152 | tf_op jit(solution)/shard_map/all_to_all | solution.py:817
  468.9 3.7 fusion.19
  478.1 4.9 convolution_convert_fusion.1
  484.3 4.7 convolution_convert_fusion.2
  491.2 5.8 collective-permute-start.6
  497.0 7.3 reduce-scatter.30.cloned.1.call-done
  507.5 27.1 %reduce-scatter.22.cloned.1.call-done = bf16[48,1536]{1,0:T(8,128)(2,1)} async-done(((bf16[192,1536]{1,0:T(8,128)(2,1)}), bf16[48,1536]{1,0:T(8,128)(2,1)}) %reduce-scatter.22.cloned.1.call-update) | async-done | bytes 147472 | tf_op jit(solution)/shard_map/reduce_scatter | solution.py:874
  534.6 5.0 collective-permute-start.4
  544.8 59.3 %reduce-scatter.20.cloned.1.call-done = bf16[128,1536]{1,0:T(8,128)(2,1)} async-done(((bf16[1024,1536]{1,0:T(8,128)(2,1)}), bf16[128,1536]{1,0:T(8,128)(2,1)}) %reduce-scatter.20.cloned.1.call-update) | async-done | bytes 393232 | tf_op jit(solution)/shard_map/reduce_scatter | solution.py:765
  606.7 67.8 %reduce-scatter.16.cloned.1.call-done = bf16[128,1536]{1,0:T(8,128)(2,1)} async-done(((bf16[1024,1536]{1,0:T(8,128)(2,1)}), bf16[128,1536]{1,0:T(8,128)(2,1)}) %reduce-scatter.16.cloned.1.call-update) | async-done | bytes 393232 | tf_op jit(solution)/shard_map/reduce_scatter | solution.py:765
  677.1 97.8 %reduce-scatter.28.cloned.1.call-done = f32[48,2]{1,0:T(8,128)} async-done(((f32[1536,2]{1,0:T(8,128)}), f32[48,2]{1,0:T(8,128)}) %reduce-scatter.28.cloned.1.call-update) | async-done | bytes 400
  (201 shorter events, 79.1 us)
Async XLA Ops:
  8.0 173.8 %reduce-scatter.14.cloned.1.call-start = ((), (), s32[]{:S(2)}) async-start(), calls=%async_computation.11 | async-start | bytes 3538944 | tf_op jit(solution)/shard_map/reduce_scatter | solution.py:765
  8.0 73.1 %collective-permute-start = (bf16[48,1536]{1,0:T(8,128)(2,1)}, bf16[48,1536]{1,0:T(8,128)(2,1)S(1)}, u32[]{:S(2)}, u32[]{:S(2)}) collective-permute-start(bf16[48,1536]{1,0:T(8,128)(2,1)} %param.16), channel_id=1, source_target_pairs={{0,0},{1,1},{2,2},{3,3},{8,4},{9,5},{10,6},{11,7},{16,8},{17,9},{1... | collective-permute-start | bytes 442376 | tf_op jit(solution)/shard_map/ppermute | solution.py:797
  11.3 81.3 %copy-start.25 = (pred[128]{0:T(512)(128)(4,1)}, pred[128]{0:T(512)(128)(4,1)S(1)}, u32[]{:S(2)}) copy-start(pred[128]{0:T(512)(128)(4,1)S(1)} %iota_compare_fusion.3) | copy-start | bytes 388
  11.3 81.2 %copy-start.27 = (f32[128]{0:T(128)}, f32[128]{0:T(128)S(1)}, u32[]{:S(2)}) copy-start(f32[128]{0:T(128)S(1)} %fusion.57) | copy-start | bytes 1540
  11.3 81.2 %copy-start.29 = (pred[128]{0:T(512)(128)(4,1)}, pred[128]{0:T(512)(128)(4,1)S(1)}, u32[]{:S(2)}) copy-start(pred[128]{0:T(512)(128)(4,1)S(1)} %get-tuple-element.122) | copy-start | bytes 388
  92.6 89.3 %copy-start.1 = (bf16[2,1,64,1536]{3,2,1,0:T(8,128)(2,1)S(1)}, bf16[2,1,64,1536]{3,2,1,0:T(8,128)(2,1)}, u32[]{:S(2)}) copy-start(bf16[2,1,64,1536]{3,2,1,0:T(8,128)(2,1)} %param.12) | copy-start | bytes 1179652
  92.6 92.7 %all-gather.10.cloned.1.call-start = ((), (), s32[]{:S(2)}) async-start(), calls=%async_computation.14 | async-start | bytes 1966080 | tf_op jit(solution)/shard_map/all_gather | solution.py:800
  93.5 16.3 %collective-permute-start.2 = (bf16[128,1536]{1,0:T(8,128)(2,1)S(1)}, bf16[128,1536]{1,0:T(8,128)(2,1)S(1)}, u32[]{:S(2)}, u32[]{:S(2)}) collective-permute-start(bf16[128,1536]{1,0:T(8,128)(2,1)S(1)} %copy-done.40), channel_id=1, source_target_pairs={{0,0},{1,1},{2,2},{3,3},{8,4},{9,5},{10,6},{11,7},{16,8},{17,9},{1... | collective-permute-start | bytes 1179656 | tf_op jit(solution)/shard_map/ppermute | solution.py:800
  110.6 88.3 %all-gather.12.cloned.1.call-start = ((), (), s32[]{:S(2)}) async-start(), calls=%async_computation.16 | async-start | bytes 3538944 | tf_op jit(solution)/shard_map/all_gather | solution.py:761
  111.2 133.2 %all-gather.8.cloned.1.call-start = ((), (), s32[]{:S(2)}) async-start(), calls=%async_computation.13 | async-start | bytes 3932160 | tf_op jit(solution)/shard_map/all_gather | solution.py:799
  111.2 1.8 collective-permute-start.1
  113.9 170.6 %all-gather.6.cloned.1.call-start = ((), (), s32[]{:S(2)}) async-start(), calls=%async_computation.12 | async-start | bytes 3538944 | tf_op jit(solution)/shard_map/all_gather | solution.py:761
  183.1 184.5 %copy-start.23 = (f32[128]{0:T(128)}, f32[128]{0:T(128)S(1)}, u32[]{:S(2)}) copy-start(f32[128]{0:T(128)S(1)} %get-tuple-element.115) | copy-start | bytes 1540
  183.1 184.5 %copy-start.33 = (f32[128]{0:T(128)}, f32[128]{0:T(128)S(1)}, u32[]{:S(2)}) copy-start(f32[128]{0:T(128)S(1)} %get-tuple-element.114) | copy-start | bytes 1540
  185.0 180.6 %reduce-scatter.18.cloned.1.call-start = ((), (), s32[]{:S(2)}) async-start(), calls=%async_computation.17 | async-start | bytes 3538944 | tf_op jit(solution)/shard_map/reduce_scatter | solution.py:765
  299.2 109.4 %all-gather.14.cloned.1.call-start = ((), (), s32[]{:S(2)}) async-start(), calls=%async_computation.18 | async-start | bytes 3538944 | tf_op jit(solution)/shard_map/all_gather | solution.py:761
  369.7 119.5 %reduce-scatter.24.cloned.1.call-start = ((), (), s32[]{:S(2)}) async-start(), calls=%async_computation.21 | async-start | bytes 3932160 | tf_op jit(solution)/shard_map/reduce_scatter | solution.py:874
  414.3 12.2 %all-to-all-start = ((bf16[4,2,4,64,128]{4,3,2,1,0:T(8,128)(2,1)}), bf16[4,2,4,64,128]{4,3,2,1,0:T(8,128)(2,1)S(1)}, u32[]{:S(2)}, u32[]{:S(2)}) async-start(bf16[4,2,4,64,128]{4,3,2,1,0:T(8,128)(2,1)} %bitcast.14), calls=%async_computation.3 | async-start | bytes 1048576 | tf_op jit(solution)/shard_map/all_to_all | solution.py:811
  418.1 73.1 %reduce-scatter.26.cloned.1.call-start = ((), (), s32[]{:S(2)}) async-start(), calls=%async_computation.22 | async-start | bytes 1966080 | tf_op jit(solution)/shard_map/reduce_scatter | solution.py:874
  423.3 81.0 %reduce-scatter.30.cloned.1.call-start = ((), (), s32[]{:S(2)}) async-start(), calls=%async_computation.24 | async-start | bytes 1474560
  473.8 60.9 %reduce-scatter.22.cloned.1.call-start = ((), (), s32[]{:S(2)}) async-start(), calls=%async_computation.20 | async-start | bytes 737280 | tf_op jit(solution)/shard_map/reduce_scatter | solution.py:874
  477.8 126.4 %reduce-scatter.20.cloned.1.call-start = ((), (), s32[]{:S(2)}) async-start(), calls=%async_computation.19 | async-start | bytes 3538944 | tf_op jit(solution)/shard_map/reduce_scatter | solution.py:765
  483.0 191.5 %reduce-scatter.16.cloned.1.call-start = ((), (), s32[]{:S(2)}) async-start(), calls=%async_computation.15 | async-start | bytes 3538944 | tf_op jit(solution)/shard_map/reduce_scatter | solution.py:765
  489.1 285.8 %reduce-scatter.28.cloned.1.call-start = ((), (), s32[]{:S(2)}) async-start(), calls=%async_computation.23 | async-start | bytes 811008
  489.2 51.4 %collective-permute-start.5 = (bf16[1536,256]{1,0:T(8,128)(2,1)}, bf16[1536,256]{1,0:T(8,128)(2,1)S(1)}, u32[]{:S(2)}, u32[]{:S(2)}) collective-permute-start(bf16[1536,256]{1,0:T(8,128)(2,1)} %reduce-scatter.24.cloned.1.call-done), channel_id=1, source_target_pairs={{0,0},{1,1},{2,16},{3,17},{4,4},{5,5},{6,20},{7,21},{8,8},{9,9},{1... | collective-permute-start | bytes 2359304 | tf_op jit(solution)/shard_map/ppermute | solution.py:876
  491.2 48.5 %collective-permute-start.6 = (bf16[128,1536]{1,0:T(8,128)(2,1)}, bf16[128,1536]{1,0:T(8,128)(2,1)S(1)}, u32[]{:S(2)}, u32[]{:S(2)}) collective-permute-start(bf16[128,1536]{1,0:T(8,128)(2,1)} %reduce-scatter.26.cloned.1.call-done), channel_id=1, source_target_pairs={{0,0},{1,1},{2,2},{3,3},{4,8},{5,9},{6,10},{7,11},{8,16},{9,17},{1... | collective-permute-start | bytes 1179656 | tf_op jit(solution)/shard_map/ppermute | solution.py:876
  504.3 39.7 %collective-permute-start.3 = (bf16[1,1536,96]{1,2,0:T(8,128)(2,1)}, bf16[1,1536,96]{1,2,0:T(8,128)(2,1)S(1)}, u32[]{:S(2)}, u32[]{:S(2)}) collective-permute-start(bf16[1,1536,96]{1,2,0:T(8,128)(2,1)} %reduce-scatter.30.cloned.1.call-done), channel_id=1, source_target_pairs={{0,0},{1,1},{16,2},{17,3},{4,4},{5,5},{20,6},{21,7},{8,8},{9,9},{2... | collective-permute-start | bytes 884744 | tf_op jit(solution)/shard_map/ppermute | solution.py:876
  534.6 8.6 %collective-permute-start.4 = (bf16[48,1536]{1,0:T(8,128)(2,1)}, bf16[48,1536]{1,0:T(8,128)(2,1)S(1)}, u32[]{:S(2)}, u32[]{:S(2)}) collective-permute-start(bf16[48,1536]{1,0:T(8,128)(2,1)} %reduce-scatter.22.cloned.1.call-done), channel_id=1, source_target_pairs={{0,0},{1,1},{2,2},{3,3},{4,8},{5,9},{6,10},{7,11},{8,16},{9,17},{1... | collective-permute-start | bytes 442376 | tf_op jit(solution)/shard_map/ppermute | solution.py:876
  540.6 133.9 %copy-start.5 = (bf16[128,1536]{1,0:T(8,128)(2,1)S(1)}, bf16[128,1536]{1,0:T(8,128)(2,1)}, u32[]{:S(2)}) copy-start(bf16[128,1536]{1,0:T(8,128)(2,1)} %reduce-scatter.18.cloned.1.call-done) | copy-start | bytes 1179652
  540.6 133.9 %copy-start.24 = (f32[128]{0:T(128)S(1)}, f32[128]{0:T(128)}, u32[]{:S(2)}) copy-start(f32[128]{0:T(128)} %copy-done.23) | copy-start | bytes 1540
  540.6 133.9 %copy-start.34 = (f32[128]{0:T(128)S(1)}, f32[128]{0:T(128)}, u32[]{:S(2)}) copy-start(f32[128]{0:T(128)} %copy-done.33) | copy-start | bytes 1540
  540.6 133.9 %copy-start.36 = (f32[128]{0:T(128)S(1)}, f32[128]{0:T(128)}, u32[]{:S(2)}) copy-start(f32[128]{0:T(128)} %copy-done.35) | copy-start | bytes 1540
  (35 other events, 359.9 us)
Sparse Core Ops, SparseCore 0:
  92.7 89.0 reduce-scatter.13
  299.3 66.3 reduce-scatter.17
  369.8 38.7 all-gather.13
Sparse Core Ops, SparseCore 1:
  110.6 41.1 all-gather.9
  153.3 45.5 all-gather.11
  201.1 43.2 all-gather.7
  246.6 37.9 all-gather.5
  377.6 44.6 reduce-scatter.23
  425.8 41.7 reduce-scatter.25
  473.8 30.4 reduce-scatter.29
  507.6 26.9 reduce-scatter.21
  536.8 67.3 reduce-scatter.19
  606.5 67.9 reduce-scatter.15
  679.4 95.4 reduce-scatter.27

commit v3 on v2

--- a/solution.py
+++ b/solution.py
@@ -403,8 +403,7 @@
             self.down(self.own, c).start()
 
         self.across(self.own, c).start()
-        if self.local is not None:
-            pltpu.make_async_copy(self.own, self.slot(c), self.local).start()
+        pltpu.make_async_copy(self.own, self.slot(c), self.local).start()
 
     def forward(self, k):
         c = self.c
@@ -429,10 +428,29 @@
 
             self.across(self.slot(c + k), c + k).start()
 
+    def take(self, at):
+        c = self.c
+
+        @pl.when(at != c)
+        def _():
+            arrived(self.slot(at), self.recv.at[self.d, at], at_device(self.d, c, self.f))
+
+            @pl.when(jnp.logical_and(at < c, c < self.n - 1))
+            def _():
+                self.up(self.slot(at), at).start()
+
+            @pl.when(jnp.logical_and(at > c, c > 0))
+            def _():
+                self.down(self.slot(at), at).start()
+
+            self.across(self.slot(at), at).start()
+
+        self.other(at)
+
     def other(self, at):
         arrived(self.whole.at[1 - self.d, at], self.recv.at[1 - self.d, at], at_device(self.d, self.c, self.f))
 
-    def finish(self):
+    def finish_sends(self):
         c = self.c
         for at in range(self.n):
 
@@ -445,8 +463,10 @@
                 left(self.slot(at), self.send.at[1, at], at_device(self.d, c, self.f))
 
             left(self.slot(at), self.send.at[2, at], at_device(self.d, c, self.f))
-        if self.local is not None:
-            pltpu.make_async_copy(self.own, self.slot(c), self.local).wait()
+
+    def finish(self):
+        self.finish_sends()
+        pltpu.make_async_copy(self.own, self.slot(self.c), self.local).wait()
 
 
 FACTOR = HD ** (-0.5)
@@ -463,10 +483,11 @@
 
 
 def first_kernel(
-    sizes, x_ref, gains_ref, w_ref, cos_ref, sin_up_ref, sin_down_ref,
-    normed_out, unit_out, att_out, wide_out, gains_out,
+    sizes, x_ref, gains_ref, w_ref, cos_ref, sin_up_ref, sin_down_ref, dy_ref, proj_ref, down_ref,
+    normed_out, unit_out, att_out, wide_out, gains_out, dy_all, proj_all, down_all,
     x_all, w_all, wide, normed, stage, unit, att_stage, att, gain_all, gain_vec,
     line_send, line_recv, line_local, w_send, w_recv, w_pass, g_send, g_recv, u_send, u_recv, a_send, a_recv, out_sem,
+    dy_send, dy_recv, dy_local, m_send, m_recv, m_pass,
 ):
     dp, ctx, fs = sizes
     n = dp * ctx * fs
@@ -554,21 +575,7 @@
     def block(step, carry):
         at = ordered(c, step, ctx)
 
-        @pl.when(at != c)
-        def _():
-            arrived(line.slot(at), line_recv.at[d, at], here)
-
-            @pl.when(jnp.logical_and(at < c, c < ctx - 1))
-            def _():
-                line.up(line.slot(at), at).start()
-
-            @pl.when(jnp.logical_and(at > c, c > 0))
-            def _():
-                line.down(line.slot(at), at).start()
-
-            line.across(line.slot(at), at).start()
-
-        line.other(at)
+        line.take(at)
         values = x_all[:, at].reshape(dp * 2 * span, D).astype(jnp.float32)
         scale = lax.rsqrt(jnp.mean(values * values, axis=-1, keepdims=True) + EPS)
         low = (values * scale * gain).astype(jnp.bfloat16)
@@ -604,6 +611,29 @@
     normed_copy.start()
     wide_copy.start()
     gains_copy.start()
+
+    to_core, to_ctx = lax.rem(c, 2), 2 * d + c // 2
+    stays = jnp.logical_and(to_core == d, to_ctx == c)
+    moved = ((proj_ref, proj_all), (down_ref, down_all))
+    for index, (shard, whole) in enumerate(moved):
+
+        @pl.when(jnp.logical_not(stays))
+        def _():
+            remote(shard, whole.at[f], m_send.at[index], m_recv.at[index, f], at_device(to_core, to_ctx, f)).start()
+
+        @pl.when(stays)
+        def _():
+            pltpu.make_async_copy(shard, whole.at[f], m_recv.at[index, f]).start()
+
+    dy_line = LineGather(ctx, dy_ref, dy_all, dy_send, dy_recv, dy_local)
+    dy_line.start()
+
+    def pass_on():
+        for index, (shard, whole) in enumerate(moved):
+            arrived(whole.at[f], m_recv.at[index, f], here)
+            for step in range(1, fs):
+                to = lax.rem(f + step, fs)
+                remote(whole.at[f], whole.at[f], m_pass.at[index, step], m_recv.at[index, f], at_device(d, c, to)).start()
 
     for at in range(ctx):
         for step in range(1, fs):
@@ -641,6 +671,11 @@
             def _():
                 att[f // 2, at, lax.rem(f, 2)] = att_stage[at, to]
 
+        if at == 0:
+            pass_on()
+        else:
+            dy_line.forward(at)
+
     for at in range(ctx):
         for step in range(1, fs):
             other = lax.rem(f + step, fs)
@@ -649,16 +684,21 @@
     att_copy.start()
 
     for at in range(ctx):
-
-        @pl.when(jnp.logical_and(at <= c, c < ctx - 1))
-        def _():
-            left(line.slot(at), line_send.at[0, at], here)
-
-        @pl.when(jnp.logical_and(at >= c, c > 0))
-        def _():
-            left(line.slot(at), line_send.at[1, at], here)
-
-        left(line.slot(at), line_send.at[2, at], here)
+        dy_line.other(at)
+    dy_line.finish()
+    for index, (shard, whole) in enumerate(moved):
+        for step in range(1, fs):
+            other = lax.rem(f + step, fs)
+            arrived(whole.at[other], m_recv.at[index, other], here)
+            left(whole.at[f], m_pass.at[index, step], here)
+
+        @pl.when(jnp.logical_not(stays))
+        def _():
+            left(shard, m_send.at[index], here)
+
+    line.finish_sends()
+    for at in range(ctx):
+
         for to in range(fs):
 
             @pl.when(to != f)
@@ -694,7 +734,7 @@
         copy.wait()
 
 
-def first(sizes, x, gains, w_qkv, cosine, sine_up, sine_down):
+def first(sizes, x, gains, w_qkv, cosine, sine_up, sine_down, dy, w_out, w_down):
     dp, ctx, fs = sizes
     n = dp * ctx * fs
     rows = x.shape[0]
@@ -707,14 +747,17 @@
         jax.ShapeDtypeStruct((dp, ctx, 2, span, 2 * LANES), low),
         jax.ShapeDtypeStruct((D, 4 * LANES), low),
         jax.ShapeDtypeStruct((8, D), wide_t),
+        jax.ShapeDtypeStruct((dp, ctx, rows, D), low),
+        jax.ShapeDtypeStruct((fs,) + w_out.shape, low),
+        jax.ShapeDtypeStruct((fs,) + w_down.shape, low),
     )
     any_spec, vm_spec = pl.BlockSpec(memory_space=ANY), pl.BlockSpec(memory_space=VM)
     return pl.pallas_call(
         functools.partial(first_kernel, sizes),
         name="first",
         out_shape=shapes,
-        in_specs=[vm_spec, vm_spec, any_spec, vm_spec, vm_spec, vm_spec],
-        out_specs=[any_spec] * 5,
+        in_specs=[vm_spec, vm_spec, any_spec, vm_spec, vm_spec, vm_spec, vm_spec, any_spec, any_spec],
+        out_specs=[any_spec] * 8,
         scratch_shapes=[
             VM((dp, ctx, rows, D), low),
             VM((4, D, HD), low),
@@ -732,9 +775,11 @@
             dma((ctx, 2 * dp)), dma((ctx, fs)),
             dma((ctx, fs)), dma((fs, ctx)),
             dma((5,)),
+            dma((3, ctx)), dma((dp, ctx)), dma,
+            dma((2,)), dma((2, fs)), dma((2, fs)),
         ],
         compiler_params=pltpu.CompilerParams(collective_id=1, has_side_effects=True, vmem_limit_bytes=60 * 1024 * 1024),
-    )(x, gains, w_qkv, cosine, sine_up, sine_down)
+    )(x, gains, w_qkv, cosine, sine_up, sine_down, dy, w_out, w_down)
 
 
 def angle_tables(ctx, fs, span):
@@ -757,6 +802,375 @@
     return cosine, sine_up, sine_down
 
 
+class LineSum:
+    def __init__(self, n, mine, out_core, in_core, out_line, in_line, total, sems):
+        self.n, self.mine, self.out_core, self.in_core = n, mine, out_core, in_core
+        self.out_line, self.in_line, self.total = out_line, in_line, total
+        self.core_send, self.core_recv, self.line_send, self.line_recv = sems
+        self.d, self.c, self.f = place()
+        self.here = at_device(self.d, self.c, self.f)
+
+    def give(self, at, both):
+        d = self.d
+        low = both.astype(jnp.bfloat16)
+
+        @pl.when(d == 0)
+        def _():
+            self.mine[at] = low[0]
+            self.out_core[at] = low[1]
+
+        @pl.when(d != 0)
+        def _():
+            self.mine[at] = low[1]
+            self.out_core[at] = low[0]
+
+        remote(
+            self.out_core.at[at], self.in_core.at[at], self.core_send.at[at], self.core_recv.at[at], at_device(1 - d, self.c, self.f)
+        ).start()
+
+    def step(self, at):
+        n, d, c, f = self.n, self.d, self.c, self.f
+        arrived(self.in_core.at[at], self.core_recv.at[at], self.here)
+        self.total[...] = self.mine[at].astype(jnp.float32) + self.in_core[at].astype(jnp.float32)
+
+        @pl.when(jnp.logical_and(at <= c, c < n - 1))
+        def _():
+            arrived(self.in_line.at[0, at], self.line_recv.at[0, at], self.here)
+            self.total[...] += self.in_line[0, at].astype(jnp.float32)
+
+        @pl.when(jnp.logical_and(at >= c, c > 0))
+        def _():
+            arrived(self.in_line.at[1, at], self.line_recv.at[1, at], self.here)
+            self.total[...] += self.in_line[1, at].astype(jnp.float32)
+
+        @pl.when(at != c)
+        def _():
+            self.out_line[at] = self.total[...].astype(jnp.bfloat16)
+
+        @pl.when(at < c)
+        def _():
+            remote(
+                self.out_line.at[at], self.in_line.at[0, at], self.line_send.at[at], self.line_recv.at[0, at], at_device(d, c - 1, f)
+            ).start()
+
+        @pl.when(at > c)
+        def _():
+            remote(
+                self.out_line.at[at], self.in_line.at[1, at], self.line_send.at[at], self.line_recv.at[1, at], at_device(d, c + 1, f)
+            ).start()
+
+    def finish(self):
+        for at in range(self.n):
+            left(self.out_core.at[at], self.core_send.at[at], self.here)
+
+            @pl.when(at != self.c)
+            def _():
+                left(self.out_line.at[at], self.line_send.at[at], self.here)
+
+    @staticmethod
+    def scratch(ctx, rows):
+        low = jnp.bfloat16
+        dma = pltpu.SemaphoreType.DMA
+        return [
+            VM((ctx, rows, D), low), VM((ctx, rows, D), low), VM((ctx, rows, D), low), VM((ctx, rows, D), low),
+            VM((2, ctx, rows, D), low), VM((rows, D), jnp.float32),
+            dma((ctx,)), dma((ctx,)), dma((ctx,)), dma((2, ctx)),
+        ]
+
+
+def greet_near(sizes):
+    dp, ctx, fs = sizes
+    d, c, f = place()
+    barrier = pltpu.get_barrier_semaphore()
+
+    def tell(device):
+        pl.semaphore_signal(barrier, inc=1, device_id=device, device_id_type=MESH)
+
+    tell(at_device(1 - d, c, f))
+    for step in range(1, fs):
+        for core in range(dp):
+            tell(at_device(core, c, lax.rem(f + step, fs)))
+
+    @pl.when(c > 0)
+    def _():
+        tell(at_device(d, c - 1, f))
+
+    @pl.when(c < ctx - 1)
+    def _():
+        tell(at_device(d, c + 1, f))
+
+    known = 1 + dp * (fs - 1)
+    ends = jnp.logical_or(c == 0, c == ctx - 1)
+
+    @pl.when(ends)
+    def _():
+        pl.semaphore_wait(barrier, known + 1)
+
+    @pl.when(jnp.logical_not(ends))
+    def _():
+        pl.semaphore_wait(barrier, known + 2)
+
+
+def middle_kernel(
+    sizes, hidden, att_ref, x_ref, dy_ref, gains_ref, proj_ref, down_ref, gate_up_ref, dy_all_ref,
+    resid_out, d_resid_out, gain_out, partial_out, unit_out, grad_up_out, grad_down_out, grad_proj_out,
+    att, dy_all, proj, down, gate_up, resid, own_two, normed_two, act, d_both, part_stage, own_d, d_resid_all, d_stage, unit,
+    grad_up, grad_down, grad_proj,
+    in_sem, gu_send, gu_recv, two_send, two_recv, two_local, dr_send, dr_recv, dr_local, u_send, u_recv, out_sem, part_sem,
+    *sums,
+):
+    dp, ctx, fs = sizes
+    d, c, f = place()
+    here = at_device(d, c, f)
+    rows = x_ref.shape[0]
+    span = rows // 2
+    both_rows = dp * rows
+    half = hidden // 2
+    line_sum = LineSum(ctx, *sums[:6], sums[6:10])
+    second_sum = LineSum(ctx, *sums[10:16], sums[16:20])
+
+    att_copy = pltpu.make_async_copy(att_ref, att, in_sem.at[0])
+    dy_copy = pltpu.make_async_copy(dy_all_ref, dy_all, in_sem.at[1])
+    down_copy = pltpu.make_async_copy(down_ref, down, in_sem.at[2])
+    att_copy.start()
+    proj[...] = jnp.zeros_like(proj)
+    each = proj_ref.shape[1]
+    proj_copies = []
+    for slot in range(fs):
+        start = slot // 2 * LANES + slot % 2 * each
+        proj_copies.append(pltpu.make_async_copy(proj_ref.at[slot], proj.at[start : start + each], in_sem.at[3 + slot]))
+        proj_copies[-1].start()
+    dy_copy.start()
+    down_copy.start()
+    greet_near(sizes)
+
+    to_core = f // 2
+    gu_slot = 2 * d + lax.rem(f, 2)
+    for to in range(fs):
+        own_place = jnp.logical_and(to_core == d, f == to)
+
+        @pl.when(jnp.logical_not(own_place))
+        def _():
+            remote(gate_up_ref, gate_up.at[gu_slot], gu_send.at[to], gu_recv.at[gu_slot], at_device(to_core, c, to)).start()
+
+        @pl.when(own_place)
+        def _():
+            pltpu.make_async_copy(gate_up_ref, gate_up.at[gu_slot], gu_recv.at[gu_slot]).start()
+
+    att_copy.wait()
+    for copy in proj_copies:
+        copy.wait()
+
+    def project(step, carry):
+        at = ordered(c, ctx - 1 - step, ctx)
+        terms = jnp.dot(att[:, at].reshape(both_rows, 2 * LANES), proj[...], preferred_element_type=jnp.float32)
+        line_sum.give(at, terms.reshape(dp, rows, D))
+        return carry
+
+    lax.fori_loop(0, ctx, project, 0)
+
+    def sum_up(step, carry):
+        line_sum.step(ordered(c, ctx - 1 - step, ctx))
+        return carry
+
+    lax.fori_loop(0, ctx, sum_up, 0)
+    gain = gains_ref[1:2, :]
+    values = x_ref[...].astype(jnp.float32) + line_sum.total[...]
+    resid[...] = values
+    scale = lax.rsqrt(jnp.mean(values * values, axis=-1, keepdims=True) + EPS)
+    own_two[...] = (values * scale * gain).astype(jnp.bfloat16)
+    resid_copy = pltpu.make_async_copy(resid, resid_out, out_sem.at[0])
+    resid_copy.start()
+    line = LineGather(ctx, own_two, normed_two, two_send, two_recv, two_local)
+    line.start()
+    line_sum.finish()
+    for slot in range(4):
+        arrived(gate_up.at[slot], gu_recv.at[slot], here)
+    dy_copy.wait()
+    down_copy.wait()
+    pltpu.make_async_copy(line.own, line.slot(c), line.local).wait()
+
+    def mlp(step, carry):
+        at = ordered(c, step, ctx)
+
+        line.take(at)
+        inputs = normed_two[:, at].reshape(both_rows, D)
+        dy_rows = dy_all[:, at].reshape(both_rows, D)
+        for part in range(2):
+            cols = slice(part * half, (part + 1) * half)
+            gate = jnp.dot(inputs, gate_up[part], preferred_element_type=jnp.float32)
+            up = jnp.dot(inputs, gate_up[2 + part], preferred_element_type=jnp.float32)
+            d_act = outer(dy_rows, down[cols, :])
+            sig = 1.0 / (1.0 + jnp.exp(-gate))
+            silu = gate * sig
+            act[:, at, :, cols] = (silu * up).astype(jnp.bfloat16).reshape(dp, rows, half)
+            d_gate = d_act * up * (sig * (1.0 + gate * (1.0 - sig)))
+            d_both[:, at, :, cols] = d_gate.astype(jnp.bfloat16).reshape(dp, rows, half)
+            d_both[:, at, :, hidden + part * half : hidden + (part + 1) * half] = (
+                (d_act * silu).astype(jnp.bfloat16).reshape(dp, rows, half)
+            )
+        terms = outer(d_both[:, at, :, 0:half].reshape(both_rows, half), gate_up[0])
+        for part in range(1, 4):
+            terms += outer(d_both[:, at, :, part * half : (part + 1) * half].reshape(both_rows, half), gate_up[part])
+        second_sum.give(at, terms.reshape(dp, rows, D))
+        return carry
+
+    lax.fori_loop(0, ctx, mlp, 0)
+
+    wide_rows = D // ctx
+
+    def grads(step):
+        first = pl.multiple_of(step * wide_rows, LANES)
+        left_rows = normed_two[:, :, :, pl.ds(first, wide_rows)].reshape(dp * ctx * rows, wide_rows)
+        for part in range(2):
+            cols = slice(part * hidden, (part + 1) * hidden)
+            grad_up[pl.ds(first, wide_rows), cols] = inner(left_rows, d_both[:, :, :, cols].reshape(dp * ctx * rows, hidden)).astype(jnp.bfloat16)
+        dy_cols = dy_all[:, :, :, pl.ds(first, wide_rows)].reshape(dp * ctx * rows, wide_rows)
+        grad_down[:, pl.ds(first, wide_rows)] = inner(act[...].reshape(dp * ctx * rows, hidden), dy_cols).astype(jnp.bfloat16)
+
+    def sum_two(step, carry):
+        second_sum.step(ordered(c, ctx - 1 - step, ctx))
+
+        @pl.when(step < ctx - 1)
+        def _():
+            grads(step)
+
+        return carry
+
+    lax.fori_loop(0, ctx, sum_two, 0)
+    values = resid[...]
+    scale = lax.rsqrt(jnp.mean(values * values, axis=-1, keepdims=True) + EPS)
+    incoming = second_sum.total[...]
+    weighted = incoming * gain
+    mean = jnp.mean(weighted * values, axis=-1, keepdims=True)
+    d_resid = dy_ref[...].astype(jnp.float32) + scale * weighted - values * (scale * scale * scale) * mean
+    own_d[...] = d_resid.astype(jnp.bfloat16)
+    d_resid_out[...] = d_resid
+    gain_out[...] = jnp.broadcast_to(jnp.sum(incoming * values * scale, axis=0, keepdims=True), gain_out.shape)
+    d_line = LineGather(ctx, own_d, d_resid_all, dr_send, dr_recv, dr_local)
+    d_line.start()
+    line.finish_sends()
+    second_sum.finish()
+    grads(ctx - 1)
+    grad_up_copy = pltpu.make_async_copy(grad_up, grad_up_out, out_sem.at[1])
+    grad_down_copy = pltpu.make_async_copy(grad_down, grad_down_out, out_sem.at[2])
+    grad_up_copy.start()
+    grad_down_copy.start()
+    pltpu.make_async_copy(d_line.own, d_line.slot(c), d_line.local).wait()
+    grad_proj[...] = jnp.zeros_like(grad_proj)
+
+    def back(step, carry):
+        at = ordered(c, step, ctx)
+
+        d_line.take(at)
+        incoming = d_resid_all[:, at].reshape(both_rows, D)
+        d_att = outer(incoming, proj[...]).astype(jnp.bfloat16)
+        d_stage[at] = d_att.reshape(2 * dp, span, 2 * LANES)
+        for to in range(2 * dp):
+
+            @pl.when(to != f)
+            def _():
+                remote(d_stage.at[at, to], unit.at[at, f], u_send.at[at, to], u_recv.at[at, f], at_device(d, c, to)).start()
+
+            @pl.when(to == f)
+            def _():
+                unit[at, f] = d_stage[at, to]
+
+        grad_proj[...] += inner(att[:, at].reshape(both_rows, 2 * LANES), incoming)
+
+        outputs = jnp.dot(act[:, at].reshape(both_rows, hidden), down[...], preferred_element_type=jnp.float32)
+        slot = lax.rem(step, 2)
+
+        @pl.when(step >= 2)
+        def _():
+            pltpu.make_async_copy(part_stage.at[slot], partial_out.at[:, at], part_sem.at[slot]).wait()
+
+        part_stage[slot] = outputs.reshape(dp, rows, D).astype(jnp.bfloat16)
+        pltpu.make_async_copy(part_stage.at[slot], partial_out.at[:, at], part_sem.at[slot]).start()
+        return carry
+
+    lax.fori_loop(0, ctx, back, 0)
+    grad_proj_copy = pltpu.make_async_copy(grad_proj, grad_proj_out, out_sem.at[3])
+    grad_proj_copy.start()
+    for at in range(ctx):
+        for step in range(1, fs):
+            other = lax.rem(f + step, fs)
+            arrived(unit.at[at, other], u_recv.at[at, other], here)
+    unit_copy = pltpu.make_async_copy(unit, unit_out, out_sem.at[4])
+    unit_copy.start()
+    d_line.finish_sends()
+    for at in range(ctx):
+        for to in range(fs):
+
+            @pl.when(to != f)
+            def _():
+                left(d_stage.at[at, to], u_send.at[at, to], here)
+
+    for to in range(fs):
+
+        @pl.when(jnp.logical_not(jnp.logical_and(to_core == d, f == to)))
+        def _():
+            left(gate_up_ref, gu_send.at[to], here)
+
+    for slot in range(2):
+        pltpu.make_async_copy(part_stage.at[slot], partial_out.at[:, 0], part_sem.at[slot]).wait()
+    for copy in (resid_copy, grad_up_copy, grad_down_copy, grad_proj_copy, unit_copy):
+        copy.wait()
+
+
+def middle(sizes, att, x, dy, gains, proj, down, w_gate_up, dy_all):
+    dp, ctx, fs = sizes
+    rows = x.shape[0]
+    span = rows // 2
+    hidden = FF // (dp * ctx)
+    low, wide_t = jnp.bfloat16, jnp.float32
+    dma = pltpu.SemaphoreType.DMA
+    any_spec, vm_spec = pl.BlockSpec(memory_space=ANY), pl.BlockSpec(memory_space=VM)
+    shapes = (
+        jax.ShapeDtypeStruct((rows, D), wide_t),
+        jax.ShapeDtypeStruct((rows, D), wide_t),
+        jax.ShapeDtypeStruct((8, D), wide_t),
+        jax.ShapeDtypeStruct((dp, ctx, rows, D), low),
+        jax.ShapeDtypeStruct((ctx, fs, span, 2 * LANES), low),
+        jax.ShapeDtypeStruct((D, 2 * hidden), low),
+        jax.ShapeDtypeStruct((hidden, D), low),
+        jax.ShapeDtypeStruct((2 * LANES, D), wide_t),
+    )
+    return pl.pallas_call(
+        functools.partial(middle_kernel, sizes, hidden),
+        name="middle",
+        out_shape=shapes,
+        in_specs=[any_spec, vm_spec, vm_spec, vm_spec, any_spec, any_spec, any_spec, any_spec],
+        out_specs=[any_spec, vm_spec, vm_spec] + [any_spec] * 5,
+        scratch_shapes=[
+            VM((dp, ctx, rows, 2 * LANES), low),
+            VM((dp, ctx, rows, D), low),
+            VM((2 * LANES, D), low),
+            VM((hidden, D), low),
+            VM((4, D, hidden // 2), low),
+            VM((rows, D), wide_t),
+            VM((rows, D), low),
+            VM((dp, ctx, rows, D), low),
+            VM((dp, ctx, rows, hidden), low),
+            VM((dp, ctx, rows, 2 * hidden), low),
+            VM((2, dp, rows, D), low),
+            VM((rows, D), low),
+            VM((dp, ctx, rows, D), low),
+            VM((ctx, 2 * dp, span, 2 * LANES), low),
+            VM((ctx, fs, span, 2 * LANES), low),
+            VM((D, 2 * hidden), low),
+            VM((hidden, D), low),
+            VM((2 * LANES, D), wide_t),
+            dma((3 + fs,)), dma((fs,)), dma((4,)),
+            dma((3, ctx)), dma((dp, ctx)), dma,
+            dma((3, ctx)), dma((dp, ctx)), dma,
+            dma((ctx, 2 * dp)), dma((ctx, fs)),
+            dma((5,)), dma((2,)),
+        ] + LineSum.scratch(ctx, rows) + LineSum.scratch(ctx, rows),
+        compiler_params=pltpu.CompilerParams(collective_id=2, has_side_effects=True, vmem_limit_bytes=63 * 1024 * 1024),
+    )(att, x, dy, gains, proj, down.reshape(hidden, D), w_gate_up, dy_all)
+
+
 def gather_tp(value):
     return lax.all_gather(value, TP, axis=0, tiled=True)
 
@@ -788,21 +1202,25 @@
     gain_rows = gain_rows.at[0, : attn_gain.shape[0]].set(attn_gain.astype(jnp.float32))
     gain_rows = gain_rows.at[1, : mlp_gain.shape[0]].set(mlp_gain.astype(jnp.float32))
     cosine, sine_up, sine_down = angle_tables(ctx, fs, span)
-    normed, unit, att, qkv, gains = first((dp, ctx, fs), x_low, gain_rows, w_qkv, cosine, sine_up, sine_down)
+    dy = cotangent.reshape(rows, D)
+    where = (dp, ctx, fs)
+    normed, unit, att, qkv, gains, dy_all, proj, down = first(
+        where, x_low, gain_rows, w_qkv, cosine, sine_up, sine_down, dy, w_out, w_down
+    )
+    att = att.reshape(dp, ctx, rows, 2 * LANES)
+    resid, d_resid, grad_two, partial, d_unit, grad_gate_up, grad_down, grad_out = middle(
+        where, att, x_low, dy, gains, proj, down, w_gate_up, dy_all
+    )
+    block_out = (resid + sum_tp(partial.reshape(dp * ctx * rows, D))).astype(jnp.bfloat16)
+    grad_two = grad_two[0]
+    grad_out = grad_out.reshape(2, LANES, D)[:, :HD].reshape(2 * HD, D)
+    d_unit = jnp.moveaxis(d_unit.reshape(length, 2, LANES), 1, 0)
     gain_one, gain_two = gains[0], gains[1]
     normed = normed.reshape(dp * ctx * rows, D)
     unit = unit.reshape(length, 4, LANES)
-    attended = att.reshape(dp * ctx * rows, 2 * LANES)
-
-    out_w = lax.all_gather(lax.ppermute(w_out, ALL, down_owner(sizes)), "fsdp", axis=0, tiled=True)
-    out_w = jnp.pad(out_w.reshape(2, HD, D), ((0, 0), (0, LANES - HD), (0, 0))).reshape(2 * LANES, D)
-    gate_up = lax.all_gather(lax.ppermute(w_gate_up, ALL, up_owner(sizes)), "fsdp", axis=1, tiled=True)
-    down = lax.all_gather(lax.ppermute(w_down, ALL, down_owner(sizes)), "fsdp", axis=0, tiled=True)
 
     x = x_low.astype(jnp.float32)
-    dy = cotangent.reshape(rows, D)
     scale_one = lax.rsqrt(jnp.mean(x * x, axis=-1, keepdims=True) + EPS)
-    dy_all = gather_tp(dy)
 
     def to_units(values):
         count = values.shape[0]
@@ -827,30 +1245,6 @@
     weights = jnp.where(allowed, jnp.exp(scores - best), 0.0)
     probs = weights / jnp.sum(weights, axis=-1, keepdims=True)
     probs_low = probs.astype(jnp.bfloat16)
-    partial = dot(attended, out_w)
-    resid = x + sum_tp(partial)
-    scale_two = lax.rsqrt(jnp.mean(resid * resid, axis=-1, keepdims=True) + EPS)
-    normed_two = gather_tp((resid * scale_two * gain_two).astype(jnp.bfloat16))
-    gate = dot(normed_two, gate_up[:, :hidden])
-    up = dot(normed_two, gate_up[:, hidden:])
-    sig = 1.0 / (1.0 + jnp.exp(-gate))
-    silu = gate * sig
-    act = (silu * up).astype(jnp.bfloat16)
-    block_out = (resid + sum_tp(dot(act, down))).astype(jnp.bfloat16)
-
-    grad_down = inner(act, dy_all)
-    d_act = outer(dy_all, down)
-    d_gate = d_act * up * (sig * (1.0 + gate * (1.0 - sig)))
-    d_up = d_act * silu
-    d_both = jnp.concatenate([d_gate, d_up], axis=1).astype(jnp.bfloat16)
-    grad_gate_up = inner(normed_two, d_both)
-    d_two = sum_tp(outer(d_both, gate_up))
-    grad_two = jnp.sum(d_two * resid * scale_two, axis=0)
-    d_resid = dy.astype(jnp.float32) + norm_back(resid, scale_two, gain_two, d_two)
-    d_resid_all = gather_tp(d_resid.astype(jnp.bfloat16))
-    grad_out = inner(attended, d_resid_all).reshape(2, LANES, D)[:, :HD].reshape(2 * HD, D)
-    d_att = outer(d_resid_all, out_w).astype(jnp.bfloat16)
-    d_unit = to_units(jnp.moveaxis(d_att.reshape(dp, ctx, mb, span, 2, LANES), 4, 0))
     d_probs = jnp.einsum("hqd,kd->hqk", d_unit, v, preferred_element_type=jnp.float32)
     delta = jnp.sum(probs * d_probs, axis=-1, keepdims=True)
     d_scores = (probs * (d_probs - delta)).astype(jnp.bfloat16)

time: 796 us -> 698 us (0.88)
  Pallas kernels: 65 us -> 240 us
  waiting for transfers between devices: 522 us -> 356 us
  matrix products: 68.3 us -> 25.2 us
  blocking collectives: 27.2 us -> 0 us
  starting transfers between devices: 27.8 us -> 17.4 us
  other arithmetic: 32.1 us -> 22.3 us
    pallas_call x0 -> x1, Pallas kernels: none -> 148 us  [middle(): pl.pallas_call(functools.partial(middle_kernel, sizes, hidden), name='mid...]
    reduce_scatter x4 -> x2, waiting for transfers between devices: 260 us -> 136 us  [sum_tp(): lax.psum_scatter(value.astype(jnp.bfloat16), TP, scatter_dimension=0, til...]
    all_gather x5 -> x0, waiting for transfers between devices: 110 us -> none  [the longest x3 70 us: gather_tp(): return lax.all_gather(value, TP, axis=0, tiled=True)]
    reduce_scatter x3, waiting for transfers between devices: 27.2 us -> 76.9 us  [reduce_rows(): lax.psum_scatter(value.astype(jnp.bfloat16), 'fsdp', scatter_dimension=di...]
    pallas_call x1, Pallas kernels: 65 us -> 92.3 us  [first(): pl.pallas_call(functools.partial(first_kernel, sizes), name='first', out_...]
    all_to_all x1 -> x0, blocking collectives: 19.5 us -> none  [to_rows(): lax.all_to_all(values, 'fsdp', split_axis=0, concat_axis=0, tiled=True)]
    dot_general x5 -> x0, matrix products: 18.4 us -> none  [the longest x4 16.5 us: dot(): return jnp.dot(left, right, preferred_element_type=jnp.float32)]
    unnamed x16 -> x9, waiting for transfers between devices: 106 us -> 124 us
  transfers between devices with their start and end apart: 22 -> 12, of which waited for: 14 -> 9; matrix products, arithmetic and copies ran while one was open for 12% -> 3% of each run, Pallas kernels for 8% -> 0%
where the time goes in v3:
time: 698 us; the launch traced here: 694 us
  waiting for transfers between devices  356 us (51%)
  Pallas kernels  240 us (34%)
  matrix products  25.2 us (4%)
  other arithmetic  22.3 us (3%)
  local copies, waits for them, and re-layouts  18.1 us (3%)
  starting transfers between devices  17.4 us (2%)
  between operations  14.5 us (2%)
    pallas_call x1, Pallas kernels, middle(): pl.pallas_call(functools.partial(middle_kernel, sizes, hidden), name='mid...  148 us
    reduce_scatter x2, waiting for transfers between devices, sum_tp(): lax.psum_scatter(value.astype(jnp.bfloat16), TP, scatter_dimension=0, til...  136 us
    unnamed x9, waiting for transfers between devices  124 us
    pallas_call x1, Pallas kernels, first(): pl.pallas_call(functools.partial(first_kernel, sizes), name='first', out_...  92.3 us
    reduce_scatter x3, waiting for transfers between devices, reduce_rows(): lax.psum_scatter(value.astype(jnp.bfloat16), 'fsdp', scatter_dimension=di...  76.9 us
  transfers between devices with their start and end apart: 12, of which 9 were waited for; matrix products, arithmetic and copies ran while one was open for 3% of the time, Pallas kernels for 0%

profile of v3, /device:TPU:13, one launch (start us, length us, event | category | flops | bytes accessed | tf_op | source)
XLA Modules:
  0.0 693.7 jit_solution(17031114852323184710)
XLA Ops:
  7.2 1.3 iota_compare_fusion
  9.9 1.9 copy.76.w_ref
  11.9 1.3 fusion.47
  13.2 92.3 %first.1 = (bf16[2,4,128,1536]{3,2,1,0:T(8,128)(2,1)}, bf16[4,4,64,512]{3,2,1,0:T(8,128)(2,1)}, bf16[2,4,2,64,256]{4,3,2,1,0:T(8,128)(2,1)}, bf16[1536,512]{1,0:...) custom-call(bf16[128,1536]{1,0:T(8,128)(2,1)} %bitcast.103, ...), custom_call_target="tpu_custom_call" | custom-call | tf_op jit(solution)/shard_map/first/pallas_call | solution.py:755
  105.5 1.3 reshape.367
  106.8 2.2 fusion.64
  109.8 147.7 %middle.1 = (f32[128,1536]{1,0:T(8,128)}, f32[128,1536]{1,0:T(8,128)}, f32[8,1536]{1,0:T(8,128)}, bf16[2,4,128,1536]{3,2,1,0:T(8,128)(2,1)}, bf16[4,4,64,256]{3,...) custom-call(bf16[2,4,128,256]{3,2,1,0:T(8,128)(2,1)} %bitcast.121, ...), custom_call_target="tpu_custom_call" | custom-call | tf_op jit(solution)/shard_map/middle/pallas_call | solution.py:1139
  258.7 9.0 %fusion.68 = (f32[2,1024]{1,0:T(2,128)S(1)}, f32[2,1024,1024]{1,2,0:T(8,128)}) fusion(pred[1024,1024]{0,1:T(8,128)(4,1)} %iota_compare_fusion, bf16[1,1024,128]{2,1,0:T(8,128)(2,1)S(1)} %bitcast.115, bf16[1,1024,128]{2,1,0:T(8,128)(2,1)} %bitcast.117, bf16[1024,1,128]{2,1,0:T(2,128)(2,1)S(1)} %get-tuple-element.111), kind=kOutput, calls=%fused_computation.106 | convolution fusion | flops 547619840 | bytes 10231808 | tf_op jit(solution)/shard_map/sub | solution.py:1245
  267.7 5.5 fusion.11
  273.6 1.3 multiply_reduce_fusion
  274.9 2.5 multiply_convert_fusion
  277.4 1.5 fusion.10
  280.8 3.4 fusion.35
  284.3 2.0 fusion.17
  288.9 3.5 all-to-all-start
  293.5 11.4 %all-to-all-done = bf16[4,4,4,64,128]{4,3,2,1,0:T(8,128)(2,1)S(1)} async-done(((bf16[4,4,4,64,128]{4,3,2,1,0:T(8,128)(2,1)}), bf16[4,4,4,64,128]{4,3,2,1,0:T(8,128)(2,1)S(1)}, u32[]{:S(2)}, u32[]{:S(2)}) %all-to-all-start) | async-done | bytes 1048608 | tf_op jit(solution)/shard_map/all_to_all | solution.py:1235
  305.6 3.7 fusion.18
  312.4 3.5 convolution_convert_fusion
  316.2 12.5 %reduce-scatter.16.cloned.1.call-done = bf16[48,1536]{1,0:T(8,128)(2,1)} async-done(((bf16[192,1536]{1,0:T(8,128)(2,1)}), bf16[48,1536]{1,0:T(8,128)(2,1)}) %reduce-scatter.16.cloned.1.call-update) | async-done | bytes 147472 | tf_op jit(solution)/shard_map/reduce_scatter | solution.py:1268
  328.7 4.9 collective-permute-start.1
  333.7 27.5 %reduce-scatter.24.cloned.1.call-done = bf16[1,1536,96]{1,2,0:T(8,128)(2,1)} async-done(((bf16[4,1536,96]{1,2,0:T(8,128)(2,1)}), bf16[1,1536,96]{1,2,0:T(8,128)(2,1)}) %reduce-scatter.24.cloned.1.call-update) | async-done | bytes 294928
  361.1 2.1 collective-permute-start
  365.7 32.2 %reduce-scatter.20.cloned.1.call-done = bf16[128,1536]{1,0:T(8,128)(2,1)} async-done(((bf16[512,1536]{1,0:T(8,128)(2,1)}), bf16[128,1536]{1,0:T(8,128)(2,1)}) %reduce-scatter.20.cloned.1.call-update) | async-done | bytes 393232 | tf_op jit(solution)/shard_map/reduce_scatter | solution.py:1268
  397.9 4.8 collective-permute-start.3
  403.6 8.0 %collective-permute-done.3 = bf16[128,1536]{1,0:T(8,128)(2,1)S(1)} collective-permute-done((bf16[128,1536]{1,0:T(8,128)(2,1)}, bf16[128,1536]{1,0:T(8,128)(2,1)S(1)}, u32[]{:S(2)}, u32[]{:S(2)}) %collective-permute-start.3) | collective-permute-done | bytes 393248 | tf_op jit(solution)/shard_map/ppermute | solution.py:1270
  412.5 32.2 %reduce-scatter.18.cloned.1.call-done = bf16[1536,256]{1,0:T(8,128)(2,1)} async-done(((bf16[1536,1024]{1,0:T(8,128)(2,1)}), bf16[1536,256]{1,0:T(8,128)(2,1)}) %reduce-scatter.18.cloned.1.call-update) | async-done | bytes 786448 | tf_op jit(solution)/shard_map/reduce_scatter | solution.py:1268
  444.7 1.8 collective-permute-start.2
  446.5 67.6 %reduce-scatter.12.cloned.1.call-done = bf16[128,1536]{1,0:T(8,128)(2,1)} async-done(((bf16[1024,1536]{1,0:T(8,128)(2,1)}), bf16[128,1536]{1,0:T(8,128)(2,1)}) %reduce-scatter.12.cloned.1.call-update) | async-done | bytes 393232 | tf_op jit(solution)/shard_map/reduce_scatter | solution.py:1179
  514.1 1.8 add_convert_fusion
  515.9 68.4 %reduce-scatter.14.cloned.1.call-done = bf16[128,1536]{1,0:T(8,128)(2,1)} async-done(((bf16[1024,1536]{1,0:T(8,128)(2,1)}), bf16[128,1536]{1,0:T(8,128)(2,1)}) %reduce-scatter.14.cloned.1.call-update) | async-done | bytes 393232 | tf_op jit(solution)/shard_map/reduce_scatter | solution.py:1179
  586.8 2.1 fusion.25
  590.2 94.6 %reduce-scatter.22.cloned.1.call-done = f32[48,2]{1,0:T(8,128)} async-done(((f32[1536,2]{1,0:T(8,128)}), f32[48,2]{1,0:T(8,128)}) %reduce-scatter.22.cloned.1.call-update) | async-done | bytes 400
  (79 shorter events, 23.4 us)
Async XLA Ops:
  11.9 1.3 copy-start.7
  267.7 5.8 copy-start.1
  267.7 5.9 copy-start.6
  274.9 2.5 copy-start.3
  286.6 5.8 copy-start.2
  288.9 16.0 %all-to-all-start = ((bf16[4,4,4,64,128]{4,3,2,1,0:T(8,128)(2,1)}), bf16[4,4,4,64,128]{4,3,2,1,0:T(8,128)(2,1)S(1)}, u32[]{:S(2)}, u32[]{:S(2)}) async-start(bf16[4,4,4,64,128]{4,3,2,1,0:T(8,128)(2,1)} %copy.88), calls=%async_computation.1 | async-start | bytes 2097152 | tf_op jit(solution)/shard_map/all_to_all | solution.py:1235
  292.4 36.3 %reduce-scatter.16.cloned.1.call-start = ((), (), s32[]{:S(2)}) async-start(), calls=%async_computation.10 | async-start | bytes 737280 | tf_op jit(solution)/shard_map/reduce_scatter | solution.py:1268
  293.5 67.7 %reduce-scatter.24.cloned.1.call-start = ((), (), s32[]{:S(2)}) async-start(), calls=%async_computation.14 | async-start | bytes 1474560
  310.4 2.0 copy-start.8
  310.4 87.5 %reduce-scatter.20.cloned.1.call-start = ((), (), s32[]{:S(2)}) async-start(), calls=%async_computation.12 | async-start | bytes 1966080 | tf_op jit(solution)/shard_map/reduce_scatter | solution.py:1268
  311.1 133.5 %reduce-scatter.18.cloned.1.call-start = ((), (), s32[]{:S(2)}) async-start(), calls=%async_computation.11 | async-start | bytes 3932160 | tf_op jit(solution)/shard_map/reduce_scatter | solution.py:1268
  311.7 202.4 %reduce-scatter.12.cloned.1.call-start = ((), (), s32[]{:S(2)}) async-start(), calls=%async_computation.8 | async-start | bytes 3538944 | tf_op jit(solution)/shard_map/reduce_scatter | solution.py:1179
  312.3 272.0 %reduce-scatter.14.cloned.1.call-start = ((), (), s32[]{:S(2)}) async-start(), calls=%async_computation.9 | async-start | bytes 3538944 | tf_op jit(solution)/shard_map/reduce_scatter | solution.py:1179
  312.4 3.6 copy-start
  315.9 198.2 %copy-start.4 = (f32[128,1536]{1,0:T(8,128)S(1)}, f32[128,1536]{1,0:T(8,128)}, u32[]{:S(2)}) copy-start(f32[128,1536]{1,0:T(8,128)} %get-tuple-element.53) | copy-start | bytes 2359300
  315.9 270.9 %copy-start.5 = (f32[128,1536]{1,0:T(8,128)S(1)}, f32[128,1536]{1,0:T(8,128)}, u32[]{:S(2)}) copy-start(f32[128,1536]{1,0:T(8,128)} %get-tuple-element.55) | copy-start | bytes 2359300
  315.9 368.9 %reduce-scatter.22.cloned.1.call-start = ((), (), s32[]{:S(2)}) async-start(), calls=%async_computation.13 | async-start | bytes 811008
  328.7 36.2 %collective-permute-start.1 = (bf16[48,1536]{1,0:T(8,128)(2,1)}, bf16[48,1536]{1,0:T(8,128)(2,1)S(1)}, u32[]{:S(2)}, u32[]{:S(2)}) collective-permute-start(bf16[48,1536]{1,0:T(8,128)(2,1)} %reduce-scatter.16.cloned.1.call-done), channel_id=1, source_target_pairs={{0,0},{1,1},{2,2},{3,3},{4,8},{5,9},{6,10},{7,11},{8,16},{9,17},{1... | collective-permute-start | bytes 442376 | tf_op jit(solution)/shard_map/ppermute | solution.py:1270
  361.1 41.5 %collective-permute-start = (bf16[1,1536,96]{1,2,0:T(8,128)(2,1)}, bf16[1,1536,96]{1,2,0:T(8,128)(2,1)S(1)}, u32[]{:S(2)}, u32[]{:S(2)}) collective-permute-start(bf16[1,1536,96]{1,2,0:T(8,128)(2,1)} %reduce-scatter.24.cloned.1.call-done), channel_id=1, source_target_pairs={{0,0},{1,1},{16,2},{17,3},{4,4},{5,5},{20,6},{21,7},{8,8},{9,9},{2... | collective-permute-start | bytes 884744 | tf_op jit(solution)/shard_map/ppermute | solution.py:1270
  397.9 13.6 %collective-permute-start.3 = (bf16[128,1536]{1,0:T(8,128)(2,1)}, bf16[128,1536]{1,0:T(8,128)(2,1)S(1)}, u32[]{:S(2)}, u32[]{:S(2)}) collective-permute-start(bf16[128,1536]{1,0:T(8,128)(2,1)} %reduce-scatter.20.cloned.1.call-done), channel_id=1, source_target_pairs={{0,0},{1,1},{2,2},{3,3},{4,8},{5,9},{6,10},{7,11},{8,16},{9,17},{1... | collective-permute-start | bytes 1179656 | tf_op jit(solution)/shard_map/ppermute | solution.py:1270
  444.7 144.2 %collective-permute-start.2 = (bf16[1536,256]{1,0:T(8,128)(2,1)}, bf16[1536,256]{1,0:T(8,128)(2,1)S(1)}, u32[]{:S(2)}, u32[]{:S(2)}) collective-permute-start(bf16[1536,256]{1,0:T(8,128)(2,1)} %reduce-scatter.18.cloned.1.call-done), channel_id=1, source_target_pairs={{0,0},{1,1},{2,16},{3,17},{4,4},{5,5},{6,20},{7,21},{8,8},{9,9},{1... | collective-permute-start | bytes 2359304 | tf_op jit(solution)/shard_map/ppermute | solution.py:1270
Sparse Core Ops, SparseCore 0:
  296.7 32.0 reduce-scatter.15
  332.2 28.8 reduce-scatter.23
  364.1 33.7 reduce-scatter.19
  400.7 43.8 reduce-scatter.17
  446.8 67.2 reduce-scatter.11
  516.2 67.9 reduce-scatter.13
  589.4 95.3 reduce-scatter.21

commit v4 on v3

--- a/solution.py
+++ b/solution.py
@@ -274,58 +274,6 @@
     )
 
 
-TP = ("dp", "ctx")
-ALL = ("dp", "ctx", "fsdp")
-
-
-def dot(left, right):
-    return jnp.dot(left, right, preferred_element_type=jnp.float32)
-
-
-def qkv_owner(sizes):
-    moves = []
-    for head in range(H + 2 * KVH):
-        if head < H:
-            group, slot = head // 2, head % 2
-        elif head < H + KVH:
-            group, slot = head - H, 2
-        else:
-            group, slot = head - H - KVH, 3
-        device = group % sizes["dp"] * sizes["ctx"] + group // sizes["dp"]
-        moves.append((head, device * sizes["fsdp"] + slot))
-    return moves
-
-
-def hidden_of(device, sizes):
-    ctx = sizes["ctx"]
-    return (device % ctx) * sizes["dp"] + device // ctx
-
-
-def down_owner(sizes):
-    n, f = sizes["dp"] * sizes["ctx"], sizes["fsdp"]
-    return [
-        (hidden_of(device, sizes) * f + slot, device * f + slot)
-        for device in range(n)
-        for slot in range(f)
-    ]
-
-
-def up_owner(sizes):
-    n, f = sizes["dp"] * sizes["ctx"], sizes["fsdp"]
-    half = n * f // 2
-    moves = []
-    for device in range(n):
-        first = hidden_of(device, sizes) * (f // 2)
-        for slot in range(f):
-            source = first + slot if slot < f // 2 else half + first + slot - f // 2
-            moves.append((source, device * f + slot))
-    return moves
-
-
-def back(moves):
-    return [(to, source) for source, to in moves]
-
-
 MESH = pl.DeviceIdType.MESH
 VM = pltpu.VMEM
 ANY = pl.ANY
@@ -581,7 +529,7 @@
         low = (values * scale * gain).astype(jnp.bfloat16)
         normed[:, at] = low.reshape(dp, 2 * span, D)
         heads = jnp.dot(low, wide[...], preferred_element_type=jnp.float32)
-        cosine, sine_up, sine_down = cos_ref[at], sin_up_ref[at], sin_down_ref[at]
+        cosine, sine_up, sine_down = cos_ref[at, f], sin_up_ref[at, f], sin_down_ref[at, f]
         for slot in range(4):
             head = heads[:, slot * LANES : (slot + 1) * LANES]
             if slot < 3:
@@ -783,9 +731,7 @@
 
 
 def angle_tables(ctx, fs, span):
-    f_index = lax.axis_index("fsdp")
-    positions = (jnp.arange(ctx, dtype=jnp.int32)[:, None] * fs + f_index) * span + jnp.arange(span, dtype=jnp.int32)[None, :]
-    return lane_tables(positions)
+    return lane_tables(jnp.arange(ctx * fs * span, dtype=jnp.int32).reshape(ctx, fs, span))
 
 
 def lane_tables(positions):
@@ -915,7 +861,7 @@
     sizes, hidden, att_ref, x_ref, dy_ref, gains_ref, proj_ref, down_ref, gate_up_ref, dy_all_ref,
     resid_out, d_resid_out, gain_out, partial_out, unit_out, grad_up_out, grad_down_out, grad_proj_out,
     att, dy_all, proj, down, gate_up, resid, own_two, normed_two, act, d_both, part_stage, own_d, d_resid_all, d_stage, unit,
-    grad_up, grad_down, grad_proj,
+    grad_up, grad_down, grad_proj, grad_proj_low,
     in_sem, gu_send, gu_recv, two_send, two_recv, two_local, dr_send, dr_recv, dr_local, u_send, u_recv, out_sem, part_sem,
     *sums,
 ):
@@ -1024,7 +970,9 @@
         left_rows = normed_two[:, :, :, pl.ds(first, wide_rows)].reshape(dp * ctx * rows, wide_rows)
         for part in range(2):
             cols = slice(part * hidden, (part + 1) * hidden)
-            grad_up[pl.ds(first, wide_rows), cols] = inner(left_rows, d_both[:, :, :, cols].reshape(dp * ctx * rows, hidden)).astype(jnp.bfloat16)
+            terms = inner(left_rows, d_both[:, :, :, cols].reshape(dp * ctx * rows, hidden)).astype(jnp.bfloat16)
+            grad_up[2 * part, pl.ds(first, wide_rows), :] = terms[:, :half]
+            grad_up[2 * part + 1, pl.ds(first, wide_rows), :] = terms[:, half:]
         dy_cols = dy_all[:, :, :, pl.ds(first, wide_rows)].reshape(dp * ctx * rows, wide_rows)
         grad_down[:, pl.ds(first, wide_rows)] = inner(act[...].reshape(dp * ctx * rows, hidden), dy_cols).astype(jnp.bfloat16)
 
@@ -1090,7 +1038,10 @@
         return carry
 
     lax.fori_loop(0, ctx, back, 0)
-    grad_proj_copy = pltpu.make_async_copy(grad_proj, grad_proj_out, out_sem.at[3])
+    for slot in range(fs):
+        start = slot // 2 * LANES + slot % 2 * each
+        grad_proj_low[slot] = grad_proj[start : start + each, :].astype(jnp.bfloat16)
+    grad_proj_copy = pltpu.make_async_copy(grad_proj_low, grad_proj_out, out_sem.at[3])
     grad_proj_copy.start()
     for at in range(ctx):
         for step in range(1, fs):
@@ -1132,9 +1083,9 @@
         jax.ShapeDtypeStruct((8, D), wide_t),
         jax.ShapeDtypeStruct((dp, ctx, rows, D), low),
         jax.ShapeDtypeStruct((ctx, fs, span, 2 * LANES), low),
-        jax.ShapeDtypeStruct((D, 2 * hidden), low),
+        jax.ShapeDtypeStruct((4, D, hidden // 2), low),
         jax.ShapeDtypeStruct((hidden, D), low),
-        jax.ShapeDtypeStruct((2 * LANES, D), wide_t),
+        jax.ShapeDtypeStruct(proj.shape, low),
     )
     return pl.pallas_call(
         functools.partial(middle_kernel, sizes, hidden),
@@ -1158,9 +1109,10 @@
             VM((dp, ctx, rows, D), low),
             VM((ctx, 2 * dp, span, 2 * LANES), low),
             VM((ctx, fs, span, 2 * LANES), low),
-            VM((D, 2 * hidden), low),
+            VM((4, D, hidden // 2), low),
             VM((hidden, D), low),
             VM((2 * LANES, D), wide_t),
+            VM(proj.shape, low),
             dma((3 + fs,)), dma((fs,)), dma((4,)),
             dma((3, ctx)), dma((dp, ctx)), dma,
             dma((3, ctx)), dma((dp, ctx)), dma,
@@ -1171,120 +1123,397 @@
     )(att, x, dy, gains, proj, down.reshape(hidden, D), w_gate_up, dy_all)
 
 
-def gather_tp(value):
-    return lax.all_gather(value, TP, axis=0, tiled=True)
-
-
-def sum_tp(value):
-    return lax.psum_scatter(value.astype(jnp.bfloat16), TP, scatter_dimension=0, tiled=True).astype(
-        jnp.float32
-    )
-
-
-def norm_back(values, scale, gain, incoming):
+def last_kernel(
+    sizes, x_ref, gains_ref, cos_ref, sin_up_ref, sin_down_ref, resid_ref, d_resid_ref, gain_two_ref,
+    unit_ref, d_unit_ref, normed_ref, wide_ref, partial_ref, up_ref, down_ref, proj_ref,
+    out_ref, d_x_ref, gains_out, qkv_out, proj_out, up_out, down_out,
+    unit, d_unit, d_k, d_v, stage, mixed, normed, wide, grad_wide, grad_heads,
+    up_land, down_land, proj_land, q_land, kv_land, down_sum, proj_sum, kv_sum, down_last, proj_last, kv_last, gain_vec, gain_stage, gain_land,
+    in_sem, up_send, up_recv, down_send, down_recv, proj_send, proj_recv, head_send, head_recv, move_send, move_recv,
+    u_send, u_recv, g_send, g_recv, mine_sem,
+    *sums,
+):
+    dp, ctx, fs = sizes
+    n = dp * ctx * fs
+    d, c, f = place()
+    here = at_device(d, c, f)
+    me = (d * ctx + c) * fs + f
+    rows = x_ref.shape[0]
+    span = rows // 2
+    both_rows = dp * rows
+    low, wide_t = jnp.bfloat16, jnp.float32
+    loads = [
+        pltpu.make_async_copy(src, dst, in_sem.at[index])
+        for index, (src, dst) in enumerate(((unit_ref, unit), (d_unit_ref, d_unit), (normed_ref, normed), (wide_ref, wide)))
+    ]
+    for load in loads:
+        load.start()
+    out_sum = LineSum(ctx, *sums[:6], sums[6:10])
+    in_sum = LineSum(ctx, *sums[10:16], sums[16:20])
+    for at in range(ctx):
+        pltpu.make_async_copy(partial_ref.at[d, at], out_sum.mine.at[at], mine_sem.at[at]).start()
+    greet_all(sizes)
+
+    for at in range(ctx):
+        remote(
+            partial_ref.at[1 - d, at], out_sum.in_core.at[at], out_sum.core_send.at[at], out_sum.core_recv.at[at], at_device(1 - d, c, f)
+        ).start()
+
+    def push(src, land, send, recv, core, fs_to):
+        to_self = jnp.logical_and(core == d, fs_to == f)
+
+        @pl.when(jnp.logical_not(to_self))
+        def _():
+            remote(src, land.at[f], send, recv.at[f], at_device(core, c, fs_to)).start()
+
+        @pl.when(to_self)
+        def _():
+            pltpu.make_async_copy(src, land.at[f], recv.at[f]).start()
+
+    def pushed(src, send, core, fs_to):
+        @pl.when(jnp.logical_not(jnp.logical_and(core == d, fs_to == f)))
+        def _():
+            left(src, send, here)
+
+    def push_down():
+        for slot in range(fs):
+            push(down_ref.at[slot], down_land, down_send.at[slot], down_recv, d, slot)
+            push(proj_ref.at[slot], proj_land, proj_send.at[slot], proj_recv, d, slot)
+
+    def push_up():
+        for slot in range(4):
+            push(up_ref.at[slot], up_land, up_send.at[slot], up_recv, slot // 2, 2 * d + slot % 2)
+
+    push_up()
+    push_down()
+    loads[0].wait()
+    loads[1].wait()
+    d_k[...] = jnp.zeros_like(d_k)
+    d_v[...] = jnp.zeros_like(d_v)
+    block = fs * span
+
+    def unturn(values, at):
+        up = pltpu.roll(values, HD // 2, 1).reshape(fs, span, LANES)
+        down = pltpu.roll(values, LANES - HD // 2, 1).reshape(fs, span, LANES)
+        return values.reshape(fs, span, LANES) * cos_ref[at] - up * sin_up_ref[at] - down * sin_down_ref[at]
+
+    for at in reversed(range(ctx)):
+        keys = block * (at + 1)
+        k_rows = unit[0 : at + 1, :, :, 2 * LANES : 3 * LANES].reshape(keys, LANES)
+        v_rows = unit[0 : at + 1, :, :, 3 * LANES : 4 * LANES].reshape(keys, LANES)
+        allowed = lax.broadcasted_iota(jnp.int32, (block, keys), 1) <= block * at + lax.broadcasted_iota(
+            jnp.int32, (block, keys), 0
+        )
+        for head in range(2):
+            lanes = slice(head * LANES, (head + 1) * LANES)
+            q_rows = unit[at, :, :, lanes].reshape(block, LANES)
+            d_rows = d_unit[at, :, :, lanes].reshape(block, LANES)
+            scores = jnp.where(allowed, outer(q_rows, k_rows) * FACTOR, NEG)
+            weights = jnp.exp(scores - jnp.max(scores, axis=-1, keepdims=True))
+            probs = weights / jnp.sum(weights, axis=-1, keepdims=True)
+            d_probs = outer(d_rows, v_rows)
+            delta = jnp.sum(probs * d_probs, axis=-1, keepdims=True)
+            d_scores = (probs * (d_probs - delta)).astype(low)
+            d_q = jnp.dot(d_scores, k_rows, preferred_element_type=wide_t) * FACTOR
+            stage[at, :, :, lanes] = unturn(d_q, at).astype(low)
+            d_k[0:keys, :] += inner(d_scores, q_rows) * FACTOR
+            d_v[0:keys, :] += inner(probs.astype(low), d_rows)
+        stage[at, :, :, 2 * LANES : 3 * LANES] = unturn(d_k[block * at : keys, :], at).astype(low)
+        stage[at, :, :, 3 * LANES : 4 * LANES] = d_v[block * at : keys, :].astype(low).reshape(fs, span, LANES)
+        for to in range(fs):
+
+            @pl.when(to != f)
+            def _():
+                remote(
+                    stage.at[at, to], mixed.at[f // 2, at, lax.rem(f, 2)], u_send.at[at, to], u_recv.at[f, at], at_device(d, c, to)
+                ).start()
+
+            @pl.when(to == f)
+            def _():
+                mixed[f // 2, at, lax.rem(f, 2)] = stage[at, to]
+
+    loads[2].wait()
+    loads[3].wait()
+
+    def give(step, carry):
+        at = ordered(c, ctx - 1 - step, ctx)
+        for move in range(1, fs):
+            other = lax.rem(f + move, fs)
+            arrived(mixed.at[other // 2, at, lax.rem(other, 2)], u_recv.at[other, at], here)
+        terms = outer(mixed[:, at].reshape(both_rows, 4 * LANES), wide[...])
+        in_sum.give(at, terms.reshape(dp, rows, D))
+        return carry
+
+    lax.fori_loop(0, ctx, give, 0)
+
+    every = dp * ctx * rows
+    quarter = D // ctx
+
+    def grads(step, carry):
+        first_row = pl.multiple_of(step * quarter, LANES)
+        rows_of = normed[:, :, :, pl.ds(first_row, quarter)].reshape(every, quarter)
+        grad_wide[pl.ds(first_row, quarter), :] = inner(rows_of, mixed[...].reshape(every, 4 * LANES)).astype(low)
+        return carry
+
+    relay_f = 2 * lax.rem(c, 2) + d
+
+    def push_heads():
+        for slot in range(4):
+            grad_heads[slot] = grad_wide[:, slot * LANES : slot * LANES + HD]
+        for slot in range(2):
+            push(grad_heads.at[slot], q_land, head_send.at[slot], head_recv.at[0], 0, 2 * d + slot)
+        for slot in range(2):
+            push(grad_heads.at[2 + slot], kv_land.at[slot], head_send.at[2 + slot], head_recv.at[1 + slot], d, relay_f)
+
+    def out_step(step, carry):
+        at = ordered(c, ctx - 1 - step, ctx)
+        pltpu.make_async_copy(partial_ref.at[d, at], out_sum.mine.at[at], mine_sem.at[at]).wait()
+        out_sum.step(at)
+        return carry
+
+    lax.fori_loop(0, ctx, out_step, 0)
+    out_ref[...] = (resid_ref[...] + out_sum.total[...]).astype(low)
+    in_sum.step(ordered(c, ctx - 1, ctx))
+    lax.fori_loop(0, ctx, grads, 0)
+    push_heads()
+
+    def in_step(step, carry):
+        in_sum.step(ordered(c, ctx - 1 - step, ctx))
+        return carry
+
+    lax.fori_loop(1, ctx - 1, in_step, 0)
+
+    def sum_of(land):
+        total = land[0].astype(wide_t)
+        for source in range(1, fs):
+            total += land[source].astype(wide_t)
+        return total
+
+    for source in range(fs):
+        arrived(down_land.at[source], down_recv.at[source], here)
+        arrived(proj_land.at[source], proj_recv.at[source], here)
+    down_sum[...] = sum_of(down_land).astype(low)
+    proj_sum[...] = sum_of(proj_land).astype(low)
+    own_core, own_ctx = c // 2, 2 * lax.rem(c, 2) + d
+    stays = jnp.logical_and(own_core == d, own_ctx == c)
+    moves = ((down_sum, down_last), (proj_sum, proj_last))
+    for index, (src, dst) in enumerate(moves):
+
+        @pl.when(jnp.logical_not(stays))
+        def _():
+            remote(src, dst, move_send.at[index], move_recv.at[index], at_device(own_core, own_ctx, f)).start()
+
+        @pl.when(stays)
+        def _():
+            pltpu.make_async_copy(src, dst, move_recv.at[index]).start()
+
+    in_sum.step(c)
+
+    gain = gains_ref[0:1, :]
+    values = x_ref[...].astype(wide_t)
+    scale = lax.rsqrt(jnp.mean(values * values, axis=-1, keepdims=True) + EPS)
+    incoming = in_sum.total[...]
     weighted = incoming * gain
     mean = jnp.mean(weighted * values, axis=-1, keepdims=True)
-    return scale * weighted - values * (scale * scale * scale) * mean
+    d_x_ref[...] = (d_resid_ref[...] + scale * weighted - values * (scale * scale * scale) * mean).astype(low)
+    gain_vec[0:1, :] = jnp.sum(incoming * values * scale, axis=0, keepdims=True)
+    gain_vec[1:2, :] = gain_two_ref[0:1, :]
+    each = D // n
+    for index in range(n):
+        gain_stage[index, :, 0:each] = gain_vec[:, index * each : (index + 1) * each]
+    gain_land[me] = gain_stage[me]
+
+    def gain_to(step, carry):
+        other = lax.rem(me + step, n)
+        remote(
+            gain_stage.at[other], gain_land.at[me], g_send.at[other], g_recv.at[me],
+            at_device(other // (ctx * fs), lax.rem(other // fs, ctx), lax.rem(other, fs)),
+        ).start()
+        return carry
+
+    lax.fori_loop(1, n, gain_to, 0)
+
+    for slot in range(2):
+        owner = slot * 2 + c // 2
+
+        @pl.when(f == relay_f)
+        def _():
+            for source in range(fs):
+                arrived(kv_land.at[slot, source], head_recv.at[1 + slot, source], here)
+            kv_sum[slot] = sum_of(kv_land.at[slot]).astype(low)
+            away = jnp.logical_or(d != 1, owner != c)
+
+            @pl.when(away)
+            def _():
+                remote(kv_sum.at[slot], kv_last, move_send.at[2 + slot], move_recv.at[2], at_device(1, owner, f)).start()
+
+            @pl.when(jnp.logical_not(away))
+            def _():
+                pltpu.make_async_copy(kv_sum.at[slot], kv_last, move_recv.at[2]).start()
+
+    for source in range(fs):
+        arrived(up_land.at[source], up_recv.at[source], here)
+    up_out[...] = sum_of(up_land)
+    for index, (src, dst) in enumerate(moves):
+        arrived(dst, move_recv.at[index], here)
+    down_out[...] = down_last[...].astype(wide_t)
+    proj_out[...] = proj_last[...].astype(wide_t)
+
+    @pl.when(d == 0)
+    def _():
+        for source in range(fs):
+            arrived(q_land.at[source], head_recv.at[0, source], here)
+        qkv_out[...] = sum_of(q_land)
+
+    @pl.when(d == 1)
+    def _():
+        arrived(kv_last, move_recv.at[2], here)
+        qkv_out[...] = kv_last[...].astype(wide_t)
+
+    def gain_from(step, carry):
+        other = lax.rem(me + step, n)
+        arrived(gain_land.at[other], g_recv.at[other], here)
+        return carry
+
+    lax.fori_loop(1, n, gain_from, 0)
+    total = gain_land[0]
+    for index in range(1, n):
+        total += gain_land[index]
+    gains_out[...] = total
+
+    for slot in range(4):
+        pushed(up_ref.at[slot], up_send.at[slot], slot // 2, 2 * d + slot % 2)
+        pushed(down_ref.at[slot], down_send.at[slot], d, slot)
+        pushed(proj_ref.at[slot], proj_send.at[slot], d, slot)
+    for slot in range(2):
+        pushed(grad_heads.at[slot], head_send.at[slot], 0, 2 * d + slot)
+        pushed(grad_heads.at[2 + slot], head_send.at[2 + slot], d, relay_f)
+        owner = slot * 2 + c // 2
+
+        @pl.when(jnp.logical_and(f == relay_f, jnp.logical_or(d != 1, owner != c)))
+        def _():
+            left(kv_sum.at[slot], move_send.at[2 + slot], here)
+
+        @pl.when(jnp.logical_not(stays))
+        def _():
+            left(moves[slot][0], move_send.at[slot], here)
+
+    for at in range(ctx):
+        for to in range(fs):
+
+            @pl.when(to != f)
+            def _():
+                left(stage.at[at, to], u_send.at[at, to], here)
+
+        left(partial_ref.at[1 - d, at], out_sum.core_send.at[at], here)
+
+        @pl.when(at != c)
+        def _():
+            left(out_sum.out_line.at[at], out_sum.line_send.at[at], here)
+
+    in_sum.finish()
+
+    def gain_left(step, carry):
+        other = lax.rem(me + step, n)
+        left(gain_stage.at[other], g_send.at[other], here)
+        return carry
+
+    lax.fori_loop(1, n, gain_left, 0)
+
+
+def last(sizes, x, gains, tables, resid, d_resid, gain_two, unit, d_unit, normed, wide, partial, grad_up, grad_down, grad_proj):
+    dp, ctx, fs = sizes
+    n = dp * ctx * fs
+    rows = x.shape[0]
+    span = rows // 2
+    low, wide_t = jnp.bfloat16, jnp.float32
+    dma = pltpu.SemaphoreType.DMA
+    any_spec, vm_spec = pl.BlockSpec(memory_space=ANY), pl.BlockSpec(memory_space=VM)
+    down_rows, proj_rows, half = grad_down.shape[0] // fs, grad_proj.shape[1], grad_up.shape[2]
+    shapes = (
+        jax.ShapeDtypeStruct((rows, D), low),
+        jax.ShapeDtypeStruct((rows, D), low),
+        jax.ShapeDtypeStruct((8, LANES), wide_t),
+        jax.ShapeDtypeStruct((D, HD), wide_t),
+        jax.ShapeDtypeStruct((proj_rows, D), wide_t),
+        jax.ShapeDtypeStruct((D, half), wide_t),
+        jax.ShapeDtypeStruct((down_rows, D), wide_t),
+    )
+    return pl.pallas_call(
+        functools.partial(last_kernel, sizes),
+        name="last",
+        out_shape=shapes,
+        in_specs=[vm_spec] * 8 + [any_spec] * 8,
+        out_specs=[vm_spec] * 7,
+        scratch_shapes=[
+            VM(unit.shape, low),
+            VM(d_unit.shape, low),
+            VM((ctx * fs * span, LANES), wide_t),
+            VM((ctx * fs * span, LANES), wide_t),
+            VM((ctx, fs, span, 4 * LANES), low),
+            VM((dp, ctx, 2, span, 4 * LANES), low),
+            VM(normed.shape, low),
+            VM(wide.shape, low),
+            VM(wide.shape, low),
+            VM((4, D, HD), low),
+            VM((fs, D, half), low),
+            VM((fs, down_rows, D), low),
+            VM((fs, proj_rows, D), low),
+            VM((fs, D, HD), low),
+            VM((2, fs, D, HD), low),
+            VM((down_rows, D), low),
+            VM((proj_rows, D), low),
+            VM((2, D, HD), low),
+            VM((down_rows, D), low),
+            VM((proj_rows, D), low),
+            VM((D, HD), low),
+            VM((8, D), wide_t),
+            VM((n, 8, LANES), wide_t),
+            VM((n, 8, LANES), wide_t),
+            dma((4,)),
+            dma((4,)), dma((fs,)), dma((fs,)), dma((fs,)), dma((fs,)), dma((fs,)),
+            dma((4,)), dma((3, fs)), dma((4,)), dma((3,)),
+            dma((ctx, fs)), dma((fs, ctx)), dma((n,)), dma((n,)), dma((ctx,)),
+        ] + LineSum.scratch(ctx, rows) + LineSum.scratch(ctx, rows),
+        compiler_params=pltpu.CompilerParams(collective_id=3, has_side_effects=True, vmem_limit_bytes=63 * 1024 * 1024),
+    )(
+        x, gains, *tables, resid, d_resid, gain_two, unit, d_unit, normed, wide, partial,
+        grad_up, grad_down.reshape(fs, down_rows, D), grad_proj,
+    )
 
 
 def on_device(tokens, cotangent, attn_gain, w_qkv, w_out, mlp_gain, w_gate_up, w_down):
-    sizes = {name: lax.axis_size(name) for name in ALL}
-    dp, ctx, fs = sizes["dp"], sizes["ctx"], sizes["fsdp"]
+    dp, ctx, fs = where = tuple(lax.axis_size(name) for name in ("dp", "ctx", "fsdp"))
     mb, _, span, _ = tokens.shape
     rows = mb * span
-    f_index = lax.axis_index("fsdp")
-    length = span * ctx * fs
-    factor = HD ** (-0.5)
-    hidden = FF // (dp * ctx)
-
-    x_low = tokens.reshape(rows, D)
-    gain_rows = jnp.zeros((8, LANES), jnp.float32)
-    gain_rows = gain_rows.at[0, : attn_gain.shape[0]].set(attn_gain.astype(jnp.float32))
-    gain_rows = gain_rows.at[1, : mlp_gain.shape[0]].set(mlp_gain.astype(jnp.float32))
-    cosine, sine_up, sine_down = angle_tables(ctx, fs, span)
+    x = tokens.reshape(rows, D)
     dy = cotangent.reshape(rows, D)
-    where = (dp, ctx, fs)
-    normed, unit, att, qkv, gains, dy_all, proj, down = first(
-        where, x_low, gain_rows, w_qkv, cosine, sine_up, sine_down, dy, w_out, w_down
+    each = attn_gain.shape[0]
+    gain_rows = jnp.concatenate([attn_gain[None], mlp_gain[None]]).astype(jnp.float32)
+    gain_rows = jnp.pad(gain_rows, ((0, 6), (0, LANES - each)))
+    tables = angle_tables(ctx, fs, span)
+    normed, unit, att, qkv, gains, dy_all, proj, down = first(where, x, gain_rows, w_qkv, *tables, dy, w_out, w_down)
+    att = att.reshape(dp, ctx, rows, 2 * LANES)
+    resid, d_resid, grad_two, partial, d_unit, grad_up, grad_down, grad_proj = middle(
+        where, att, x, dy, gains, proj, down, w_gate_up, dy_all
     )
-    att = att.reshape(dp, ctx, rows, 2 * LANES)
-    resid, d_resid, grad_two, partial, d_unit, grad_gate_up, grad_down, grad_out = middle(
-        where, att, x_low, dy, gains, proj, down, w_gate_up, dy_all
+    block_out, grad_tokens, gain_grads, grad_qkv, grad_out, grad_gate_up, grad_down = last(
+        where, x, gains, tables, resid, d_resid, grad_two, unit, d_unit, normed, qkv, partial, grad_up, grad_down, grad_proj
     )
-    block_out = (resid + sum_tp(partial.reshape(dp * ctx * rows, D))).astype(jnp.bfloat16)
-    grad_two = grad_two[0]
-    grad_out = grad_out.reshape(2, LANES, D)[:, :HD].reshape(2 * HD, D)
-    d_unit = jnp.moveaxis(d_unit.reshape(length, 2, LANES), 1, 0)
-    gain_one, gain_two = gains[0], gains[1]
-    normed = normed.reshape(dp * ctx * rows, D)
-    unit = unit.reshape(length, 4, LANES)
-
-    x = x_low.astype(jnp.float32)
-    scale_one = lax.rsqrt(jnp.mean(x * x, axis=-1, keepdims=True) + EPS)
-
-    def to_units(values):
-        count = values.shape[0]
-        values = values.transpose(1, 3, 0, 2, 4, 5)
-        values = values.reshape(dp * mb, count, ctx, span, -1)
-        values = lax.all_to_all(values, "fsdp", split_axis=0, concat_axis=0, tiled=True)
-        return values.transpose(1, 2, 0, 3, 4).reshape(count, length, -1)
-
-    def to_rows(values):
-        count = values.shape[0]
-        values = values.reshape(count, ctx, fs, span, -1).transpose(2, 0, 1, 3, 4)
-        values = lax.all_to_all(values, "fsdp", split_axis=0, concat_axis=0, tiled=True)
-        values = values.reshape(dp, mb, count, ctx, span, -1).transpose(2, 0, 3, 1, 4, 5)
-        return values.reshape(count, dp * ctx * rows, -1)
-
-    q = jnp.stack([unit[:, 0], unit[:, 1]])
-    k, v = unit[:, 2], unit[:, 3]
-    scores = jnp.einsum("hqd,kd->hqk", q, k, preferred_element_type=jnp.float32) * factor
-    allowed = jnp.arange(length)[None, :] <= jnp.arange(length)[:, None]
-    scores = jnp.where(allowed, scores, NEG)
-    best = jnp.max(scores, axis=-1, keepdims=True)
-    weights = jnp.where(allowed, jnp.exp(scores - best), 0.0)
-    probs = weights / jnp.sum(weights, axis=-1, keepdims=True)
-    probs_low = probs.astype(jnp.bfloat16)
-    d_probs = jnp.einsum("hqd,kd->hqk", d_unit, v, preferred_element_type=jnp.float32)
-    delta = jnp.sum(probs * d_probs, axis=-1, keepdims=True)
-    d_scores = (probs * (d_probs - delta)).astype(jnp.bfloat16)
-    d_q = jnp.einsum("hqk,kd->hqd", d_scores, k, preferred_element_type=jnp.float32) * factor
-    d_k = jnp.einsum("hqk,hqd->kd", d_scores, q, preferred_element_type=jnp.float32) * factor
-    d_v = jnp.einsum("hqk,hqd->kd", probs_low, d_unit, preferred_element_type=jnp.float32)
-    cos_u, up_u, down_u = lane_tables(jnp.arange(length, dtype=jnp.int32))
-
-    def unturn(values):
-        return values * cos_u - jnp.roll(values, HD // 2, -1) * up_u - jnp.roll(values, -(HD // 2), -1) * down_u
-
-    d_heads = jnp.concatenate([unturn(d_q), unturn(d_k)[None], d_v[None]]).astype(jnp.bfloat16)
-    d_mixed = to_rows(d_heads)
-    d_mixed = jnp.moveaxis(d_mixed, 0, 1).reshape(dp * ctx * rows, 4 * LANES)
-    grad_qkv = jnp.moveaxis(inner(normed, d_mixed).reshape(D, 4, LANES)[:, :, :HD], 1, 0)
-    d_normed = sum_tp(outer(d_mixed, qkv))
-    grad_one = jnp.sum(d_normed * x * scale_one, axis=0)
-    grad_tokens = (d_resid + norm_back(x, scale_one, gain_one, d_normed)).astype(jnp.bfloat16)
-
-    def reduce_rows(value, dim, moves):
-        value = lax.psum_scatter(value.astype(jnp.bfloat16), "fsdp", scatter_dimension=dim, tiled=True)
-        if moves is not None:
-            value = lax.ppermute(value, ALL, back(moves))
-        return value.astype(jnp.float32)
-
-    gain_grads = lax.psum_scatter(jnp.stack([grad_one, grad_two]), ALL, scatter_dimension=1, tiled=True)
     return (
         block_out.reshape(tokens.shape),
         grad_tokens.reshape(tokens.shape),
-        gain_grads[0],
-        reduce_rows(grad_qkv, 0, qkv_owner(sizes)).reshape(D, HD),
-        reduce_rows(grad_out, 0, down_owner(sizes)),
-        gain_grads[1],
-        reduce_rows(grad_gate_up, 1, up_owner(sizes)),
-        reduce_rows(grad_down, 0, down_owner(sizes)),
+        gain_grads[0, :each],
+        grad_qkv,
+        grad_out,
+        gain_grads[1, :each],
+        grad_gate_up,
+        grad_down,
     )
 
 
 def fits(mesh):
-    return mesh.shape["dp"] * mesh.shape["ctx"] == KVH and mesh.shape["fsdp"] == 4
+    return mesh.shape["dp"] == 2 and mesh.shape["ctx"] == 4 and mesh.shape["fsdp"] == 4
 
 
 def solution(mesh):

time: 698 us -> 423 us (0.61)
  waiting for transfers between devices: 356 us -> 0 us
  Pallas kernels: 240 us -> 403 us
  matrix products: 25.2 us -> 0 us
  other arithmetic: 22.3 us -> 4.47 us
  starting transfers between devices: 17.4 us -> 0 us
  between operations: 14.5 us -> 0.7 us
  local copies, waits for them, and re-layouts: 18.1 us -> 10.3 us
    reduce_scatter x5 -> x0, waiting for transfers between devices: 213 us -> none  [the longest x2 136 us: sum_tp(): lax.psum_scatter(value.astype(jnp.bfloat16), TP, scatter_dimension=0, til...]
    pallas_call x0 -> x1, Pallas kernels: none -> 163 us  [last(): pl.pallas_call(functools.partial(last_kernel, sizes), name='last', out_sh...]
    unnamed x9 -> x0, waiting for transfers between devices: 124 us -> none
    dot_general x6 -> x0, matrix products: 16.2 us -> none  [the longest x1 5.49 us: on_device(): jnp.einsum('hqk,hqd->kd', probs_low, d_unit, preferred_element_type=jnp.f...]
    ppermute x4 -> x0, starting transfers between devices: 13.6 us -> none  [reduce_rows(): value = lax.ppermute(value, ALL, back(moves))]
    all_to_all x1 -> x0, waiting for transfers between devices: 11.4 us -> none  [to_rows(): lax.all_to_all(values, 'fsdp', split_axis=0, concat_axis=0, tiled=True)]
    convert_element_type x6 -> x0, other arithmetic: 9.32 us -> none  [the longest x3 2.95 us: reduce_rows(): return value.astype(jnp.float32)]
    sub x1 -> x0, matrix products: 8.99 us -> none  [on_device(): weights = jnp.where(allowed, jnp.exp(scores - best), 0.0)]
  transfers between devices with their start and end apart: 12 -> 0, of which waited for: 9 -> 0; matrix products, arithmetic and copies ran while one was open for 3% -> 0% of each run, Pallas kernels for 0% -> 0%
where the time goes in v4:
time: 423 us; the launch traced here: 419 us
  Pallas kernels  403 us (95%)
  local copies, waits for them, and re-layouts  10.3 us (2%)
  other arithmetic  4.47 us (1%)
    pallas_call x1, Pallas kernels, last(): pl.pallas_call(functools.partial(last_kernel, sizes), name='last', out_sh...  163 us
    pallas_call x1, Pallas kernels, middle(): pl.pallas_call(functools.partial(middle_kernel, sizes, hidden), name='mid...  148 us
    pallas_call x1, Pallas kernels, first(): pl.pallas_call(functools.partial(first_kernel, sizes), name='first', out_...  92.5 us
    unnamed x17, local copies, waits for them, and re-layouts  8.99 us

profile of v4, /device:TPU:13, one launch (start us, length us, event | category | flops | bytes accessed | tf_op | source)
XLA Modules:
  0.0 418.7 jit_solution(3163044938168069917)
XLA Ops:
  0.7 1.3 fusion.10.gains_ref
  2.0 1.9 copy.16.w_ref
  3.8 3.2 fusion.2
  7.0 92.5 %first.1 = (bf16[2,4,128,1536]{3,2,1,0:T(8,128)(2,1)}, bf16[4,4,64,512]{3,2,1,0:T(8,128)(2,1)}, bf16[2,4,2,64,256]{4,3,2,1,0:T(8,128)(2,1)}, bf16[1536,512]{1,0:...) custom-call(bf16[128,1536]{1,0:T(8,128)(2,1)} %bitcast.17, ...), custom_call_target="tpu_custom_call" | custom-call | tf_op jit(solution)/shard_map/first/pallas_call | solution.py:703
  99.5 147.7 %middle.1 = (f32[128,1536]{1,0:T(8,128)}, f32[128,1536]{1,0:T(8,128)}, f32[8,1536]{1,0:T(8,128)}, bf16[2,4,128,1536]{3,2,1,0:T(8,128)(2,1)}, bf16[4,4,64,256]{3,...) custom-call(bf16[2,4,128,256]{3,2,1,0:T(8,128)(2,1)} %bitcast.24, ...), custom_call_target="tpu_custom_call" | custom-call | tf_op jit(solution)/shard_map/middle/pallas_call | solution.py:1090
  247.3 163.0 %last.1 = (bf16[128,1536]{1,0:T(8,128)(2,1)}, bf16[128,1536]{1,0:T(8,128)(2,1)}, f32[8,128]{1,0:T(8,128)}, f32[1536,96]{1,0:T(8,128)}, f32[48,1536]{1,0:T(8,128)...) custom-call(bf16[128,1536]{1,0:T(8,128)(2,1)} %bitcast.19, f32[8,1536]{1,0:T(8,128)} %get-tuple-element.31.gains_ref, ...), custom_call_target="tpu_custom_call" | custom-call | tf_op jit(solution)/shard_map/last/pallas_call | solution.py:1442
  410.3 0.0 copy-start.3
  410.3 0.0 copy-start.2
  410.3 0.0 copy-start.4
  410.3 1.3 slice_bitcast_fusion
  411.6 0.0 copy-start
  411.6 2.3 copy.19
  413.9 0.0 copy-done.3
  413.9 0.7 copy.25
  414.7 0.0 copy-done.2
  414.7 0.7 copy.26
  415.4 0.0 copy-done.4
  415.4 0.7 copy.27
  416.1 0.0 copy-done
  416.1 0.0 copy-start.1
  416.1 1.1 copy.28
  417.3 0.5 copy-done.1
  417.8 0.9 copy.29
  (4 shorter events, 0.0 us)
Async XLA Ops:
  410.3 3.6 copy-start.3
  410.3 4.4 %copy-start.2 = (bf16[128,1536]{1,0:T(8,128)(2,1)S(1)}, bf16[128,1536]{1,0:T(8,128)(2,1)}, u32[]{:S(2)}) copy-start(bf16[128,1536]{1,0:T(8,128)(2,1)} %get-tuple-element.48) | copy-start | bytes 1179652
  410.3 5.1 %copy-start.4 = (f32[48,1536]{1,0:T(8,128)S(1)}, f32[48,1536]{1,0:T(8,128)}, u32[]{:S(2)}) copy-start(f32[48,1536]{1,0:T(8,128)} %get-tuple-element.81) | copy-start | bytes 884740
  411.6 4.5 %copy-start = (f32[1536,256]{1,0:T(8,128)S(1)}, f32[1536,256]{1,0:T(8,128)}, u32[]{:S(2)}) copy-start(f32[1536,256]{1,0:T(8,128)} %get-tuple-element.83) | copy-start | bytes 4718596
  416.1 1.7 copy-start.1

commit v5 on v4

--- a/solution.py
+++ b/solution.py
@@ -301,7 +301,7 @@
     remote(src, src, send, send, device).wait_send()
 
 
-def greet_all(sizes):
+def tell_all(sizes):
     dp, ctx, fs = sizes
     n = dp * ctx * fs
     d, c, f = place()
@@ -319,7 +319,11 @@
         return carry
 
     lax.fori_loop(1, n, tell, 0)
-    pl.semaphore_wait(barrier, n - 1)
+
+
+def hear_all(sizes):
+    dp, ctx, fs = sizes
+    pl.semaphore_wait(pltpu.get_barrier_semaphore(), dp * ctx * fs - 1)
 
 
 class LineGather:
@@ -431,32 +435,40 @@
 
 
 def first_kernel(
-    sizes, x_ref, gains_ref, w_ref, cos_ref, sin_up_ref, sin_down_ref, dy_ref, proj_ref, down_ref,
-    normed_out, unit_out, att_out, wide_out, gains_out, dy_all, proj_all, down_all,
-    x_all, w_all, wide, normed, stage, unit, att_stage, att, gain_all, gain_vec,
+    sizes, parts, x_ref, gains_ref, w_ref, block_ref, step_ref, dy_ref, proj_ref, gate_up_ref,
+    normed_out, unit_out, att_out, wide_out, gains_out, dy_all, proj_all, gate_up_all,
+    x_all, wide, normed, stage, unit, att_stage, att, gain_all, gain_vec,
     line_send, line_recv, line_local, w_send, w_recv, w_pass, g_send, g_recv, u_send, u_recv, a_send, a_recv, out_sem,
-    dy_send, dy_recv, dy_local, m_send, m_recv, m_pass,
+    dy_send, dy_recv, dy_local, m_send, m_recv, m_pass, gu_send, gu_recv,
 ):
     dp, ctx, fs = sizes
     n = dp * ctx * fs
     d, c, f = place()
     here = at_device(d, c, f)
     span = stage.shape[2]
-    greet_all(sizes)
+    tell_all(sizes)
+    for slot in range(4):
+        wide[slot * LANES + HD : (slot + 1) * LANES, :] = jnp.zeros((LANES - HD, D), jnp.bfloat16)
+    hear_all(sizes)
+
+    def head_rows(slot):
+        return wide.at[pl.ds(pl.multiple_of(slot * LANES, LANES), HD)]
 
     q_core = f // 2
     kv_slot = 2 + c // 2
     kv_ctx = 2 * lax.rem(c, 2) + f // 2
     kv_core = lax.rem(f, 2)
-    relay = f == 2 * lax.rem(c, 2) + d
-
-    @pl.when(jnp.logical_and(d == 1, jnp.logical_or(kv_core != 1, kv_ctx != c)))
+    kv_f = lax.rem(f + 2 * (c // 2), fs)
+    kv_away = jnp.logical_or(jnp.logical_or(kv_core != d, kv_ctx != c), kv_f != f)
+    relay_of = {slot: f == lax.rem(2 * lax.rem(c, 2) + d + 2 * (slot - 2), fs) for slot in (2, 3)}
+
+    @pl.when(jnp.logical_and(d == 1, kv_away))
     def _():
-        remote(w_ref, w_all.at[kv_slot], w_send.at[0], w_recv.at[kv_slot], at_device(kv_core, kv_ctx, f)).start()
-
-    @pl.when(jnp.logical_and(d == 1, jnp.logical_and(kv_core == 1, kv_ctx == c)))
+        remote(w_ref, head_rows(kv_slot), w_send.at[0], w_recv.at[kv_slot], at_device(kv_core, kv_ctx, kv_f)).start()
+
+    @pl.when(jnp.logical_and(d == 1, jnp.logical_not(kv_away)))
     def _():
-        pltpu.make_async_copy(w_ref, w_all.at[kv_slot], w_recv.at[kv_slot]).start()
+        pltpu.make_async_copy(w_ref, head_rows(kv_slot), w_recv.at[kv_slot]).start()
 
     line = LineGather(ctx, x_ref, x_all, line_send, line_recv, line_local)
     line.start()
@@ -468,11 +480,11 @@
 
             @pl.when(jnp.logical_or(q_core != 0, to != f))
             def _():
-                remote(w_ref, w_all.at[slot], w_send.at[to], w_recv.at[slot], at_device(q_core, c, to)).start()
+                remote(w_ref, head_rows(slot), w_send.at[to], w_recv.at[slot], at_device(q_core, c, to)).start()
 
             @pl.when(jnp.logical_and(q_core == 0, to == f))
             def _():
-                pltpu.make_async_copy(w_ref, w_all.at[slot], w_recv.at[slot]).start()
+                pltpu.make_async_copy(w_ref, head_rows(slot), w_recv.at[slot]).start()
 
     me = (d * ctx + c) * fs + f
 
@@ -487,13 +499,35 @@
     lax.fori_loop(1, n, gain_to, 0)
     gain_all[me] = gains_ref[...]
 
-    @pl.when(relay)
-    def _():
-        for slot in (2, 3):
-            arrived(w_all.at[slot], w_recv.at[slot], here)
+    for slot in (2, 3):
+
+        @pl.when(relay_of[slot])
+        def _():
+            arrived(head_rows(slot), w_recv.at[slot], here)
             for step in range(1, fs):
                 to = lax.rem(f + step, fs)
-                remote(w_all.at[slot], w_all.at[slot], w_pass.at[slot - 2, step], w_recv.at[slot], at_device(d, c, to)).start()
+                remote(head_rows(slot), head_rows(slot), w_pass.at[slot - 2, step], w_recv.at[slot], at_device(d, c, to)).start()
+
+    gu_core = f // 2
+    gu_slot = 2 * d + lax.rem(f, 2)
+    part_rows = gate_up_ref.shape[0] // parts
+
+    def push_part(part):
+        first_row = part * part_rows
+        src = gate_up_ref.at[first_row : first_row + part_rows]
+        dst = gate_up_all.at[gu_slot, first_row : first_row + part_rows]
+        for to in range(fs):
+            own_place = jnp.logical_and(gu_core == d, f == to)
+
+            @pl.when(jnp.logical_not(own_place))
+            def _():
+                remote(src, dst, gu_send.at[part, to], gu_recv.at[part, gu_slot], at_device(gu_core, c, to)).start()
+
+            @pl.when(own_place)
+            def _():
+                pltpu.make_async_copy(src, dst, gu_recv.at[part, gu_slot]).start()
+
+    push_part(0)
 
     def gain_from(step, carry):
         other = lax.rem(me + step, n)
@@ -506,17 +540,14 @@
         gain_vec[:, index * each : (index + 1) * each] = gain_all[index][:, :each]
     gain = gain_vec[0:1, :]
 
-    wide[...] = jnp.zeros_like(wide)
-    for slot in (0, 1, 2, 3):
+    for slot in range(4):
         if slot < 2:
-            arrived(w_all.at[slot], w_recv.at[slot], here)
+            arrived(head_rows(slot), w_recv.at[slot], here)
         else:
 
-            @pl.when(jnp.logical_not(relay))
-            def _():
-                arrived(w_all.at[slot], w_recv.at[slot], here)
-
-        wide[:, slot * LANES : slot * LANES + HD] = w_all[slot]
+            @pl.when(jnp.logical_not(relay_of[slot]))
+            def _():
+                arrived(head_rows(slot), w_recv.at[slot], here)
 
     pltpu.make_async_copy(line.own, line.slot(c), line.local).wait()
 
@@ -528,8 +559,8 @@
         scale = lax.rsqrt(jnp.mean(values * values, axis=-1, keepdims=True) + EPS)
         low = (values * scale * gain).astype(jnp.bfloat16)
         normed[:, at] = low.reshape(dp, 2 * span, D)
-        heads = jnp.dot(low, wide[...], preferred_element_type=jnp.float32)
-        cosine, sine_up, sine_down = cos_ref[at, f], sin_up_ref[at, f], sin_down_ref[at, f]
+        heads = outer(low, wide[...])
+        cosine, sine_up, sine_down = turns(block_ref, step_ref, at * fs + f)
         for slot in range(4):
             head = heads[:, slot * LANES : (slot + 1) * LANES]
             if slot < 3:
@@ -562,7 +593,7 @@
 
     to_core, to_ctx = lax.rem(c, 2), 2 * d + c // 2
     stays = jnp.logical_and(to_core == d, to_ctx == c)
-    moved = ((proj_ref, proj_all), (down_ref, down_all))
+    moved = ((proj_ref, proj_all),)
     for index, (shard, whole) in enumerate(moved):
 
         @pl.when(jnp.logical_not(stays))
@@ -621,8 +652,11 @@
 
         if at == 0:
             pass_on()
-        else:
-            dy_line.forward(at)
+        elif at == 1:
+            dy_line.forward(1)
+        elif at == ctx - 1:
+            for part in range(1, gu_send.shape[0]):
+                push_part(part)
 
     for at in range(ctx):
         for step in range(1, fs):
@@ -631,6 +665,8 @@
     att_copy = pltpu.make_async_copy(att, att_out, out_sem.at[4])
     att_copy.start()
 
+    for k in range(2, ctx):
+        dy_line.forward(k)
     for at in range(ctx):
         dy_line.other(at)
     dy_line.finish()
@@ -644,6 +680,16 @@
         def _():
             left(shard, m_send.at[index], here)
 
+    for part in range(gu_send.shape[0]):
+        src = gate_up_ref.at[part * part_rows : (part + 1) * part_rows]
+        for slot in range(4):
+            arrived(gate_up_all.at[slot, part * part_rows : (part + 1) * part_rows], gu_recv.at[part, slot], here)
+        for to in range(fs):
+
+            @pl.when(jnp.logical_not(jnp.logical_and(gu_core == d, f == to)))
+            def _():
+                left(src, gu_send.at[part, to], here)
+
     line.finish_sends()
     for at in range(ctx):
 
@@ -654,7 +700,7 @@
                 left(stage.at[at, to], u_send.at[at, to], here)
                 left(att_stage.at[at, to], a_send.at[at, to], here)
 
-    @pl.when(jnp.logical_and(d == 1, jnp.logical_or(kv_core != 1, kv_ctx != c)))
+    @pl.when(jnp.logical_and(d == 1, kv_away))
     def _():
         left(w_ref, w_send.at[0], here)
 
@@ -666,11 +712,12 @@
             def _():
                 left(w_ref, w_send.at[to], here)
 
-    @pl.when(relay)
-    def _():
-        for slot in (2, 3):
+    for slot in (2, 3):
+
+        @pl.when(relay_of[slot])
+        def _():
             for step in range(1, fs):
-                left(w_all.at[slot], w_pass.at[slot - 2, step], here)
+                left(head_rows(slot), w_pass.at[slot - 2, step], here)
 
     def gain_left(step, carry):
         other = lax.rem(me + step, n)
@@ -682,7 +729,7 @@
         copy.wait()
 
 
-def first(sizes, x, gains, w_qkv, cosine, sine_up, sine_down, dy, w_out, w_down):
+def first(sizes, parts, sent, x, gains, w_qkv, blocks, steps, dy, w_out, w_gate_up):
     dp, ctx, fs = sizes
     n = dp * ctx * fs
     rows = x.shape[0]
@@ -693,23 +740,22 @@
         jax.ShapeDtypeStruct((dp, ctx, rows, D), low),
         jax.ShapeDtypeStruct((ctx, fs, span, 4 * LANES), low),
         jax.ShapeDtypeStruct((dp, ctx, 2, span, 2 * LANES), low),
-        jax.ShapeDtypeStruct((D, 4 * LANES), low),
+        jax.ShapeDtypeStruct((4 * LANES, D), low),
         jax.ShapeDtypeStruct((8, D), wide_t),
         jax.ShapeDtypeStruct((dp, ctx, rows, D), low),
         jax.ShapeDtypeStruct((fs,) + w_out.shape, low),
-        jax.ShapeDtypeStruct((fs,) + w_down.shape, low),
+        jax.ShapeDtypeStruct((4, D // parts * sent, w_gate_up.shape[1]), low),
     )
     any_spec, vm_spec = pl.BlockSpec(memory_space=ANY), pl.BlockSpec(memory_space=VM)
     return pl.pallas_call(
-        functools.partial(first_kernel, sizes),
+        functools.partial(first_kernel, sizes, parts),
         name="first",
         out_shape=shapes,
-        in_specs=[vm_spec, vm_spec, any_spec, vm_spec, vm_spec, vm_spec, vm_spec, any_spec, any_spec],
+        in_specs=[vm_spec] * 8,
         out_specs=[any_spec] * 8,
         scratch_shapes=[
             VM((dp, ctx, rows, D), low),
-            VM((4, D, HD), low),
-            VM((D, 4 * LANES), low),
+            VM((4 * LANES, D), low),
             VM((dp, ctx, rows, D), low),
             VM((ctx, 2 * dp, span, 4 * LANES), low),
             VM((ctx, fs, span, 4 * LANES), low),
@@ -724,28 +770,33 @@
             dma((ctx, fs)), dma((fs, ctx)),
             dma((5,)),
             dma((3, ctx)), dma((dp, ctx)), dma,
-            dma((2,)), dma((2, fs)), dma((2, fs)),
+            dma((1,)), dma((1, fs)), dma((1, fs)),
+            dma((sent, fs)), dma((sent, 4)),
         ],
         compiler_params=pltpu.CompilerParams(collective_id=1, has_side_effects=True, vmem_limit_bytes=60 * 1024 * 1024),
-    )(x, gains, w_qkv, cosine, sine_up, sine_down, dy, w_out, w_down)
-
-
-def angle_tables(ctx, fs, span):
-    return lane_tables(jnp.arange(ctx * fs * span, dtype=jnp.int32).reshape(ctx, fs, span))
-
-
-def lane_tables(positions):
+    )(x, gains, w_qkv, blocks, steps, dy, w_out, w_gate_up)
+
+
+def angle_tables(count, span):
     lane = jnp.arange(LANES, dtype=jnp.int32)
-    pair = (lane % (HD // 2)).astype(jnp.float32)
-    frequency = THETA ** (-(pair * 2.0) / HD)
-    angles = positions.astype(jnp.float32)[..., None] * frequency
-    inside = lane < HD
-    low_half = lane < HD // 2
-    cosine = jnp.where(inside, jnp.cos(angles), 0.0)
-    sine = jnp.sin(angles)
-    sine_up = jnp.where(jnp.logical_and(inside, jnp.logical_not(low_half)), sine, 0.0)
-    sine_down = jnp.where(low_half, -sine, 0.0)
-    return cosine, sine_up, sine_down
+    frequency = THETA ** (-((lane % (HD // 2)).astype(jnp.float32) * 2.0) / HD)
+
+    def both(positions):
+        angles = positions.astype(jnp.float32)[:, None] * frequency
+        return jnp.stack([jnp.cos(angles), jnp.sin(angles)])
+
+    return both(jnp.arange(count, dtype=jnp.int32) * span), both(jnp.arange(span, dtype=jnp.int32))
+
+
+def turns(block_ref, step_ref, block):
+    cos_b, sin_b = block_ref[0, pl.ds(block, 1)], block_ref[1, pl.ds(block, 1)]
+    cos_s, sin_s = step_ref[0], step_ref[1]
+    cosine = cos_b * cos_s - sin_b * sin_s
+    sine = sin_b * cos_s + cos_b * sin_s
+    lane = lax.broadcasted_iota(jnp.int32, sine.shape, 1)
+    first_half = lane < HD // 2
+    sine_up = jnp.where(jnp.logical_and(lane >= HD // 2, lane < HD), sine, 0.0)
+    return cosine, sine_up, jnp.where(first_half, -sine, 0.0)
 
 
 class LineSum:
@@ -824,45 +875,46 @@
         ]
 
 
-def greet_near(sizes):
+def down_route(d, c):
+    return (lax.rem(c, 2), 2 * d + c // 2), (c // 2, 2 * lax.rem(c, 2) + d)
+
+
+def near_devices(sizes):
     dp, ctx, fs = sizes
     d, c, f = place()
-    barrier = pltpu.get_barrier_semaphore()
-
-    def tell(device):
-        pl.semaphore_signal(barrier, inc=1, device_id=device, device_id_type=MESH)
-
-    tell(at_device(1 - d, c, f))
+    yes = c >= 0
+    found = [(at_device(1 - d, c, f), yes)]
     for step in range(1, fs):
         for core in range(dp):
-            tell(at_device(core, c, lax.rem(f + step, fs)))
-
-    @pl.when(c > 0)
-    def _():
-        tell(at_device(d, c - 1, f))
-
-    @pl.when(c < ctx - 1)
-    def _():
-        tell(at_device(d, c + 1, f))
-
-    known = 1 + dp * (fs - 1)
-    ends = jnp.logical_or(c == 0, c == ctx - 1)
-
-    @pl.when(ends)
-    def _():
-        pl.semaphore_wait(barrier, known + 1)
-
-    @pl.when(jnp.logical_not(ends))
-    def _():
-        pl.semaphore_wait(barrier, known + 2)
+            found.append((at_device(core, c, lax.rem(f + step, fs)), yes))
+    found.append((at_device(d, c - 1, f), c > 0))
+    found.append((at_device(d, c + 1, f), c < ctx - 1))
+    for core, place_ in down_route(d, c):
+        found.append((at_device(core, place_, f), jnp.logical_or(core != d, place_ != c)))
+    return found
+
+
+def tell_near(sizes):
+    barrier = pltpu.get_barrier_semaphore()
+    for device, counts in near_devices(sizes):
+
+        @pl.when(counts)
+        def _():
+            pl.semaphore_signal(barrier, inc=1, device_id=device, device_id_type=MESH)
+
+
+def hear_near(sizes):
+    peers = sum(jnp.where(counts, 1, 0) for _, counts in near_devices(sizes))
+    pl.semaphore_wait(pltpu.get_barrier_semaphore(), peers)
 
 
 def middle_kernel(
-    sizes, hidden, att_ref, x_ref, dy_ref, gains_ref, proj_ref, down_ref, gate_up_ref, dy_all_ref,
-    resid_out, d_resid_out, gain_out, partial_out, unit_out, grad_up_out, grad_down_out, grad_proj_out,
+    sizes, hidden, parts, sent, att_ref, x_ref, dy_ref, gains_ref, proj_ref, down_ref, gate_up_ref, gate_up_part_ref, dy_all_ref,
+    resid_out, d_resid_out, gain_out, partial_out, unit_out, grad_proj_out, up_land, down_land,
     att, dy_all, proj, down, gate_up, resid, own_two, normed_two, act, d_both, part_stage, own_d, d_resid_all, d_stage, unit,
     grad_up, grad_down, grad_proj, grad_proj_low,
-    in_sem, gu_send, gu_recv, two_send, two_recv, two_local, dr_send, dr_recv, dr_local, u_send, u_recv, out_sem, part_sem,
+    in_sem, gu_send, gu_recv, m_send, m_recv, m_pass, two_send, two_recv, two_local, dr_send, dr_recv, dr_local, u_send, u_recv,
+    out_sem, part_sem, gup_send, gup_recv, gdn_send, gdn_recv,
     *sums,
 ):
     dp, ctx, fs = sizes
@@ -874,10 +926,12 @@
     half = hidden // 2
     line_sum = LineSum(ctx, *sums[:6], sums[6:10])
     second_sum = LineSum(ctx, *sums[10:16], sums[16:20])
+    part_rows = D // parts
+    tell_near(sizes)
 
     att_copy = pltpu.make_async_copy(att_ref, att, in_sem.at[0])
     dy_copy = pltpu.make_async_copy(dy_all_ref, dy_all, in_sem.at[1])
-    down_copy = pltpu.make_async_copy(down_ref, down, in_sem.at[2])
+    part_copy = pltpu.make_async_copy(gate_up_part_ref, gate_up.at[:, 0 : part_rows * sent], in_sem.at[2])
     att_copy.start()
     proj[...] = jnp.zeros_like(proj)
     each = proj_ref.shape[1]
@@ -887,21 +941,33 @@
         proj_copies.append(pltpu.make_async_copy(proj_ref.at[slot], proj.at[start : start + each], in_sem.at[3 + slot]))
         proj_copies[-1].start()
     dy_copy.start()
-    down_copy.start()
-    greet_near(sizes)
-
-    to_core = f // 2
+    part_copy.start()
+    hear_near(sizes)
+
+    (to_core, to_ctx), _ = down_route(d, c)
+    stays = jnp.logical_and(to_core == d, to_ctx == c)
+
+    @pl.when(jnp.logical_not(stays))
+    def _():
+        remote(down_ref, down.at[f], m_send, m_recv.at[f], at_device(to_core, to_ctx, f)).start()
+
+    @pl.when(stays)
+    def _():
+        pltpu.make_async_copy(down_ref, down.at[f], m_recv.at[f]).start()
+
+    gu_core = f // 2
     gu_slot = 2 * d + lax.rem(f, 2)
+    rest = slice(part_rows * sent, D)
     for to in range(fs):
-        own_place = jnp.logical_and(to_core == d, f == to)
+        own_place = jnp.logical_and(gu_core == d, f == to)
 
         @pl.when(jnp.logical_not(own_place))
         def _():
-            remote(gate_up_ref, gate_up.at[gu_slot], gu_send.at[to], gu_recv.at[gu_slot], at_device(to_core, c, to)).start()
+            remote(gate_up_ref.at[rest], gate_up.at[gu_slot, rest], gu_send.at[to], gu_recv.at[gu_slot], at_device(gu_core, c, to)).start()
 
         @pl.when(own_place)
         def _():
-            pltpu.make_async_copy(gate_up_ref, gate_up.at[gu_slot], gu_recv.at[gu_slot]).start()
+            pltpu.make_async_copy(gate_up_ref.at[rest], gate_up.at[gu_slot, rest], gu_recv.at[gu_slot]).start()
 
     att_copy.wait()
     for copy in proj_copies:
@@ -915,11 +981,18 @@
 
     lax.fori_loop(0, ctx, project, 0)
 
+    line_sum.step(ordered(c, ctx - 1, ctx))
+    line_sum.step(ordered(c, ctx - 2, ctx))
+    arrived(down.at[f], m_recv.at[f], here)
+    for step in range(1, fs):
+        to = lax.rem(f + step, fs)
+        remote(down.at[f], down.at[f], m_pass.at[step], m_recv.at[f], at_device(d, c, to)).start()
+
     def sum_up(step, carry):
         line_sum.step(ordered(c, ctx - 1 - step, ctx))
         return carry
 
-    lax.fori_loop(0, ctx, sum_up, 0)
+    lax.fori_loop(2, ctx, sum_up, 0)
     gain = gains_ref[1:2, :]
     values = x_ref[...].astype(jnp.float32) + line_sum.total[...]
     resid[...] = values
@@ -931,9 +1004,12 @@
     line.start()
     line_sum.finish()
     for slot in range(4):
-        arrived(gate_up.at[slot], gu_recv.at[slot], here)
+        arrived(gate_up.at[slot, rest], gu_recv.at[slot], here)
     dy_copy.wait()
-    down_copy.wait()
+    part_copy.wait()
+    for step in range(1, fs):
+        other = lax.rem(f + step, fs)
+        arrived(down.at[other], m_recv.at[other], here)
     pltpu.make_async_copy(line.own, line.slot(c), line.local).wait()
 
     def mlp(step, carry):
@@ -946,7 +1022,7 @@
             cols = slice(part * half, (part + 1) * half)
             gate = jnp.dot(inputs, gate_up[part], preferred_element_type=jnp.float32)
             up = jnp.dot(inputs, gate_up[2 + part], preferred_element_type=jnp.float32)
-            d_act = outer(dy_rows, down[cols, :])
+            d_act = outer(dy_rows, down[2 * part : 2 * part + 2].reshape(half, D))
             sig = 1.0 / (1.0 + jnp.exp(-gate))
             silu = gate * sig
             act[:, at, :, cols] = (silu * up).astype(jnp.bfloat16).reshape(dp, rows, half)
@@ -965,6 +1041,17 @@
 
     wide_rows = D // ctx
 
+    def push(src, dst, send, recv, core, to):
+        to_self = jnp.logical_and(core == d, to == f)
+
+        @pl.when(jnp.logical_not(to_self))
+        def _():
+            remote(src, dst, send, recv, at_device(core, c, to)).start()
+
+        @pl.when(to_self)
+        def _():
+            pltpu.make_async_copy(src, dst, recv).start()
+
     def grads(step):
         first = pl.multiple_of(step * wide_rows, LANES)
         left_rows = normed_two[:, :, :, pl.ds(first, wide_rows)].reshape(dp * ctx * rows, wide_rows)
@@ -974,7 +1061,17 @@
             grad_up[2 * part, pl.ds(first, wide_rows), :] = terms[:, :half]
             grad_up[2 * part + 1, pl.ds(first, wide_rows), :] = terms[:, half:]
         dy_cols = dy_all[:, :, :, pl.ds(first, wide_rows)].reshape(dp * ctx * rows, wide_rows)
-        grad_down[:, pl.ds(first, wide_rows)] = inner(act[...].reshape(dp * ctx * rows, hidden), dy_cols).astype(jnp.bfloat16)
+        terms = inner(act[...].reshape(dp * ctx * rows, hidden), dy_cols).astype(jnp.bfloat16)
+        grad_down[:, :, pl.ds(first, wide_rows)] = terms.reshape(fs, hidden // fs, wide_rows)
+        for slot in range(4):
+            push(
+                grad_up.at[slot, pl.ds(first, wide_rows)], up_land.at[f, pl.ds(first, wide_rows)],
+                gup_send.at[slot, step], gup_recv.at[f, step], slot // 2, 2 * d + slot % 2,
+            )
+            push(
+                grad_down.at[slot, :, pl.ds(first, wide_rows)], down_land.at[f, :, pl.ds(first, wide_rows)],
+                gdn_send.at[slot, step], gdn_recv.at[f, step], d, slot,
+            )
 
     def sum_two(step, carry):
         second_sum.step(ordered(c, ctx - 1 - step, ctx))
@@ -1000,10 +1097,6 @@
     line.finish_sends()
     second_sum.finish()
     grads(ctx - 1)
-    grad_up_copy = pltpu.make_async_copy(grad_up, grad_up_out, out_sem.at[1])
-    grad_down_copy = pltpu.make_async_copy(grad_down, grad_down_out, out_sem.at[2])
-    grad_up_copy.start()
-    grad_down_copy.start()
     pltpu.make_async_copy(d_line.own, d_line.slot(c), d_line.local).wait()
     grad_proj[...] = jnp.zeros_like(grad_proj)
 
@@ -1026,7 +1119,7 @@
 
         grad_proj[...] += inner(att[:, at].reshape(both_rows, 2 * LANES), incoming)
 
-        outputs = jnp.dot(act[:, at].reshape(both_rows, hidden), down[...], preferred_element_type=jnp.float32)
+        outputs = jnp.dot(act[:, at].reshape(both_rows, hidden), down[...].reshape(hidden, D), preferred_element_type=jnp.float32)
         slot = lax.rem(step, 2)
 
         @pl.when(step >= 2)
@@ -1041,13 +1134,13 @@
     for slot in range(fs):
         start = slot // 2 * LANES + slot % 2 * each
         grad_proj_low[slot] = grad_proj[start : start + each, :].astype(jnp.bfloat16)
-    grad_proj_copy = pltpu.make_async_copy(grad_proj_low, grad_proj_out, out_sem.at[3])
+    grad_proj_copy = pltpu.make_async_copy(grad_proj_low, grad_proj_out, out_sem.at[1])
     grad_proj_copy.start()
     for at in range(ctx):
         for step in range(1, fs):
             other = lax.rem(f + step, fs)
             arrived(unit.at[at, other], u_recv.at[at, other], here)
-    unit_copy = pltpu.make_async_copy(unit, unit_out, out_sem.at[4])
+    unit_copy = pltpu.make_async_copy(unit, unit_out, out_sem.at[2])
     unit_copy.start()
     d_line.finish_sends()
     for at in range(ctx):
@@ -1059,17 +1152,42 @@
 
     for to in range(fs):
 
-        @pl.when(jnp.logical_not(jnp.logical_and(to_core == d, f == to)))
-        def _():
-            left(gate_up_ref, gu_send.at[to], here)
-
+        @pl.when(jnp.logical_not(jnp.logical_and(gu_core == d, f == to)))
+        def _():
+            left(gate_up_ref.at[rest], gu_send.at[to], here)
+
+    @pl.when(jnp.logical_not(stays))
+    def _():
+        left(down_ref, m_send, here)
+
+    for step in range(1, fs):
+        left(down.at[f], m_pass.at[step], here)
+
+    def settle(step, carry):
+        first = pl.multiple_of(step * wide_rows, LANES)
+        for slot in range(4):
+            up_src, down_src = grad_up.at[slot, pl.ds(first, wide_rows)], grad_down.at[slot, :, pl.ds(first, wide_rows)]
+            arrived(up_land.at[slot, pl.ds(first, wide_rows)], gup_recv.at[slot, step], here)
+            arrived(down_land.at[slot, :, pl.ds(first, wide_rows)], gdn_recv.at[slot, step], here)
+
+            @pl.when(jnp.logical_or(slot // 2 != d, 2 * d + slot % 2 != f))
+            def _():
+                left(up_src, gup_send.at[slot, step], here)
+
+            @pl.when(slot != f)
+            def _():
+                left(down_src, gdn_send.at[slot, step], here)
+
+        return carry
+
+    lax.fori_loop(0, ctx, settle, 0)
     for slot in range(2):
         pltpu.make_async_copy(part_stage.at[slot], partial_out.at[:, 0], part_sem.at[slot]).wait()
-    for copy in (resid_copy, grad_up_copy, grad_down_copy, grad_proj_copy, unit_copy):
+    for copy in (resid_copy, grad_proj_copy, unit_copy):
         copy.wait()
 
 
-def middle(sizes, att, x, dy, gains, proj, down, w_gate_up, dy_all):
+def middle(sizes, parts, sent, att, x, dy, gains, proj, w_down, w_gate_up, gate_up_part, dy_all):
     dp, ctx, fs = sizes
     rows = x.shape[0]
     span = rows // 2
@@ -1083,21 +1201,21 @@
         jax.ShapeDtypeStruct((8, D), wide_t),
         jax.ShapeDtypeStruct((dp, ctx, rows, D), low),
         jax.ShapeDtypeStruct((ctx, fs, span, 2 * LANES), low),
-        jax.ShapeDtypeStruct((4, D, hidden // 2), low),
-        jax.ShapeDtypeStruct((hidden, D), low),
         jax.ShapeDtypeStruct(proj.shape, low),
+        jax.ShapeDtypeStruct((fs, D, hidden // 2), low),
+        jax.ShapeDtypeStruct((fs, hidden // fs, D), low),
     )
     return pl.pallas_call(
-        functools.partial(middle_kernel, sizes, hidden),
+        functools.partial(middle_kernel, sizes, hidden, parts, sent),
         name="middle",
         out_shape=shapes,
-        in_specs=[any_spec, vm_spec, vm_spec, vm_spec, any_spec, any_spec, any_spec, any_spec],
+        in_specs=[any_spec, vm_spec, vm_spec, vm_spec, any_spec, vm_spec, vm_spec, any_spec, any_spec],
         out_specs=[any_spec, vm_spec, vm_spec] + [any_spec] * 5,
         scratch_shapes=[
             VM((dp, ctx, rows, 2 * LANES), low),
             VM((dp, ctx, rows, D), low),
             VM((2 * LANES, D), low),
-            VM((hidden, D), low),
+            VM((fs, hidden // fs, D), low),
             VM((4, D, hidden // 2), low),
             VM((rows, D), wide_t),
             VM((rows, D), low),
@@ -1110,26 +1228,27 @@
             VM((ctx, 2 * dp, span, 2 * LANES), low),
             VM((ctx, fs, span, 2 * LANES), low),
             VM((4, D, hidden // 2), low),
-            VM((hidden, D), low),
+            VM((fs, hidden // fs, D), low),
             VM((2 * LANES, D), wide_t),
             VM(proj.shape, low),
-            dma((3 + fs,)), dma((fs,)), dma((4,)),
+            dma((3 + fs,)), dma((fs,)), dma((4,)), dma, dma((fs,)), dma((fs,)),
             dma((3, ctx)), dma((dp, ctx)), dma,
             dma((3, ctx)), dma((dp, ctx)), dma,
             dma((ctx, 2 * dp)), dma((ctx, fs)),
-            dma((5,)), dma((2,)),
+            dma((3,)), dma((2,)),
+            dma((4, ctx)), dma((fs, ctx)), dma((fs, ctx)), dma((fs, ctx)),
         ] + LineSum.scratch(ctx, rows) + LineSum.scratch(ctx, rows),
         compiler_params=pltpu.CompilerParams(collective_id=2, has_side_effects=True, vmem_limit_bytes=63 * 1024 * 1024),
-    )(att, x, dy, gains, proj, down.reshape(hidden, D), w_gate_up, dy_all)
+    )(att, x, dy, gains, proj, w_down, w_gate_up, gate_up_part, dy_all)
 
 
 def last_kernel(
-    sizes, x_ref, gains_ref, cos_ref, sin_up_ref, sin_down_ref, resid_ref, d_resid_ref, gain_two_ref,
-    unit_ref, d_unit_ref, normed_ref, wide_ref, partial_ref, up_ref, down_ref, proj_ref,
+    sizes, x_ref, gains_ref, block_ref, step_ref, resid_ref, d_resid_ref, gain_two_ref, proj_ref,
+    unit_ref, d_unit_ref, normed_ref, wide_ref, partial_ref, up_land_ref, down_land_ref,
     out_ref, d_x_ref, gains_out, qkv_out, proj_out, up_out, down_out,
-    unit, d_unit, d_k, d_v, stage, mixed, normed, wide, grad_wide, grad_heads,
+    unit, d_unit, d_k, d_v, stage, mixed, normed, wide, grad_heads,
     up_land, down_land, proj_land, q_land, kv_land, down_sum, proj_sum, kv_sum, down_last, proj_last, kv_last, gain_vec, gain_stage, gain_land,
-    in_sem, up_send, up_recv, down_send, down_recv, proj_send, proj_recv, head_send, head_recv, move_send, move_recv,
+    in_sem, proj_send, proj_recv, head_send, head_recv, move_send, move_recv,
     u_send, u_recv, g_send, g_recv, mine_sem,
     *sums,
 ):
@@ -1144,15 +1263,20 @@
     low, wide_t = jnp.bfloat16, jnp.float32
     loads = [
         pltpu.make_async_copy(src, dst, in_sem.at[index])
-        for index, (src, dst) in enumerate(((unit_ref, unit), (d_unit_ref, d_unit), (normed_ref, normed), (wide_ref, wide)))
+        for index, (src, dst) in enumerate((
+            (unit_ref, unit), (d_unit_ref, d_unit), (normed_ref, normed), (wide_ref, wide), (down_land_ref, down_land), (up_land_ref, up_land),
+        ))
     ]
+    tell_all(sizes)
     for load in loads:
         load.start()
     out_sum = LineSum(ctx, *sums[:6], sums[6:10])
     in_sum = LineSum(ctx, *sums[10:16], sums[16:20])
     for at in range(ctx):
         pltpu.make_async_copy(partial_ref.at[d, at], out_sum.mine.at[at], mine_sem.at[at]).start()
-    greet_all(sizes)
+    d_k[...] = jnp.zeros_like(d_k)
+    d_v[...] = jnp.zeros_like(d_v)
+    hear_all(sizes)
 
     for at in range(ctx):
         remote(
@@ -1175,27 +1299,40 @@
         def _():
             left(src, send, here)
 
-    def push_down():
-        for slot in range(fs):
-            push(down_ref.at[slot], down_land, down_send.at[slot], down_recv, d, slot)
-            push(proj_ref.at[slot], proj_land, proj_send.at[slot], proj_recv, d, slot)
-
-    def push_up():
-        for slot in range(4):
-            push(up_ref.at[slot], up_land, up_send.at[slot], up_recv, slot // 2, 2 * d + slot % 2)
-
-    push_up()
-    push_down()
+    def sum_of(land):
+        total = land[0].astype(wide_t)
+        for source in range(1, fs):
+            total += land[source].astype(wide_t)
+        return total
+
+    _, (own_core, own_ctx) = down_route(d, c)
+    stays = jnp.logical_and(own_core == d, own_ctx == c)
+
+    def move(index, src, dst):
+        @pl.when(jnp.logical_not(stays))
+        def _():
+            remote(src, dst, move_send.at[index], move_recv.at[index], at_device(own_core, own_ctx, f)).start()
+
+        @pl.when(stays)
+        def _():
+            pltpu.make_async_copy(src, dst, move_recv.at[index]).start()
+
+    loads[4].wait()
+    down_sum[...] = sum_of(down_land).astype(low)
+    move(0, down_sum, down_last)
     loads[0].wait()
     loads[1].wait()
-    d_k[...] = jnp.zeros_like(d_k)
-    d_v[...] = jnp.zeros_like(d_v)
     block = fs * span
 
     def unturn(values, at):
-        up = pltpu.roll(values, HD // 2, 1).reshape(fs, span, LANES)
-        down = pltpu.roll(values, LANES - HD // 2, 1).reshape(fs, span, LANES)
-        return values.reshape(fs, span, LANES) * cos_ref[at] - up * sin_up_ref[at] - down * sin_down_ref[at]
+        up = pltpu.roll(values, HD // 2, 1)
+        down = pltpu.roll(values, LANES - HD // 2, 1)
+        pieces = []
+        for index in range(fs):
+            own = slice(index * span, (index + 1) * span)
+            cosine, sine_up, sine_down = turns(block_ref, step_ref, at * fs + index)
+            pieces.append(values[own] * cosine - up[own] * sine_up - down[own] * sine_down)
+        return jnp.concatenate(pieces, axis=0).reshape(fs, span, LANES)
 
     for at in reversed(range(ctx)):
         keys = block * (at + 1)
@@ -1232,81 +1369,75 @@
             def _():
                 mixed[f // 2, at, lax.rem(f, 2)] = stage[at, to]
 
+    for slot in range(fs):
+        push(proj_ref.at[slot], proj_land, proj_send.at[slot], proj_recv, d, slot)
     loads[2].wait()
     loads[3].wait()
 
     def give(step, carry):
         at = ordered(c, ctx - 1 - step, ctx)
-        for move in range(1, fs):
-            other = lax.rem(f + move, fs)
+        for step_ in range(1, fs):
+            other = lax.rem(f + step_, fs)
             arrived(mixed.at[other // 2, at, lax.rem(other, 2)], u_recv.at[other, at], here)
-        terms = outer(mixed[:, at].reshape(both_rows, 4 * LANES), wide[...])
+        terms = jnp.dot(mixed[:, at].reshape(both_rows, 4 * LANES), wide[...], preferred_element_type=wide_t)
         in_sum.give(at, terms.reshape(dp, rows, D))
         return carry
 
     lax.fori_loop(0, ctx, give, 0)
+    in_sum.step(ordered(c, ctx - 1, ctx))
 
     every = dp * ctx * rows
-    quarter = D // ctx
-
-    def grads(step, carry):
-        first_row = pl.multiple_of(step * quarter, LANES)
-        rows_of = normed[:, :, :, pl.ds(first_row, quarter)].reshape(every, quarter)
-        grad_wide[pl.ds(first_row, quarter), :] = inner(rows_of, mixed[...].reshape(every, 4 * LANES)).astype(low)
-        return carry
-
-    relay_f = 2 * lax.rem(c, 2) + d
-
-    def push_heads():
-        for slot in range(4):
-            grad_heads[slot] = grad_wide[:, slot * LANES : slot * LANES + HD]
-        for slot in range(2):
+    k_relay = 2 * lax.rem(c, 2) + d
+    relays = (k_relay, lax.rem(k_relay + 2, fs))
+    for slot in (2, 3, 0, 1):
+        heads = inner(mixed[:, :, :, :, slot * LANES : (slot + 1) * LANES].reshape(every, LANES), normed[...].reshape(every, D))
+        grad_heads[slot] = heads[:HD].astype(low)
+        if slot < 2:
             push(grad_heads.at[slot], q_land, head_send.at[slot], head_recv.at[0], 0, 2 * d + slot)
-        for slot in range(2):
-            push(grad_heads.at[2 + slot], kv_land.at[slot], head_send.at[2 + slot], head_recv.at[1 + slot], d, relay_f)
-
-    def out_step(step, carry):
+        else:
+            push(grad_heads.at[slot], kv_land.at[slot - 2], head_send.at[slot], head_recv.at[slot - 1], d, relays[slot - 2])
+
+    def steps(step, carry):
         at = ordered(c, ctx - 1 - step, ctx)
         pltpu.make_async_copy(partial_ref.at[d, at], out_sum.mine.at[at], mine_sem.at[at]).wait()
         out_sum.step(at)
+
+        @pl.when(step < ctx - 2)
+        def _():
+            in_sum.step(ordered(c, ctx - 2 - step, ctx))
+
         return carry
 
-    lax.fori_loop(0, ctx, out_step, 0)
+    lax.fori_loop(0, ctx, steps, 0)
     out_ref[...] = (resid_ref[...] + out_sum.total[...]).astype(low)
-    in_sum.step(ordered(c, ctx - 1, ctx))
-    lax.fori_loop(0, ctx, grads, 0)
-    push_heads()
-
-    def in_step(step, carry):
-        in_sum.step(ordered(c, ctx - 1 - step, ctx))
-        return carry
-
-    lax.fori_loop(1, ctx - 1, in_step, 0)
-
-    def sum_of(land):
-        total = land[0].astype(wide_t)
-        for source in range(1, fs):
-            total += land[source].astype(wide_t)
-        return total
-
     for source in range(fs):
-        arrived(down_land.at[source], down_recv.at[source], here)
         arrived(proj_land.at[source], proj_recv.at[source], here)
-    down_sum[...] = sum_of(down_land).astype(low)
     proj_sum[...] = sum_of(proj_land).astype(low)
-    own_core, own_ctx = c // 2, 2 * lax.rem(c, 2) + d
-    stays = jnp.logical_and(own_core == d, own_ctx == c)
-    moves = ((down_sum, down_last), (proj_sum, proj_last))
-    for index, (src, dst) in enumerate(moves):
-
-        @pl.when(jnp.logical_not(stays))
-        def _():
-            remote(src, dst, move_send.at[index], move_recv.at[index], at_device(own_core, own_ctx, f)).start()
-
-        @pl.when(stays)
-        def _():
-            pltpu.make_async_copy(src, dst, move_recv.at[index]).start()
-
+    move(1, proj_sum, proj_last)
+
+    def kv_route(slot):
+        owner, owner_f = slot * 2 + c // 2, k_relay
+        return owner, owner_f, jnp.logical_or(jnp.logical_or(d != 1, owner != c), owner_f != f)
+
+    for slot in range(2):
+        owner, owner_f, away = kv_route(slot)
+
+        @pl.when(f == relays[slot])
+        def _():
+            for source in range(fs):
+                arrived(kv_land.at[slot, source], head_recv.at[1 + slot, source], here)
+            kv_sum[slot] = sum_of(kv_land.at[slot]).astype(low)
+
+            @pl.when(away)
+            def _():
+                remote(kv_sum.at[slot], kv_last, move_send.at[2 + slot], move_recv.at[2], at_device(1, owner, owner_f)).start()
+
+            @pl.when(jnp.logical_not(away))
+            def _():
+                pltpu.make_async_copy(kv_sum.at[slot], kv_last, move_recv.at[2]).start()
+
+    loads[5].wait()
+    up_out[...] = sum_of(up_land)
     in_sum.step(c)
 
     gain = gains_ref[0:1, :]
@@ -1333,28 +1464,7 @@
 
     lax.fori_loop(1, n, gain_to, 0)
 
-    for slot in range(2):
-        owner = slot * 2 + c // 2
-
-        @pl.when(f == relay_f)
-        def _():
-            for source in range(fs):
-                arrived(kv_land.at[slot, source], head_recv.at[1 + slot, source], here)
-            kv_sum[slot] = sum_of(kv_land.at[slot]).astype(low)
-            away = jnp.logical_or(d != 1, owner != c)
-
-            @pl.when(away)
-            def _():
-                remote(kv_sum.at[slot], kv_last, move_send.at[2 + slot], move_recv.at[2], at_device(1, owner, f)).start()
-
-            @pl.when(jnp.logical_not(away))
-            def _():
-                pltpu.make_async_copy(kv_sum.at[slot], kv_last, move_recv.at[2]).start()
-
-    for source in range(fs):
-        arrived(up_land.at[source], up_recv.at[source], here)
-    up_out[...] = sum_of(up_land)
-    for index, (src, dst) in enumerate(moves):
+    for index, dst in enumerate((down_last, proj_last)):
         arrived(dst, move_recv.at[index], here)
     down_out[...] = down_last[...].astype(wide_t)
     proj_out[...] = proj_last[...].astype(wide_t)
@@ -1381,22 +1491,20 @@
         total += gain_land[index]
     gains_out[...] = total
 
-    for slot in range(4):
-        pushed(up_ref.at[slot], up_send.at[slot], slot // 2, 2 * d + slot % 2)
-        pushed(down_ref.at[slot], down_send.at[slot], d, slot)
+    for slot in range(fs):
         pushed(proj_ref.at[slot], proj_send.at[slot], d, slot)
     for slot in range(2):
         pushed(grad_heads.at[slot], head_send.at[slot], 0, 2 * d + slot)
-        pushed(grad_heads.at[2 + slot], head_send.at[2 + slot], d, relay_f)
-        owner = slot * 2 + c // 2
-
-        @pl.when(jnp.logical_and(f == relay_f, jnp.logical_or(d != 1, owner != c)))
+        pushed(grad_heads.at[2 + slot], head_send.at[2 + slot], d, relays[slot])
+        away = kv_route(slot)[2]
+
+        @pl.when(jnp.logical_and(f == relays[slot], away))
         def _():
             left(kv_sum.at[slot], move_send.at[2 + slot], here)
 
         @pl.when(jnp.logical_not(stays))
         def _():
-            left(moves[slot][0], move_send.at[slot], here)
+            left((down_sum, proj_sum)[slot], move_send.at[slot], here)
 
     for at in range(ctx):
         for to in range(fs):
@@ -1421,7 +1529,7 @@
     lax.fori_loop(1, n, gain_left, 0)
 
 
-def last(sizes, x, gains, tables, resid, d_resid, gain_two, unit, d_unit, normed, wide, partial, grad_up, grad_down, grad_proj):
+def last(sizes, x, gains, tables, resid, d_resid, gain_two, grad_proj, unit, d_unit, normed, wide, partial, up_land, down_land):
     dp, ctx, fs = sizes
     n = dp * ctx * fs
     rows = x.shape[0]
@@ -1429,12 +1537,12 @@
     low, wide_t = jnp.bfloat16, jnp.float32
     dma = pltpu.SemaphoreType.DMA
     any_spec, vm_spec = pl.BlockSpec(memory_space=ANY), pl.BlockSpec(memory_space=VM)
-    down_rows, proj_rows, half = grad_down.shape[0] // fs, grad_proj.shape[1], grad_up.shape[2]
+    down_rows, proj_rows, half = down_land.shape[1], grad_proj.shape[1], up_land.shape[2]
     shapes = (
         jax.ShapeDtypeStruct((rows, D), low),
         jax.ShapeDtypeStruct((rows, D), low),
         jax.ShapeDtypeStruct((8, LANES), wide_t),
-        jax.ShapeDtypeStruct((D, HD), wide_t),
+        jax.ShapeDtypeStruct((HD, D), wide_t),
         jax.ShapeDtypeStruct((proj_rows, D), wide_t),
         jax.ShapeDtypeStruct((D, half), wide_t),
         jax.ShapeDtypeStruct((down_rows, D), wide_t),
@@ -1443,7 +1551,7 @@
         functools.partial(last_kernel, sizes),
         name="last",
         out_shape=shapes,
-        in_specs=[vm_spec] * 8 + [any_spec] * 8,
+        in_specs=[vm_spec] * 8 + [any_spec] * 7,
         out_specs=[vm_spec] * 7,
         scratch_shapes=[
             VM(unit.shape, low),
@@ -1454,32 +1562,27 @@
             VM((dp, ctx, 2, span, 4 * LANES), low),
             VM(normed.shape, low),
             VM(wide.shape, low),
-            VM(wide.shape, low),
-            VM((4, D, HD), low),
+            VM((4, HD, D), low),
             VM((fs, D, half), low),
             VM((fs, down_rows, D), low),
             VM((fs, proj_rows, D), low),
-            VM((fs, D, HD), low),
-            VM((2, fs, D, HD), low),
+            VM((fs, HD, D), low),
+            VM((2, fs, HD, D), low),
             VM((down_rows, D), low),
             VM((proj_rows, D), low),
-            VM((2, D, HD), low),
+            VM((2, HD, D), low),
             VM((down_rows, D), low),
             VM((proj_rows, D), low),
-            VM((D, HD), low),
+            VM((HD, D), low),
             VM((8, D), wide_t),
             VM((n, 8, LANES), wide_t),
             VM((n, 8, LANES), wide_t),
-            dma((4,)),
-            dma((4,)), dma((fs,)), dma((fs,)), dma((fs,)), dma((fs,)), dma((fs,)),
+            dma((6,)), dma((fs,)), dma((fs,)),
             dma((4,)), dma((3, fs)), dma((4,)), dma((3,)),
             dma((ctx, fs)), dma((fs, ctx)), dma((n,)), dma((n,)), dma((ctx,)),
         ] + LineSum.scratch(ctx, rows) + LineSum.scratch(ctx, rows),
         compiler_params=pltpu.CompilerParams(collective_id=3, has_side_effects=True, vmem_limit_bytes=63 * 1024 * 1024),
-    )(
-        x, gains, *tables, resid, d_resid, gain_two, unit, d_unit, normed, wide, partial,
-        grad_up, grad_down.reshape(fs, down_rows, D), grad_proj,
-    )
+    )(x, gains, *tables, resid, d_resid, gain_two, grad_proj, unit, d_unit, normed, wide, partial, up_land, down_land)
 
 
 def on_device(tokens, cotangent, attn_gain, w_qkv, w_out, mlp_gain, w_gate_up, w_down):
@@ -1491,20 +1594,23 @@
     each = attn_gain.shape[0]
     gain_rows = jnp.concatenate([attn_gain[None], mlp_gain[None]]).astype(jnp.float32)
     gain_rows = jnp.pad(gain_rows, ((0, 6), (0, LANES - each)))
-    tables = angle_tables(ctx, fs, span)
-    normed, unit, att, qkv, gains, dy_all, proj, down = first(where, x, gain_rows, w_qkv, *tables, dy, w_out, w_down)
+    tables = angle_tables(ctx * fs, span)
+    parts, sent = 4, 3
+    normed, unit, att, qkv, gains, dy_all, proj, gate_up = first(
+        where, parts, sent, x, gain_rows, w_qkv.T, *tables, dy, w_out, w_gate_up
+    )
     att = att.reshape(dp, ctx, rows, 2 * LANES)
-    resid, d_resid, grad_two, partial, d_unit, grad_up, grad_down, grad_proj = middle(
-        where, att, x, dy, gains, proj, down, w_gate_up, dy_all
+    resid, d_resid, grad_two, partial, d_unit, grad_proj, up_land, down_land = middle(
+        where, parts, sent, att, x, dy, gains, proj, w_down, w_gate_up, gate_up, dy_all
     )
     block_out, grad_tokens, gain_grads, grad_qkv, grad_out, grad_gate_up, grad_down = last(
-        where, x, gains, tables, resid, d_resid, grad_two, unit, d_unit, normed, qkv, partial, grad_up, grad_down, grad_proj
+        where, x, gains, tables, resid, d_resid, grad_two, grad_proj, unit, d_unit, normed, qkv, partial, up_land, down_land
     )
     return (
         block_out.reshape(tokens.shape),
         grad_tokens.reshape(tokens.shape),
         gain_grads[0, :each],
-        grad_qkv,
+        grad_qkv.T,
         grad_out,
         gain_grads[1, :each],
         grad_gate_up,

time: 423 us -> 350 us (0.83)
  Pallas kernels: 403 us -> 334 us
    pallas_call x1, Pallas kernels: 163 us -> 94.3 us  [last(): pl.pallas_call(functools.partial(last_kernel, sizes), name='last', out_sh...]
    unnamed x17 -> x12, local copies, waits for them, and re-layouts: 8.99 us -> 8.27 us
where the time goes in v5:
time: 350 us; the launch traced here: 348 us
  Pallas kernels  334 us (95%)
  local copies, waits for them, and re-layouts  9.6 us (3%)
    pallas_call x1, Pallas kernels, middle(): pl.pallas_call(functools.partial(middle_kernel, sizes, hidden, parts, sen...  149 us
    pallas_call x1, Pallas kernels, last(): pl.pallas_call(functools.partial(last_kernel, sizes), name='last', out_sh...  94.3 us
    pallas_call x1, Pallas kernels, first(): pl.pallas_call(functools.partial(first_kernel, sizes, parts), name='first...  91.3 us
    unnamed x12, local copies, waits for them, and re-layouts  8.27 us

profile of v5, /device:TPU:13, one launch (start us, length us, event | category | flops | bytes accessed | tf_op | source)
XLA Modules:
  0.0 347.6 jit_solution(102904378672490171)
XLA Ops:
  0.7 1.3 fusion.6.gains_ref
  1.9 0.1 multiply_cosine_fusion.1
  2.1 0.6 pad_maximum_fusion.1.block_ref
  2.7 0.2 multiply_cosine_fusion
  2.9 0.6 pad_maximum_fusion.step_ref
  3.5 91.3 %first.1 = (bf16[2,4,128,1536]{3,2,1,0:T(8,128)(2,1)}, bf16[4,4,64,512]{3,2,1,0:T(8,128)(2,1)}, bf16[2,4,2,64,256]{4,3,2,1,0:T(8,128)(2,1)}, bf16[512,1536]{1,0:...) custom-call(bf16[128,1536]{1,0:T(8,128)(2,1)} %bitcast.17, ...), custom_call_target="tpu_custom_call" | custom-call | tf_op jit(solution)/shard_map/first/pallas_call | solution.py:750
  94.8 148.8 %middle.1 = (f32[128,1536]{1,0:T(8,128)}, f32[128,1536]{1,0:T(8,128)}, f32[8,1536]{1,0:T(8,128)}, bf16[2,4,128,1536]{3,2,1,0:T(8,128)(2,1)}, bf16[4,4,64,256]{3,...) custom-call(bf16[2,4,128,256]{3,2,1,0:T(8,128)(2,1)} %bitcast.23, ...), custom_call_target="tpu_custom_call" | custom-call | tf_op jit(solution)/shard_map/middle/pallas_call | solution.py:1208
  243.7 94.3 %last.1 = (bf16[128,1536]{1,0:T(8,128)(2,1)}, bf16[128,1536]{1,0:T(8,128)(2,1)}, f32[8,128]{1,0:T(8,128)}, f32[96,1536]{1,0:T(8,128)}, f32[48,1536]{1,0:T(8,128)...) custom-call(bf16[128,1536]{1,0:T(8,128)(2,1)} %bitcast.19, f32[8,1536]{1,0:T(8,128)} %get-tuple-element.31.gains_ref, ...), custom_call_target="tpu_custom_call" | custom-call | tf_op jit(solution)/shard_map/last/pallas_call | solution.py:1550
  338.0 0.0 copy-start.2
  338.0 0.0 copy-start
  338.0 1.3 slice_bitcast_fusion
  339.4 1.8 copy.24
  341.1 1.8 copy.25
  342.9 0.0 copy-start.1
  342.9 2.0 copy.26
  344.9 0.0 copy-done.2
  344.9 0.7 copy.27
  345.6 0.0 copy-done
  345.6 1.1 copy.28
  346.7 0.0 copy-done.1
  346.7 0.9 copy.29
  (3 shorter events, 0.0 us)
Async XLA Ops:
  338.0 6.9 %copy-start.2 = (f32[48,1536]{1,0:T(8,128)S(1)}, f32[48,1536]{1,0:T(8,128)}, u32[]{:S(2)}) copy-start(f32[48,1536]{1,0:T(8,128)} %get-tuple-element.80) | copy-start | bytes 884740
  338.0 7.6 %copy-start = (f32[1536,256]{1,0:T(8,128)S(1)}, f32[1536,256]{1,0:T(8,128)}, u32[]{:S(2)}) copy-start(f32[1536,256]{1,0:T(8,128)} %get-tuple-element.82) | copy-start | bytes 4718596
  342.9 3.9 %copy-start.1 = (f32[128,1536]{1,0:T(8,128)S(1)}, f32[128,1536]{1,0:T(8,128)}, u32[]{:S(2)}) copy-start(f32[128,1536]{1,0:T(8,128)} %get-tuple-element.83) | copy-start | bytes 2359300

commit v6 on v5

--- a/solution.py
+++ b/solution.py
@@ -326,95 +326,94 @@
     pl.semaphore_wait(pltpu.get_barrier_semaphore(), dp * ctx * fs - 1)
 
 
+HALVES = 2
+
+
+def half(ref, index):
+    rows = ref.shape[-2] // HALVES
+    return ref.at[index * rows : (index + 1) * rows]
+
+
 class LineGather:
     def __init__(self, n, own, whole, send, recv, local):
         self.n, self.own, self.whole, self.send, self.recv, self.local = n, own, whole, send, recv, local
         self.d, self.c, self.f = place()
+        self.here = at_device(self.d, self.c, self.f)
 
     def slot(self, at):
         return self.whole.at[self.d, at]
 
-    def up(self, src, at):
-        return remote(src, self.slot(at), self.send.at[0, at], self.recv.at[self.d, at], at_device(self.d, self.c + 1, self.f))
-
-    def down(self, src, at):
-        return remote(src, self.slot(at), self.send.at[1, at], self.recv.at[self.d, at], at_device(self.d, self.c - 1, self.f))
-
-    def across(self, src, at):
-        return remote(src, self.slot(at), self.send.at[2, at], self.recv.at[self.d, at], at_device(1 - self.d, self.c, self.f))
+    def along(self, way, block, at, part):
+        to = (at_device(self.d, self.c + 1, self.f), at_device(self.d, self.c - 1, self.f), at_device(1 - self.d, self.c, self.f))[way]
+        return remote(half(block, part), half(self.slot(at), part), self.send.at[way, at, part], self.recv.at[self.d, at, part], to)
 
     def start(self):
         c = self.c
-
-        @pl.when(c < self.n - 1)
-        def _():
-            self.up(self.own, c).start()
-
-        @pl.when(c > 0)
-        def _():
-            self.down(self.own, c).start()
-
-        self.across(self.own, c).start()
+        for part in range(HALVES):
+
+            @pl.when(c < self.n - 1)
+            def _():
+                self.along(0, self.own, c, part).start()
+
+            @pl.when(c > 0)
+            def _():
+                self.along(1, self.own, c, part).start()
+
+        for part in range(HALVES):
+            self.along(2, self.own, c, part).start()
         pltpu.make_async_copy(self.own, self.slot(c), self.local).start()
 
     def forward(self, k):
         c = self.c
-
-        @pl.when(c - k >= 0)
-        def _():
-            arrived(self.slot(c - k), self.recv.at[self.d, c - k], at_device(self.d, c, self.f))
-
-            @pl.when(c < self.n - 1)
-            def _():
-                self.up(self.slot(c - k), c - k).start()
-
-            self.across(self.slot(c - k), c - k).start()
-
-        @pl.when(c + k < self.n)
-        def _():
-            arrived(self.slot(c + k), self.recv.at[self.d, c + k], at_device(self.d, c, self.f))
-
-            @pl.when(c > 0)
-            def _():
-                self.down(self.slot(c + k), c + k).start()
-
-            self.across(self.slot(c + k), c + k).start()
-
-    def take(self, at):
-        c = self.c
-
-        @pl.when(at != c)
-        def _():
-            arrived(self.slot(at), self.recv.at[self.d, at], at_device(self.d, c, self.f))
-
-            @pl.when(jnp.logical_and(at < c, c < self.n - 1))
-            def _():
-                self.up(self.slot(at), at).start()
-
-            @pl.when(jnp.logical_and(at > c, c > 0))
-            def _():
-                self.down(self.slot(at), at).start()
-
-            self.across(self.slot(at), at).start()
-
-        self.other(at)
+        for part in range(HALVES):
+
+            @pl.when(c - k >= 0)
+            def _():
+                arrived(half(self.slot(c - k), part), self.recv.at[self.d, c - k, part], self.here)
+
+                @pl.when(c < self.n - 1)
+                def _():
+                    self.along(0, self.slot(c - k), c - k, part).start()
+
+                self.along(2, self.slot(c - k), c - k, part).start()
+
+            @pl.when(c + k < self.n)
+            def _():
+                arrived(half(self.slot(c + k), part), self.recv.at[self.d, c + k, part], self.here)
+
+                @pl.when(c > 0)
+                def _():
+                    self.along(1, self.slot(c + k), c + k, part).start()
+
+                self.along(2, self.slot(c + k), c + k, part).start()
+
+    def reach(self, step):
+        now = jnp.abs(ordered(self.c, step, self.n) - self.c)
+        before = jnp.abs(ordered(self.c, step - 1, self.n) - self.c)
+
+        @pl.when(jnp.logical_and(step > 0, now != before))
+        def _():
+            self.forward(now)
 
     def other(self, at):
-        arrived(self.whole.at[1 - self.d, at], self.recv.at[1 - self.d, at], at_device(self.d, self.c, self.f))
+        for part in range(HALVES):
+            arrived(half(self.whole.at[1 - self.d, at], part), self.recv.at[1 - self.d, at, part], self.here)
 
     def finish_sends(self):
         c = self.c
         for at in range(self.n):
-
-            @pl.when(jnp.logical_and(at <= c, c < self.n - 1))
-            def _():
-                left(self.slot(at), self.send.at[0, at], at_device(self.d, c, self.f))
-
-            @pl.when(jnp.logical_and(at >= c, c > 0))
-            def _():
-                left(self.slot(at), self.send.at[1, at], at_device(self.d, c, self.f))
-
-            left(self.slot(at), self.send.at[2, at], at_device(self.d, c, self.f))
+            for part in range(HALVES):
+                block = half(self.slot(at), part)
+
+                @pl.when(jnp.logical_and(at <= c, c < self.n - 1))
+                def _():
+                    left(block, self.send.at[0, at, part], self.here)
+
+                @pl.when(jnp.logical_and(at >= c, c > 0))
+                def _():
+                    left(block, self.send.at[1, at, part], self.here)
+
+                left(block, self.send.at[2, at, part], self.here)
 
     def finish(self):
         self.finish_sends()
@@ -434,12 +433,25 @@
     return at
 
 
+def towards(c, step, n):
+    at = c
+    for here in range(n):
+        due = []
+        for to in range(n):
+            if to != here:
+                hops = here if to > here else n - 1 - here
+                due.append((hops + (n - 1 - to if to > here else to), -hops, to))
+        for index, (_, _, to) in enumerate(sorted(due)):
+            at = jnp.where(jnp.logical_and(c == here, step == index), to, at)
+    return at
+
+
 def first_kernel(
-    sizes, parts, x_ref, gains_ref, w_ref, block_ref, step_ref, dy_ref, proj_ref, gate_up_ref,
-    normed_out, unit_out, att_out, wide_out, gains_out, dy_all, proj_all, gate_up_all,
+    sizes, parts, x_ref, gains_ref, w_ref, block_ref, step_ref, dy_ref, proj_ref, down_ref, gate_up_ref,
+    normed_out, unit_out, att_out, wide_out, gains_out, dy_all, proj_all, down_out, gate_up_all,
     x_all, wide, normed, stage, unit, att_stage, att, gain_all, gain_vec,
     line_send, line_recv, line_local, w_send, w_recv, w_pass, g_send, g_recv, u_send, u_recv, a_send, a_recv, out_sem,
-    dy_send, dy_recv, dy_local, m_send, m_recv, m_pass, gu_send, gu_recv,
+    dy_send, dy_recv, dy_local, m_send, m_recv, m_pass, down_send, down_recv, gu_send, gu_recv,
 ):
     dp, ctx, fs = sizes
     n = dp * ctx * fs
@@ -462,30 +474,6 @@
     kv_away = jnp.logical_or(jnp.logical_or(kv_core != d, kv_ctx != c), kv_f != f)
     relay_of = {slot: f == lax.rem(2 * lax.rem(c, 2) + d + 2 * (slot - 2), fs) for slot in (2, 3)}
 
-    @pl.when(jnp.logical_and(d == 1, kv_away))
-    def _():
-        remote(w_ref, head_rows(kv_slot), w_send.at[0], w_recv.at[kv_slot], at_device(kv_core, kv_ctx, kv_f)).start()
-
-    @pl.when(jnp.logical_and(d == 1, jnp.logical_not(kv_away)))
-    def _():
-        pltpu.make_async_copy(w_ref, head_rows(kv_slot), w_recv.at[kv_slot]).start()
-
-    line = LineGather(ctx, x_ref, x_all, line_send, line_recv, line_local)
-    line.start()
-
-    @pl.when(d == 0)
-    def _():
-        slot = lax.rem(f, 2)
-        for to in range(fs):
-
-            @pl.when(jnp.logical_or(q_core != 0, to != f))
-            def _():
-                remote(w_ref, head_rows(slot), w_send.at[to], w_recv.at[slot], at_device(q_core, c, to)).start()
-
-            @pl.when(jnp.logical_and(q_core == 0, to == f))
-            def _():
-                pltpu.make_async_copy(w_ref, head_rows(slot), w_recv.at[slot]).start()
-
     me = (d * ctx + c) * fs + f
 
     def gain_to(step, carry):
@@ -499,6 +487,30 @@
     lax.fori_loop(1, n, gain_to, 0)
     gain_all[me] = gains_ref[...]
 
+    @pl.when(jnp.logical_and(d == 1, kv_away))
+    def _():
+        remote(w_ref, head_rows(kv_slot), w_send.at[0], w_recv.at[kv_slot], at_device(kv_core, kv_ctx, kv_f)).start()
+
+    @pl.when(jnp.logical_and(d == 1, jnp.logical_not(kv_away)))
+    def _():
+        pltpu.make_async_copy(w_ref, head_rows(kv_slot), w_recv.at[kv_slot]).start()
+
+    line = LineGather(ctx, x_ref, x_all, line_send, line_recv, line_local)
+    line.start()
+
+    @pl.when(d == 0)
+    def _():
+        slot = lax.rem(f, 2)
+        for to in range(fs):
+
+            @pl.when(jnp.logical_or(q_core != 0, to != f))
+            def _():
+                remote(w_ref, head_rows(slot), w_send.at[to], w_recv.at[slot], at_device(q_core, c, to)).start()
+
+            @pl.when(jnp.logical_and(q_core == 0, to == f))
+            def _():
+                pltpu.make_async_copy(w_ref, head_rows(slot), w_recv.at[slot]).start()
+
     for slot in (2, 3):
 
         @pl.when(relay_of[slot])
@@ -527,8 +539,6 @@
             def _():
                 pltpu.make_async_copy(src, dst, gu_recv.at[part, gu_slot]).start()
 
-    push_part(0)
-
     def gain_from(step, carry):
         other = lax.rem(me + step, n)
         arrived(gain_all.at[other], g_recv.at[other], here)
@@ -540,6 +550,10 @@
         gain_vec[:, index * each : (index + 1) * each] = gain_all[index][:, :each]
     gain = gain_vec[0:1, :]
 
+    for k in range(1, ctx - 1):
+        line.forward(k)
+    dy_line = LineGather(ctx, dy_ref, dy_all, dy_send, dy_recv, dy_local)
+    dy_line.start()
     for slot in range(4):
         if slot < 2:
             arrived(head_rows(slot), w_recv.at[slot], here)
@@ -549,12 +563,13 @@
             def _():
                 arrived(head_rows(slot), w_recv.at[slot], here)
 
+    push_part(0)
     pltpu.make_async_copy(line.own, line.slot(c), line.local).wait()
 
     def block(step, carry):
         at = ordered(c, step, ctx)
 
-        line.take(at)
+        line.other(at)
         values = x_all[:, at].reshape(dp * 2 * span, D).astype(jnp.float32)
         scale = lax.rsqrt(jnp.mean(values * values, axis=-1, keepdims=True) + EPS)
         low = (values * scale * gain).astype(jnp.bfloat16)
@@ -583,7 +598,14 @@
 
         return carry
 
-    lax.fori_loop(0, ctx, block, 0)
+    def near(step, carry):
+        @pl.when(step == ctx - 1)
+        def _():
+            line.forward(ctx - 1)
+
+        return block(step, carry)
+
+    lax.fori_loop(0, ctx, near, 0)
     normed_copy = pltpu.make_async_copy(normed, normed_out, out_sem.at[0])
     wide_copy = pltpu.make_async_copy(wide, wide_out, out_sem.at[1])
     gains_copy = pltpu.make_async_copy(gain_vec, gains_out, out_sem.at[2])
@@ -604,8 +626,9 @@
         def _():
             pltpu.make_async_copy(shard, whole.at[f], m_recv.at[index, f]).start()
 
-    dy_line = LineGather(ctx, dy_ref, dy_all, dy_send, dy_recv, dy_local)
-    dy_line.start()
+
+    push_part(1)
+    dy_line.forward(1)
 
     def pass_on():
         for index, (shard, whole) in enumerate(moved):
@@ -652,11 +675,19 @@
 
         if at == 0:
             pass_on()
-        elif at == 1:
-            dy_line.forward(1)
         elif at == ctx - 1:
-            for part in range(1, gu_send.shape[0]):
+            for part in range(2, gu_send.shape[0]):
                 push_part(part)
+            dy_line.forward(2)
+
+            @pl.when(jnp.logical_not(stays))
+            def _():
+                remote(down_ref, down_out, down_send, down_recv, at_device(to_core, to_ctx, f)).start()
+
+            @pl.when(stays)
+            def _():
+                pltpu.make_async_copy(down_ref, down_out, down_recv).start()
+
 
     for at in range(ctx):
         for step in range(1, fs):
@@ -665,7 +696,7 @@
     att_copy = pltpu.make_async_copy(att, att_out, out_sem.at[4])
     att_copy.start()
 
-    for k in range(2, ctx):
+    for k in range(3, ctx):
         dy_line.forward(k)
     for at in range(ctx):
         dy_line.other(at)
@@ -680,6 +711,12 @@
         def _():
             left(shard, m_send.at[index], here)
 
+    arrived(down_out, down_recv, here)
+
+    @pl.when(jnp.logical_not(stays))
+    def _():
+        left(down_ref, down_send, here)
+
     for part in range(gu_send.shape[0]):
         src = gate_up_ref.at[part * part_rows : (part + 1) * part_rows]
         for slot in range(4):
@@ -729,7 +766,7 @@
         copy.wait()
 
 
-def first(sizes, parts, sent, x, gains, w_qkv, blocks, steps, dy, w_out, w_gate_up):
+def first(sizes, parts, sent, x, gains, w_qkv, blocks, steps, dy, w_out, w_down, w_gate_up):
     dp, ctx, fs = sizes
     n = dp * ctx * fs
     rows = x.shape[0]
@@ -744,6 +781,7 @@
         jax.ShapeDtypeStruct((8, D), wide_t),
         jax.ShapeDtypeStruct((dp, ctx, rows, D), low),
         jax.ShapeDtypeStruct((fs,) + w_out.shape, low),
+        jax.ShapeDtypeStruct(w_down.shape, low),
         jax.ShapeDtypeStruct((4, D // parts * sent, w_gate_up.shape[1]), low),
     )
     any_spec, vm_spec = pl.BlockSpec(memory_space=ANY), pl.BlockSpec(memory_space=VM)
@@ -751,8 +789,8 @@
         functools.partial(first_kernel, sizes, parts),
         name="first",
         out_shape=shapes,
-        in_specs=[vm_spec] * 8,
-        out_specs=[any_spec] * 8,
+        in_specs=[vm_spec] * 9,
+        out_specs=[any_spec] * 9,
         scratch_shapes=[
             VM((dp, ctx, rows, D), low),
             VM((4 * LANES, D), low),
@@ -763,18 +801,18 @@
             VM((dp, ctx, 2, span, 2 * LANES), low),
             VM((n, 8, LANES), wide_t),
             VM((8, D), wide_t),
-            dma((3, ctx)), dma((dp, ctx)), dma,
+            dma((3, ctx, HALVES)), dma((dp, ctx, HALVES)), dma,
             dma((fs,)), dma((4,)), dma((2, fs)),
             dma((n,)), dma((n,)),
             dma((ctx, 2 * dp)), dma((ctx, fs)),
             dma((ctx, fs)), dma((fs, ctx)),
             dma((5,)),
-            dma((3, ctx)), dma((dp, ctx)), dma,
-            dma((1,)), dma((1, fs)), dma((1, fs)),
+            dma((3, ctx, HALVES)), dma((dp, ctx, HALVES)), dma,
+            dma((1,)), dma((1, fs)), dma((1, fs)), dma, dma,
             dma((sent, fs)), dma((sent, 4)),
         ],
         compiler_params=pltpu.CompilerParams(collective_id=1, has_side_effects=True, vmem_limit_bytes=60 * 1024 * 1024),
-    )(x, gains, w_qkv, blocks, steps, dy, w_out, w_gate_up)
+    )(x, gains, w_qkv, blocks, steps, dy, w_out, w_down, w_gate_up)
 
 
 def angle_tables(count, span):
@@ -808,6 +846,10 @@
         self.here = at_device(self.d, self.c, self.f)
 
     def give(self, at, both):
+        self.keep(at, both)
+        self.hand(at)
+
+    def keep(self, at, both):
         d = self.d
         low = both.astype(jnp.bfloat16)
 
@@ -821,48 +863,47 @@
             self.mine[at] = low[1]
             self.out_core[at] = low[0]
 
+    def hand(self, at):
         remote(
-            self.out_core.at[at], self.in_core.at[at], self.core_send.at[at], self.core_recv.at[at], at_device(1 - d, self.c, self.f)
+            self.out_core.at[at], self.in_core.at[at], self.core_send.at[at], self.core_recv.at[at], at_device(1 - self.d, self.c, self.f)
         ).start()
 
     def step(self, at):
         n, d, c, f = self.n, self.d, self.c, self.f
         arrived(self.in_core.at[at], self.core_recv.at[at], self.here)
-        self.total[...] = self.mine[at].astype(jnp.float32) + self.in_core[at].astype(jnp.float32)
-
-        @pl.when(jnp.logical_and(at <= c, c < n - 1))
-        def _():
-            arrived(self.in_line.at[0, at], self.line_recv.at[0, at], self.here)
-            self.total[...] += self.in_line[0, at].astype(jnp.float32)
-
-        @pl.when(jnp.logical_and(at >= c, c > 0))
-        def _():
-            arrived(self.in_line.at[1, at], self.line_recv.at[1, at], self.here)
-            self.total[...] += self.in_line[1, at].astype(jnp.float32)
-
-        @pl.when(at != c)
-        def _():
-            self.out_line[at] = self.total[...].astype(jnp.bfloat16)
-
-        @pl.when(at < c)
-        def _():
-            remote(
-                self.out_line.at[at], self.in_line.at[0, at], self.line_send.at[at], self.line_recv.at[0, at], at_device(d, c - 1, f)
-            ).start()
-
-        @pl.when(at > c)
-        def _():
-            remote(
-                self.out_line.at[at], self.in_line.at[1, at], self.line_send.at[at], self.line_recv.at[1, at], at_device(d, c + 1, f)
-            ).start()
+        rows = self.total.shape[0] // HALVES
+        for part in range(HALVES):
+            own = slice(part * rows, (part + 1) * rows)
+            self.total[own] = self.mine[at, own].astype(jnp.float32) + self.in_core[at, own].astype(jnp.float32)
+            for way, comes in enumerate((jnp.logical_and(at <= c, c < n - 1), jnp.logical_and(at >= c, c > 0))):
+
+                @pl.when(comes)
+                def _():
+                    arrived(self.in_line.at[way, at, own], self.line_recv.at[way, at, part], self.here)
+                    self.total[own] += self.in_line[way, at, own].astype(jnp.float32)
+
+            @pl.when(at != c)
+            def _():
+                self.out_line[at, own] = self.total[own].astype(jnp.bfloat16)
+
+            for way, (goes, to) in enumerate(((at < c, c - 1), (at > c, c + 1))):
+
+                @pl.when(goes)
+                def _():
+                    remote(
+                        self.out_line.at[at, own], self.in_line.at[way, at, own],
+                        self.line_send.at[at, part], self.line_recv.at[way, at, part], at_device(d, to, f),
+                    ).start()
 
     def finish(self):
+        rows = self.total.shape[0] // HALVES
         for at in range(self.n):
             left(self.out_core.at[at], self.core_send.at[at], self.here)
 
             @pl.when(at != self.c)
             def _():
-                left(self.out_line.at[at], self.line_send.at[at], self.here)
+                for part in range(HALVES):
+                    left(self.out_line.at[at, part * rows : (part + 1) * rows], self.line_send.at[at, part], self.here)
 
     @staticmethod
     def scratch(ctx, rows):
@@ -871,7 +912,7 @@
         return [
             VM((ctx, rows, D), low), VM((ctx, rows, D), low), VM((ctx, rows, D), low), VM((ctx, rows, D), low),
             VM((2, ctx, rows, D), low), VM((rows, D), jnp.float32),
-            dma((ctx,)), dma((ctx,)), dma((ctx,)), dma((2, ctx)),
+            dma((ctx,)), dma((ctx,)), dma((ctx, HALVES)), dma((2, ctx, HALVES)),
         ]
 
 
@@ -889,8 +930,6 @@
             found.append((at_device(core, c, lax.rem(f + step, fs)), yes))
     found.append((at_device(d, c - 1, f), c > 0))
     found.append((at_device(d, c + 1, f), c < ctx - 1))
-    for core, place_ in down_route(d, c):
-        found.append((at_device(core, place_, f), jnp.logical_or(core != d, place_ != c)))
     return found
 
 
@@ -910,11 +949,11 @@
 
 def middle_kernel(
     sizes, hidden, parts, sent, att_ref, x_ref, dy_ref, gains_ref, proj_ref, down_ref, gate_up_ref, gate_up_part_ref, dy_all_ref,
-    resid_out, d_resid_out, gain_out, partial_out, unit_out, grad_proj_out, up_land, down_land,
-    att, dy_all, proj, down, gate_up, resid, own_two, normed_two, act, d_both, part_stage, own_d, d_resid_all, d_stage, unit,
+    out_ref, d_resid_out, gain_out, unit_out, grad_proj_out, up_land, down_land,
+    att, dy_all, proj, down, gate_up, resid, own_two, normed_two, act, d_both, own_d, d_resid_all, d_stage, unit,
     grad_up, grad_down, grad_proj, grad_proj_low,
-    in_sem, gu_send, gu_recv, m_send, m_recv, m_pass, two_send, two_recv, two_local, dr_send, dr_recv, dr_local, u_send, u_recv,
-    out_sem, part_sem, gup_send, gup_recv, gdn_send, gdn_recv,
+    in_sem, gu_send, gu_recv, m_recv, m_pass, two_send, two_recv, two_local, dr_send, dr_recv, dr_local, u_send, u_recv,
+    out_sem, gup_send, gup_recv, gdn_send, gdn_recv,
     *sums,
 ):
     dp, ctx, fs = sizes
@@ -926,6 +965,7 @@
     half = hidden // 2
     line_sum = LineSum(ctx, *sums[:6], sums[6:10])
     second_sum = LineSum(ctx, *sums[10:16], sums[16:20])
+    out_sum = LineSum(ctx, *sums[20:26], sums[26:30])
     part_rows = D // parts
     tell_near(sizes)
 
@@ -942,18 +982,27 @@
         proj_copies[-1].start()
     dy_copy.start()
     part_copy.start()
+    att_copy.wait()
+    for copy in proj_copies:
+        copy.wait()
+
+    def project(step, carry):
+        at = towards(c, step, ctx)
+        terms = jnp.dot(att[:, at].reshape(both_rows, 2 * LANES), proj[...], preferred_element_type=jnp.float32)
+        line_sum.keep(at, terms.reshape(dp, rows, D))
+        return carry
+
+    lax.fori_loop(0, ctx, project, 0)
     hear_near(sizes)
 
-    (to_core, to_ctx), _ = down_route(d, c)
-    stays = jnp.logical_and(to_core == d, to_ctx == c)
-
-    @pl.when(jnp.logical_not(stays))
-    def _():
-        remote(down_ref, down.at[f], m_send, m_recv.at[f], at_device(to_core, to_ctx, f)).start()
-
-    @pl.when(stays)
-    def _():
-        pltpu.make_async_copy(down_ref, down.at[f], m_recv.at[f]).start()
+    pltpu.make_async_copy(down_ref, down.at[f], m_recv.at[f]).start()
+    for step in range(1, fs):
+        to = lax.rem(f + step, fs)
+        remote(down_ref, down.at[f], m_pass.at[step], m_recv.at[f], at_device(d, c, to)).start()
+    ends = jnp.logical_or(c == 0, c == ctx - 1)
+
+    for step in range(ctx):
+        line_sum.hand(towards(c, step, ctx))
 
     gu_core = f // 2
     gu_slot = 2 * d + lax.rem(f, 2)
@@ -969,53 +1018,35 @@
         def _():
             pltpu.make_async_copy(gate_up_ref.at[rest], gate_up.at[gu_slot, rest], gu_recv.at[gu_slot]).start()
 
-    att_copy.wait()
-    for copy in proj_copies:
-        copy.wait()
-
-    def project(step, carry):
-        at = ordered(c, ctx - 1 - step, ctx)
-        terms = jnp.dot(att[:, at].reshape(both_rows, 2 * LANES), proj[...], preferred_element_type=jnp.float32)
-        line_sum.give(at, terms.reshape(dp, rows, D))
-        return carry
-
-    lax.fori_loop(0, ctx, project, 0)
-
-    line_sum.step(ordered(c, ctx - 1, ctx))
-    line_sum.step(ordered(c, ctx - 2, ctx))
-    arrived(down.at[f], m_recv.at[f], here)
-    for step in range(1, fs):
-        to = lax.rem(f + step, fs)
-        remote(down.at[f], down.at[f], m_pass.at[step], m_recv.at[f], at_device(d, c, to)).start()
-
-    def sum_up(step, carry):
-        line_sum.step(ordered(c, ctx - 1 - step, ctx))
-        return carry
-
-    lax.fori_loop(2, ctx, sum_up, 0)
+    line_sum.step(towards(c, 0, ctx))
+    line_sum.step(towards(c, 1, ctx))
+    line_sum.step(towards(c, 2, ctx))
+    line_sum.step(c)
     gain = gains_ref[1:2, :]
     values = x_ref[...].astype(jnp.float32) + line_sum.total[...]
     resid[...] = values
     scale = lax.rsqrt(jnp.mean(values * values, axis=-1, keepdims=True) + EPS)
     own_two[...] = (values * scale * gain).astype(jnp.bfloat16)
-    resid_copy = pltpu.make_async_copy(resid, resid_out, out_sem.at[0])
-    resid_copy.start()
     line = LineGather(ctx, own_two, normed_two, two_send, two_recv, two_local)
     line.start()
-    line_sum.finish()
+    line.forward(1)
     for slot in range(4):
         arrived(gate_up.at[slot, rest], gu_recv.at[slot], here)
     dy_copy.wait()
     part_copy.wait()
-    for step in range(1, fs):
-        other = lax.rem(f + step, fs)
-        arrived(down.at[other], m_recv.at[other], here)
+    for slot in range(fs):
+        arrived(down.at[slot], m_recv.at[slot], here)
     pltpu.make_async_copy(line.own, line.slot(c), line.local).wait()
 
     def mlp(step, carry):
         at = ordered(c, step, ctx)
 
-        line.take(at)
+
+        @pl.when(lax.rem(step, 2) == 1)
+        def _():
+            line.forward(2 + step // 2)
+
+        line.other(at)
         inputs = normed_two[:, at].reshape(both_rows, D)
         dy_rows = dy_all[:, at].reshape(both_rows, D)
         for part in range(2):
@@ -1053,7 +1084,7 @@
             pltpu.make_async_copy(src, dst, recv).start()
 
     def grads(step):
-        first = pl.multiple_of(step * wide_rows, LANES)
+        first = step * wide_rows
         left_rows = normed_two[:, :, :, pl.ds(first, wide_rows)].reshape(dp * ctx * rows, wide_rows)
         for part in range(2):
             cols = slice(part * hidden, (part + 1) * hidden)
@@ -1073,16 +1104,20 @@
                 gdn_send.at[slot, step], gdn_recv.at[f, step], d, slot,
             )
 
-    def sum_two(step, carry):
-        second_sum.step(ordered(c, ctx - 1 - step, ctx))
-
-        @pl.when(step < ctx - 1)
-        def _():
-            grads(step)
-
-        return carry
-
-    lax.fori_loop(0, ctx, sum_two, 0)
+    def out_terms(step):
+        at = towards(c, step, ctx)
+        terms = jnp.dot(act[:, at].reshape(both_rows, hidden), down[...].reshape(hidden, D), preferred_element_type=jnp.float32)
+        out_sum.give(at, terms.reshape(dp, rows, D))
+
+    second_sum.step(towards(c, 0, ctx))
+    grads(0)
+    out_terms(0)
+    second_sum.step(towards(c, 1, ctx))
+    second_sum.step(towards(c, 2, ctx))
+    for step in range(1, ctx - 1):
+        grads(step)
+        out_terms(step)
+    second_sum.step(c)
     values = resid[...]
     scale = lax.rsqrt(jnp.mean(values * values, axis=-1, keepdims=True) + EPS)
     incoming = second_sum.total[...]
@@ -1094,8 +1129,15 @@
     gain_out[...] = jnp.broadcast_to(jnp.sum(incoming * values * scale, axis=0, keepdims=True), gain_out.shape)
     d_line = LineGather(ctx, own_d, d_resid_all, dr_send, dr_recv, dr_local)
     d_line.start()
-    line.finish_sends()
-    second_sum.finish()
+    def out_step(step, carry):
+        out_sum.step(towards(c, step, ctx))
+        return carry
+
+    @pl.when(ends)
+    def _():
+        lax.fori_loop(0, ctx - 1, out_step, 0)
+
+    out_terms(ctx - 1)
     grads(ctx - 1)
     pltpu.make_async_copy(d_line.own, d_line.slot(c), d_line.local).wait()
     grad_proj[...] = jnp.zeros_like(grad_proj)
@@ -1103,7 +1145,8 @@
     def back(step, carry):
         at = ordered(c, step, ctx)
 
-        d_line.take(at)
+        d_line.reach(step)
+        d_line.other(at)
         incoming = d_resid_all[:, at].reshape(both_rows, D)
         d_att = outer(incoming, proj[...]).astype(jnp.bfloat16)
         d_stage[at] = d_att.reshape(2 * dp, span, 2 * LANES)
@@ -1119,18 +1162,21 @@
 
         grad_proj[...] += inner(att[:, at].reshape(both_rows, 2 * LANES), incoming)
 
-        outputs = jnp.dot(act[:, at].reshape(both_rows, hidden), down[...].reshape(hidden, D), preferred_element_type=jnp.float32)
-        slot = lax.rem(step, 2)
-
-        @pl.when(step >= 2)
-        def _():
-            pltpu.make_async_copy(part_stage.at[slot], partial_out.at[:, at], part_sem.at[slot]).wait()
-
-        part_stage[slot] = outputs.reshape(dp, rows, D).astype(jnp.bfloat16)
-        pltpu.make_async_copy(part_stage.at[slot], partial_out.at[:, at], part_sem.at[slot]).start()
+        @pl.when(jnp.logical_and(jnp.logical_not(ends), step == ctx - 2))
+        def _():
+            out_sum.step(towards(c, 0, ctx))
+
         return carry
 
     lax.fori_loop(0, ctx, back, 0)
+
+    @pl.when(jnp.logical_not(ends))
+    def _():
+        lax.fori_loop(1, ctx - 1, out_step, 0)
+
+    line_sum.finish()
+    line.finish_sends()
+    second_sum.finish()
     for slot in range(fs):
         start = slot // 2 * LANES + slot % 2 * each
         grad_proj_low[slot] = grad_proj[start : start + each, :].astype(jnp.bfloat16)
@@ -1142,7 +1188,10 @@
             arrived(unit.at[at, other], u_recv.at[at, other], here)
     unit_copy = pltpu.make_async_copy(unit, unit_out, out_sem.at[2])
     unit_copy.start()
+    out_step(ctx - 1, 0)
+    out_ref[...] = (resid[...] + out_sum.total[...]).astype(jnp.bfloat16)
     d_line.finish_sends()
+    out_sum.finish()
     for at in range(ctx):
         for to in range(fs):
 
@@ -1156,34 +1205,34 @@
         def _():
             left(gate_up_ref.at[rest], gu_send.at[to], here)
 
-    @pl.when(jnp.logical_not(stays))
-    def _():
-        left(down_ref, m_send, here)
-
     for step in range(1, fs):
-        left(down.at[f], m_pass.at[step], here)
-
-    def settle(step, carry):
+        left(down_ref, m_pass.at[step], here)
+
+    def settle_up(step, carry):
         first = pl.multiple_of(step * wide_rows, LANES)
         for slot in range(4):
-            up_src, down_src = grad_up.at[slot, pl.ds(first, wide_rows)], grad_down.at[slot, :, pl.ds(first, wide_rows)]
             arrived(up_land.at[slot, pl.ds(first, wide_rows)], gup_recv.at[slot, step], here)
+
+            @pl.when(jnp.logical_or(slot // 2 != d, 2 * d + slot % 2 != f))
+            def _():
+                left(grad_up.at[slot, pl.ds(first, wide_rows)], gup_send.at[slot, step], here)
+
+        return carry
+
+    def settle_down(step, carry):
+        first = pl.multiple_of(step * wide_rows, LANES)
+        for slot in range(4):
             arrived(down_land.at[slot, :, pl.ds(first, wide_rows)], gdn_recv.at[slot, step], here)
 
-            @pl.when(jnp.logical_or(slot // 2 != d, 2 * d + slot % 2 != f))
-            def _():
-                left(up_src, gup_send.at[slot, step], here)
-
             @pl.when(slot != f)
             def _():
-                left(down_src, gdn_send.at[slot, step], here)
+                left(grad_down.at[slot, :, pl.ds(first, wide_rows)], gdn_send.at[slot, step], here)
 
         return carry
 
-    lax.fori_loop(0, ctx, settle, 0)
-    for slot in range(2):
-        pltpu.make_async_copy(part_stage.at[slot], partial_out.at[:, 0], part_sem.at[slot]).wait()
-    for copy in (resid_copy, grad_proj_copy, unit_copy):
+    lax.fori_loop(0, ctx, settle_up, 0)
+    lax.fori_loop(0, ctx, settle_down, 0)
+    for copy in (grad_proj_copy, unit_copy):
         copy.wait()
 
 
@@ -1196,10 +1245,9 @@
     dma = pltpu.SemaphoreType.DMA
     any_spec, vm_spec = pl.BlockSpec(memory_space=ANY), pl.BlockSpec(memory_space=VM)
     shapes = (
-        jax.ShapeDtypeStruct((rows, D), wide_t),
+        jax.ShapeDtypeStruct((rows, D), low),
         jax.ShapeDtypeStruct((rows, D), wide_t),
         jax.ShapeDtypeStruct((8, D), wide_t),
-        jax.ShapeDtypeStruct((dp, ctx, rows, D), low),
         jax.ShapeDtypeStruct((ctx, fs, span, 2 * LANES), low),
         jax.ShapeDtypeStruct(proj.shape, low),
         jax.ShapeDtypeStruct((fs, D, hidden // 2), low),
@@ -1210,7 +1258,7 @@
         name="middle",
         out_shape=shapes,
         in_specs=[any_spec, vm_spec, vm_spec, vm_spec, any_spec, vm_spec, vm_spec, any_spec, any_spec],
-        out_specs=[any_spec, vm_spec, vm_spec] + [any_spec] * 5,
+        out_specs=[vm_spec] * 3 + [any_spec] * 4,
         scratch_shapes=[
             VM((dp, ctx, rows, 2 * LANES), low),
             VM((dp, ctx, rows, D), low),
@@ -1222,7 +1270,6 @@
             VM((dp, ctx, rows, D), low),
             VM((dp, ctx, rows, hidden), low),
             VM((dp, ctx, rows, 2 * hidden), low),
-            VM((2, dp, rows, D), low),
             VM((rows, D), low),
             VM((dp, ctx, rows, D), low),
             VM((ctx, 2 * dp, span, 2 * LANES), low),
@@ -1231,25 +1278,25 @@
             VM((fs, hidden // fs, D), low),
             VM((2 * LANES, D), wide_t),
             VM(proj.shape, low),
-            dma((3 + fs,)), dma((fs,)), dma((4,)), dma, dma((fs,)), dma((fs,)),
-            dma((3, ctx)), dma((dp, ctx)), dma,
-            dma((3, ctx)), dma((dp, ctx)), dma,
+            dma((3 + fs,)), dma((fs,)), dma((4,)), dma((fs,)), dma((fs,)),
+            dma((3, ctx, HALVES)), dma((dp, ctx, HALVES)), dma,
+            dma((3, ctx, HALVES)), dma((dp, ctx, HALVES)), dma,
             dma((ctx, 2 * dp)), dma((ctx, fs)),
-            dma((3,)), dma((2,)),
+            dma((3,)),
             dma((4, ctx)), dma((fs, ctx)), dma((fs, ctx)), dma((fs, ctx)),
-        ] + LineSum.scratch(ctx, rows) + LineSum.scratch(ctx, rows),
+        ] + LineSum.scratch(ctx, rows) * 3,
         compiler_params=pltpu.CompilerParams(collective_id=2, has_side_effects=True, vmem_limit_bytes=63 * 1024 * 1024),
     )(att, x, dy, gains, proj, w_down, w_gate_up, gate_up_part, dy_all)
 
 
 def last_kernel(
-    sizes, x_ref, gains_ref, block_ref, step_ref, resid_ref, d_resid_ref, gain_two_ref, proj_ref,
-    unit_ref, d_unit_ref, normed_ref, wide_ref, partial_ref, up_land_ref, down_land_ref,
-    out_ref, d_x_ref, gains_out, qkv_out, proj_out, up_out, down_out,
+    sizes, x_ref, gains_ref, block_ref, step_ref, d_resid_ref, gain_two_ref, proj_ref,
+    unit_ref, d_unit_ref, normed_ref, wide_ref, up_land_ref, down_land_ref,
+    d_x_ref, gains_out, qkv_out, proj_out, up_out, down_out,
     unit, d_unit, d_k, d_v, stage, mixed, normed, wide, grad_heads,
     up_land, down_land, proj_land, q_land, kv_land, down_sum, proj_sum, kv_sum, down_last, proj_last, kv_last, gain_vec, gain_stage, gain_land,
     in_sem, proj_send, proj_recv, head_send, head_recv, move_send, move_recv,
-    u_send, u_recv, g_send, g_recv, mine_sem,
+    u_send, u_recv, g_send, g_recv,
     *sums,
 ):
     dp, ctx, fs = sizes
@@ -1270,18 +1317,9 @@
     tell_all(sizes)
     for load in loads:
         load.start()
-    out_sum = LineSum(ctx, *sums[:6], sums[6:10])
-    in_sum = LineSum(ctx, *sums[10:16], sums[16:20])
-    for at in range(ctx):
-        pltpu.make_async_copy(partial_ref.at[d, at], out_sum.mine.at[at], mine_sem.at[at]).start()
+    in_sum = LineSum(ctx, *sums[:6], sums[6:10])
     d_k[...] = jnp.zeros_like(d_k)
     d_v[...] = jnp.zeros_like(d_v)
-    hear_all(sizes)
-
-    for at in range(ctx):
-        remote(
-            partial_ref.at[1 - d, at], out_sum.in_core.at[at], out_sum.core_send.at[at], out_sum.core_recv.at[at], at_device(1 - d, c, f)
-        ).start()
 
     def push(src, land, send, recv, core, fs_to):
         to_self = jnp.logical_and(core == d, fs_to == f)
@@ -1317,9 +1355,6 @@
         def _():
             pltpu.make_async_copy(src, dst, move_recv.at[index]).start()
 
-    loads[4].wait()
-    down_sum[...] = sum_of(down_land).astype(low)
-    move(0, down_sum, down_last)
     loads[0].wait()
     loads[1].wait()
     block = fs * span
@@ -1357,6 +1392,10 @@
             d_v[0:keys, :] += inner(probs.astype(low), d_rows)
         stage[at, :, :, 2 * LANES : 3 * LANES] = unturn(d_k[block * at : keys, :], at).astype(low)
         stage[at, :, :, 3 * LANES : 4 * LANES] = d_v[block * at : keys, :].astype(low).reshape(fs, span, LANES)
+        if at == ctx - 1:
+            hear_all(sizes)
+            for slot in range(fs):
+                push(proj_ref.at[slot], proj_land, proj_send.at[slot], proj_recv, d, slot)
         for to in range(fs):
 
             @pl.when(to != f)
@@ -1369,85 +1408,52 @@
             def _():
                 mixed[f // 2, at, lax.rem(f, 2)] = stage[at, to]
 
-    for slot in range(fs):
-        push(proj_ref.at[slot], proj_land, proj_send.at[slot], proj_recv, d, slot)
+        if at == ctx - 1:
+            loads[4].wait()
+            down_sum[...] = sum_of(down_land).astype(low)
+            move(0, down_sum, down_last)
+    for source in range(fs):
+        arrived(proj_land.at[source], proj_recv.at[source], here)
+    proj_sum[...] = sum_of(proj_land).astype(low)
+    move(1, proj_sum, proj_last)
+
     loads[2].wait()
     loads[3].wait()
 
+    ends = jnp.logical_or(c == 0, c == ctx - 1)
+
     def give(step, carry):
-        at = ordered(c, ctx - 1 - step, ctx)
-        for step_ in range(1, fs):
-            other = lax.rem(f + step_, fs)
+        at = towards(c, step, ctx)
+        for move_ in range(1, fs):
+            other = lax.rem(f + move_, fs)
             arrived(mixed.at[other // 2, at, lax.rem(other, 2)], u_recv.at[other, at], here)
         terms = jnp.dot(mixed[:, at].reshape(both_rows, 4 * LANES), wide[...], preferred_element_type=wide_t)
         in_sum.give(at, terms.reshape(dp, rows, D))
+
+        @pl.when(jnp.logical_and(ends, step > 0))
+        def _():
+            in_sum.step(towards(c, step - 1, ctx))
+
         return carry
 
     lax.fori_loop(0, ctx, give, 0)
-    in_sum.step(ordered(c, ctx - 1, ctx))
 
     every = dp * ctx * rows
     k_relay = 2 * lax.rem(c, 2) + d
     relays = (k_relay, lax.rem(k_relay + 2, fs))
+    gain_terms = jnp.zeros((1, D), wide_t)
     for slot in (2, 3, 0, 1):
         heads = inner(mixed[:, :, :, :, slot * LANES : (slot + 1) * LANES].reshape(every, LANES), normed[...].reshape(every, D))
         grad_heads[slot] = heads[:HD].astype(low)
+        weights = wide[slot * LANES : slot * LANES + HD, :].astype(wide_t)
+        gain_terms += jnp.sum(heads[:HD] * weights, axis=0, keepdims=True)
         if slot < 2:
             push(grad_heads.at[slot], q_land, head_send.at[slot], head_recv.at[0], 0, 2 * d + slot)
         else:
             push(grad_heads.at[slot], kv_land.at[slot - 2], head_send.at[slot], head_recv.at[slot - 1], d, relays[slot - 2])
 
-    def steps(step, carry):
-        at = ordered(c, ctx - 1 - step, ctx)
-        pltpu.make_async_copy(partial_ref.at[d, at], out_sum.mine.at[at], mine_sem.at[at]).wait()
-        out_sum.step(at)
-
-        @pl.when(step < ctx - 2)
-        def _():
-            in_sum.step(ordered(c, ctx - 2 - step, ctx))
-
-        return carry
-
-    lax.fori_loop(0, ctx, steps, 0)
-    out_ref[...] = (resid_ref[...] + out_sum.total[...]).astype(low)
-    for source in range(fs):
-        arrived(proj_land.at[source], proj_recv.at[source], here)
-    proj_sum[...] = sum_of(proj_land).astype(low)
-    move(1, proj_sum, proj_last)
-
-    def kv_route(slot):
-        owner, owner_f = slot * 2 + c // 2, k_relay
-        return owner, owner_f, jnp.logical_or(jnp.logical_or(d != 1, owner != c), owner_f != f)
-
-    for slot in range(2):
-        owner, owner_f, away = kv_route(slot)
-
-        @pl.when(f == relays[slot])
-        def _():
-            for source in range(fs):
-                arrived(kv_land.at[slot, source], head_recv.at[1 + slot, source], here)
-            kv_sum[slot] = sum_of(kv_land.at[slot]).astype(low)
-
-            @pl.when(away)
-            def _():
-                remote(kv_sum.at[slot], kv_last, move_send.at[2 + slot], move_recv.at[2], at_device(1, owner, owner_f)).start()
-
-            @pl.when(jnp.logical_not(away))
-            def _():
-                pltpu.make_async_copy(kv_sum.at[slot], kv_last, move_recv.at[2]).start()
-
-    loads[5].wait()
-    up_out[...] = sum_of(up_land)
-    in_sum.step(c)
-
     gain = gains_ref[0:1, :]
-    values = x_ref[...].astype(wide_t)
-    scale = lax.rsqrt(jnp.mean(values * values, axis=-1, keepdims=True) + EPS)
-    incoming = in_sum.total[...]
-    weighted = incoming * gain
-    mean = jnp.mean(weighted * values, axis=-1, keepdims=True)
-    d_x_ref[...] = (d_resid_ref[...] + scale * weighted - values * (scale * scale * scale) * mean).astype(low)
-    gain_vec[0:1, :] = jnp.sum(incoming * values * scale, axis=0, keepdims=True)
+    gain_vec[0:1, :] = gain_terms / gain
     gain_vec[1:2, :] = gain_two_ref[0:1, :]
     each = D // n
     for index in range(n):
@@ -1464,16 +1470,56 @@
 
     lax.fori_loop(1, n, gain_to, 0)
 
-    for index, dst in enumerate((down_last, proj_last)):
-        arrived(dst, move_recv.at[index], here)
-    down_out[...] = down_last[...].astype(wide_t)
-    proj_out[...] = proj_last[...].astype(wide_t)
+    def middle_step(step, carry):
+        in_sum.step(towards(c, step, ctx))
+        return carry
+
+    @pl.when(jnp.logical_not(ends))
+    def _():
+        lax.fori_loop(0, ctx - 1, middle_step, 0)
+
+    def kv_route(slot):
+        owner, owner_f = slot * 2 + c // 2, k_relay
+        return owner, owner_f, jnp.logical_or(jnp.logical_or(d != 1, owner != c), owner_f != f)
+
+    for slot in range(2):
+        owner, owner_f, away = kv_route(slot)
+
+        @pl.when(f == relays[slot])
+        def _():
+            for source in range(fs):
+                arrived(kv_land.at[slot, source], head_recv.at[1 + slot, source], here)
+            kv_sum[slot] = sum_of(kv_land.at[slot]).astype(low)
+
+            @pl.when(away)
+            def _():
+                remote(kv_sum.at[slot], kv_last, move_send.at[2 + slot], move_recv.at[2], at_device(1, owner, owner_f)).start()
+
+            @pl.when(jnp.logical_not(away))
+            def _():
+                pltpu.make_async_copy(kv_sum.at[slot], kv_last, move_recv.at[2]).start()
+
+    loads[5].wait()
+    up_out[...] = sum_of(up_land)
+    in_sum.step(c)
+
+    values = x_ref[...].astype(wide_t)
+    scale = lax.rsqrt(jnp.mean(values * values, axis=-1, keepdims=True) + EPS)
+    incoming = in_sum.total[...]
+    weighted = incoming * gain
+    mean = jnp.mean(weighted * values, axis=-1, keepdims=True)
+    d_x_ref[...] = (d_resid_ref[...] + scale * weighted - values * (scale * scale * scale) * mean).astype(low)
 
     @pl.when(d == 0)
     def _():
         for source in range(fs):
             arrived(q_land.at[source], head_recv.at[0, source], here)
         qkv_out[...] = sum_of(q_land)
+
+    for index, dst in enumerate((down_last, proj_last)):
+        arrived(dst, move_recv.at[index], here)
+    down_out[...] = down_last[...].astype(wide_t)
+    proj_out[...] = proj_last[...].astype(wide_t)
 
     @pl.when(d == 1)
     def _():
@@ -1513,12 +1559,6 @@
             def _():
                 left(stage.at[at, to], u_send.at[at, to], here)
 
-        left(partial_ref.at[1 - d, at], out_sum.core_send.at[at], here)
-
-        @pl.when(at != c)
-        def _():
-            left(out_sum.out_line.at[at], out_sum.line_send.at[at], here)
-
     in_sum.finish()
 
     def gain_left(step, carry):
@@ -1529,7 +1569,7 @@
     lax.fori_loop(1, n, gain_left, 0)
 
 
-def last(sizes, x, gains, tables, resid, d_resid, gain_two, grad_proj, unit, d_unit, normed, wide, partial, up_land, down_land):
+def last(sizes, x, gains, tables, d_resid, gain_two, grad_proj, unit, d_unit, normed, wide, up_land, down_land):
     dp, ctx, fs = sizes
     n = dp * ctx * fs
     rows = x.shape[0]
@@ -1539,7 +1579,6 @@
     any_spec, vm_spec = pl.BlockSpec(memory_space=ANY), pl.BlockSpec(memory_space=VM)
     down_rows, proj_rows, half = down_land.shape[1], grad_proj.shape[1], up_land.shape[2]
     shapes = (
-        jax.ShapeDtypeStruct((rows, D), low),
         jax.ShapeDtypeStruct((rows, D), low),
         jax.ShapeDtypeStruct((8, LANES), wide_t),
         jax.ShapeDtypeStruct((HD, D), wide_t),
@@ -1551,8 +1590,8 @@
         functools.partial(last_kernel, sizes),
         name="last",
         out_shape=shapes,
-        in_specs=[vm_spec] * 8 + [any_spec] * 7,
-        out_specs=[vm_spec] * 7,
+        in_specs=[vm_spec] * 7 + [any_spec] * 6,
+        out_specs=[vm_spec] * 6,
         scratch_shapes=[
             VM(unit.shape, low),
             VM(d_unit.shape, low),
@@ -1563,7 +1602,7 @@
             VM(normed.shape, low),
             VM(wide.shape, low),
             VM((4, HD, D), low),
-            VM((fs, D, half), low),
+            VM(up_land.shape, low),
             VM((fs, down_rows, D), low),
             VM((fs, proj_rows, D), low),
             VM((fs, HD, D), low),
@@ -1579,10 +1618,42 @@
             VM((n, 8, LANES), wide_t),
             dma((6,)), dma((fs,)), dma((fs,)),
             dma((4,)), dma((3, fs)), dma((4,)), dma((3,)),
-            dma((ctx, fs)), dma((fs, ctx)), dma((n,)), dma((n,)), dma((ctx,)),
-        ] + LineSum.scratch(ctx, rows) + LineSum.scratch(ctx, rows),
+            dma((ctx, fs)), dma((fs, ctx)), dma((n,)), dma((n,)),
+        ] + LineSum.scratch(ctx, rows),
         compiler_params=pltpu.CompilerParams(collective_id=3, has_side_effects=True, vmem_limit_bytes=63 * 1024 * 1024),
-    )(x, gains, *tables, resid, d_resid, gain_two, grad_proj, unit, d_unit, normed, wide, partial, up_land, down_land)
+    )(x, gains, *tables, d_resid, gain_two, grad_proj, unit, d_unit, normed, wide, up_land, down_land)
+
+
+def emit_kernel(count, gains_ref, *refs):
+    sources, outs, one_ref, two_ref = refs[:count], refs[count : 2 * count], refs[2 * count], refs[2 * count + 1]
+    held, in_sem, out_sem = refs[2 * count + 2 : 3 * count + 2], refs[-2], refs[-1]
+    loads = [pltpu.make_async_copy(sources[i], held[i], in_sem.at[i]) for i in range(count)]
+    stores = [pltpu.make_async_copy(held[i], outs[i], out_sem.at[i]) for i in range(count)]
+    for load in loads:
+        load.start()
+    each = one_ref.shape[0]
+    one_ref[...] = gains_ref[0, :each]
+    two_ref[...] = gains_ref[1, :each]
+    for load, store in zip(loads, stores):
+        load.wait()
+        store.start()
+    for store in stores:
+        store.wait()
+
+
+def emit(each, gains, *arrays):
+    count = len(arrays)
+    any_spec, vm_spec = pl.BlockSpec(memory_space=ANY), pl.BlockSpec(memory_space=VM)
+    gain = jax.ShapeDtypeStruct((each,), jnp.float32)
+    return pl.pallas_call(
+        functools.partial(emit_kernel, count),
+        name="emit",
+        out_shape=[jax.ShapeDtypeStruct(a.shape, a.dtype) for a in arrays] + [gain, gain],
+        in_specs=[vm_spec] + [any_spec] * count,
+        out_specs=[any_spec] * count + [vm_spec] * 2,
+        scratch_shapes=[VM(a.shape, a.dtype) for a in arrays] + [pltpu.SemaphoreType.DMA((count,))] * 2,
+        compiler_params=pltpu.CompilerParams(vmem_limit_bytes=63 * 1024 * 1024),
+    )(gains, *arrays)
 
 
 def on_device(tokens, cotangent, attn_gain, w_qkv, w_out, mlp_gain, w_gate_up, w_down):
@@ -1596,23 +1667,26 @@
     gain_rows = jnp.pad(gain_rows, ((0, 6), (0, LANES - each)))
     tables = angle_tables(ctx * fs, span)
     parts, sent = 4, 3
-    normed, unit, att, qkv, gains, dy_all, proj, gate_up = first(
-        where, parts, sent, x, gain_rows, w_qkv.T, *tables, dy, w_out, w_gate_up
+    normed, unit, att, qkv, gains, dy_all, proj, down, gate_up = first(
+        where, parts, sent, x, gain_rows, w_qkv.T, *tables, dy, w_out, w_down, w_gate_up
     )
     att = att.reshape(dp, ctx, rows, 2 * LANES)
-    resid, d_resid, grad_two, partial, d_unit, grad_proj, up_land, down_land = middle(
-        where, parts, sent, att, x, dy, gains, proj, w_down, w_gate_up, gate_up, dy_all
+    block_out, d_resid, grad_two, d_unit, grad_proj, up_land, down_land = middle(
+        where, parts, sent, att, x, dy, gains, proj, down, w_gate_up, gate_up, dy_all
     )
-    block_out, grad_tokens, gain_grads, grad_qkv, grad_out, grad_gate_up, grad_down = last(
-        where, x, gains, tables, resid, d_resid, grad_two, grad_proj, unit, d_unit, normed, qkv, partial, up_land, down_land
+    grad_tokens, gain_grads, grad_qkv, grad_out, grad_gate_up, grad_down = last(
+        where, x, gains, tables, d_resid, grad_two, grad_proj, unit, d_unit, normed, qkv, up_land, down_land
+    )
+    block_out, grad_tokens, grad_qkv, grad_out, grad_gate_up, grad_down, grad_one, grad_two = emit(
+        each, gain_grads, block_out, grad_tokens, grad_qkv, grad_out, grad_gate_up, grad_down
     )
     return (
         block_out.reshape(tokens.shape),
         grad_tokens.reshape(tokens.shape),
-        gain_grads[0, :each],
+        grad_one,
         grad_qkv.T,
         grad_out,
-        gain_grads[1, :each],
+        grad_two,
         grad_gate_up,
         grad_down,
     )

time: 350 us -> 295 us (0.84)
  Pallas kernels: 334 us -> 291 us
  local copies, waits for them, and re-layouts: 9.6 us -> 0 us
    pallas_call x1, Pallas kernels: 94.3 us -> 63.2 us  [last(): pl.pallas_call(functools.partial(last_kernel, sizes), name='last', out_sh...]
    pallas_call x1, Pallas kernels: 91.3 us -> 80.4 us  [first(): pl.pallas_call(functools.partial(first_kernel, sizes, parts), name='first...]
    unnamed x12 -> x0, local copies, waits for them, and re-layouts: 8.27 us -> none
    pallas_call x1, Pallas kernels: 149 us -> 143 us  [middle(): pl.pallas_call(functools.partial(middle_kernel, sizes, hidden, parts, sen...]
    pallas_call x0 -> x1, Pallas kernels: none -> 4.79 us  [emit(): pl.pallas_call(functools.partial(emit_kernel, count), name='emit', out_sh...]
where the time goes in v6:
time: 295 us
  Pallas kernels  291 us (99%)
    pallas_call x1, Pallas kernels, middle(): pl.pallas_call(functools.partial(middle_kernel, sizes, hidden, parts, sen...  143 us
    pallas_call x1, Pallas kernels, first(): pl.pallas_call(functools.partial(first_kernel, sizes, parts), name='first...  80.4 us
    pallas_call x1, Pallas kernels, last(): pl.pallas_call(functools.partial(last_kernel, sizes), name='last', out_sh...  63.2 us

profile of v6, /device:TPU:13, one launch (start us, length us, event | category | flops | bytes accessed | tf_op | source)
XLA Modules:
  0.0 294.8 jit_solution(4967301294428733115)
XLA Ops:
  0.7 1.3 fusion.6.gains_ref
  1.9 0.1 multiply_cosine_fusion.1
  2.1 0.6 pad_maximum_fusion.1.block_ref
  2.7 0.2 multiply_cosine_fusion
  2.9 0.6 pad_maximum_fusion.step_ref
  3.5 80.4 %first.1 = (bf16[2,4,128,1536]{3,2,1,0:T(8,128)(2,1)}, bf16[4,4,64,512]{3,2,1,0:T(8,128)(2,1)}, bf16[2,4,2,64,256]{4,3,2,1,0:T(8,128)(2,1)}, bf16[512,1536]{1,0:...) custom-call(bf16[128,1536]{1,0:T(8,128)(2,1)} %bitcast.13, ...), custom_call_target="tpu_custom_call" | custom-call | tf_op jit(solution)/shard_map/first/pallas_call | solution.py:788
  83.9 142.8 %middle.1 = (bf16[128,1536]{1,0:T(8,128)(2,1)}, f32[128,1536]{1,0:T(8,128)}, f32[8,1536]{1,0:T(8,128)}, bf16[4,4,64,256]{3,2,1,0:T(8,128)(2,1)}, bf16[4,48,1536]...) custom-call(bf16[2,4,128,256]{3,2,1,0:T(8,128)(2,1)} %bitcast.18, ...), custom_call_target="tpu_custom_call" | custom-call | tf_op jit(solution)/shard_map/middle/pallas_call | solution.py:1256
  226.7 63.2 %last.1 = (bf16[128,1536]{1,0:T(8,128)(2,1)}, f32[8,128]{1,0:T(8,128)}, f32[96,1536]{1,0:T(8,128)}, f32[48,1536]{1,0:T(8,128)}, f32[1536,256]{1,0:T(8,128)}, /*index=5*/f32[128,1536]{1,0:T(8,128)}) custom-call(bf16[128,1536]{1,0:T(8,128)(2,1)} %bitcast.15, f32[8,1536]{1,0:T(8,128)} %get-tuple-element.38.gains_ref, ...), custom_call_target="tpu_custom_call" | custom-call | tf_op jit(solution)/shard_map/last/pallas_call | solution.py:1589
  289.9 4.8 %emit.1 = (bf16[128,1536]{1,0:T(8,128)(2,1)}, bf16[128,1536]{1,0:T(8,128)(2,1)}, f32[96,1536]{1,0:T(8,128)}, f32[48,1536]{1,0:T(8,128)}, f32[1536,256]{1,0:T(8,1...) custom-call(f32[8,128]{1,0:T(8,128)} %get-tuple-element.53.gains_ref, ...), custom_call_target="tpu_custom_call" | custom-call | tf_op jit(solution)/shard_map/emit/pallas_call | solution.py:1648
  (3 shorter events, 0.0 us)

commit v7 on v6

--- a/solution.py
+++ b/solution.py
@@ -329,23 +329,39 @@
 HALVES = 2
 
 
-def half(ref, index):
+def part_of(ref, index):
     rows = ref.shape[-2] // HALVES
     return ref.at[index * rows : (index + 1) * rows]
 
 
+def near_or_inner(c, at, n):
+    ends = jnp.logical_or(c == 0, c == n - 1)
+    return jnp.logical_or(jnp.logical_not(ends), jnp.abs(at - c) <= 1)
+
+
 class LineGather:
-    def __init__(self, n, own, whole, send, recv, local):
+    def __init__(self, n, own, whole, send, recv, local, short=False):
         self.n, self.own, self.whole, self.send, self.recv, self.local = n, own, whole, send, recv, local
+        self.short = short
         self.d, self.c, self.f = place()
         self.here = at_device(self.d, self.c, self.f)
 
     def slot(self, at):
         return self.whole.at[self.d, at]
 
+    def held(self, at):
+        valid = jnp.logical_and(at >= 0, at < self.n)
+        return jnp.logical_and(valid, near_or_inner(self.c, at, self.n)) if self.short else valid
+
+    def passes(self, way, at):
+        ahead = self.n - 2 - self.c if way == 0 else self.c - 1
+        inside = at <= self.c if way == 0 else at >= self.c
+        goes = jnp.logical_and(inside, ahead >= 0)
+        return jnp.logical_and(goes, jnp.logical_or(at == self.c, ahead > 0)) if self.short else goes
+
     def along(self, way, block, at, part):
         to = (at_device(self.d, self.c + 1, self.f), at_device(self.d, self.c - 1, self.f), at_device(1 - self.d, self.c, self.f))[way]
-        return remote(half(block, part), half(self.slot(at), part), self.send.at[way, at, part], self.recv.at[self.d, at, part], to)
+        return remote(part_of(block, part), part_of(self.slot(at), part), self.send.at[way, at, part], self.recv.at[self.d, at, part], to)
 
     def start(self):
         c = self.c
@@ -364,28 +380,18 @@
         pltpu.make_async_copy(self.own, self.slot(c), self.local).start()
 
     def forward(self, k):
-        c = self.c
         for part in range(HALVES):
-
-            @pl.when(c - k >= 0)
-            def _():
-                arrived(half(self.slot(c - k), part), self.recv.at[self.d, c - k, part], self.here)
-
-                @pl.when(c < self.n - 1)
+            for way, at in enumerate((self.c - k, self.c + k)):
+
+                @pl.when(self.held(at))
                 def _():
-                    self.along(0, self.slot(c - k), c - k, part).start()
-
-                self.along(2, self.slot(c - k), c - k, part).start()
-
-            @pl.when(c + k < self.n)
-            def _():
-                arrived(half(self.slot(c + k), part), self.recv.at[self.d, c + k, part], self.here)
-
-                @pl.when(c > 0)
-                def _():
-                    self.along(1, self.slot(c + k), c + k, part).start()
-
-                self.along(2, self.slot(c + k), c + k, part).start()
+                    arrived(part_of(self.slot(at), part), self.recv.at[self.d, at, part], self.here)
+
+                    @pl.when(self.passes(way, at))
+                    def _():
+                        self.along(way, self.slot(at), at, part).start()
+
+                    self.along(2, self.slot(at), at, part).start()
 
     def reach(self, step):
         now = jnp.abs(ordered(self.c, step, self.n) - self.c)
@@ -396,24 +402,20 @@
             self.forward(now)
 
     def other(self, at):
-        for part in range(HALVES):
-            arrived(half(self.whole.at[1 - self.d, at], part), self.recv.at[1 - self.d, at, part], self.here)
+        @pl.when(self.held(at))
+        def _():
+            for part in range(HALVES):
+                arrived(part_of(self.whole.at[1 - self.d, at], part), self.recv.at[1 - self.d, at, part], self.here)
 
     def finish_sends(self):
-        c = self.c
         for at in range(self.n):
             for part in range(HALVES):
-                block = half(self.slot(at), part)
-
-                @pl.when(jnp.logical_and(at <= c, c < self.n - 1))
-                def _():
-                    left(block, self.send.at[0, at, part], self.here)
-
-                @pl.when(jnp.logical_and(at >= c, c > 0))
-                def _():
-                    left(block, self.send.at[1, at, part], self.here)
-
-                left(block, self.send.at[2, at, part], self.here)
+                block = part_of(self.slot(at), part)
+                for way in range(3):
+
+                    @pl.when(self.passes(way, at) if way < 2 else self.held(at))
+                    def _():
+                        left(block, self.send.at[way, at, part], self.here)
 
     def finish(self):
         self.finish_sends()
@@ -552,7 +554,21 @@
 
     for k in range(1, ctx - 1):
         line.forward(k)
-    dy_line = LineGather(ctx, dy_ref, dy_all, dy_send, dy_recv, dy_local)
+    to_core, to_ctx = lax.rem(c, 2), 2 * d + c // 2
+    stays = jnp.logical_and(to_core == d, to_ctx == c)
+    moved = ((proj_ref, proj_all),)
+    for index, (shard, whole) in enumerate(moved):
+
+        @pl.when(jnp.logical_not(stays))
+        def _():
+            remote(shard, whole.at[f], m_send.at[index], m_recv.at[index, f], at_device(to_core, to_ctx, f)).start()
+
+        @pl.when(stays)
+        def _():
+            pltpu.make_async_copy(shard, whole.at[f], m_recv.at[index, f]).start()
+
+
+    dy_line = LineGather(ctx, dy_ref, dy_all, dy_send, dy_recv, dy_local, short=True)
     dy_line.start()
     for slot in range(4):
         if slot < 2:
@@ -563,7 +579,8 @@
             def _():
                 arrived(head_rows(slot), w_recv.at[slot], here)
 
-    push_part(0)
+    for part in range(gu_send.shape[0]):
+        push_part(part)
     pltpu.make_async_copy(line.own, line.slot(c), line.local).wait()
 
     def block(step, carry):
@@ -613,29 +630,21 @@
     wide_copy.start()
     gains_copy.start()
 
-    to_core, to_ctx = lax.rem(c, 2), 2 * d + c // 2
-    stays = jnp.logical_and(to_core == d, to_ctx == c)
-    moved = ((proj_ref, proj_all),)
+    @pl.when(jnp.logical_not(stays))
+    def _():
+        remote(down_ref, down_out, down_send, down_recv, at_device(to_core, to_ctx, f)).start()
+
+    @pl.when(stays)
+    def _():
+        pltpu.make_async_copy(down_ref, down_out, down_recv).start()
+
     for index, (shard, whole) in enumerate(moved):
-
-        @pl.when(jnp.logical_not(stays))
-        def _():
-            remote(shard, whole.at[f], m_send.at[index], m_recv.at[index, f], at_device(to_core, to_ctx, f)).start()
-
-        @pl.when(stays)
-        def _():
-            pltpu.make_async_copy(shard, whole.at[f], m_recv.at[index, f]).start()
-
-
-    push_part(1)
+        arrived(whole.at[f], m_recv.at[index, f], here)
+        for step in range(1, fs):
+            to = lax.rem(f + step, fs)
+            remote(whole.at[f], whole.at[f], m_pass.at[index, step], m_recv.at[index, f], at_device(d, c, to)).start()
+
     dy_line.forward(1)
-
-    def pass_on():
-        for index, (shard, whole) in enumerate(moved):
-            arrived(whole.at[f], m_recv.at[index, f], here)
-            for step in range(1, fs):
-                to = lax.rem(f + step, fs)
-                remote(whole.at[f], whole.at[f], m_pass.at[index, step], m_recv.at[index, f], at_device(d, c, to)).start()
 
     for at in range(ctx):
         for step in range(1, fs):
@@ -673,21 +682,8 @@
             def _():
                 att[f // 2, at, lax.rem(f, 2)] = att_stage[at, to]
 
-        if at == 0:
-            pass_on()
-        elif at == ctx - 1:
-            for part in range(2, gu_send.shape[0]):
-                push_part(part)
+        if at == ctx - 1:
             dy_line.forward(2)
-
-            @pl.when(jnp.logical_not(stays))
-            def _():
-                remote(down_ref, down_out, down_send, down_recv, at_device(to_core, to_ctx, f)).start()
-
-            @pl.when(stays)
-            def _():
-                pltpu.make_async_copy(down_ref, down_out, down_recv).start()
-
 
     for at in range(ctx):
         for step in range(1, fs):
@@ -696,8 +692,6 @@
     att_copy = pltpu.make_async_copy(att, att_out, out_sem.at[4])
     att_copy.start()
 
-    for k in range(3, ctx):
-        dy_line.forward(k)
     for at in range(ctx):
         dy_line.other(at)
     dy_line.finish()
@@ -952,8 +946,8 @@
     out_ref, d_resid_out, gain_out, unit_out, grad_proj_out, up_land, down_land,
     att, dy_all, proj, down, gate_up, resid, own_two, normed_two, act, d_both, own_d, d_resid_all, d_stage, unit,
     grad_up, grad_down, grad_proj, grad_proj_low,
-    in_sem, gu_send, gu_recv, m_recv, m_pass, two_send, two_recv, two_local, dr_send, dr_recv, dr_local, u_send, u_recv,
-    out_sem, gup_send, gup_recv, gdn_send, gdn_recv,
+    in_sem, dy_sem, gu_send, gu_recv, m_recv, m_pass, two_send, two_recv, two_local, dr_send, dr_recv, dr_local, u_send, u_recv,
+    late_send, late_recv, late_pass, out_sem, gup_send, gup_recv, gdn_send, gdn_recv,
     *sums,
 ):
     dp, ctx, fs = sizes
@@ -970,7 +964,6 @@
     tell_near(sizes)
 
     att_copy = pltpu.make_async_copy(att_ref, att, in_sem.at[0])
-    dy_copy = pltpu.make_async_copy(dy_all_ref, dy_all, in_sem.at[1])
     part_copy = pltpu.make_async_copy(gate_up_part_ref, gate_up.at[:, 0 : part_rows * sent], in_sem.at[2])
     att_copy.start()
     proj[...] = jnp.zeros_like(proj)
@@ -980,7 +973,16 @@
         start = slot // 2 * LANES + slot % 2 * each
         proj_copies.append(pltpu.make_async_copy(proj_ref.at[slot], proj.at[start : start + each], in_sem.at[3 + slot]))
         proj_copies[-1].start()
-    dy_copy.start()
+
+    def dy_load(at):
+        return pltpu.make_async_copy(dy_all_ref.at[:, at], dy_all.at[:, at], dy_sem.at[at])
+
+    for at in range(ctx):
+
+        @pl.when(near_or_inner(c, at, ctx))
+        def _():
+            dy_load(at).start()
+
     part_copy.start()
     att_copy.wait()
     for copy in proj_copies:
@@ -995,12 +997,32 @@
     lax.fori_loop(0, ctx, project, 0)
     hear_near(sizes)
 
+    ends = jnp.logical_or(c == 0, c == ctx - 1)
+    last_hops = ((c == 1, -1), (c == ctx - 2, 1))
+
+    def late(way, at, part):
+        src, dst = part_of(dy_all_ref.at[d, at], part), part_of(dy_all.at[d, at], part)
+        return remote(src, dst, late_send.at[at, part], late_recv.at[d, at, part], at_device(d, c + way, f))
+
+    for sends, way in last_hops:
+        for step in range(1, ctx - 1):
+
+            @pl.when(sends)
+            def _():
+                for part in range(HALVES):
+                    late(way, c - way * step, part).start()
+
+    def late_across(at, part):
+        block = part_of(dy_all.at[d, at], part)
+        return remote(block, block, late_pass.at[at, part], late_recv.at[d, at, part], at_device(1 - d, c, f))
+
+    def far(step):
+        return jnp.where(c == 0, 1 + step, ctx - 2 - step)
+
     pltpu.make_async_copy(down_ref, down.at[f], m_recv.at[f]).start()
     for step in range(1, fs):
         to = lax.rem(f + step, fs)
         remote(down_ref, down.at[f], m_pass.at[step], m_recv.at[f], at_device(d, c, to)).start()
-    ends = jnp.logical_or(c == 0, c == ctx - 1)
-
     for step in range(ctx):
         line_sum.hand(towards(c, step, ctx))
 
@@ -1021,6 +1043,14 @@
     line_sum.step(towards(c, 0, ctx))
     line_sum.step(towards(c, 1, ctx))
     line_sum.step(towards(c, 2, ctx))
+
+    @pl.when(ends)
+    def _():
+        for step in range(1, ctx - 1):
+            for part in range(HALVES):
+                arrived(part_of(dy_all.at[d, far(step)], part), late_recv.at[d, far(step), part], here)
+                late_across(far(step), part).start()
+
     line_sum.step(c)
     gain = gains_ref[1:2, :]
     values = x_ref[...].astype(jnp.float32) + line_sum.total[...]
@@ -1032,7 +1062,17 @@
     line.forward(1)
     for slot in range(4):
         arrived(gate_up.at[slot, rest], gu_recv.at[slot], here)
-    dy_copy.wait()
+    for at in range(ctx):
+
+        @pl.when(near_or_inner(c, at, ctx))
+        def _():
+            dy_load(at).wait()
+
+    @pl.when(ends)
+    def _():
+        for step in range(1, ctx - 1):
+            for part in range(HALVES):
+                arrived(part_of(dy_all.at[1 - d, far(step)], part), late_recv.at[1 - d, far(step), part], here)
     part_copy.wait()
     for slot in range(fs):
         arrived(down.at[slot], m_recv.at[slot], here)
@@ -1084,7 +1124,7 @@
             pltpu.make_async_copy(src, dst, recv).start()
 
     def grads(step):
-        first = step * wide_rows
+        first = pl.multiple_of(step * wide_rows, LANES)
         left_rows = normed_two[:, :, :, pl.ds(first, wide_rows)].reshape(dp * ctx * rows, wide_rows)
         for part in range(2):
             cols = slice(part * hidden, (part + 1) * hidden)
@@ -1109,14 +1149,22 @@
         terms = jnp.dot(act[:, at].reshape(both_rows, hidden), down[...].reshape(hidden, D), preferred_element_type=jnp.float32)
         out_sum.give(at, terms.reshape(dp, rows, D))
 
-    second_sum.step(towards(c, 0, ctx))
-    grads(0)
-    out_terms(0)
-    second_sum.step(towards(c, 1, ctx))
-    second_sum.step(towards(c, 2, ctx))
-    for step in range(1, ctx - 1):
+    def second_steps():
+        def body(step, carry):
+            second_sum.step(towards(c, step, ctx))
+            return carry
+
+        lax.fori_loop(0, ctx - 1, body, 0)
+
+    def local_terms(step, carry):
         grads(step)
         out_terms(step)
+        return carry
+
+    pl.when(ends)(second_steps)
+    lax.fori_loop(0, ctx - 1, local_terms, 0)
+    pl.when(jnp.logical_not(ends))(second_steps)
+    local_terms(ctx - 1, 0)
     second_sum.step(c)
     values = resid[...]
     scale = lax.rsqrt(jnp.mean(values * values, axis=-1, keepdims=True) + EPS)
@@ -1137,8 +1185,6 @@
     def _():
         lax.fori_loop(0, ctx - 1, out_step, 0)
 
-    out_terms(ctx - 1)
-    grads(ctx - 1)
     pltpu.make_async_copy(d_line.own, d_line.slot(c), d_line.local).wait()
     grad_proj[...] = jnp.zeros_like(grad_proj)
 
@@ -1207,6 +1253,19 @@
 
     for step in range(1, fs):
         left(down_ref, m_pass.at[step], here)
+    for sends, way in last_hops:
+        for step in range(1, ctx - 1):
+
+            @pl.when(sends)
+            def _():
+                for part in range(HALVES):
+                    left(part_of(dy_all_ref.at[d, c - way * step], part), late_send.at[c - way * step, part], here)
+
+    @pl.when(ends)
+    def _():
+        for step in range(1, ctx - 1):
+            for part in range(HALVES):
+                left(part_of(dy_all.at[d, far(step)], part), late_pass.at[far(step), part], here)
 
     def settle_up(step, carry):
         first = pl.multiple_of(step * wide_rows, LANES)
@@ -1278,11 +1337,11 @@
             VM((fs, hidden // fs, D), low),
             VM((2 * LANES, D), wide_t),
             VM(proj.shape, low),
-            dma((3 + fs,)), dma((fs,)), dma((4,)), dma((fs,)), dma((fs,)),
+            dma((3 + fs,)), dma((ctx,)), dma((fs,)), dma((4,)), dma((fs,)), dma((fs,)),
             dma((3, ctx, HALVES)), dma((dp, ctx, HALVES)), dma,
             dma((3, ctx, HALVES)), dma((dp, ctx, HALVES)), dma,
             dma((ctx, 2 * dp)), dma((ctx, fs)),
-            dma((3,)),
+            dma((ctx, HALVES)), dma((dp, ctx, HALVES)), dma((ctx, HALVES)), dma((3,)),
             dma((4, ctx)), dma((fs, ctx)), dma((fs, ctx)), dma((fs, ctx)),
         ] + LineSum.scratch(ctx, rows) * 3,
         compiler_params=pltpu.CompilerParams(collective_id=2, has_side_effects=True, vmem_limit_bytes=63 * 1024 * 1024),
@@ -1394,8 +1453,6 @@
         stage[at, :, :, 3 * LANES : 4 * LANES] = d_v[block * at : keys, :].astype(low).reshape(fs, span, LANES)
         if at == ctx - 1:
             hear_all(sizes)
-            for slot in range(fs):
-                push(proj_ref.at[slot], proj_land, proj_send.at[slot], proj_recv, d, slot)
         for to in range(fs):
 
             @pl.when(to != f)
@@ -1412,11 +1469,8 @@
             loads[4].wait()
             down_sum[...] = sum_of(down_land).astype(low)
             move(0, down_sum, down_last)
-    for source in range(fs):
-        arrived(proj_land.at[source], proj_recv.at[source], here)
-    proj_sum[...] = sum_of(proj_land).astype(low)
-    move(1, proj_sum, proj_last)
-
+    for slot in range(fs):
+        push(proj_ref.at[slot], proj_land, proj_send.at[slot], proj_recv, d, slot)
     loads[2].wait()
     loads[3].wait()
 
@@ -1430,7 +1484,7 @@
         terms = jnp.dot(mixed[:, at].reshape(both_rows, 4 * LANES), wide[...], preferred_element_type=wide_t)
         in_sum.give(at, terms.reshape(dp, rows, D))
 
-        @pl.when(jnp.logical_and(ends, step > 0))
+        @pl.when(jnp.logical_and(ends, jnp.logical_and(step > 0, step < ctx - 1)))
         def _():
             in_sum.step(towards(c, step - 1, ctx))
 
@@ -1470,13 +1524,16 @@
 
     lax.fori_loop(1, n, gain_to, 0)
 
+    for source in range(fs):
+        arrived(proj_land.at[source], proj_recv.at[source], here)
+    proj_sum[...] = sum_of(proj_land).astype(low)
+    move(1, proj_sum, proj_last)
+
     def middle_step(step, carry):
         in_sum.step(towards(c, step, ctx))
         return carry
 
-    @pl.when(jnp.logical_not(ends))
-    def _():
-        lax.fori_loop(0, ctx - 1, middle_step, 0)
+    lax.fori_loop(jnp.where(ends, ctx - 2, 0), ctx - 1, middle_step, 0)
 
     def kv_route(slot):
         owner, owner_f = slot * 2 + c // 2, k_relay
@@ -1666,7 +1723,7 @@
     gain_rows = jnp.concatenate([attn_gain[None], mlp_gain[None]]).astype(jnp.float32)
     gain_rows = jnp.pad(gain_rows, ((0, 6), (0, LANES - each)))
     tables = angle_tables(ctx * fs, span)
-    parts, sent = 4, 3
+    parts, sent = 4, 1
     normed, unit, att, qkv, gains, dy_all, proj, down, gate_up = first(
         where, parts, sent, x, gain_rows, w_qkv.T, *tables, dy, w_out, w_down, w_gate_up
     )

time: 295 us -> 267 us (0.905)
  Pallas kernels: 291 us -> 263 us
    pallas_call x1, Pallas kernels: 80.4 us -> 64.7 us  [first(): pl.pallas_call(functools.partial(first_kernel, sizes, parts), name='first...]
    pallas_call x1, Pallas kernels: 143 us -> 133 us  [middle(): pl.pallas_call(functools.partial(middle_kernel, sizes, hidden, parts, sen...]
where the time goes in v7:
time: 267 us
  Pallas kernels  263 us (99%)
  other arithmetic  2.85 us (1%)
    pallas_call x1, Pallas kernels, middle(): pl.pallas_call(functools.partial(middle_kernel, sizes, hidden, parts, sen...  133 us
    pallas_call x1, Pallas kernels, first(): pl.pallas_call(functools.partial(first_kernel, sizes, parts), name='first...  64.7 us
    pallas_call x1, Pallas kernels, last(): pl.pallas_call(functools.partial(last_kernel, sizes), name='last', out_sh...  60.2 us

profile of v7, /device:TPU:13, one launch (start us, length us, event | category | flops | bytes accessed | tf_op | source)
XLA Modules:
  0.0 266.9 jit_solution(6547937870725312691)
XLA Ops:
  0.7 1.3 fusion.6.gains_ref
  1.9 0.1 multiply_cosine_fusion.1
  2.1 0.6 pad_maximum_fusion.1.block_ref
  2.7 0.2 multiply_cosine_fusion
  2.9 0.6 pad_maximum_fusion.step_ref
  3.5 64.7 %first.1 = (bf16[2,4,128,1536]{3,2,1,0:T(8,128)(2,1)}, bf16[4,4,64,512]{3,2,1,0:T(8,128)(2,1)}, bf16[2,4,2,64,256]{4,3,2,1,0:T(8,128)(2,1)}, bf16[512,1536]{1,0:...) custom-call(bf16[128,1536]{1,0:T(8,128)(2,1)} %bitcast.13, ...), custom_call_target="tpu_custom_call" | custom-call | tf_op jit(solution)/shard_map/first/pallas_call | solution.py:782
  68.2 133.5 %middle.1 = (bf16[128,1536]{1,0:T(8,128)(2,1)}, f32[128,1536]{1,0:T(8,128)}, f32[8,1536]{1,0:T(8,128)}, bf16[4,4,64,256]{3,2,1,0:T(8,128)(2,1)}, bf16[4,48,1536]...) custom-call(bf16[2,4,128,256]{3,2,1,0:T(8,128)(2,1)} %bitcast.18, ...), custom_call_target="tpu_custom_call" | custom-call | tf_op jit(solution)/shard_map/middle/pallas_call | solution.py:1315
  201.7 60.2 %last.1 = (bf16[128,1536]{1,0:T(8,128)(2,1)}, f32[8,128]{1,0:T(8,128)}, f32[96,1536]{1,0:T(8,128)}, f32[48,1536]{1,0:T(8,128)}, f32[1536,256]{1,0:T(8,128)}, /*index=5*/f32[128,1536]{1,0:T(8,128)}) custom-call(bf16[128,1536]{1,0:T(8,128)(2,1)} %bitcast.15, f32[8,1536]{1,0:T(8,128)} %get-tuple-element.38.gains_ref, ...), custom_call_target="tpu_custom_call" | custom-call | tf_op jit(solution)/shard_map/last/pallas_call | solution.py:1646
  261.9 4.8 %emit.1 = (bf16[128,1536]{1,0:T(8,128)(2,1)}, bf16[128,1536]{1,0:T(8,128)(2,1)}, f32[96,1536]{1,0:T(8,128)}, f32[48,1536]{1,0:T(8,128)}, f32[1536,256]{1,0:T(8,1...) custom-call(f32[8,128]{1,0:T(8,128)} %get-tuple-element.53.gains_ref, ...), custom_call_target="tpu_custom_call" | custom-call | tf_op jit(solution)/shard_map/emit/pallas_call | solution.py:1705
  (3 shorter events, 0.0 us)

commit v8 on v7

--- a/solution.py
+++ b/solution.py
@@ -1,4 +1,5 @@
 import functools
+import math
 
 import jax
 import jax.numpy as jnp
@@ -448,22 +449,120 @@
     return at
 
 
-def first_kernel(
-    sizes, parts, x_ref, gains_ref, w_ref, block_ref, step_ref, dy_ref, proj_ref, down_ref, gate_up_ref,
-    normed_out, unit_out, att_out, wide_out, gains_out, dy_all, proj_all, down_out, gate_up_all,
-    x_all, wide, normed, stage, unit, att_stage, att, gain_all, gain_vec,
-    line_send, line_recv, line_local, w_send, w_recv, w_pass, g_send, g_recv, u_send, u_recv, a_send, a_recv, out_sem,
-    dy_send, dy_recv, dy_local, m_send, m_recv, m_pass, down_send, down_recv, gu_send, gu_recv,
+class LineSum:
+    def __init__(self, n, mine, out_core, in_core, out_line, in_line, total, sems):
+        self.n, self.mine, self.out_core, self.in_core = n, mine, out_core, in_core
+        self.out_line, self.in_line, self.total = out_line, in_line, total
+        self.core_send, self.core_recv, self.line_send, self.line_recv = sems
+        self.d, self.c, self.f = place()
+        self.here = at_device(self.d, self.c, self.f)
+
+    def give(self, at, both):
+        self.keep(at, both)
+        self.hand(at)
+
+    def keep(self, at, both):
+        d = self.d
+        low = both.astype(jnp.bfloat16)
+
+        @pl.when(d == 0)
+        def _():
+            self.mine[at] = low[0]
+            self.out_core[at] = low[1]
+
+        @pl.when(d != 0)
+        def _():
+            self.mine[at] = low[1]
+            self.out_core[at] = low[0]
+
+    def hand(self, at):
+        remote(
+            self.out_core.at[at], self.in_core.at[at], self.core_send.at[at], self.core_recv.at[at], at_device(1 - self.d, self.c, self.f)
+        ).start()
+
+    def step(self, at):
+        n, d, c, f = self.n, self.d, self.c, self.f
+        arrived(self.in_core.at[at], self.core_recv.at[at], self.here)
+        rows = self.total.shape[0] // HALVES
+        for part in range(HALVES):
+            own = slice(part * rows, (part + 1) * rows)
+            self.total[own] = self.mine[at, own].astype(jnp.float32) + self.in_core[at, own].astype(jnp.float32)
+            for way, comes in enumerate((jnp.logical_and(at <= c, c < n - 1), jnp.logical_and(at >= c, c > 0))):
+
+                @pl.when(comes)
+                def _():
+                    arrived(self.in_line.at[way, at, own], self.line_recv.at[way, at, part], self.here)
+                    self.total[own] += self.in_line[way, at, own].astype(jnp.float32)
+
+            @pl.when(at != c)
+            def _():
+                self.out_line[at, own] = self.total[own].astype(jnp.bfloat16)
+
+            for way, (goes, to) in enumerate(((at < c, c - 1), (at > c, c + 1))):
+
+                @pl.when(goes)
+                def _():
+                    remote(
+                        self.out_line.at[at, own], self.in_line.at[way, at, own],
+                        self.line_send.at[at, part], self.line_recv.at[way, at, part], at_device(d, to, f),
+                    ).start()
+
+    def finish(self):
+        rows = self.total.shape[0] // HALVES
+        for at in range(self.n):
+            left(self.out_core.at[at], self.core_send.at[at], self.here)
+
+            @pl.when(at != self.c)
+            def _():
+                for part in range(HALVES):
+                    left(self.out_line.at[at, part * rows : (part + 1) * rows], self.line_send.at[at, part], self.here)
+
+    @staticmethod
+    def scratch(ctx, rows):
+        low = jnp.bfloat16
+        dma = pltpu.SemaphoreType.DMA
+        return [
+            VM((ctx, rows, D), low), VM((ctx, rows, D), low), VM((ctx, rows, D), low), VM((ctx, rows, D), low),
+            VM((2, ctx, rows, D), low), VM((rows, D), jnp.float32),
+            dma((ctx,)), dma((ctx,)), dma((ctx, HALVES)), dma((2, ctx, HALVES)),
+        ]
+
+
+def down_route(d, c):
+    return (lax.rem(c, 2), 2 * d + c // 2), (c // 2, 2 * lax.rem(c, 2) + d)
+
+
+def front_kernel(
+    sizes, hidden, parts, x_ref, one_ref, two_ref, w_ref, dy_ref, proj_ref, down_ref, gate_up_ref,
+    out_ref, d_resid_out, gain_out, block_ref, step_ref, normed_out, qkv_out, wide_out, gains_out, unit_out, grad_proj_out, up_land, down_land,
+    x_all, wide, normed, stage, qkv_unit, att_stage, att, gain_all, gain_vec,
+    dy_all, proj, down_mid, down, gate_up, resid, own_two, normed_two, act, d_both, own_d, d_stage, unit,
+    grad_up, grad_down, grad_proj, grad_proj_low, gains_ref,
+    line_send, line_recv, line_local, w_send, w_recv, w_pass, g_send, g_recv, q_send, q_recv, a_send, a_recv, out_sem,
+    dy_send, dy_recv, dy_local, m_send, m_recv, m_pass, down_send, down_recv, d_recv, d_pass, gu_send, gu_recv,
+    two_send, two_recv, two_local, dr_send, dr_recv, dr_local, u_send, u_recv, gup_send, gup_recv, gdn_send, gdn_recv,
+    *sums,
 ):
+    d_resid_all = x_all
     dp, ctx, fs = sizes
     n = dp * ctx * fs
     d, c, f = place()
     here = at_device(d, c, f)
     span = stage.shape[2]
     tell_all(sizes)
+    fill_tables(block_ref, step_ref)
+    gains_ref[0:1, 0 : D // n] = one_ref[...].astype(jnp.float32).reshape(1, D // n)
+    gains_ref[1:2, 0 : D // n] = two_ref[...].astype(jnp.float32).reshape(1, D // n)
     for slot in range(4):
         wide[slot * LANES + HD : (slot + 1) * LANES, :] = jnp.zeros((LANES - HD, D), jnp.bfloat16)
+    each_proj = proj_ref.shape[0]
+    for start in range(2 * each_proj, 2 * LANES, LANES):
+        proj[start : start + LANES - 2 * each_proj, :] = jnp.zeros((LANES - 2 * each_proj, D), jnp.bfloat16)
     hear_all(sizes)
+
+    def proj_rows(slot):
+        start = slot // 2 * LANES + lax.rem(slot, 2) * each_proj
+        return proj.at[pl.ds(pl.multiple_of(start, 16), each_proj)]
 
     def head_rows(slot):
         return wide.at[pl.ds(pl.multiple_of(slot * LANES, LANES), HD)]
@@ -497,8 +596,8 @@
     def _():
         pltpu.make_async_copy(w_ref, head_rows(kv_slot), w_recv.at[kv_slot]).start()
 
-    line = LineGather(ctx, x_ref, x_all, line_send, line_recv, line_local)
-    line.start()
+    x_line = LineGather(ctx, x_ref, x_all, line_send, line_recv, line_local)
+    x_line.start()
 
     @pl.when(d == 0)
     def _():
@@ -529,7 +628,7 @@
     def push_part(part):
         first_row = part * part_rows
         src = gate_up_ref.at[first_row : first_row + part_rows]
-        dst = gate_up_all.at[gu_slot, first_row : first_row + part_rows]
+        dst = gate_up.at[gu_slot, first_row : first_row + part_rows]
         for to in range(fs):
             own_place = jnp.logical_and(gu_core == d, f == to)
 
@@ -553,22 +652,19 @@
     gain = gain_vec[0:1, :]
 
     for k in range(1, ctx - 1):
-        line.forward(k)
+        x_line.forward(k)
     to_core, to_ctx = lax.rem(c, 2), 2 * d + c // 2
     stays = jnp.logical_and(to_core == d, to_ctx == c)
-    moved = ((proj_ref, proj_all),)
-    for index, (shard, whole) in enumerate(moved):
-
-        @pl.when(jnp.logical_not(stays))
-        def _():
-            remote(shard, whole.at[f], m_send.at[index], m_recv.at[index, f], at_device(to_core, to_ctx, f)).start()
-
-        @pl.when(stays)
-        def _():
-            pltpu.make_async_copy(shard, whole.at[f], m_recv.at[index, f]).start()
-
-
-    dy_line = LineGather(ctx, dy_ref, dy_all, dy_send, dy_recv, dy_local, short=True)
+
+    @pl.when(jnp.logical_not(stays))
+    def _():
+        remote(proj_ref, proj_rows(f), m_send, m_recv.at[f], at_device(to_core, to_ctx, f)).start()
+
+    @pl.when(stays)
+    def _():
+        pltpu.make_async_copy(proj_ref, proj_rows(f), m_recv.at[f]).start()
+
+    dy_line = LineGather(ctx, dy_ref, dy_all, dy_send, dy_recv, dy_local)
     dy_line.start()
     for slot in range(4):
         if slot < 2:
@@ -579,14 +675,13 @@
             def _():
                 arrived(head_rows(slot), w_recv.at[slot], here)
 
-    for part in range(gu_send.shape[0]):
-        push_part(part)
-    pltpu.make_async_copy(line.own, line.slot(c), line.local).wait()
+    push_part(0)
+    pltpu.make_async_copy(x_line.own, x_line.slot(c), x_line.local).wait()
 
     def block(step, carry):
         at = ordered(c, step, ctx)
 
-        line.other(at)
+        x_line.other(at)
         values = x_all[:, at].reshape(dp * 2 * span, D).astype(jnp.float32)
         scale = lax.rsqrt(jnp.mean(values * values, axis=-1, keepdims=True) + EPS)
         low = (values * scale * gain).astype(jnp.bfloat16)
@@ -607,62 +702,61 @@
 
             @pl.when(to != f)
             def _():
-                remote(stage.at[at, to], unit.at[at, f], u_send.at[at, to], u_recv.at[at, f], at_device(d, c, to)).start()
+                remote(stage.at[at, to], qkv_unit.at[at, f], q_send.at[at, to], q_recv.at[at, f], at_device(d, c, to)).start()
 
             @pl.when(to == f)
             def _():
-                unit[at, f] = stage[at, to]
+                qkv_unit[at, f] = stage[at, to]
 
         return carry
 
     def near(step, carry):
         @pl.when(step == ctx - 1)
         def _():
-            line.forward(ctx - 1)
+            x_line.forward(ctx - 1)
 
         return block(step, carry)
 
     lax.fori_loop(0, ctx, near, 0)
-    normed_copy = pltpu.make_async_copy(normed, normed_out, out_sem.at[0])
-    wide_copy = pltpu.make_async_copy(wide, wide_out, out_sem.at[1])
-    gains_copy = pltpu.make_async_copy(gain_vec, gains_out, out_sem.at[2])
+    normed_copy = pltpu.make_async_copy(normed, normed_out, out_sem.at[3])
+    wide_copy = pltpu.make_async_copy(wide, wide_out, out_sem.at[4])
+    gains_copy = pltpu.make_async_copy(gain_vec, gains_out, out_sem.at[5])
     normed_copy.start()
     wide_copy.start()
     gains_copy.start()
 
     @pl.when(jnp.logical_not(stays))
     def _():
-        remote(down_ref, down_out, down_send, down_recv, at_device(to_core, to_ctx, f)).start()
+        remote(down_ref, down_mid, down_send, down_recv, at_device(to_core, to_ctx, f)).start()
 
     @pl.when(stays)
     def _():
-        pltpu.make_async_copy(down_ref, down_out, down_recv).start()
-
-    for index, (shard, whole) in enumerate(moved):
-        arrived(whole.at[f], m_recv.at[index, f], here)
-        for step in range(1, fs):
-            to = lax.rem(f + step, fs)
-            remote(whole.at[f], whole.at[f], m_pass.at[index, step], m_recv.at[index, f], at_device(d, c, to)).start()
+        pltpu.make_async_copy(down_ref, down_mid, down_recv).start()
+
+    arrived(proj_rows(f), m_recv.at[f], here)
+    for step in range(1, fs):
+        to = lax.rem(f + step, fs)
+        remote(proj_rows(f), proj_rows(f), m_pass.at[step], m_recv.at[f], at_device(d, c, to)).start()
 
     dy_line.forward(1)
 
     for at in range(ctx):
         for step in range(1, fs):
             other = lax.rem(f + step, fs)
-            arrived(unit.at[at, other], u_recv.at[at, other], here)
-    unit_copy = pltpu.make_async_copy(unit, unit_out, out_sem.at[3])
-    unit_copy.start()
-
-    rows = fs * span
-    for at in range(ctx):
-        keys = rows * (at + 1)
-        k_rows = unit[0 : at + 1, :, :, 2 * LANES : 3 * LANES].reshape(keys, LANES)
-        v_rows = unit[0 : at + 1, :, :, 3 * LANES : 4 * LANES].reshape(keys, LANES)
-        allowed = lax.broadcasted_iota(jnp.int32, (rows, keys), 1) <= rows * at + lax.broadcasted_iota(
-            jnp.int32, (rows, keys), 0
+            arrived(qkv_unit.at[at, other], q_recv.at[at, other], here)
+    qkv_copy = pltpu.make_async_copy(qkv_unit, qkv_out, out_sem.at[0])
+    qkv_copy.start()
+
+    block_rows = fs * span
+    for at in (0, ctx - 1, *range(1, ctx - 1)):
+        keys = block_rows * (at + 1)
+        k_rows = qkv_unit[0 : at + 1, :, :, 2 * LANES : 3 * LANES].reshape(keys, LANES)
+        v_rows = qkv_unit[0 : at + 1, :, :, 3 * LANES : 4 * LANES].reshape(keys, LANES)
+        allowed = lax.broadcasted_iota(jnp.int32, (block_rows, keys), 1) <= block_rows * at + lax.broadcasted_iota(
+            jnp.int32, (block_rows, keys), 0
         )
         for head in range(2):
-            q_rows = unit[at, :, :, head * LANES : (head + 1) * LANES].reshape(rows, LANES)
+            q_rows = qkv_unit[at, :, :, head * LANES : (head + 1) * LANES].reshape(block_rows, LANES)
             scores = outer(q_rows, k_rows) * FACTOR
             scores = jnp.where(allowed, scores, NEG)
             best = jnp.max(scores, axis=-1, keepdims=True)
@@ -682,377 +776,60 @@
             def _():
                 att[f // 2, at, lax.rem(f, 2)] = att_stage[at, to]
 
-        if at == ctx - 1:
-            dy_line.forward(2)
-
-    for at in range(ctx):
-        for step in range(1, fs):
-            other = lax.rem(f + step, fs)
-            arrived(att.at[other // 2, at, lax.rem(other, 2)], a_recv.at[other, at], here)
-    att_copy = pltpu.make_async_copy(att, att_out, out_sem.at[4])
-    att_copy.start()
-
-    for at in range(ctx):
-        dy_line.other(at)
-    dy_line.finish()
-    for index, (shard, whole) in enumerate(moved):
-        for step in range(1, fs):
-            other = lax.rem(f + step, fs)
-            arrived(whole.at[other], m_recv.at[index, other], here)
-            left(whole.at[f], m_pass.at[index, step], here)
-
-        @pl.when(jnp.logical_not(stays))
-        def _():
-            left(shard, m_send.at[index], here)
-
-    arrived(down_out, down_recv, here)
-
-    @pl.when(jnp.logical_not(stays))
+
+    ends = jnp.logical_or(c == 0, c == ctx - 1)
+
+    @pl.when(jnp.logical_not(ends))
     def _():
-        left(down_ref, down_send, here)
-
-    for part in range(gu_send.shape[0]):
-        src = gate_up_ref.at[part * part_rows : (part + 1) * part_rows]
-        for slot in range(4):
-            arrived(gate_up_all.at[slot, part * part_rows : (part + 1) * part_rows], gu_recv.at[part, slot], here)
-        for to in range(fs):
-
-            @pl.when(jnp.logical_not(jnp.logical_and(gu_core == d, f == to)))
-            def _():
-                left(src, gu_send.at[part, to], here)
-
-    line.finish_sends()
-    for at in range(ctx):
-
-        for to in range(fs):
-
-            @pl.when(to != f)
-            def _():
-                left(stage.at[at, to], u_send.at[at, to], here)
-                left(att_stage.at[at, to], a_send.at[at, to], here)
-
-    @pl.when(jnp.logical_and(d == 1, kv_away))
-    def _():
-        left(w_ref, w_send.at[0], here)
-
-    @pl.when(d == 0)
-    def _():
-        for to in range(fs):
-
-            @pl.when(jnp.logical_or(q_core != 0, to != f))
-            def _():
-                left(w_ref, w_send.at[to], here)
-
-    for slot in (2, 3):
-
-        @pl.when(relay_of[slot])
-        def _():
-            for step in range(1, fs):
-                left(head_rows(slot), w_pass.at[slot - 2, step], here)
-
-    def gain_left(step, carry):
-        other = lax.rem(me + step, n)
-        left(gains_ref, g_send.at[other], here)
-        return carry
-
-    lax.fori_loop(1, n, gain_left, 0)
-    for copy in (normed_copy, wide_copy, gains_copy, unit_copy, att_copy):
-        copy.wait()
-
-
-def first(sizes, parts, sent, x, gains, w_qkv, blocks, steps, dy, w_out, w_down, w_gate_up):
-    dp, ctx, fs = sizes
-    n = dp * ctx * fs
-    rows = x.shape[0]
-    span = rows // 2
-    low, wide_t = jnp.bfloat16, jnp.float32
-    dma = pltpu.SemaphoreType.DMA
-    shapes = (
-        jax.ShapeDtypeStruct((dp, ctx, rows, D), low),
-        jax.ShapeDtypeStruct((ctx, fs, span, 4 * LANES), low),
-        jax.ShapeDtypeStruct((dp, ctx, 2, span, 2 * LANES), low),
-        jax.ShapeDtypeStruct((4 * LANES, D), low),
-        jax.ShapeDtypeStruct((8, D), wide_t),
-        jax.ShapeDtypeStruct((dp, ctx, rows, D), low),
-        jax.ShapeDtypeStruct((fs,) + w_out.shape, low),
-        jax.ShapeDtypeStruct(w_down.shape, low),
-        jax.ShapeDtypeStruct((4, D // parts * sent, w_gate_up.shape[1]), low),
-    )
-    any_spec, vm_spec = pl.BlockSpec(memory_space=ANY), pl.BlockSpec(memory_space=VM)
-    return pl.pallas_call(
-        functools.partial(first_kernel, sizes, parts),
-        name="first",
-        out_shape=shapes,
-        in_specs=[vm_spec] * 9,
-        out_specs=[any_spec] * 9,
-        scratch_shapes=[
-            VM((dp, ctx, rows, D), low),
-            VM((4 * LANES, D), low),
-            VM((dp, ctx, rows, D), low),
-            VM((ctx, 2 * dp, span, 4 * LANES), low),
-            VM((ctx, fs, span, 4 * LANES), low),
-            VM((ctx, fs, span, 2 * LANES), low),
-            VM((dp, ctx, 2, span, 2 * LANES), low),
-            VM((n, 8, LANES), wide_t),
-            VM((8, D), wide_t),
-            dma((3, ctx, HALVES)), dma((dp, ctx, HALVES)), dma,
-            dma((fs,)), dma((4,)), dma((2, fs)),
-            dma((n,)), dma((n,)),
-            dma((ctx, 2 * dp)), dma((ctx, fs)),
-            dma((ctx, fs)), dma((fs, ctx)),
-            dma((5,)),
-            dma((3, ctx, HALVES)), dma((dp, ctx, HALVES)), dma,
-            dma((1,)), dma((1, fs)), dma((1, fs)), dma, dma,
-            dma((sent, fs)), dma((sent, 4)),
-        ],
-        compiler_params=pltpu.CompilerParams(collective_id=1, has_side_effects=True, vmem_limit_bytes=60 * 1024 * 1024),
-    )(x, gains, w_qkv, blocks, steps, dy, w_out, w_down, w_gate_up)
-
-
-def angle_tables(count, span):
-    lane = jnp.arange(LANES, dtype=jnp.int32)
-    frequency = THETA ** (-((lane % (HD // 2)).astype(jnp.float32) * 2.0) / HD)
-
-    def both(positions):
-        angles = positions.astype(jnp.float32)[:, None] * frequency
-        return jnp.stack([jnp.cos(angles), jnp.sin(angles)])
-
-    return both(jnp.arange(count, dtype=jnp.int32) * span), both(jnp.arange(span, dtype=jnp.int32))
-
-
-def turns(block_ref, step_ref, block):
-    cos_b, sin_b = block_ref[0, pl.ds(block, 1)], block_ref[1, pl.ds(block, 1)]
-    cos_s, sin_s = step_ref[0], step_ref[1]
-    cosine = cos_b * cos_s - sin_b * sin_s
-    sine = sin_b * cos_s + cos_b * sin_s
-    lane = lax.broadcasted_iota(jnp.int32, sine.shape, 1)
-    first_half = lane < HD // 2
-    sine_up = jnp.where(jnp.logical_and(lane >= HD // 2, lane < HD), sine, 0.0)
-    return cosine, sine_up, jnp.where(first_half, -sine, 0.0)
-
-
-class LineSum:
-    def __init__(self, n, mine, out_core, in_core, out_line, in_line, total, sems):
-        self.n, self.mine, self.out_core, self.in_core = n, mine, out_core, in_core
-        self.out_line, self.in_line, self.total = out_line, in_line, total
-        self.core_send, self.core_recv, self.line_send, self.line_recv = sems
-        self.d, self.c, self.f = place()
-        self.here = at_device(self.d, self.c, self.f)
-
-    def give(self, at, both):
-        self.keep(at, both)
-        self.hand(at)
-
-    def keep(self, at, both):
-        d = self.d
-        low = both.astype(jnp.bfloat16)
-
-        @pl.when(d == 0)
-        def _():
-            self.mine[at] = low[0]
-            self.out_core[at] = low[1]
-
-        @pl.when(d != 0)
-        def _():
-            self.mine[at] = low[1]
-            self.out_core[at] = low[0]
-
-    def hand(self, at):
-        remote(
-            self.out_core.at[at], self.in_core.at[at], self.core_send.at[at], self.core_recv.at[at], at_device(1 - self.d, self.c, self.f)
-        ).start()
-
-    def step(self, at):
-        n, d, c, f = self.n, self.d, self.c, self.f
-        arrived(self.in_core.at[at], self.core_recv.at[at], self.here)
-        rows = self.total.shape[0] // HALVES
-        for part in range(HALVES):
-            own = slice(part * rows, (part + 1) * rows)
-            self.total[own] = self.mine[at, own].astype(jnp.float32) + self.in_core[at, own].astype(jnp.float32)
-            for way, comes in enumerate((jnp.logical_and(at <= c, c < n - 1), jnp.logical_and(at >= c, c > 0))):
-
-                @pl.when(comes)
-                def _():
-                    arrived(self.in_line.at[way, at, own], self.line_recv.at[way, at, part], self.here)
-                    self.total[own] += self.in_line[way, at, own].astype(jnp.float32)
-
-            @pl.when(at != c)
-            def _():
-                self.out_line[at, own] = self.total[own].astype(jnp.bfloat16)
-
-            for way, (goes, to) in enumerate(((at < c, c - 1), (at > c, c + 1))):
-
-                @pl.when(goes)
-                def _():
-                    remote(
-                        self.out_line.at[at, own], self.in_line.at[way, at, own],
-                        self.line_send.at[at, part], self.line_recv.at[way, at, part], at_device(d, to, f),
-                    ).start()
-
-    def finish(self):
-        rows = self.total.shape[0] // HALVES
-        for at in range(self.n):
-            left(self.out_core.at[at], self.core_send.at[at], self.here)
-
-            @pl.when(at != self.c)
-            def _():
-                for part in range(HALVES):
-                    left(self.out_line.at[at, part * rows : (part + 1) * rows], self.line_send.at[at, part], self.here)
-
-    @staticmethod
-    def scratch(ctx, rows):
-        low = jnp.bfloat16
-        dma = pltpu.SemaphoreType.DMA
-        return [
-            VM((ctx, rows, D), low), VM((ctx, rows, D), low), VM((ctx, rows, D), low), VM((ctx, rows, D), low),
-            VM((2, ctx, rows, D), low), VM((rows, D), jnp.float32),
-            dma((ctx,)), dma((ctx,)), dma((ctx, HALVES)), dma((2, ctx, HALVES)),
-        ]
-
-
-def down_route(d, c):
-    return (lax.rem(c, 2), 2 * d + c // 2), (c // 2, 2 * lax.rem(c, 2) + d)
-
-
-def near_devices(sizes):
-    dp, ctx, fs = sizes
-    d, c, f = place()
-    yes = c >= 0
-    found = [(at_device(1 - d, c, f), yes)]
+        dy_line.forward(2)
+
     for step in range(1, fs):
-        for core in range(dp):
-            found.append((at_device(core, c, lax.rem(f + step, fs)), yes))
-    found.append((at_device(d, c - 1, f), c > 0))
-    found.append((at_device(d, c + 1, f), c < ctx - 1))
-    return found
-
-
-def tell_near(sizes):
-    barrier = pltpu.get_barrier_semaphore()
-    for device, counts in near_devices(sizes):
-
-        @pl.when(counts)
-        def _():
-            pl.semaphore_signal(barrier, inc=1, device_id=device, device_id_type=MESH)
-
-
-def hear_near(sizes):
-    peers = sum(jnp.where(counts, 1, 0) for _, counts in near_devices(sizes))
-    pl.semaphore_wait(pltpu.get_barrier_semaphore(), peers)
-
-
-def middle_kernel(
-    sizes, hidden, parts, sent, att_ref, x_ref, dy_ref, gains_ref, proj_ref, down_ref, gate_up_ref, gate_up_part_ref, dy_all_ref,
-    out_ref, d_resid_out, gain_out, unit_out, grad_proj_out, up_land, down_land,
-    att, dy_all, proj, down, gate_up, resid, own_two, normed_two, act, d_both, own_d, d_resid_all, d_stage, unit,
-    grad_up, grad_down, grad_proj, grad_proj_low,
-    in_sem, dy_sem, gu_send, gu_recv, m_recv, m_pass, two_send, two_recv, two_local, dr_send, dr_recv, dr_local, u_send, u_recv,
-    late_send, late_recv, late_pass, out_sem, gup_send, gup_recv, gdn_send, gdn_recv,
-    *sums,
-):
-    dp, ctx, fs = sizes
-    d, c, f = place()
-    here = at_device(d, c, f)
+        other = lax.rem(f + step, fs)
+        arrived(proj_rows(other), m_recv.at[other], here)
     rows = x_ref.shape[0]
-    span = rows // 2
     both_rows = dp * rows
     half = hidden // 2
     line_sum = LineSum(ctx, *sums[:6], sums[6:10])
     second_sum = LineSum(ctx, *sums[10:16], sums[16:20])
-    out_sum = LineSum(ctx, *sums[20:26], sums[26:30])
-    part_rows = D // parts
-    tell_near(sizes)
-
-    att_copy = pltpu.make_async_copy(att_ref, att, in_sem.at[0])
-    part_copy = pltpu.make_async_copy(gate_up_part_ref, gate_up.at[:, 0 : part_rows * sent], in_sem.at[2])
-    att_copy.start()
-    proj[...] = jnp.zeros_like(proj)
-    each = proj_ref.shape[1]
-    proj_copies = []
-    for slot in range(fs):
-        start = slot // 2 * LANES + slot % 2 * each
-        proj_copies.append(pltpu.make_async_copy(proj_ref.at[slot], proj.at[start : start + each], in_sem.at[3 + slot]))
-        proj_copies[-1].start()
-
-    def dy_load(at):
-        return pltpu.make_async_copy(dy_all_ref.at[:, at], dy_all.at[:, at], dy_sem.at[at])
-
-    for at in range(ctx):
-
-        @pl.when(near_or_inner(c, at, ctx))
-        def _():
-            dy_load(at).start()
-
-    part_copy.start()
-    att_copy.wait()
-    for copy in proj_copies:
-        copy.wait()
+    out_sum = line_sum
 
     def project(step, carry):
         at = towards(c, step, ctx)
+        for move in range(1, fs):
+            other = lax.rem(f + move, fs)
+            arrived(att.at[other // 2, at, lax.rem(other, 2)], a_recv.at[other, at], here)
         terms = jnp.dot(att[:, at].reshape(both_rows, 2 * LANES), proj[...], preferred_element_type=jnp.float32)
-        line_sum.keep(at, terms.reshape(dp, rows, D))
+        line_sum.give(at, terms.reshape(dp, rows, D))
+
+        @pl.when(jnp.logical_and(ends, step > 0))
+        def _():
+            line_sum.step(towards(c, step - 1, ctx))
+
         return carry
 
     lax.fori_loop(0, ctx, project, 0)
-    hear_near(sizes)
-
-    ends = jnp.logical_or(c == 0, c == ctx - 1)
-    last_hops = ((c == 1, -1), (c == ctx - 2, 1))
-
-    def late(way, at, part):
-        src, dst = part_of(dy_all_ref.at[d, at], part), part_of(dy_all.at[d, at], part)
-        return remote(src, dst, late_send.at[at, part], late_recv.at[d, at, part], at_device(d, c + way, f))
-
-    for sends, way in last_hops:
-        for step in range(1, ctx - 1):
-
-            @pl.when(sends)
-            def _():
-                for part in range(HALVES):
-                    late(way, c - way * step, part).start()
-
-    def late_across(at, part):
-        block = part_of(dy_all.at[d, at], part)
-        return remote(block, block, late_pass.at[at, part], late_recv.at[d, at, part], at_device(1 - d, c, f))
-
-    def far(step):
-        return jnp.where(c == 0, 1 + step, ctx - 2 - step)
-
-    pltpu.make_async_copy(down_ref, down.at[f], m_recv.at[f]).start()
+
+    arrived(down_mid, down_recv, here)
+    pltpu.make_async_copy(down_mid, down.at[f], d_recv.at[f]).start()
     for step in range(1, fs):
         to = lax.rem(f + step, fs)
-        remote(down_ref, down.at[f], m_pass.at[step], m_recv.at[f], at_device(d, c, to)).start()
-    for step in range(ctx):
-        line_sum.hand(towards(c, step, ctx))
-
-    gu_core = f // 2
-    gu_slot = 2 * d + lax.rem(f, 2)
-    rest = slice(part_rows * sent, D)
-    for to in range(fs):
-        own_place = jnp.logical_and(gu_core == d, f == to)
-
-        @pl.when(jnp.logical_not(own_place))
-        def _():
-            remote(gate_up_ref.at[rest], gate_up.at[gu_slot, rest], gu_send.at[to], gu_recv.at[gu_slot], at_device(gu_core, c, to)).start()
-
-        @pl.when(own_place)
-        def _():
-            pltpu.make_async_copy(gate_up_ref.at[rest], gate_up.at[gu_slot, rest], gu_recv.at[gu_slot]).start()
-
-    line_sum.step(towards(c, 0, ctx))
-    line_sum.step(towards(c, 1, ctx))
-    line_sum.step(towards(c, 2, ctx))
+        remote(down_mid, down.at[f], d_pass.at[step], d_recv.at[f], at_device(d, c, to)).start()
+    for part in range(1, parts):
+        push_part(part)
+
+    def sum_step(step, carry):
+        line_sum.step(towards(c, step, ctx))
+        return carry
+
+    lax.fori_loop(jnp.where(ends, ctx - 1, 0), ctx - 1, sum_step, 0)
 
     @pl.when(ends)
     def _():
-        for step in range(1, ctx - 1):
-            for part in range(HALVES):
-                arrived(part_of(dy_all.at[d, far(step)], part), late_recv.at[d, far(step), part], here)
-                late_across(far(step), part).start()
+        for k in range(2, ctx):
+            dy_line.forward(k)
 
     line_sum.step(c)
-    gain = gains_ref[1:2, :]
+    gain = gain_vec[1:2, :]
     values = x_ref[...].astype(jnp.float32) + line_sum.total[...]
     resid[...] = values
     scale = lax.rsqrt(jnp.mean(values * values, axis=-1, keepdims=True) + EPS)
@@ -1060,22 +837,68 @@
     line = LineGather(ctx, own_two, normed_two, two_send, two_recv, two_local)
     line.start()
     line.forward(1)
-    for slot in range(4):
-        arrived(gate_up.at[slot, rest], gu_recv.at[slot], here)
+    line_sum.finish()
+    x_line.finish_sends()
+    for part in range(parts):
+        for slot in range(4):
+            arrived(gate_up.at[slot, part * part_rows : (part + 1) * part_rows], gu_recv.at[part, slot], here)
+    for slot in range(fs):
+        arrived(down.at[slot], d_recv.at[slot], here)
+    pltpu.make_async_copy(dy_line.own, dy_line.slot(c), dy_line.local).wait()
+    for part in range(parts):
+        src = gate_up_ref.at[part * part_rows : (part + 1) * part_rows]
+        for to in range(fs):
+
+            @pl.when(jnp.logical_not(jnp.logical_and(gu_core == d, f == to)))
+            def _():
+                left(src, gu_send.at[part, to], here)
+
     for at in range(ctx):
 
-        @pl.when(near_or_inner(c, at, ctx))
-        def _():
-            dy_load(at).wait()
-
-    @pl.when(ends)
+        for to in range(fs):
+
+            @pl.when(to != f)
+            def _():
+                left(stage.at[at, to], q_send.at[at, to], here)
+                left(att_stage.at[at, to], a_send.at[at, to], here)
+
+    @pl.when(jnp.logical_and(d == 1, kv_away))
     def _():
-        for step in range(1, ctx - 1):
-            for part in range(HALVES):
-                arrived(part_of(dy_all.at[1 - d, far(step)], part), late_recv.at[1 - d, far(step), part], here)
-    part_copy.wait()
-    for slot in range(fs):
-        arrived(down.at[slot], m_recv.at[slot], here)
+        left(w_ref, w_send.at[0], here)
+
+    @pl.when(d == 0)
+    def _():
+        for to in range(fs):
+
+            @pl.when(jnp.logical_or(q_core != 0, to != f))
+            def _():
+                left(w_ref, w_send.at[to], here)
+
+    for slot in (2, 3):
+
+        @pl.when(relay_of[slot])
+        def _():
+            for step in range(1, fs):
+                left(head_rows(slot), w_pass.at[slot - 2, step], here)
+
+    def gain_left(step, carry):
+        other = lax.rem(me + step, n)
+        left(gains_ref, g_send.at[other], here)
+        return carry
+
+    lax.fori_loop(1, n, gain_left, 0)
+    for copy in (normed_copy, wide_copy, gains_copy, qkv_copy):
+        copy.wait()
+    for step in range(1, fs):
+        left(down_mid, d_pass.at[step], here)
+        left(proj_rows(f), m_pass.at[step], here)
+
+    @pl.when(jnp.logical_not(stays))
+    def _():
+        left(proj_ref, m_send, here)
+        left(down_ref, down_send, here)
+
+    dy_line.finish_sends()
     pltpu.make_async_copy(line.own, line.slot(c), line.local).wait()
 
     def mlp(step, carry):
@@ -1087,6 +910,7 @@
             line.forward(2 + step // 2)
 
         line.other(at)
+        dy_line.other(at)
         inputs = normed_two[:, at].reshape(both_rows, D)
         dy_rows = dy_all[:, at].reshape(both_rows, D)
         for part in range(2):
@@ -1185,6 +1009,8 @@
     def _():
         lax.fori_loop(0, ctx - 1, out_step, 0)
 
+    line.finish_sends()
+    second_sum.finish()
     pltpu.make_async_copy(d_line.own, d_line.slot(c), d_line.local).wait()
     grad_proj[...] = jnp.zeros_like(grad_proj)
 
@@ -1220,12 +1046,9 @@
     def _():
         lax.fori_loop(1, ctx - 1, out_step, 0)
 
-    line_sum.finish()
-    line.finish_sends()
-    second_sum.finish()
     for slot in range(fs):
-        start = slot // 2 * LANES + slot % 2 * each
-        grad_proj_low[slot] = grad_proj[start : start + each, :].astype(jnp.bfloat16)
+        start = slot // 2 * LANES + slot % 2 * each_proj
+        grad_proj_low[slot] = grad_proj[start : start + each_proj, :].astype(jnp.bfloat16)
     grad_proj_copy = pltpu.make_async_copy(grad_proj_low, grad_proj_out, out_sem.at[1])
     grad_proj_copy.start()
     for at in range(ctx):
@@ -1234,38 +1057,13 @@
             arrived(unit.at[at, other], u_recv.at[at, other], here)
     unit_copy = pltpu.make_async_copy(unit, unit_out, out_sem.at[2])
     unit_copy.start()
-    out_step(ctx - 1, 0)
-    out_ref[...] = (resid[...] + out_sum.total[...]).astype(jnp.bfloat16)
     d_line.finish_sends()
-    out_sum.finish()
     for at in range(ctx):
         for to in range(fs):
 
             @pl.when(to != f)
             def _():
                 left(d_stage.at[at, to], u_send.at[at, to], here)
-
-    for to in range(fs):
-
-        @pl.when(jnp.logical_not(jnp.logical_and(gu_core == d, f == to)))
-        def _():
-            left(gate_up_ref.at[rest], gu_send.at[to], here)
-
-    for step in range(1, fs):
-        left(down_ref, m_pass.at[step], here)
-    for sends, way in last_hops:
-        for step in range(1, ctx - 1):
-
-            @pl.when(sends)
-            def _():
-                for part in range(HALVES):
-                    left(part_of(dy_all_ref.at[d, c - way * step], part), late_send.at[c - way * step, part], here)
-
-    @pl.when(ends)
-    def _():
-        for step in range(1, ctx - 1):
-            for part in range(HALVES):
-                left(part_of(dy_all.at[d, far(step)], part), late_pass.at[far(step), part], here)
 
     def settle_up(step, carry):
         first = pl.multiple_of(step * wide_rows, LANES)
@@ -1291,37 +1089,56 @@
 
     lax.fori_loop(0, ctx, settle_up, 0)
     lax.fori_loop(0, ctx, settle_down, 0)
+    out_step(ctx - 1, 0)
+    out_ref[...] = (resid[...] + out_sum.total[...]).astype(jnp.bfloat16)
+    out_sum.finish()
     for copy in (grad_proj_copy, unit_copy):
         copy.wait()
 
-
-def middle(sizes, parts, sent, att, x, dy, gains, proj, w_down, w_gate_up, gate_up_part, dy_all):
+def front(sizes, parts, x, attn_gain, mlp_gain, w_qkv, dy, w_out, w_down, w_gate_up):
     dp, ctx, fs = sizes
+    n = dp * ctx * fs
     rows = x.shape[0]
     span = rows // 2
     hidden = FF // (dp * ctx)
     low, wide_t = jnp.bfloat16, jnp.float32
     dma = pltpu.SemaphoreType.DMA
     any_spec, vm_spec = pl.BlockSpec(memory_space=ANY), pl.BlockSpec(memory_space=VM)
+    line_sems = [dma((3, ctx, HALVES)), dma((dp, ctx, HALVES)), dma]
     shapes = (
         jax.ShapeDtypeStruct((rows, D), low),
         jax.ShapeDtypeStruct((rows, D), wide_t),
         jax.ShapeDtypeStruct((8, D), wide_t),
+        jax.ShapeDtypeStruct((2, ctx * fs, LANES), wide_t),
+        jax.ShapeDtypeStruct((2, span, LANES), wide_t),
+        jax.ShapeDtypeStruct((dp, ctx, rows, D), low),
+        jax.ShapeDtypeStruct((ctx, fs, span, 4 * LANES), low),
+        jax.ShapeDtypeStruct((4 * LANES, D), low),
+        jax.ShapeDtypeStruct((8, D), wide_t),
         jax.ShapeDtypeStruct((ctx, fs, span, 2 * LANES), low),
-        jax.ShapeDtypeStruct(proj.shape, low),
+        jax.ShapeDtypeStruct((fs,) + w_out.shape, low),
         jax.ShapeDtypeStruct((fs, D, hidden // 2), low),
         jax.ShapeDtypeStruct((fs, hidden // fs, D), low),
     )
     return pl.pallas_call(
-        functools.partial(middle_kernel, sizes, hidden, parts, sent),
-        name="middle",
+        functools.partial(front_kernel, sizes, hidden, parts),
+        name="front",
         out_shape=shapes,
-        in_specs=[any_spec, vm_spec, vm_spec, vm_spec, any_spec, vm_spec, vm_spec, any_spec, any_spec],
-        out_specs=[vm_spec] * 3 + [any_spec] * 4,
+        in_specs=[vm_spec] * 3 + [any_spec] + [vm_spec] * 4,
+        out_specs=[vm_spec] * 5 + [any_spec] * 8,
         scratch_shapes=[
-            VM((dp, ctx, rows, 2 * LANES), low),
+            VM((dp, ctx, rows, D), low),
+            VM((4 * LANES, D), low),
+            VM((dp, ctx, rows, D), low),
+            VM((ctx, 2 * dp, span, 4 * LANES), low),
+            VM((ctx, fs, span, 4 * LANES), low),
+            VM((ctx, fs, span, 2 * LANES), low),
+            VM((dp, ctx, 2, span, 2 * LANES), low),
+            VM((n, 8, LANES), wide_t),
+            VM((8, D), wide_t),
             VM((dp, ctx, rows, D), low),
             VM((2 * LANES, D), low),
+            VM(w_down.shape, low),
             VM((fs, hidden // fs, D), low),
             VM((4, D, hidden // 2), low),
             VM((rows, D), wide_t),
@@ -1330,22 +1147,48 @@
             VM((dp, ctx, rows, hidden), low),
             VM((dp, ctx, rows, 2 * hidden), low),
             VM((rows, D), low),
-            VM((dp, ctx, rows, D), low),
             VM((ctx, 2 * dp, span, 2 * LANES), low),
             VM((ctx, fs, span, 2 * LANES), low),
             VM((4, D, hidden // 2), low),
             VM((fs, hidden // fs, D), low),
             VM((2 * LANES, D), wide_t),
-            VM(proj.shape, low),
-            dma((3 + fs,)), dma((ctx,)), dma((fs,)), dma((4,)), dma((fs,)), dma((fs,)),
-            dma((3, ctx, HALVES)), dma((dp, ctx, HALVES)), dma,
-            dma((3, ctx, HALVES)), dma((dp, ctx, HALVES)), dma,
+            VM((fs,) + w_out.shape, low),
+            VM((8, LANES), wide_t),
+            *line_sems,
+            dma((fs,)), dma((4,)), dma((2, fs)), dma((n,)), dma((n,)),
+            dma((ctx, 2 * dp)), dma((ctx, fs)), dma((ctx, fs)), dma((fs, ctx)), dma((6,)),
+            *line_sems,
+            dma, dma((fs,)), dma((fs,)), dma, dma, dma((fs,)), dma((fs,)), dma((parts, fs)), dma((parts, 4)),
+            *line_sems,
+            *line_sems,
             dma((ctx, 2 * dp)), dma((ctx, fs)),
-            dma((ctx, HALVES)), dma((dp, ctx, HALVES)), dma((ctx, HALVES)), dma((3,)),
             dma((4, ctx)), dma((fs, ctx)), dma((fs, ctx)), dma((fs, ctx)),
-        ] + LineSum.scratch(ctx, rows) * 3,
-        compiler_params=pltpu.CompilerParams(collective_id=2, has_side_effects=True, vmem_limit_bytes=63 * 1024 * 1024),
-    )(att, x, dy, gains, proj, w_down, w_gate_up, gate_up_part, dy_all)
+        ] + LineSum.scratch(ctx, rows) * 2,
+        compiler_params=pltpu.CompilerParams(collective_id=1, has_side_effects=True, vmem_limit_bytes=67043328),
+    )(x, attn_gain, mlp_gain, w_qkv, dy, w_out, w_down, w_gate_up)
+
+
+def fill_tables(block_ref, step_ref):
+    span = step_ref.shape[1]
+    for ref, scale in ((block_ref, span), (step_ref, 1)):
+        shape = ref.shape[1:]
+        lane = lax.broadcasted_iota(jnp.int32, shape, 1)
+        pair = jnp.where(lane >= HD // 2, lane - HD // 2, lane).astype(jnp.float32)
+        frequency = jnp.exp(pair * (-2.0 * math.log(THETA) / HD))
+        angles = (lax.broadcasted_iota(jnp.int32, shape, 0) * scale).astype(jnp.float32) * frequency
+        ref[0] = jnp.cos(angles)
+        ref[1] = jnp.sin(angles)
+
+
+def turns(block_ref, step_ref, block):
+    cos_b, sin_b = block_ref[0, pl.ds(block, 1)], block_ref[1, pl.ds(block, 1)]
+    cos_s, sin_s = step_ref[0], step_ref[1]
+    cosine = cos_b * cos_s - sin_b * sin_s
+    sine = sin_b * cos_s + cos_b * sin_s
+    lane = lax.broadcasted_iota(jnp.int32, sine.shape, 1)
+    first_half = lane < HD // 2
+    sine_up = jnp.where(jnp.logical_and(lane >= HD // 2, lane < HD), sine, 0.0)
+    return cosine, sine_up, jnp.where(first_half, -sine, 0.0)
 
 
 def last_kernel(
@@ -1353,9 +1196,9 @@
     unit_ref, d_unit_ref, normed_ref, wide_ref, up_land_ref, down_land_ref,
     d_x_ref, gains_out, qkv_out, proj_out, up_out, down_out,
     unit, d_unit, d_k, d_v, stage, mixed, normed, wide, grad_heads,
-    up_land, down_land, proj_land, q_land, kv_land, down_sum, proj_sum, kv_sum, down_last, proj_last, kv_last, gain_vec, gain_stage, gain_land,
+    up_land, down_land, proj_land, q_land, kv_land, down_sum, proj_sum, kv_sum, down_last, proj_last, kv_last, gain_vec, gain_stage, gain_land, up_sum,
     in_sem, proj_send, proj_recv, head_send, head_recv, move_send, move_recv,
-    u_send, u_recv, g_send, g_recv,
+    u_send, u_recv, g_send, g_recv, up_sem,
     *sums,
 ):
     dp, ctx, fs = sizes
@@ -1557,7 +1400,46 @@
                 pltpu.make_async_copy(kv_sum.at[slot], kv_last, move_recv.at[2]).start()
 
     loads[5].wait()
-    up_out[...] = sum_of(up_land)
+    up_sum[...] = sum_of(up_land)
+    up_copy = pltpu.make_async_copy(up_sum, up_out, up_sem)
+    up_copy.start()
+    @pl.when(d == 0)
+    def _():
+        for source in range(fs):
+            arrived(q_land.at[source], head_recv.at[0, source], here)
+        qkv_out[...] = sum_of(q_land)
+
+    for slot in range(fs):
+        pushed(proj_ref.at[slot], proj_send.at[slot], d, slot)
+    for slot in range(2):
+        pushed(grad_heads.at[slot], head_send.at[slot], 0, 2 * d + slot)
+        pushed(grad_heads.at[2 + slot], head_send.at[2 + slot], d, relays[slot])
+
+    for at in range(ctx):
+        for to in range(fs):
+
+            @pl.when(to != f)
+            def _():
+                left(stage.at[at, to], u_send.at[at, to], here)
+
+    def gain_from(step, carry):
+        other = lax.rem(me + step, n)
+        arrived(gain_land.at[other], g_recv.at[other], here)
+        return carry
+
+    lax.fori_loop(1, n, gain_from, 0)
+    total = gain_land[0]
+    for index in range(1, n):
+        total += gain_land[index]
+    gains_out[...] = total
+
+    def gain_left(step, carry):
+        other = lax.rem(me + step, n)
+        left(gain_stage.at[other], g_send.at[other], here)
+        return carry
+
+    lax.fori_loop(1, n, gain_left, 0)
+
     in_sum.step(c)
 
     values = x_ref[...].astype(wide_t)
@@ -1567,12 +1449,6 @@
     mean = jnp.mean(weighted * values, axis=-1, keepdims=True)
     d_x_ref[...] = (d_resid_ref[...] + scale * weighted - values * (scale * scale * scale) * mean).astype(low)
 
-    @pl.when(d == 0)
-    def _():
-        for source in range(fs):
-            arrived(q_land.at[source], head_recv.at[0, source], here)
-        qkv_out[...] = sum_of(q_land)
-
     for index, dst in enumerate((down_last, proj_last)):
         arrived(dst, move_recv.at[index], here)
     down_out[...] = down_last[...].astype(wide_t)
@@ -1583,22 +1459,7 @@
         arrived(kv_last, move_recv.at[2], here)
         qkv_out[...] = kv_last[...].astype(wide_t)
 
-    def gain_from(step, carry):
-        other = lax.rem(me + step, n)
-        arrived(gain_land.at[other], g_recv.at[other], here)
-        return carry
-
-    lax.fori_loop(1, n, gain_from, 0)
-    total = gain_land[0]
-    for index in range(1, n):
-        total += gain_land[index]
-    gains_out[...] = total
-
-    for slot in range(fs):
-        pushed(proj_ref.at[slot], proj_send.at[slot], d, slot)
     for slot in range(2):
-        pushed(grad_heads.at[slot], head_send.at[slot], 0, 2 * d + slot)
-        pushed(grad_heads.at[2 + slot], head_send.at[2 + slot], d, relays[slot])
         away = kv_route(slot)[2]
 
         @pl.when(jnp.logical_and(f == relays[slot], away))
@@ -1609,21 +1470,8 @@
         def _():
             left((down_sum, proj_sum)[slot], move_send.at[slot], here)
 
-    for at in range(ctx):
-        for to in range(fs):
-
-            @pl.when(to != f)
-            def _():
-                left(stage.at[at, to], u_send.at[at, to], here)
-
     in_sum.finish()
-
-    def gain_left(step, carry):
-        other = lax.rem(me + step, n)
-        left(gain_stage.at[other], g_send.at[other], here)
-        return carry
-
-    lax.fori_loop(1, n, gain_left, 0)
+    up_copy.wait()
 
 
 def last(sizes, x, gains, tables, d_resid, gain_two, grad_proj, unit, d_unit, normed, wide, up_land, down_land):
@@ -1648,7 +1496,7 @@
         name="last",
         out_shape=shapes,
         in_specs=[vm_spec] * 7 + [any_spec] * 6,
-        out_specs=[vm_spec] * 6,
+        out_specs=[vm_spec] * 4 + [any_spec, vm_spec],
         scratch_shapes=[
             VM(unit.shape, low),
             VM(d_unit.shape, low),
@@ -1673,9 +1521,10 @@
             VM((8, D), wide_t),
             VM((n, 8, LANES), wide_t),
             VM((n, 8, LANES), wide_t),
+            VM((D, half), wide_t),
             dma((6,)), dma((fs,)), dma((fs,)),
             dma((4,)), dma((3, fs)), dma((4,)), dma((3,)),
-            dma((ctx, fs)), dma((fs, ctx)), dma((n,)), dma((n,)),
+            dma((ctx, fs)), dma((fs, ctx)), dma((n,)), dma((n,)), dma,
         ] + LineSum.scratch(ctx, rows),
         compiler_params=pltpu.CompilerParams(collective_id=3, has_side_effects=True, vmem_limit_bytes=63 * 1024 * 1024),
     )(x, gains, *tables, d_resid, gain_two, grad_proj, unit, d_unit, normed, wide, up_land, down_land)
@@ -1720,16 +1569,8 @@
     x = tokens.reshape(rows, D)
     dy = cotangent.reshape(rows, D)
     each = attn_gain.shape[0]
-    gain_rows = jnp.concatenate([attn_gain[None], mlp_gain[None]]).astype(jnp.float32)
-    gain_rows = jnp.pad(gain_rows, ((0, 6), (0, LANES - each)))
-    tables = angle_tables(ctx * fs, span)
-    parts, sent = 4, 1
-    normed, unit, att, qkv, gains, dy_all, proj, down, gate_up = first(
-        where, parts, sent, x, gain_rows, w_qkv.T, *tables, dy, w_out, w_down, w_gate_up
-    )
-    att = att.reshape(dp, ctx, rows, 2 * LANES)
-    block_out, d_resid, grad_two, d_unit, grad_proj, up_land, down_land = middle(
-        where, parts, sent, att, x, dy, gains, proj, down, w_gate_up, gate_up, dy_all
+    block_out, d_resid, grad_two, *tables, normed, unit, qkv, gains, d_unit, grad_proj, up_land, down_land = front(
+        where, 4, x, attn_gain, mlp_gain, w_qkv.T, dy, w_out, w_down, w_gate_up
     )
     grad_tokens, gain_grads, grad_qkv, grad_out, grad_gate_up, grad_down = last(
         where, x, gains, tables, d_resid, grad_two, grad_proj, unit, d_unit, normed, qkv, up_land, down_land

time: 267 us -> 260 us (0.974)
  Pallas kernels: 263 us -> 259 us
  other arithmetic: 2.85 us -> 0 us
    pallas_call x2 -> x1, Pallas kernels: 198 us -> 196 us  [front(): pl.pallas_call(functools.partial(front_kernel, sizes, hidden, parts), nam...]
where the time goes in v8:
time: 260 us
  Pallas kernels  259 us (100%)
    pallas_call x1, Pallas kernels, front(): pl.pallas_call(functools.partial(front_kernel, sizes, hidden, parts), nam...  196 us
    pallas_call x1, Pallas kernels, last(): pl.pallas_call(functools.partial(last_kernel, sizes), name='last', out_sh...  58.2 us

profile of v8, /device:TPU:13, one launch (start us, length us, event | category | flops | bytes accessed | tf_op | source)
XLA Modules:
  0.0 260.1 jit_solution(4746287053290652905)
XLA Ops:
  0.6 196.3 %front.1 = (bf16[128,1536]{1,0:T(8,128)(2,1)}, f32[128,1536]{1,0:T(8,128)}, f32[8,1536]{1,0:T(8,128)}, f32[2,16,128]{2,1,0:T(8,128)}, f32[2,64,128]{2,1,0:T(8,12...) custom-call(bf16[128,1536]{1,0:T(8,128)(2,1)} %bitcast.10, ...), custom_call_target="tpu_custom_call" | custom-call | tf_op jit(solution)/shard_map/front/pallas_call | solution.py:1123
  196.9 58.2 %last.1 = (bf16[128,1536]{1,0:T(8,128)(2,1)}, f32[8,128]{1,0:T(8,128)}, f32[96,1536]{1,0:T(8,128)}, f32[48,1536]{1,0:T(8,128)}, f32[1536,256]{1,0:T(8,128)}, /*index=5*/f32[128,1536]{1,0:T(8,128)}) custom-call(bf16[128,1536]{1,0:T(8,128)(2,1)} %bitcast.11, f32[8,1536]{1,0:T(8,128)} %get-tuple-element.35.gains_ref, ...), custom_call_target="tpu_custom_call" | custom-call | tf_op jit(solution)/shard_map/last/pallas_call | solution.py:1494
  255.2 4.8 %emit.1 = (bf16[128,1536]{1,0:T(8,128)(2,1)}, bf16[128,1536]{1,0:T(8,128)(2,1)}, f32[96,1536]{1,0:T(8,128)}, f32[48,1536]{1,0:T(8,128)}, f32[1536,256]{1,0:T(8,1...) custom-call(f32[8,128]{1,0:T(8,128)} %get-tuple-element.47.gains_ref, ...), custom_call_target="tpu_custom_call" | custom-call | tf_op jit(solution)/shard_map/emit/pallas_call | solution.py:1554

commit v9 on v8

--- a/solution.py
+++ b/solution.py
@@ -537,7 +537,7 @@
     out_ref, d_resid_out, gain_out, block_ref, step_ref, normed_out, qkv_out, wide_out, gains_out, unit_out, grad_proj_out, up_land, down_land,
     x_all, wide, normed, stage, qkv_unit, att_stage, att, gain_all, gain_vec,
     dy_all, proj, down_mid, down, gate_up, resid, own_two, normed_two, act, d_both, own_d, d_stage, unit,
-    grad_up, grad_down, grad_proj, grad_proj_low, gains_ref,
+    grad_up, grad_down, grad_proj, grad_proj_low, gains_ref, d_resid_held,
     line_send, line_recv, line_local, w_send, w_recv, w_pass, g_send, g_recv, q_send, q_recv, a_send, a_recv, out_sem,
     dy_send, dy_recv, dy_local, m_send, m_recv, m_pass, down_send, down_recv, d_recv, d_pass, gu_send, gu_recv,
     two_send, two_recv, two_local, dr_send, dr_recv, dr_local, u_send, u_recv, gup_send, gup_recv, gdn_send, gdn_recv,
@@ -738,7 +738,12 @@
         to = lax.rem(f + step, fs)
         remote(proj_rows(f), proj_rows(f), m_pass.at[step], m_recv.at[f], at_device(d, c, to)).start()
 
-    dy_line.forward(1)
+    ends = jnp.logical_or(c == 0, c == ctx - 1)
+
+    @pl.when(jnp.logical_not(ends))
+    def _():
+        dy_line.forward(1)
+
 
     for at in range(ctx):
         for step in range(1, fs):
@@ -825,7 +830,7 @@
 
     @pl.when(ends)
     def _():
-        for k in range(2, ctx):
+        for k in range(1, ctx):
             dy_line.forward(k)
 
     line_sum.step(c)
@@ -997,7 +1002,9 @@
     mean = jnp.mean(weighted * values, axis=-1, keepdims=True)
     d_resid = dy_ref[...].astype(jnp.float32) + scale * weighted - values * (scale * scale * scale) * mean
     own_d[...] = d_resid.astype(jnp.bfloat16)
-    d_resid_out[...] = d_resid
+    d_resid_held[...] = d_resid
+    d_resid_copy = pltpu.make_async_copy(d_resid_held, d_resid_out, out_sem.at[6])
+    d_resid_copy.start()
     gain_out[...] = jnp.broadcast_to(jnp.sum(incoming * values * scale, axis=0, keepdims=True), gain_out.shape)
     d_line = LineGather(ctx, own_d, d_resid_all, dr_send, dr_recv, dr_local)
     d_line.start()
@@ -1092,7 +1099,7 @@
     out_step(ctx - 1, 0)
     out_ref[...] = (resid[...] + out_sum.total[...]).astype(jnp.bfloat16)
     out_sum.finish()
-    for copy in (grad_proj_copy, unit_copy):
+    for copy in (d_resid_copy, grad_proj_copy, unit_copy):
         copy.wait()
 
 def front(sizes, parts, x, attn_gain, mlp_gain, w_qkv, dy, w_out, w_down, w_gate_up):
@@ -1125,7 +1132,7 @@
         name="front",
         out_shape=shapes,
         in_specs=[vm_spec] * 3 + [any_spec] + [vm_spec] * 4,
-        out_specs=[vm_spec] * 5 + [any_spec] * 8,
+        out_specs=[vm_spec, any_spec] + [vm_spec] * 3 + [any_spec] * 8,
         scratch_shapes=[
             VM((dp, ctx, rows, D), low),
             VM((4 * LANES, D), low),
@@ -1154,9 +1161,10 @@
             VM((2 * LANES, D), wide_t),
             VM((fs,) + w_out.shape, low),
             VM((8, LANES), wide_t),
+            VM((rows, D), wide_t),
             *line_sems,
             dma((fs,)), dma((4,)), dma((2, fs)), dma((n,)), dma((n,)),
-            dma((ctx, 2 * dp)), dma((ctx, fs)), dma((ctx, fs)), dma((fs, ctx)), dma((6,)),
+            dma((ctx, 2 * dp)), dma((ctx, fs)), dma((ctx, fs)), dma((fs, ctx)), dma((7,)),
             *line_sems,
             dma, dma((fs,)), dma((fs,)), dma, dma, dma((fs,)), dma((fs,)), dma((parts, fs)), dma((parts, 4)),
             *line_sems,
@@ -1192,13 +1200,13 @@
 
 
 def last_kernel(
-    sizes, x_ref, gains_ref, block_ref, step_ref, d_resid_ref, gain_two_ref, proj_ref,
-    unit_ref, d_unit_ref, normed_ref, wide_ref, up_land_ref, down_land_ref,
+    sizes, x_ref, gains_ref, block_ref, step_ref, gain_two_ref, proj_ref,
+    d_resid_in, unit_ref, d_unit_ref, normed_ref, wide_ref, up_land_ref, down_land_ref,
     d_x_ref, gains_out, qkv_out, proj_out, up_out, down_out,
-    unit, d_unit, d_k, d_v, stage, mixed, normed, wide, grad_heads,
-    up_land, down_land, proj_land, q_land, kv_land, down_sum, proj_sum, kv_sum, down_last, proj_last, kv_last, gain_vec, gain_stage, gain_land, up_sum,
+    unit, d_unit, d_k, d_v, stage, mixed, packed, normed, wide, grad_heads,
+    up_land, down_land, proj_land, q_land, kv_land, down_sum, proj_sum, kv_sum, down_last, proj_last, kv_last, gain_vec, gain_stage, gain_land, up_sum, d_resid_ref,
     in_sem, proj_send, proj_recv, head_send, head_recv, move_send, move_recv,
-    u_send, u_recv, g_send, g_recv, up_sem,
+    u_send, u_recv, g_send, g_recv, up_sem, wide_sem,
     *sums,
 ):
     dp, ctx, fs = sizes
@@ -1213,11 +1221,17 @@
     loads = [
         pltpu.make_async_copy(src, dst, in_sem.at[index])
         for index, (src, dst) in enumerate((
-            (unit_ref, unit), (d_unit_ref, d_unit), (normed_ref, normed), (wide_ref, wide), (down_land_ref, down_land), (up_land_ref, up_land),
+            (unit_ref, unit), (d_unit_ref, d_unit), (normed_ref, normed), (d_resid_in, d_resid_ref), (down_land_ref, down_land), (up_land_ref, up_land),
         ))
     ]
+    wide_loads = [
+        pltpu.make_async_copy(
+            wide_ref.at[slot * LANES : slot * LANES + HD], wide.at[slot * HD : (slot + 1) * HD], wide_sem.at[slot]
+        )
+        for slot in range(4)
+    ]
     tell_all(sizes)
-    for load in loads:
+    for load in loads + wide_loads:
         load.start()
     in_sum = LineSum(ctx, *sums[:6], sums[6:10])
     d_k[...] = jnp.zeros_like(d_k)
@@ -1269,7 +1283,7 @@
             own = slice(index * span, (index + 1) * span)
             cosine, sine_up, sine_down = turns(block_ref, step_ref, at * fs + index)
             pieces.append(values[own] * cosine - up[own] * sine_up - down[own] * sine_down)
-        return jnp.concatenate(pieces, axis=0).reshape(fs, span, LANES)
+        return jnp.concatenate(pieces, axis=0)
 
     for at in reversed(range(ctx)):
         keys = block * (at + 1)
@@ -1289,11 +1303,12 @@
             delta = jnp.sum(probs * d_probs, axis=-1, keepdims=True)
             d_scores = (probs * (d_probs - delta)).astype(low)
             d_q = jnp.dot(d_scores, k_rows, preferred_element_type=wide_t) * FACTOR
-            stage[at, :, :, lanes] = unturn(d_q, at).astype(low)
+            packed[:, head * HD : (head + 1) * HD] = unturn(d_q, at)[:, :HD]
             d_k[0:keys, :] += inner(d_scores, q_rows) * FACTOR
             d_v[0:keys, :] += inner(probs.astype(low), d_rows)
-        stage[at, :, :, 2 * LANES : 3 * LANES] = unturn(d_k[block * at : keys, :], at).astype(low)
-        stage[at, :, :, 3 * LANES : 4 * LANES] = d_v[block * at : keys, :].astype(low).reshape(fs, span, LANES)
+        packed[:, 2 * HD : 3 * HD] = unturn(d_k[block * at : keys, :], at)[:, :HD]
+        packed[:, 3 * HD : 4 * HD] = d_v[block * at : keys, :HD]
+        stage[at] = packed[...].astype(low).reshape(fs, span, 4 * HD)
         if at == ctx - 1:
             hear_all(sizes)
         for to in range(fs):
@@ -1312,10 +1327,9 @@
             loads[4].wait()
             down_sum[...] = sum_of(down_land).astype(low)
             move(0, down_sum, down_last)
-    for slot in range(fs):
-        push(proj_ref.at[slot], proj_land, proj_send.at[slot], proj_recv, d, slot)
     loads[2].wait()
-    loads[3].wait()
+    for load in wide_loads:
+        load.wait()
 
     ends = jnp.logical_or(c == 0, c == ctx - 1)
 
@@ -1324,7 +1338,7 @@
         for move_ in range(1, fs):
             other = lax.rem(f + move_, fs)
             arrived(mixed.at[other // 2, at, lax.rem(other, 2)], u_recv.at[other, at], here)
-        terms = jnp.dot(mixed[:, at].reshape(both_rows, 4 * LANES), wide[...], preferred_element_type=wide_t)
+        terms = jnp.dot(mixed[:, at].reshape(both_rows, 4 * HD), wide[...], preferred_element_type=wide_t)
         in_sum.give(at, terms.reshape(dp, rows, D))
 
         @pl.when(jnp.logical_and(ends, jnp.logical_and(step > 0, step < ctx - 1)))
@@ -1340,14 +1354,21 @@
     relays = (k_relay, lax.rem(k_relay + 2, fs))
     gain_terms = jnp.zeros((1, D), wide_t)
     for slot in (2, 3, 0, 1):
-        heads = inner(mixed[:, :, :, :, slot * LANES : (slot + 1) * LANES].reshape(every, LANES), normed[...].reshape(every, D))
-        grad_heads[slot] = heads[:HD].astype(low)
-        weights = wide[slot * LANES : slot * LANES + HD, :].astype(wide_t)
-        gain_terms += jnp.sum(heads[:HD] * weights, axis=0, keepdims=True)
+        if slot % 2 == 0:
+            both_heads = inner(
+                mixed[...].reshape(every, 4 * HD)[:, slot * HD : (slot + 2) * HD], normed[...].reshape(every, D)
+            )
+        heads = both_heads[slot % 2 * HD : (slot % 2 + 1) * HD]
+        grad_heads[slot] = heads.astype(low)
+        weights = wide[slot * HD : (slot + 1) * HD, :].astype(wide_t)
+        gain_terms += jnp.sum(heads * weights, axis=0, keepdims=True)
         if slot < 2:
             push(grad_heads.at[slot], q_land, head_send.at[slot], head_recv.at[0], 0, 2 * d + slot)
         else:
             push(grad_heads.at[slot], kv_land.at[slot - 2], head_send.at[slot], head_recv.at[slot - 1], d, relays[slot - 2])
+
+    for slot in range(fs):
+        push(proj_ref.at[slot], proj_land, proj_send.at[slot], proj_recv, d, slot)
 
     gain = gains_ref[0:1, :]
     gain_vec[0:1, :] = gain_terms / gain
@@ -1367,37 +1388,37 @@
 
     lax.fori_loop(1, n, gain_to, 0)
 
+    def middle_step(step, carry):
+        in_sum.step(towards(c, step, ctx))
+        return carry
+
+    lax.fori_loop(jnp.where(ends, ctx - 2, 0), ctx - 1, middle_step, 0)
+
+    def kv_route(slot):
+        owner, owner_f = slot * 2 + c // 2, k_relay
+        return owner, owner_f, jnp.logical_or(jnp.logical_or(d != 1, owner != c), owner_f != f)
+
+    for slot in range(2):
+        owner, owner_f, away = kv_route(slot)
+
+        @pl.when(f == relays[slot])
+        def _():
+            for source in range(fs):
+                arrived(kv_land.at[slot, source], head_recv.at[1 + slot, source], here)
+            kv_sum[slot] = sum_of(kv_land.at[slot]).astype(low)
+
+            @pl.when(away)
+            def _():
+                remote(kv_sum.at[slot], kv_last, move_send.at[2 + slot], move_recv.at[2], at_device(1, owner, owner_f)).start()
+
+            @pl.when(jnp.logical_not(away))
+            def _():
+                pltpu.make_async_copy(kv_sum.at[slot], kv_last, move_recv.at[2]).start()
+
     for source in range(fs):
         arrived(proj_land.at[source], proj_recv.at[source], here)
     proj_sum[...] = sum_of(proj_land).astype(low)
     move(1, proj_sum, proj_last)
-
-    def middle_step(step, carry):
-        in_sum.step(towards(c, step, ctx))
-        return carry
-
-    lax.fori_loop(jnp.where(ends, ctx - 2, 0), ctx - 1, middle_step, 0)
-
-    def kv_route(slot):
-        owner, owner_f = slot * 2 + c // 2, k_relay
-        return owner, owner_f, jnp.logical_or(jnp.logical_or(d != 1, owner != c), owner_f != f)
-
-    for slot in range(2):
-        owner, owner_f, away = kv_route(slot)
-
-        @pl.when(f == relays[slot])
-        def _():
-            for source in range(fs):
-                arrived(kv_land.at[slot, source], head_recv.at[1 + slot, source], here)
-            kv_sum[slot] = sum_of(kv_land.at[slot]).astype(low)
-
-            @pl.when(away)
-            def _():
-                remote(kv_sum.at[slot], kv_last, move_send.at[2 + slot], move_recv.at[2], at_device(1, owner, owner_f)).start()
-
-            @pl.when(jnp.logical_not(away))
-            def _():
-                pltpu.make_async_copy(kv_sum.at[slot], kv_last, move_recv.at[2]).start()
 
     loads[5].wait()
     up_sum[...] = sum_of(up_land)
@@ -1440,6 +1461,7 @@
 
     lax.fori_loop(1, n, gain_left, 0)
 
+    loads[3].wait()
     in_sum.step(c)
 
     values = x_ref[...].astype(wide_t)
@@ -1495,17 +1517,18 @@
         functools.partial(last_kernel, sizes),
         name="last",
         out_shape=shapes,
-        in_specs=[vm_spec] * 7 + [any_spec] * 6,
+        in_specs=[vm_spec] * 6 + [any_spec] * 7,
         out_specs=[vm_spec] * 4 + [any_spec, vm_spec],
         scratch_shapes=[
             VM(unit.shape, low),
             VM(d_unit.shape, low),
             VM((ctx * fs * span, LANES), wide_t),
             VM((ctx * fs * span, LANES), wide_t),
-            VM((ctx, fs, span, 4 * LANES), low),
-            VM((dp, ctx, 2, span, 4 * LANES), low),
+            VM((ctx, fs, span, 4 * HD), low),
+            VM((dp, ctx, 2, span, 4 * HD), low),
+            VM((fs * span, 4 * HD), wide_t),
             VM(normed.shape, low),
-            VM(wide.shape, low),
+            VM((4 * HD, D), low),
             VM((4, HD, D), low),
             VM(up_land.shape, low),
             VM((fs, down_rows, D), low),
@@ -1522,12 +1545,13 @@
             VM((n, 8, LANES), wide_t),
             VM((n, 8, LANES), wide_t),
             VM((D, half), wide_t),
+            VM((rows, D), wide_t),
             dma((6,)), dma((fs,)), dma((fs,)),
             dma((4,)), dma((3, fs)), dma((4,)), dma((3,)),
-            dma((ctx, fs)), dma((fs, ctx)), dma((n,)), dma((n,)), dma,
+            dma((ctx, fs)), dma((fs, ctx)), dma((n,)), dma((n,)), dma, dma((4,)),
         ] + LineSum.scratch(ctx, rows),
         compiler_params=pltpu.CompilerParams(collective_id=3, has_side_effects=True, vmem_limit_bytes=63 * 1024 * 1024),
-    )(x, gains, *tables, d_resid, gain_two, grad_proj, unit, d_unit, normed, wide, up_land, down_land)
+    )(x, gains, *tables, gain_two, grad_proj, d_resid, unit, d_unit, normed, wide, up_land, down_land)
 
 
 def emit_kernel(count, gains_ref, *refs):
@@ -1570,7 +1594,7 @@
     dy = cotangent.reshape(rows, D)
     each = attn_gain.shape[0]
     block_out, d_resid, grad_two, *tables, normed, unit, qkv, gains, d_unit, grad_proj, up_land, down_land = front(
-        where, 4, x, attn_gain, mlp_gain, w_qkv.T, dy, w_out, w_down, w_gate_up
+        where, 8, x, attn_gain, mlp_gain, w_qkv.T, dy, w_out, w_down, w_gate_up
     )
     grad_tokens, gain_grads, grad_qkv, grad_out, grad_gate_up, grad_down = last(
         where, x, gains, tables, d_resid, grad_two, grad_proj, unit, d_unit, normed, qkv, up_land, down_land

time: 260 us -> 257 us (0.988); the launches traced: 260 us -> 254 us
  Pallas kernels: 259 us -> 253 us
    pallas_call x1, Pallas kernels: 58.2 us -> 54.3 us  [last(): pl.pallas_call(functools.partial(last_kernel, sizes), name='last', out_sh...]
where the time goes in v9:
time: 257 us; the launch traced here: 254 us
  Pallas kernels  253 us (98%)
    pallas_call x1, Pallas kernels, front(): pl.pallas_call(functools.partial(front_kernel, sizes, hidden, parts), nam...  194 us
    pallas_call x1, Pallas kernels, last(): pl.pallas_call(functools.partial(last_kernel, sizes), name='last', out_sh...  54.3 us

profile of v9, /device:TPU:13, one launch (start us, length us, event | category | flops | bytes accessed | tf_op | source)
XLA Modules:
  0.0 254.1 jit_solution(17951624277768085839)
XLA Ops:
  0.6 194.2 %front.1 = (bf16[128,1536]{1,0:T(8,128)(2,1)}, f32[128,1536]{1,0:T(8,128)}, f32[8,1536]{1,0:T(8,128)}, f32[2,16,128]{2,1,0:T(8,128)}, f32[2,64,128]{2,1,0:T(8,12...) custom-call(bf16[128,1536]{1,0:T(8,128)(2,1)} %bitcast.10, ...), custom_call_target="tpu_custom_call" | custom-call | tf_op jit(solution)/shard_map/front/pallas_call | solution.py:1130
  194.8 54.3 %last.1 = (bf16[128,1536]{1,0:T(8,128)(2,1)}, f32[8,128]{1,0:T(8,128)}, f32[96,1536]{1,0:T(8,128)}, f32[48,1536]{1,0:T(8,128)}, f32[1536,256]{1,0:T(8,128)}, /*index=5*/f32[128,1536]{1,0:T(8,128)}) custom-call(bf16[128,1536]{1,0:T(8,128)(2,1)} %bitcast.11, f32[8,1536]{1,0:T(8,128)} %get-tuple-element.35.gains_ref, ...), custom_call_target="tpu_custom_call" | custom-call | tf_op jit(solution)/shard_map/last/pallas_call | solution.py:1516
  249.1 4.8 %emit.1 = (bf16[128,1536]{1,0:T(8,128)(2,1)}, bf16[128,1536]{1,0:T(8,128)(2,1)}, f32[96,1536]{1,0:T(8,128)}, f32[48,1536]{1,0:T(8,128)}, f32[1536,256]{1,0:T(8,1...) custom-call(f32[8,128]{1,0:T(8,128)} %get-tuple-element.47.gains_ref, ...), custom_call_target="tpu_custom_call" | custom-call | tf_op jit(solution)/shard_map/emit/pallas_call | solution.py:1578

commit v10 on v9

--- a/solution.py
+++ b/solution.py
@@ -1131,7 +1131,7 @@
         functools.partial(front_kernel, sizes, hidden, parts),
         name="front",
         out_shape=shapes,
-        in_specs=[vm_spec] * 3 + [any_spec] + [vm_spec] * 4,
+        in_specs=[vm_spec] * 3 + [any_spec, vm_spec] + [any_spec] * 3,
         out_specs=[vm_spec, any_spec] + [vm_spec] * 3 + [any_spec] * 8,
         scratch_shapes=[
             VM((dp, ctx, rows, D), low),
@@ -1517,7 +1517,7 @@
         functools.partial(last_kernel, sizes),
         name="last",
         out_shape=shapes,
-        in_specs=[vm_spec] * 6 + [any_spec] * 7,
+        in_specs=[vm_spec] * 5 + [any_spec] * 8,
         out_specs=[vm_spec] * 4 + [any_spec, vm_spec],
         scratch_shapes=[
             VM(unit.shape, low),
@@ -1554,11 +1554,20 @@
     )(x, gains, *tables, gain_two, grad_proj, d_resid, unit, d_unit, normed, wide, up_land, down_land)
 
 
+PIECES = 4
+
+
 def emit_kernel(count, gains_ref, *refs):
     sources, outs, one_ref, two_ref = refs[:count], refs[count : 2 * count], refs[2 * count], refs[2 * count + 1]
     held, in_sem, out_sem = refs[2 * count + 2 : 3 * count + 2], refs[-2], refs[-1]
-    loads = [pltpu.make_async_copy(sources[i], held[i], in_sem.at[i]) for i in range(count)]
-    stores = [pltpu.make_async_copy(held[i], outs[i], out_sem.at[i]) for i in range(count)]
+    loads, stores = [], []
+    for index in range(count):
+        rows = held[index].shape[0]
+        pieces = PIECES if rows % (PIECES * 16) == 0 else 1
+        for piece in range(pieces):
+            own = slice(piece * rows // pieces, (piece + 1) * rows // pieces)
+            loads.append(pltpu.make_async_copy(sources[index].at[own], held[index].at[own], in_sem.at[len(loads)]))
+            stores.append(pltpu.make_async_copy(held[index].at[own], outs[index].at[own], out_sem.at[len(stores)]))
     for load in loads:
         load.start()
     each = one_ref.shape[0]
@@ -1581,7 +1590,7 @@
         out_shape=[jax.ShapeDtypeStruct(a.shape, a.dtype) for a in arrays] + [gain, gain],
         in_specs=[vm_spec] + [any_spec] * count,
         out_specs=[any_spec] * count + [vm_spec] * 2,
-        scratch_shapes=[VM(a.shape, a.dtype) for a in arrays] + [pltpu.SemaphoreType.DMA((count,))] * 2,
+        scratch_shapes=[VM(a.shape, a.dtype) for a in arrays] + [pltpu.SemaphoreType.DMA((count * PIECES,))] * 2,
         compiler_params=pltpu.CompilerParams(vmem_limit_bytes=63 * 1024 * 1024),
     )(gains, *arrays)
 

time: 257 us -> 256 us (level)
  no operation moved by 1% of the time
where the time goes in v10:
time: 256 us; the launch traced here: 254 us
  Pallas kernels  253 us (99%)
    pallas_call x1, Pallas kernels, front(): pl.pallas_call(functools.partial(front_kernel, sizes, hidden, parts), nam...  194 us
    pallas_call x1, Pallas kernels, last(): pl.pallas_call(functools.partial(last_kernel, sizes), name='last', out_sh...  53.9 us
    pallas_call x1, Pallas kernels, emit(): pl.pallas_call(functools.partial(emit_kernel, count), name='emit', out_sh...  5.17 us

profile of v10, /device:TPU:13, one launch (start us, length us, event | category | flops | bytes accessed | tf_op | source)
XLA Modules:
  0.0 253.8 jit_solution(10857140537342000609)
XLA Ops:
  0.6 193.9 %front.1 = (bf16[128,1536]{1,0:T(8,128)(2,1)}, f32[128,1536]{1,0:T(8,128)}, f32[8,1536]{1,0:T(8,128)}, f32[2,16,128]{2,1,0:T(8,128)}, f32[2,64,128]{2,1,0:T(8,12...) custom-call(bf16[128,1536]{1,0:T(8,128)(2,1)} %bitcast.10, ...), custom_call_target="tpu_custom_call" | custom-call | tf_op jit(solution)/shard_map/front/pallas_call | solution.py:1130
  194.6 53.9 %last.1 = (bf16[128,1536]{1,0:T(8,128)(2,1)}, f32[8,128]{1,0:T(8,128)}, f32[96,1536]{1,0:T(8,128)}, f32[48,1536]{1,0:T(8,128)}, f32[1536,256]{1,0:T(8,128)}, /*index=5*/f32[128,1536]{1,0:T(8,128)}) custom-call(bf16[128,1536]{1,0:T(8,128)(2,1)} %bitcast.11, f32[8,1536]{1,0:T(8,128)} %get-tuple-element.35.gains_ref, ...), custom_call_target="tpu_custom_call" | custom-call | tf_op jit(solution)/shard_map/last/pallas_call | solution.py:1516
  248.5 5.2 %emit.1 = (bf16[128,1536]{1,0:T(8,128)(2,1)}, bf16[128,1536]{1,0:T(8,128)(2,1)}, f32[96,1536]{1,0:T(8,128)}, f32[48,1536]{1,0:T(8,128)}, f32[1536,256]{1,0:T(8,1...) custom-call(f32[8,128]{1,0:T(8,128)} %get-tuple-element.47.gains_ref, ...), custom_call_target="tpu_custom_call" | custom-call | tf_op jit(solution)/shard_map/emit/pallas_call | solution.py:1587

commit v11 on v10

--- a/solution.py
+++ b/solution.py
@@ -1462,18 +1462,18 @@
     lax.fori_loop(1, n, gain_left, 0)
 
     loads[3].wait()
-    in_sum.step(c)
-
+    arrived(down_last, move_recv.at[0], here)
+    down_out[...] = down_last[...].astype(wide_t)
     values = x_ref[...].astype(wide_t)
     scale = lax.rsqrt(jnp.mean(values * values, axis=-1, keepdims=True) + EPS)
+    in_sum.step(c)
+
     incoming = in_sum.total[...]
     weighted = incoming * gain
     mean = jnp.mean(weighted * values, axis=-1, keepdims=True)
     d_x_ref[...] = (d_resid_ref[...] + scale * weighted - values * (scale * scale * scale) * mean).astype(low)
 
-    for index, dst in enumerate((down_last, proj_last)):
-        arrived(dst, move_recv.at[index], here)
-    down_out[...] = down_last[...].astype(wide_t)
+    arrived(proj_last, move_recv.at[1], here)
     proj_out[...] = proj_last[...].astype(wide_t)
 
     @pl.when(d == 1)

time: 256 us -> 256 us (level)
  no operation moved by 1% of the time
where the time goes in v11:
time: 256 us; the launch traced here: 254 us
  Pallas kernels  253 us (99%)
    pallas_call x1, Pallas kernels, front(): pl.pallas_call(functools.partial(front_kernel, sizes, hidden, parts), nam...  194 us
    pallas_call x1, Pallas kernels, last(): pl.pallas_call(functools.partial(last_kernel, sizes), name='last', out_sh...  53.9 us
    pallas_call x1, Pallas kernels, emit(): pl.pallas_call(functools.partial(emit_kernel, count), name='emit', out_sh...  5.17 us

profile of v11, /device:TPU:13, one launch (start us, length us, event | category | flops | bytes accessed | tf_op | source)
XLA Modules:
  0.0 253.8 jit_solution(5020474141371729935)
XLA Ops:
  0.6 193.9 %front.1 = (bf16[128,1536]{1,0:T(8,128)(2,1)}, f32[128,1536]{1,0:T(8,128)}, f32[8,1536]{1,0:T(8,128)}, f32[2,16,128]{2,1,0:T(8,128)}, f32[2,64,128]{2,1,0:T(8,12...) custom-call(bf16[128,1536]{1,0:T(8,128)(2,1)} %bitcast.10, ...), custom_call_target="tpu_custom_call" | custom-call | tf_op jit(solution)/shard_map/front/pallas_call | solution.py:1130
  194.6 53.9 %last.1 = (bf16[128,1536]{1,0:T(8,128)(2,1)}, f32[8,128]{1,0:T(8,128)}, f32[96,1536]{1,0:T(8,128)}, f32[48,1536]{1,0:T(8,128)}, f32[1536,256]{1,0:T(8,128)}, /*index=5*/f32[128,1536]{1,0:T(8,128)}) custom-call(bf16[128,1536]{1,0:T(8,128)(2,1)} %bitcast.11, f32[8,1536]{1,0:T(8,128)} %get-tuple-element.35.gains_ref, ...), custom_call_target="tpu_custom_call" | custom-call | tf_op jit(solution)/shard_map/last/pallas_call | solution.py:1516
  248.5 5.2 %emit.1 = (bf16[128,1536]{1,0:T(8,128)(2,1)}, bf16[128,1536]{1,0:T(8,128)(2,1)}, f32[96,1536]{1,0:T(8,128)}, f32[48,1536]{1,0:T(8,128)}, f32[1536,256]{1,0:T(8,1...) custom-call(f32[8,128]{1,0:T(8,128)} %get-tuple-element.47.gains_ref, ...), custom_call_target="tpu_custom_call" | custom-call | tf_op jit(solution)/shard_map/emit/pallas_call | solution.py:1587
